TPU v7x, 32 devices: a whole 2x2x4 slice. The times are simulated.
32 devices in a mesh: dp: 4 (over z), ctx: 8 (over y, x, core).
Axes of the slice: x: 2, y: 2, z: 4, core: 2. Of those that a mesh axis runs over, the one named last changes fastest.
Arguments:
- layer_input: bfloat16 [4, 2048, 2048], P('dp', 'ctx'), may hold values from -6 to 6
- doc_ids: int32 [4, 2048], P('dp', 'ctx'), may hold values from 0 to 3, never falling along the last dimension, each value on 1 to 1024 neighbouring positions
- route_ids: int32 [4, 2048, 8], P('dp', 'ctx'), may hold values from 0 to 15, all different within a row; in each aligned block of 256 rows (0 to 255, 256 to 511, ..., all dimensions but the last counted through in order) at most 144 rows name the same one
- route_probs: float32 [4, 2048, 8], P('dp', 'ctx'), may hold values from 0.04 to 0.4
- attn_gain: bfloat16 [2048], P(('dp', 'ctx')), may hold values from 0.5 to 1.5
- ffn_gain: bfloat16 [2048], P(('dp', 'ctx')), may hold values from 0.5 to 1.5
- query_gain: bfloat16 [128], P(('dp', 'ctx')), may hold values from 0.5 to 1.5
- key_gain: bfloat16 [128], P(('dp', 'ctx')), may hold values from 0.5 to 1.5
- w_query: bfloat16 [2048, 4096], P(('dp', 'ctx')), may hold values from -0.125 to 0.125
- w_key: bfloat16 [2048, 512], P(('dp', 'ctx')), may hold values from -0.125 to 0.125
- w_value: bfloat16 [2048, 512], P(('dp', 'ctx')), may hold values from -0.125 to 0.125
- w_out: bfloat16 [4096, 2048], P(('dp', 'ctx')), may hold values from -1 to 1
- w_gate: bfloat16 [16, 2048, 768], P('ctx', 'dp'), may hold values from -0.125 to 0.125
- w_up: bfloat16 [16, 2048, 768], P('ctx', 'dp'), may hold values from -0.125 to 0.125
- w_down: bfloat16 [16, 768, 2048], P('ctx', None, 'dp'), may hold values from -0.875 to 0.875
- out_grad: bfloat16 [4, 2048, 2048], P('dp', 'ctx'), may hold values from -6 to 6
Outputs:
- layer_output: bfloat16 [4, 2048, 2048], P('dp', 'ctx')
- input_grad: float32 [4, 2048, 2048], P('dp', 'ctx')
- attn_gain_grad: float32 [2048], P(('dp', 'ctx'))
- ffn_gain_grad: float32 [2048], P(('dp', 'ctx'))
- query_gain_grad: float32 [128], P(('dp', 'ctx'))
- key_gain_grad: float32 [128], P(('dp', 'ctx'))
- w_query_grad: float32 [2048, 4096], P(('dp', 'ctx'))
- w_key_grad: float32 [2048, 512], P(('dp', 'ctx'))
- w_value_grad: float32 [2048, 512], P(('dp', 'ctx'))
- w_out_grad: float32 [4096, 2048], P(('dp', 'ctx'))
- w_gate_grad: float32 [16, 2048, 768], P('ctx', 'dp')
- w_up_grad: float32 [16, 2048, 768], P('ctx', 'dp')
- w_down_grad: float32 [16, 768, 2048], P('ctx', None, 'dp')
Inputs may be any that keep to these rules, and one draw needn't show every extreme that they name: `doc_ids`: in each sequence the document numbers never fall; each document has 1 to 1024 tokens, some exactly 1024. `route_ids`: each token names 8 different experts; among the tokens of one device no expert is named more than 144 times, and in every draw some expert exactly 144 times.
All inputs are finite; a program needn't handle non-finite values.
Results may differ from a plain program's by a relative error of at most 0.017.
Values may be sent and summed in bfloat16 or wider, within the bound.
A program may use at most 384 MiB of HBM per device.

v0:
```python
import math

import jax
import jax.numpy as jnp
from jax import lax
from jax.sharding import PartitionSpec as P

HQ = 32
KV = 4
HD = 128
TOP = 8
MOST = 1024
HOPS = 4


EPS = 1e-06
ROPE_BASE = 1000000.0


def entering(part, axis, combine, identity):
    place = lax.axis_index(axis)
    gathered = lax.all_gather(part, axis)
    state = jnp.zeros_like(part) + jnp.asarray(identity, part.dtype)

    def one(hop, state):
        return combine(state, lax.dynamic_index_in_dim(gathered, hop, 0, False))

    return lax.fori_loop(0, place, one, state)


def shifted(block, axis, distance):
    devices = range(lax.axis_size(axis))
    route = [(i - distance, i) for i in devices if i - distance in devices]
    return lax.ppermute(block, axis, route)


def rms_scale(values, gain):
    return values * lax.rsqrt(jnp.mean(values * values, axis=-1, keepdims=True) + EPS) * gain


def rotate_heads(values, cosine, sine):
    half_width = values.shape[-1] // 2
    first_half = values[..., :half_width]
    second_half = values[..., half_width:]
    cos_b = cosine[:, None, :]
    sin_b = sine[:, None, :]
    return jnp.concatenate(
        [first_half * cos_b - second_half * sin_b, second_half * cos_b + first_half * sin_b],
        axis=-1,
    )


def swiglu(gate_lin, up_lin):
    return jax.nn.silu(gate_lin) * up_lin


def per_device(
    layer_input,
    doc_ids,
    route_ids,
    route_probs,
    attn_gain,
    ffn_gain,
    query_gain,
    key_gain,
    w_query,
    w_key,
    w_value,
    w_out,
    w_gate,
    w_up,
    w_down,
    out_grad,
):
    tokens = layer_input.shape[1]
    width = layer_input.shape[2]
    n_ctx = lax.axis_size("ctx")
    ctx_index = lax.axis_index("ctx")
    per_group = HQ // KV
    score_scale = 1.0 / math.sqrt(HD)
    inputs_full = layer_input.reshape(tokens, width).astype(jnp.float32)
    doc_local = doc_ids.reshape(tokens)
    route_local = route_ids.reshape(tokens * TOP)
    prob_local = route_probs.reshape(tokens, TOP)
    top_grad = out_grad.reshape(tokens, width).astype(jnp.float32)
    full_query, full_key, full_value, full_out, gain_attn, gain_ffn, gain_query, gain_key = (
        lax.all_gather(w_query, ("dp", "ctx"), axis=0, tiled=True),
        lax.all_gather(w_key, ("dp", "ctx"), axis=0, tiled=True),
        lax.all_gather(w_value, ("dp", "ctx"), axis=0, tiled=True),
        lax.all_gather(w_out, ("dp", "ctx"), axis=0, tiled=True),
        lax.all_gather(attn_gain, ("dp", "ctx"), axis=0, tiled=True),
        lax.all_gather(ffn_gain, ("dp", "ctx"), axis=0, tiled=True),
        lax.all_gather(query_gain, ("dp", "ctx"), axis=0, tiled=True),
        lax.all_gather(key_gain, ("dp", "ctx"), axis=0, tiled=True),
    )
    full_gate, full_up, full_down = (
        lax.all_gather(w_gate, "dp", axis=1, tiled=True),
        lax.all_gather(w_up, "dp", axis=1, tiled=True),
        lax.all_gather(w_down, "dp", axis=2, tiled=True),
    )
    normed, norm_pull = jax.vjp(rms_scale, inputs_full, gain_attn.astype(jnp.float32))
    normed_low = normed.astype(jnp.bfloat16)
    query_lin = jnp.dot(normed_low, full_query, preferred_element_type=jnp.float32)
    key_lin = jnp.dot(normed_low, full_key, preferred_element_type=jnp.float32)
    value_lin = jnp.dot(normed_low, full_value, preferred_element_type=jnp.float32)
    token_range = jnp.arange(tokens, dtype=jnp.int32)
    query_pos = ctx_index * tokens + token_range
    inverse = 1.0 / ROPE_BASE ** (jnp.arange(HD // 2, dtype=jnp.float32) * 2.0 / HD)
    angles = query_pos.astype(jnp.float32)[:, None] * inverse[None, :]
    cosine = jnp.cos(angles)
    sine = jnp.sin(angles)

    def head_post(query_in, key_in, query_scale, key_scale):
        query_heads = rotate_heads(
            rms_scale(query_in.reshape(tokens, HQ, HD), query_scale), cosine, sine
        )
        key_heads = rotate_heads(rms_scale(key_in.reshape(tokens, KV, HD), key_scale), cosine, sine)
        return (query_heads, key_heads)

    (query_rot, key_rot), post_pull = jax.vjp(
        head_post, query_lin, key_lin, gain_query.astype(jnp.float32), gain_key.astype(jnp.float32)
    )
    query_low = query_rot.astype(jnp.bfloat16).reshape(tokens, KV, per_group, HD)
    key_low = key_rot.astype(jnp.bfloat16)
    value_low = value_lin.astype(jnp.bfloat16).reshape(tokens, KV, HD)
    doc_count = 2 * tokens * n_ctx // MOST
    doc_range = jnp.arange(doc_count, dtype=jnp.int32)
    doc_match = doc_local[:, None] == doc_range[None, :]
    local_counts = jnp.sum(doc_match.astype(jnp.int32), axis=0)
    lower_counts = entering(
        local_counts,
        "ctx",
        lambda earlier, later: earlier + later,
        jnp.zeros((doc_count,), jnp.int32),
    )
    through_here = lower_counts + local_counts
    doc_begin = jnp.cumsum(through_here) - through_here
    query_start = jnp.sum(jnp.where(doc_match, doc_begin[None, :], 0), axis=1)
    moving = jnp.stack([key_low, value_low])
    key_parts = [key_low]
    value_parts = [value_low]
    for hop_index in range(HOPS):
        moving = shifted(moving, "ctx", 1)
        key_parts.append(moving[0])
        value_parts.append(moving[1])
    key_all = jnp.concatenate(key_parts, axis=0)
    value_all = jnp.concatenate(value_parts, axis=0)
    hop_range = jnp.arange(HOPS + 1, dtype=jnp.int32)
    source_dev = ctx_index - hop_range
    key_pos = (source_dev[:, None] * tokens + token_range[None, :]).reshape(-1)
    key_live = jnp.repeat(source_dev >= 0, tokens)
    allowed = (
        key_live[None, :]
        & (key_pos[None, :] <= query_pos[:, None])
        & (key_pos[None, :] >= query_start[:, None])
    )

    def exp_scores(head_group):
        scores = (
            jnp.einsum(
                "tjd,sd->jts",
                query_low[:, head_group],
                key_all[:, head_group],
                preferred_element_type=jnp.float32,
            )
            * score_scale
        )
        return jnp.where(allowed[None], jnp.exp(scores), 0.0)

    attn_parts = []
    row_totals = []
    for head_group in range(KV):
        exp_part = exp_scores(head_group)
        row_total = jnp.sum(exp_part, axis=-1)
        summed = jnp.einsum(
            "jts,sd->tjd",
            exp_part.astype(jnp.bfloat16),
            value_all[:, head_group],
            preferred_element_type=jnp.float32,
        )
        attn_parts.append(summed / jnp.transpose(row_total)[:, :, None])
        row_totals.append(row_total)
    attn_full = jnp.stack(attn_parts, axis=1)
    attn_low = attn_full.reshape(tokens, HQ * HD).astype(jnp.bfloat16)
    after_attn = inputs_full + jnp.dot(attn_low, full_out, preferred_element_type=jnp.float32)
    normed2, norm2_pull = jax.vjp(rms_scale, after_attn, gain_ffn.astype(jnp.float32))
    normed2_low = normed2.astype(jnp.bfloat16)
    experts_dev = w_gate.shape[0]
    n_experts = experts_dev * n_ctx
    capacity = 9 * tokens * TOP // (8 * n_experts)
    onehot = (route_local[:, None] == jnp.arange(n_experts, dtype=jnp.int32)[None, :]).astype(
        jnp.int32
    )
    slot_rank = jnp.sum((jnp.cumsum(onehot, axis=0) - onehot) * onehot, axis=1)
    slot_index = route_local * capacity + slot_rank
    send_rows = (
        jnp.zeros((n_experts * capacity, width), jnp.bfloat16)
        .at[slot_index]
        .set(jnp.repeat(normed2_low, TOP, axis=0))
    )
    arrived = lax.all_to_all(
        send_rows.reshape(n_ctx, experts_dev, capacity, width),
        "ctx",
        split_axis=0,
        concat_axis=2,
        tiled=True,
    )
    arrived = arrived.reshape(experts_dev, n_ctx * capacity, width)
    gate_lin = jnp.einsum("erd,edf->erf", arrived, full_gate, preferred_element_type=jnp.float32)
    up_lin = jnp.einsum("erd,edf->erf", arrived, full_up, preferred_element_type=jnp.float32)
    act_full, act_pull = jax.vjp(swiglu, gate_lin, up_lin)
    act_low = act_full.astype(jnp.bfloat16)
    expert_out = jnp.einsum(
        "erf,efd->erd", act_low, full_down, preferred_element_type=jnp.float32
    ).astype(jnp.bfloat16)
    returned = lax.all_to_all(
        expert_out.reshape(1, experts_dev, n_ctx * capacity, width),
        "ctx",
        split_axis=2,
        concat_axis=0,
        tiled=True,
    )
    back_rows = returned.reshape(n_experts * capacity, width)[slot_index].reshape(
        tokens, TOP, width
    )
    moe_out = jnp.sum(back_rows.astype(jnp.float32) * prob_local[:, :, None], axis=1)
    layer_output = (after_attn + moe_out).astype(jnp.bfloat16)
    full_gate, full_up, full_down = (
        lax.all_gather(w_gate, "dp", axis=1, tiled=True),
        lax.all_gather(w_up, "dp", axis=1, tiled=True),
        lax.all_gather(w_down, "dp", axis=2, tiled=True),
    )
    full_query, full_key, full_value, full_out = (
        lax.all_gather(w_query, ("dp", "ctx"), axis=0, tiled=True),
        lax.all_gather(w_key, ("dp", "ctx"), axis=0, tiled=True),
        lax.all_gather(w_value, ("dp", "ctx"), axis=0, tiled=True),
        lax.all_gather(w_out, ("dp", "ctx"), axis=0, tiled=True),
    )
    route_grad = (
        (top_grad[:, None, :] * prob_local[:, :, None])
        .astype(jnp.bfloat16)
        .reshape(tokens * TOP, width)
    )
    grad_send = (
        jnp.zeros((n_experts * capacity, width), jnp.bfloat16).at[slot_index].set(route_grad)
    )
    grad_arrived = lax.all_to_all(
        grad_send.reshape(n_ctx, experts_dev, capacity, width),
        "ctx",
        split_axis=0,
        concat_axis=2,
        tiled=True,
    )
    grad_arrived = grad_arrived.reshape(experts_dev, n_ctx * capacity, width)
    act_grad = jnp.einsum(
        "erd,efd->erf", grad_arrived, full_down, preferred_element_type=jnp.float32
    )
    down_grad = jnp.einsum(
        "erf,erd->efd", act_low, grad_arrived, preferred_element_type=jnp.float32
    )
    gate_grad_full, up_grad_full = act_pull(act_grad)
    gate_grad_low = gate_grad_full.astype(jnp.bfloat16)
    up_grad_low = up_grad_full.astype(jnp.bfloat16)
    gate_wgrad = jnp.einsum(
        "erd,erf->edf", arrived, gate_grad_low, preferred_element_type=jnp.float32
    )
    up_wgrad = jnp.einsum("erd,erf->edf", arrived, up_grad_low, preferred_element_type=jnp.float32)
    row_grad = (
        jnp.einsum("erf,edf->erd", gate_grad_low, full_gate, preferred_element_type=jnp.float32)
        + jnp.einsum("erf,edf->erd", up_grad_low, full_up, preferred_element_type=jnp.float32)
    ).astype(jnp.bfloat16)
    row_back = lax.all_to_all(
        row_grad.reshape(1, experts_dev, n_ctx * capacity, width),
        "ctx",
        split_axis=2,
        concat_axis=0,
        tiled=True,
    )
    routed_grad = row_back.reshape(n_experts * capacity, width)[slot_index].reshape(
        tokens, TOP, width
    )
    normed2_grad = jnp.sum(routed_grad.astype(jnp.float32), axis=1)
    mid_norm_grad, ffn_gain_part = norm2_pull(normed2_grad)
    mid_grad = top_grad + mid_norm_grad
    gate_out, up_out, down_out = (
        lax.psum_scatter(
            gate_wgrad.astype(jnp.bfloat16), "dp", scatter_dimension=1, tiled=True
        ).astype(jnp.float32),
        lax.psum_scatter(
            up_wgrad.astype(jnp.bfloat16), "dp", scatter_dimension=1, tiled=True
        ).astype(jnp.float32),
        lax.psum_scatter(
            down_grad.astype(jnp.bfloat16), "dp", scatter_dimension=2, tiled=True
        ).astype(jnp.float32),
    )
    branch_low = mid_grad.astype(jnp.bfloat16)
    out_wgrad = jnp.einsum("tc,td->cd", attn_low, branch_low, preferred_element_type=jnp.float32)
    attn_grad = jnp.einsum("td,cd->tc", branch_low, full_out, preferred_element_type=jnp.float32)
    attn_grad = attn_grad.reshape(tokens, KV, per_group, HD)
    query_grads = []
    key_grads = []
    value_grads = []
    for head_group in range(KV):
        head_grad = attn_grad[:, head_group]
        row_total = row_totals[head_group]
        delta = jnp.sum(head_grad * attn_full[:, head_group], axis=-1)
        summed_grad = (head_grad / jnp.transpose(row_total)[:, :, None]).astype(jnp.bfloat16)
        exp_part = exp_scores(head_group)
        value_prod = jnp.einsum(
            "tjd,sd->jts", summed_grad, value_all[:, head_group], preferred_element_type=jnp.float32
        )
        score_grad = (
            exp_part * value_prod
            - exp_part / row_total[:, :, None] * jnp.transpose(delta)[:, :, None]
        ).astype(jnp.bfloat16)
        query_grads.append(
            score_scale
            * jnp.einsum(
                "jts,sd->tjd",
                score_grad,
                key_all[:, head_group],
                preferred_element_type=jnp.float32,
            )
        )
        key_grads.append(
            score_scale
            * jnp.einsum(
                "jts,tjd->sd",
                score_grad,
                query_low[:, head_group],
                preferred_element_type=jnp.float32,
            )
        )
        value_grads.append(
            jnp.einsum(
                "jts,tjd->sd",
                exp_part.astype(jnp.bfloat16),
                summed_grad,
                preferred_element_type=jnp.float32,
            )
        )
    query_rot_grad = jnp.stack(query_grads, axis=1).reshape(tokens, HQ, HD)
    key_all_grad = jnp.stack(key_grads, axis=1).reshape(HOPS + 1, tokens, KV, HD)
    value_all_grad = jnp.stack(value_grads, axis=1).reshape(HOPS + 1, tokens, KV, HD)
    grad_pieces = jnp.stack([key_all_grad, value_all_grad], axis=1)
    carried = grad_pieces[HOPS]
    for hop_index in range(HOPS - 1, -1, -1):
        carried = (
            shifted(carried.astype(jnp.bfloat16), "ctx", -1).astype(carried.dtype)
            + grad_pieces[hop_index]
        )
    query_lin_grad, key_lin_grad, query_gain_part, key_gain_part = post_pull(
        (query_rot_grad, carried[0])
    )
    query_grad_low = query_lin_grad.astype(jnp.bfloat16)
    key_grad_low = key_lin_grad.astype(jnp.bfloat16)
    value_grad_low = carried[1].reshape(tokens, KV * HD).astype(jnp.bfloat16)
    query_wgrad = jnp.einsum(
        "td,tc->dc", normed_low, query_grad_low, preferred_element_type=jnp.float32
    )
    key_wgrad = jnp.einsum(
        "td,tc->dc", normed_low, key_grad_low, preferred_element_type=jnp.float32
    )
    value_wgrad = jnp.einsum(
        "td,tc->dc", normed_low, value_grad_low, preferred_element_type=jnp.float32
    )
    normed_grad = (
        jnp.einsum("tc,dc->td", query_grad_low, full_query, preferred_element_type=jnp.float32)
        + jnp.einsum("tc,dc->td", key_grad_low, full_key, preferred_element_type=jnp.float32)
        + jnp.einsum("tc,dc->td", value_grad_low, full_value, preferred_element_type=jnp.float32)
    )
    input_norm_grad, attn_gain_part = norm_pull(normed_grad)
    input_grad = mid_grad + input_norm_grad
    (
        query_out,
        key_out,
        value_out,
        out_out,
        attn_gain_out,
        ffn_gain_out,
        query_gain_out,
        key_gain_out,
    ) = (
        lax.psum_scatter(query_wgrad, ("dp", "ctx"), scatter_dimension=0, tiled=True),
        lax.psum_scatter(key_wgrad, ("dp", "ctx"), scatter_dimension=0, tiled=True),
        lax.psum_scatter(value_wgrad, ("dp", "ctx"), scatter_dimension=0, tiled=True),
        lax.psum_scatter(out_wgrad, ("dp", "ctx"), scatter_dimension=0, tiled=True),
        lax.psum_scatter(attn_gain_part, ("dp", "ctx"), scatter_dimension=0, tiled=True),
        lax.psum_scatter(ffn_gain_part, ("dp", "ctx"), scatter_dimension=0, tiled=True),
        lax.psum_scatter(query_gain_part, ("dp", "ctx"), scatter_dimension=0, tiled=True),
        lax.psum_scatter(key_gain_part, ("dp", "ctx"), scatter_dimension=0, tiled=True),
    )
    return (
        layer_output.reshape(1, tokens, width),
        input_grad.reshape(1, tokens, width),
        attn_gain_out,
        ffn_gain_out,
        query_gain_out,
        key_gain_out,
        query_out,
        key_out,
        value_out,
        out_out,
        gate_out,
        up_out,
        down_out,
    )


def solution(mesh):
    in_specs = (
        P("dp", "ctx", None),
        P("dp", "ctx"),
        P("dp", "ctx", None),
        P("dp", "ctx", None),
        P(("dp", "ctx")),
        P(("dp", "ctx")),
        P(("dp", "ctx")),
        P(("dp", "ctx")),
        P(("dp", "ctx"), None),
        P(("dp", "ctx"), None),
        P(("dp", "ctx"), None),
        P(("dp", "ctx"), None),
        P("ctx", "dp", None),
        P("ctx", "dp", None),
        P("ctx", None, "dp"),
        P("dp", "ctx", None),
    )
    out_specs = (
        P("dp", "ctx", None),
        P("dp", "ctx", None),
        P(("dp", "ctx")),
        P(("dp", "ctx")),
        P(("dp", "ctx")),
        P(("dp", "ctx")),
        P(("dp", "ctx"), None),
        P(("dp", "ctx"), None),
        P(("dp", "ctx"), None),
        P(("dp", "ctx"), None),
        P("ctx", "dp", None),
        P("ctx", "dp", None),
        P("ctx", None, "dp"),
    )
    return jax.shard_map(
        per_device, mesh=mesh, in_specs=in_specs, out_specs=out_specs, check_vma=False
    )
```

profile of v0, /device:TPU:14, one launch (start us, length us, event | category | flops | bytes accessed | tf_op | source)
XLA Modules:
  0.0 2270.6 jit_solution(5737399541496214657)
XLA Ops:
  19.2 18.2 scatter_custom_fusion.1
  45.3 108.8 %all-reduce.6 = s32[32]{0:T(128)S(1)} all-reduce(s32[32]{0:T(128)S(1)} %dynamic-update-slice.2), channel_id=2, replica_groups=mesh['dp'=4,'ctx'=8] {'ctx'}, use_global_device_ids=true, to_apply=%add.6 | all-reduce | flops 32 | bytes 256
  155.5 42.8 %all-reduce.14 = (bf16[2048]{0:T(1024)(128)(2,1)S(1)}, bf16[128]{0:T(256)(128)(2,1)}, bf16[128]{0:T(256)(128)(2,1)S(1)}, bf16[2048]{0:T(1024)(128)(2,1)}) all-reduce(bf16[2048]{0:T(1024)(128)(2,1)S(1)} %dynamic-update-slice, bf16[128]{0:T(256)(128)(2,1)S(1)} %dynamic-update-slice.3, ...), channel_id=1, replica_groups=mesh['dp'=4,'ctx'=8] {'dp','ctx'}, use_global_device_ids=true, to_apply=%add.4 | all-reduce | flops 4352 | bytes 17408
  208.9 13.3 collective-permute-done
  237.6 16.6 collective-permute-done.2
  259.0 17.1 collective-permute-done.3
  277.0 20.9 all-gather.13.cloned.1.call-done
  297.9 22.5 copy.161
  320.4 8.7 multiply_reduce_fusion.2
  359.6 19.0 fusion.22
  398.7 14.5 all-gather.15.cloned.1.call-done
  413.2 8.3 multiply_reduce_fusion.5
  423.0 17.9 scatter_custom_fusion
  448.1 9.4 copy.180
  457.5 92.9 %all-to-all-done = bf16[8,2,144,2048]{3,2,1,0:T(8,128)(2,1)} async-done(((bf16[8,2,144,2048]{3,2,1,0:T(8,128)(2,1)}), bf16[8,2,144,2048]{3,2,1,0:T(8,128)(2,1)}, u32[]{:S(2)}, u32[]{:S(2)}) %all-to-all-start) | async-done | bytes 9437216 | tf_op jit(solution)/shard_map/all_to_all | solution.py:201
  550.4 9.2 copy.175
  559.6 13.8 fusion.199
  573.4 68.7 %all-gather.17.cloned.1.call-done = bf16[2,2048,768]{2,1,0:T(8,128)(2,1)} async-done(((bf16[2,512,768]{2,1,0:T(8,128)(2,1)}), bf16[2,2048,768]{2,1,0:T(8,128)(2,1)}) %all-gather.17.cloned.1.call-update) | async-done | bytes 6291472 | tf_op jit(solution)/shard_map/all_gather | solution.py:97
  642.1 13.7 fusion.198
  655.8 101.4 %all-gather.21.cloned.1.call-done = bf16[2,768,2048]{2,1,0:T(8,128)(2,1)} async-done(((bf16[2,768,512]{2,1,0:T(8,128)(2,1)}), bf16[2,768,2048]{2,1,0:T(8,128)(2,1)}) %all-gather.21.cloned.1.call-update) | async-done | bytes 6291472 | tf_op jit(solution)/shard_map/all_gather | solution.py:99
  757.2 18.2 multiply_convert_fusion
  775.5 14.1 convolution_convert_fusion.1
  789.6 10.7 fusion.10
  800.2 27.9 %copy.176 = bf16[1,2,1152,2048]{3,1,0,2:T(2,128)(2,1)} copy(bf16[1,2,1152,2048]{3,2,1,0:T(8,128)(2,1)S(1)} %fusion.10) | data formatting | bytes 18874368 | tf_op jit(solution)/shard_map/reshape | solution.py:217
  833.7 13.0 convolution_convert_fusion.2
  846.8 14.5 fusion.200
  861.2 16.2 fusion.11
  877.4 18.2 copy.181
  895.7 41.0 %all-to-all-done.1 = bf16[1,2,1152,2048]{3,1,0,2:T(2,128)(2,1)} async-done(((bf16[1,2,1152,2048]{3,1,0,2:T(2,128)(2,1)}), bf16[1,2,1152,2048]{3,1,0,2:T(2,128)(2,1)}, u32[]{:S(2)}, u32[]{:S(2)}) %all-to-all-start.1) | async-done | bytes 9437216 | tf_op jit(solution)/shard_map/all_to_all | solution.py:216
  946.1 23.8 %select_convert_fusion.3 = (bf16[1280,256,8]{1,0,2:T(8,128)(2,1)}, bf16[1280,256,8]{1,0,2:T(8,128)(2,1)}, bf16[1280,256,8]{1,0,2:T(8,128)(2,1)}, bf16[1280,256,8]{1,0,2:T(8,128)(2,1)}) fusion(f32[1280,256,8]{1,0,2:T(8,128)} %get-tuple-element.100, pred[1280,256]{1,0:T(8,128)(4,1)S(1)} %compare_and_fusion, f32[1280,256,8]{1,0,2:T(8,128)} %fusion.157, ...), kind=kLoop, calls=%fused_computation.32 | loop fusion | flops 31457280 | bytes 63242240 | tf_op jit(solution)/shard_map/convert_element_type | solution.py:177
  969.9 12.5 convolution_convert_fusion.3
  982.5 11.6 copy.177
  994.1 53.1 %all-to-all-done.3 = bf16[1,2,1152,2048]{3,1,0,2:T(2,128)(2,1)} async-done(((bf16[1,2,1152,2048]{3,1,0,2:T(2,128)(2,1)}), bf16[1,2,1152,2048]{3,1,0,2:T(2,128)(2,1)}, u32[]{:S(2)}, u32[]{:S(2)}) %all-to-all-start.3) | async-done | bytes 9437216 | tf_op jit(solution)/shard_map/all_to_all | solution.py:272
  1047.2 11.8 copy.182
  1059.0 21.2 gather_fusion
  1080.2 21.6 gather_fusion.1
  1101.9 11.6 convert_reduce_fusion
  1116.2 12.7 fusion
  1133.0 9.0 fusion.150
  1165.5 8.0 fusion.5
  1177.0 8.4 fusion.9
  1254.0 15.0 fusion.148
  1288.8 13.6 fusion.111
  1302.5 12.5 fusion.201
  1320.1 47.2 %all-reduce.13 = (f32[2048]{0:T(1024)S(1)}, f32[2048]{0:T(1024)S(1)}, f32[128]{0:T(128)S(1)}, f32[128]{0:T(128)S(1)}) all-reduce(f32[2048]{0:T(1024)S(1)} %get-tuple-element.45, f32[2048]{0:T(1024)S(1)} %copy-done.67, f32[128]{0:T(128)S(1)} %get-tuple-element.37, ...), channel_id=3, replica_groups=mesh['dp'=4,'ctx'=8] {'dp','ctx'}, use_global_device_ids=true, to_apply=%region_29.30.clone | all-reduce | flops 4352 | bytes 34816
  1383.2 123.1 %reduce-scatter.10.cloned.1.call-done = f32[64,512]{1,0:T(8,128)} async-done(((f32[2048,512]{1,0:T(8,128)}), f32[64,512]{1,0:T(8,128)}) %reduce-scatter.10.cloned.1.call-update) | async-done | bytes 131088 | tf_op jit(solution)/shard_map/reduce_scatter | solution.py:385
  1506.3 392.6 %reduce-scatter.14.cloned.1.call-done = f32[128,2048]{1,0:T(8,128)} async-done(((f32[4096,2048]{1,0:T(8,128)}), f32[128,2048]{1,0:T(8,128)}) %reduce-scatter.14.cloned.1.call-update) | async-done | bytes 1048592 | tf_op jit(solution)/shard_map/reduce_scatter | solution.py:387
  1899.0 364.8 %reduce-scatter.8.cloned.1.call-done = f32[64,4096]{1,0:T(8,128)} async-done(((f32[2048,4096]{1,0:T(8,128)}), f32[64,4096]{1,0:T(8,128)}) %reduce-scatter.8.cloned.1.call-update) | async-done | bytes 1048592 | tf_op jit(solution)/shard_map/reduce_scatter | solution.py:384
  (451 shorter events, 268.0 us)
Async XLA Ops:
  7.2 192.1 %all-gather.9.cloned.1.call-start = ((), (), s32[]{:S(2)}) async-start(), calls=%async_computation.11 | async-start | bytes 2162688 | tf_op jit(solution)/shard_map/all_gather | solution.py:89
  7.9 193.8 %all-gather.11.cloned.1.call-start = ((), (), s32[]{:S(2)}) async-start(), calls=%async_computation.12 | async-start | bytes 2162688 | tf_op jit(solution)/shard_map/all_gather | solution.py:88
  8.7 289.2 %all-gather.13.cloned.1.call-start = ((), (), s32[]{:S(2)}) async-start(), calls=%async_computation.13 | async-start | bytes 17301504 | tf_op jit(solution)/shard_map/all_gather | solution.py:87
  9.4 403.8 %all-gather.15.cloned.1.call-start = ((), (), s32[]{:S(2)}) async-start(), calls=%async_computation.14 | async-start | bytes 17301504 | tf_op jit(solution)/shard_map/all_gather | solution.py:90
  10.0 549.6 %all-gather.19.cloned.1.call-start = ((), (), s32[]{:S(2)}) async-start(), calls=%async_computation.16 | async-start | bytes 7864320 | tf_op jit(solution)/shard_map/all_gather | solution.py:98
  37.4 116.7 %copy-start.6 = (bf16[1,256,2048]{2,1,0:T(8,128)(2,1)S(1)}, bf16[1,256,2048]{2,1,0:T(8,128)(2,1)}, u32[]{:S(2)}) copy-start(bf16[1,256,2048]{2,1,0:T(8,128)(2,1)} %param.18) | copy-start | bytes 3145732
  37.4 117.1 %copy-start.90 = (bf16[4]{0:T(256)(128)(2,1)S(1)}, bf16[4]{0:T(256)(128)(2,1)}, u32[]{:S(2)}) copy-start(bf16[4]{0:T(256)(128)(2,1)} %param.24) | copy-start | bytes 28
  37.4 117.4 %copy-start.91 = (bf16[4]{0:T(256)(128)(2,1)S(1)}, bf16[4]{0:T(256)(128)(2,1)}, u32[]{:S(2)}) copy-start(bf16[4]{0:T(256)(128)(2,1)} %param.25) | copy-start | bytes 28
  37.4 117.6 %copy-start.92 = (bf16[64]{0:T(256)(128)(2,1)S(1)}, bf16[64]{0:T(256)(128)(2,1)}, u32[]{:S(2)}) copy-start(bf16[64]{0:T(256)(128)(2,1)} %param.22) | copy-start | bytes 388
  37.4 117.9 %copy-start.93 = (bf16[64]{0:T(256)(128)(2,1)S(1)}, bf16[64]{0:T(256)(128)(2,1)}, u32[]{:S(2)}) copy-start(bf16[64]{0:T(256)(128)(2,1)} %param.23) | copy-start | bytes 388
  37.4 403.5 %all-to-all-start.2 = ((bf16[8,2,144,2048]{3,2,1,0:T(8,128)(2,1)}), bf16[8,2,144,2048]{3,2,1,0:T(8,128)(2,1)}, u32[]{:S(2)}, u32[]{:S(2)}) async-start(bf16[8,2,144,2048]{3,2,1,0:T(8,128)(2,1)} %bitcast.578), calls=%async_computation.2 | async-start | bytes 18874368 | tf_op jit(solution)/shard_map/all_to_all | solution.py:247
  43.1 599.0 %all-gather.17.cloned.1.call-start = ((), (), s32[]{:S(2)}) async-start(), calls=%async_computation.15 | async-start | bytes 7864320 | tf_op jit(solution)/shard_map/all_gather | solution.py:97
  154.4 166.0 %copy-start.60 = (f32[256]{0:T(256)}, f32[256]{0:T(256)S(1)}, u32[]{:S(2)}) copy-start(f32[256]{0:T(256)S(1)} %fusion.174) | copy-start | bytes 3076
  198.9 121.5 %copy-start.50 = (f32[2048]{0:T(1024)}, f32[2048]{0:T(1024)S(1)}, u32[]{:S(2)}) copy-start(f32[2048]{0:T(1024)S(1)} %convert_element_type.271) | copy-start | bytes 24580
  199.2 130.6 %copy-start.46 = (f32[256,64]{0,1:T(8,128)}, f32[256,64]{0,1:T(8,128)S(1)}, u32[]{:S(2)}) copy-start(f32[256,64]{0,1:T(8,128)S(1)} %get-tuple-element.94) | copy-start | bytes 196612
  199.2 130.6 %copy-start.48 = (f32[256,64]{0,1:T(8,128)}, f32[256,64]{0,1:T(8,128)S(1)}, u32[]{:S(2)}) copy-start(f32[256,64]{0,1:T(8,128)S(1)} %get-tuple-element.95) | copy-start | bytes 196612
  206.6 15.5 collective-permute-start
  222.1 10.5 collective-permute-start.1
  224.2 96.2 %copy-start.71 = (pred[1280]{0:T(1024)(128)(4,1)}, pred[1280]{0:T(1024)(128)(4,1)S(1)}, u32[]{:S(2)}) copy-start(pred[1280]{0:T(1024)(128)(4,1)S(1)} %and.30) | copy-start | bytes 3844
  225.7 103.5 %copy-start.85 = (f32[128]{0:T(128)}, f32[128]{0:T(128)S(1)}, u32[]{:S(2)}) copy-start(f32[128]{0:T(128)S(1)} %convert_element_type.280) | copy-start | bytes 1540
  225.7 94.7 %copy-start.63 = (s32[1280]{0:T(1024)}, s32[1280]{0:T(1024)S(1)}, u32[]{:S(2)}) copy-start(s32[1280]{0:T(1024)S(1)} %add.197) | copy-start | bytes 15364
  226.4 195.7 %copy-start.56 = (f32[2048]{0:T(1024)}, f32[2048]{0:T(1024)S(1)}, u32[]{:S(2)}) copy-start(f32[2048]{0:T(1024)S(1)} %convert_element_type.288) | copy-start | bytes 24580
  226.4 94.0 %copy-start.87 = (s32[256]{0:T(256)}, s32[256]{0:T(256)S(1)}, u32[]{:S(2)}) copy-start(s32[256]{0:T(256)S(1)} %iota_add_fusion.1) | copy-start | bytes 3076
  227.2 93.2 %copy-start.77 = (s32[256]{0:T(256)}, s32[256]{0:T(256)S(1)}, u32[]{:S(2)}) copy-start(s32[256]{0:T(256)S(1)} %select_reduce_fusion) | copy-start | bytes 3076
  232.6 21.6 collective-permute-start.2
  254.3 21.8 collective-permute-start.3
  440.9 109.5 %all-to-all-start = ((bf16[8,2,144,2048]{3,2,1,0:T(8,128)(2,1)}), bf16[8,2,144,2048]{3,2,1,0:T(8,128)(2,1)}, u32[]{:S(2)}, u32[]{:S(2)}) async-start(bf16[8,2,144,2048]{3,2,1,0:T(8,128)(2,1)} %bitcast.579), calls=%async_computation | async-start | bytes 18874368 | tf_op jit(solution)/shard_map/all_to_all | solution.py:201
  447.4 309.9 %all-gather.21.cloned.1.call-start = ((), (), s32[]{:S(2)}) async-start(), calls=%async_computation.17 | async-start | bytes 7864320 | tf_op jit(solution)/shard_map/all_gather | solution.py:99
  448.1 925.0 %reduce-scatter.20.cloned.1.call-start = ((), (), s32[]{:S(2)}) async-start(), calls=%async_computation.24 | async-start | bytes 7864320 | tf_op jit(solution)/shard_map/reduce_scatter | solution.py:292
  828.1 108.6 %all-to-all-start.1 = ((bf16[1,2,1152,2048]{3,1,0,2:T(2,128)(2,1)}), bf16[1,2,1152,2048]{3,1,0,2:T(2,128)(2,1)}, u32[]{:S(2)}, u32[]{:S(2)}) async-start(bf16[1,2,1152,2048]{3,1,0,2:T(2,128)(2,1)} %copy.176), calls=%async_computation.1 | async-start | bytes 18874368 | tf_op jit(solution)/shard_map/all_to_all | solution.py:216
  833.7 542.9 %reduce-scatter.18.cloned.1.call-start = ((), (), s32[]{:S(2)}) async-start(), calls=%async_computation.23 | async-start | bytes 7864320 | tf_op jit(solution)/shard_map/reduce_scatter | solution.py:289
  895.7 48.6 %copy-start.70 = (s32[2048,1]{0,1:T(1,128)S(1)}, s32[2048,1]{0,1:T(1,128)}, u32[]{:S(2)}) copy-start(s32[2048,1]{0,1:T(1,128)} %copy-done.69) | copy-start | bytes 24580
  895.7 49.2 %copy-start.64 = (s32[1280]{0:T(1024)S(1)}, s32[1280]{0:T(1024)}, u32[]{:S(2)}) copy-start(s32[1280]{0:T(1024)} %copy-done.63) | copy-start | bytes 15364
  895.7 49.2 %copy-start.72 = (pred[1280]{0:T(1024)(128)(4,1)S(1)}, pred[1280]{0:T(1024)(128)(4,1)}, u32[]{:S(2)}) copy-start(pred[1280]{0:T(1024)(128)(4,1)} %copy-done.71) | copy-start | bytes 3844
  895.7 49.2 %copy-start.78 = (s32[256]{0:T(256)S(1)}, s32[256]{0:T(256)}, u32[]{:S(2)}) copy-start(s32[256]{0:T(256)} %copy-done.77) | copy-start | bytes 3076
  895.7 49.2 %copy-start.88 = (s32[256]{0:T(256)S(1)}, s32[256]{0:T(256)}, u32[]{:S(2)}) copy-start(s32[256]{0:T(256)} %copy-done.87) | copy-start | bytes 3076
  936.7 110.5 %all-to-all-start.3 = ((bf16[1,2,1152,2048]{3,1,0,2:T(2,128)(2,1)}), bf16[1,2,1152,2048]{3,1,0,2:T(2,128)(2,1)}, u32[]{:S(2)}, u32[]{:S(2)}) async-start(bf16[1,2,1152,2048]{3,1,0,2:T(2,128)(2,1)} %copy.181), calls=%async_computation.3 | async-start | bytes 18874368 | tf_op jit(solution)/shard_map/all_to_all | solution.py:272
  944.1 435.8 %reduce-scatter.16.cloned.1.call-start = ((), (), s32[]{:S(2)}) async-start(), calls=%async_computation.22 | async-start | bytes 7864320 | tf_op jit(solution)/shard_map/reduce_scatter | solution.py:286
  982.4 400.8 %reduce-scatter.12.cloned.1.call-start = ((), (), s32[]{:S(2)}) async-start(), calls=%async_computation.20 | async-start | bytes 4325376 | tf_op jit(solution)/shard_map/reduce_scatter | solution.py:386
  1203.6 8.6 collective-permute-start.4
  1212.4 10.6 collective-permute-start.5
  1223.2 10.5 collective-permute-start.6
  1233.9 10.5 collective-permute-start.7
  1248.2 258.1 %reduce-scatter.10.cloned.1.call-start = ((), (), s32[]{:S(2)}) async-start(), calls=%async_computation.19 | async-start | bytes 4325376 | tf_op jit(solution)/shard_map/reduce_scatter | solution.py:385
  1252.4 646.5 %reduce-scatter.14.cloned.1.call-start = ((), (), s32[]{:S(2)}) async-start(), calls=%async_computation.21 | async-start | bytes 34603008 | tf_op jit(solution)/shard_map/reduce_scatter | solution.py:387
  1269.0 994.8 %reduce-scatter.8.cloned.1.call-start = ((), (), s32[]{:S(2)}) async-start(), calls=%async_computation.18 | async-start | bytes 34603008 | tf_op jit(solution)/shard_map/reduce_scatter | solution.py:384
  1317.6 52.0 %copy-start.80 = (f32[256]{0:T(256)S(1)}, f32[256]{0:T(256)}, u32[]{:S(2)}) copy-start(f32[256]{0:T(256)} %copy-done.79) | copy-start | bytes 3076
  1317.6 52.0 %copy-start.19 = (f32[256,2048]{1,0:T(8,128)S(1)}, f32[256,2048]{1,0:T(8,128)}, u32[]{:S(2)}) copy-start(f32[256,2048]{1,0:T(8,128)} %copy-done.18) | copy-start | bytes 6291460
  (101 other events, 784.8 us)
Sparse Core Ops, SparseCore 0:
  10.9 73.9 all-gather.8
  87.7 79.7 all-gather.10
  170.4 127.4 all-gather.12
  300.6 112.5 all-gather.14
  414.6 112.5 all-gather.18
  528.6 113.5 all-gather.16
  643.7 113.5 all-gather.20
  789.7 111.7 reduce-scatter.19
  903.8 111.2 reduce-scatter.17
  1017.3 111.2 reduce-scatter.15
  1248.3 116.6 reduce-scatter.11
  1367.7 138.5 reduce-scatter.9
  1509.2 389.7 reduce-scatter.13
  1901.7 362.0 reduce-scatter.7
where the time goes:
time: 2280 us; the launch traced here: 2270 us
  waiting for transfers between devices  1360 us (60%)
  matrix products  325 us (14%)
  local copies, waits for them, and re-layouts  214 us (9%)
  blocking collectives  199 us (9%)
  other arithmetic  113 us (5%)
  starting transfers between devices  46.6 us (2%)
    reduce_scatter x1, waiting for transfers between devices, per_device(): lax.psum_scatter(out_wgrad, ('dp', 'ctx'), scatter_dimension=0, tiled=True)  393 us
    reduce_scatter x1, waiting for transfers between devices, per_device(): lax.psum_scatter(query_wgrad, ('dp', 'ctx'), scatter_dimension=0, tiled=T...  365 us
    unnamed x3, blocking collectives  199 us
    reduce_scatter x1, waiting for transfers between devices, per_device(): lax.psum_scatter(key_wgrad, ('dp', 'ctx'), scatter_dimension=0, tiled=True)  123 us
    all_gather x1, waiting for transfers between devices, per_device(): lax.all_gather(w_down, 'dp', axis=2, tiled=True)  101 us
    all_to_all x1, waiting for transfers between devices, per_device(): lax.all_to_all(send_rows.reshape(n_ctx, experts_dev, capacity, width), 'c...  92.9 us
    ppermute x8, waiting for transfers between devices, shifted(): return lax.ppermute(block, axis, route)  79.2 us
    all_gather x1, waiting for transfers between devices, per_device(): lax.all_gather(w_gate, 'dp', axis=1, tiled=True)  68.7 us
  transfers between devices with their start and end apart: 26, of which 18 were waited for; matrix products, arithmetic and copies ran while one was open for 27% of the time, Pallas kernels for 0%

commit v1 on v0

v1 whole, which is shorter than its diff:
```python
import functools
import math

import jax
import jax.numpy as jnp
from jax import lax
from jax.experimental import pallas as pl
from jax.experimental.pallas import tpu as pltpu
from jax.sharding import PartitionSpec as P

HQ = 32
KV = 4
HD = 128
TOP = 8
MOST = 1024
EPS = 1e-06
ROPE_BASE = 1000000.0
F32 = jnp.float32
BF16 = jnp.bfloat16
SCALE = 1.0 / math.sqrt(HD)
VMEM_LIMIT = 60 * 1024 * 1024


def dot(left, right, dims=((1,), (0,))):
    return lax.dot_general(left, right, (dims, ((), ())), preferred_element_type=F32)


NT = ((1,), (1,))
TN = ((0,), (0,))


def rms_parts(values):
    return lax.rsqrt(jnp.mean(values * values, axis=-1, keepdims=True) + EPS)


def rms_back(grad, unit, inv, gain):
    scaled = grad * gain
    return inv * (scaled - unit * jnp.mean(scaled * unit, axis=-1, keepdims=True))


def head_forward(lin, gain, cosine, sine):
    unit = lin * rms_parts(lin) * gain
    return unit * cosine + pltpu.roll(unit, HD // 2, 1) * sine


def head_backward(lin, gain, cosine, sine, rot_grad):
    grad = rot_grad * cosine + pltpu.roll(rot_grad * sine, HD // 2, 1)
    inv = rms_parts(lin)
    unit = lin * inv
    return rms_back(grad, unit, inv, gain), jnp.sum(grad * unit, axis=0, keepdims=True)


def attn_forward_kernel(
    heads,
    back,
    normed_ref,
    wqkv_ref,
    wout_ref,
    cos_ref,
    sin_ref,
    qgain_ref,
    kgain_ref,
    docc_ref,
    docr_ref,
    qlin_ref,
    klin_ref,
    q_ref,
    k_ref,
    v_ref,
    attn_ref,
    total_ref,
    part_ref,
    acc_ref,
    sum_ref,
):
    step = pl.program_id(0)
    rows = normed_ref.shape[0]
    lin = dot(normed_ref[...], wqkv_ref[...])
    here = pl.ds(step * rows, rows)
    cosine = cos_ref[...]
    sine = sin_ref[...]
    qw = heads * HD
    for head in range(heads):
        cols = slice(head * HD, (head + 1) * HD)
        part = lin[:, cols]
        qlin_ref[:, cols] = part
        q_ref[:, cols] = head_forward(part, qgain_ref[...], cosine, sine).astype(BF16)
    key_lin = lin[:, qw : qw + HD]
    klin_ref[...] = key_lin
    k_ref[here, :] = head_forward(key_lin, kgain_ref[...], cosine, sine).astype(BF16)
    v_ref[here, :] = lin[:, qw + HD :].astype(BF16)
    acc_ref[...] = jnp.zeros_like(acc_ref)
    sum_ref[...] = jnp.zeros_like(sum_ref)
    row_pos = step * rows + lax.broadcasted_iota(jnp.int32, (rows, rows), 0)
    col_off = lax.broadcasted_iota(jnp.int32, (rows, rows), 1)

    def one(block, carry):
        at = pl.ds(pl.multiple_of(block * rows, rows), rows)
        key = k_ref[at, :]
        val = v_ref[at, :]
        allowed = (docc_ref[...] == docr_ref[:, at]) & (block * rows + col_off <= row_pos)
        for head in range(heads):
            cols = slice(head * HD, (head + 1) * HD)
            score = dot(q_ref[:, cols], key, NT) * SCALE
            expo = jnp.where(allowed, jnp.exp(score), 0.0)
            folded = expo[:, :HD]
            for piece in range(1, rows // HD):
                folded = folded + expo[:, piece * HD : (piece + 1) * HD]
            sum_ref[:, cols] += folded
            acc_ref[:, cols] += dot(expo.astype(BF16), val)
        return carry

    lax.fori_loop(jnp.maximum(step - back, 0), step + 1, one, 0)
    lane = lax.broadcasted_iota(jnp.int32, (rows, HD), 1)
    totals = jnp.ones((rows, HD), F32)
    for head in range(heads):
        cols = slice(head * HD, (head + 1) * HD)
        total = jnp.sum(sum_ref[:, cols], axis=-1, keepdims=True)
        totals = jnp.where(lane == head, total, totals)
        attn_ref[:, cols] = (acc_ref[:, cols] / total).astype(BF16)
    total_ref[...] = totals
    part_ref[...] = dot(attn_ref[...], wout_ref[...]).astype(BF16)


def attn_forward(normed, wqkv, wout, cosine, sine, qgain, kgain, doc, rows):
    length, width = normed.shape
    qw = wout.shape[0]
    heads = qw // HD
    blk = lambda cols: pl.BlockSpec((rows, cols), lambda i: (i, 0))
    whole = lambda shape: pl.BlockSpec(shape, lambda i: (0, 0))
    shape = jax.ShapeDtypeStruct
    return pl.pallas_call(
        functools.partial(attn_forward_kernel, heads, MOST // rows),
        grid=(length // rows,),
        in_specs=[
            blk(width),
            whole(wqkv.shape),
            whole(wout.shape),
            blk(HD),
            blk(HD),
            whole((1, HD)),
            whole((1, HD)),
            blk(1),
            whole((1, length)),
        ],
        out_specs=[
            blk(qw),
            blk(HD),
            blk(qw),
            whole((length, HD)),
            whole((length, HD)),
            blk(qw),
            blk(HD),
            blk(width),
        ],
        out_shape=[
            shape((length, qw), F32),
            shape((length, HD), F32),
            shape((length, qw), BF16),
            shape((length, HD), BF16),
            shape((length, HD), BF16),
            shape((length, qw), BF16),
            shape((length, HD), F32),
            shape((length, width), BF16),
        ],
        scratch_shapes=[pltpu.VMEM((rows, qw), F32), pltpu.VMEM((rows, qw), F32)],
        compiler_params=pltpu.CompilerParams(vmem_limit_bytes=VMEM_LIMIT),
        name="attn_forward",
    )(normed, wqkv, wout, cosine, sine, qgain, kgain, doc[:, None], doc[None, :])


def attn_backward_kernel(
    heads,
    back,
    branch_ref,
    wout_ref,
    attn_ref,
    total_ref,
    q_ref,
    k_ref,
    v_ref,
    qlin_ref,
    klin_ref,
    cos_ref,
    sin_ref,
    qgain_ref,
    kgain_ref,
    docc_ref,
    docr_ref,
    dq_ref,
    dkv_ref,
    gains_ref,
    dk_ref,
    dv_ref,
    dqa_ref,
):
    step = pl.program_id(0)
    rows = branch_ref.shape[0]
    here = pl.ds(pl.multiple_of(step * rows, rows), rows)

    @pl.when(step == 0)
    def _():
        gains_ref[...] = jnp.zeros_like(gains_ref)

    dk_ref[here, :] = jnp.zeros((rows, HD), F32)
    dv_ref[here, :] = jnp.zeros((rows, HD), F32)
    dqa_ref[...] = jnp.zeros_like(dqa_ref)
    attn_grad = dot(branch_ref[...], wout_ref[...], NT)
    grads = []
    shifts = []
    for head in range(heads):
        cols = slice(head * HD, (head + 1) * HD)
        part = attn_grad[:, cols]
        inv_total = 1.0 / total_ref[:, head : head + 1]
        delta = jnp.sum(part * attn_ref[:, cols].astype(F32), axis=-1, keepdims=True)
        grads.append((part * inv_total).astype(BF16))
        shifts.append(delta * inv_total)
    row_pos = step * rows + lax.broadcasted_iota(jnp.int32, (rows, rows), 0)
    col_off = lax.broadcasted_iota(jnp.int32, (rows, rows), 1)

    def one(block, carry):
        at = pl.ds(pl.multiple_of(block * rows, rows), rows)
        key = k_ref[at, :]
        val = v_ref[at, :]
        allowed = (docc_ref[...] == docr_ref[:, at]) & (block * rows + col_off <= row_pos)
        dk = jnp.zeros((rows, HD), F32)
        dv = jnp.zeros((rows, HD), F32)
        for head in range(heads):
            cols = slice(head * HD, (head + 1) * HD)
            query = q_ref[:, cols]
            score = dot(query, key, NT) * SCALE
            expo = jnp.where(allowed, jnp.exp(score), 0.0)
            prod = dot(grads[head], val, NT)
            score_grad = (expo * (prod - shifts[head])).astype(BF16)
            dv += dot(expo.astype(BF16), grads[head], TN)
            dk += dot(score_grad, query, TN)
            dqa_ref[:, cols] += dot(score_grad, key)
        dk_ref[at, :] += dk
        dv_ref[at, :] += dv
        return carry

    lax.fori_loop(jnp.maximum(step - back, 0), step + 1, one, 0)
    cosine = cos_ref[here, :]
    sine = sin_ref[here, :]
    for head in range(heads):
        cols = slice(head * HD, (head + 1) * HD)
        grad, gain_part = head_backward(
            qlin_ref[:, cols], qgain_ref[...], cosine, sine, dqa_ref[:, cols] * SCALE
        )
        dq_ref[:, cols] = grad.astype(BF16)
        gains_ref[0:1, :] += gain_part

    @pl.when(step == pl.num_programs(0) - 1)
    def _():
        def finish(block, carry):
            at = pl.ds(pl.multiple_of(block * rows, rows), rows)
            grad, gain_part = head_backward(
                klin_ref[at, :], kgain_ref[...], cos_ref[at, :], sin_ref[at, :], dk_ref[at, :] * SCALE
            )
            dkv_ref[at, :HD] = grad.astype(BF16)
            dkv_ref[at, HD:] = dv_ref[at, :].astype(BF16)
            gains_ref[1:2, :] += gain_part
            return carry

        lax.fori_loop(0, pl.num_programs(0), finish, 0)


def attn_backward(branch, wout, attn, total, q, k, v, qlin, klin, cosine, sine, qgain, kgain, doc, rows):
    length, width = branch.shape
    qw = wout.shape[0]
    heads = qw // HD
    blk = lambda cols: pl.BlockSpec((rows, cols), lambda i: (i, 0))
    whole = lambda shape: pl.BlockSpec(shape, lambda i: (0, 0))
    shape = jax.ShapeDtypeStruct
    full = whole((length, HD))
    return pl.pallas_call(
        functools.partial(attn_backward_kernel, heads, MOST // rows),
        grid=(length // rows,),
        in_specs=[
            blk(width),
            whole(wout.shape),
            blk(qw),
            blk(HD),
            blk(qw),
            full,
            full,
            blk(qw),
            full,
            full,
            full,
            whole((1, HD)),
            whole((1, HD)),
            blk(1),
            whole((1, length)),
        ],
        out_specs=[blk(qw), whole((length, 2 * HD)), whole((8, HD))],
        out_shape=[
            shape((length, qw), BF16),
            shape((length, 2 * HD), BF16),
            shape((8, HD), F32),
        ],
        scratch_shapes=[
            pltpu.VMEM((length, HD), F32),
            pltpu.VMEM((length, HD), F32),
            pltpu.VMEM((rows, qw), F32),
        ],
        compiler_params=pltpu.CompilerParams(vmem_limit_bytes=VMEM_LIMIT),
        name="attn_backward",
    )(branch, wout, attn, total, q, k, v, qlin, klin, cosine, sine, qgain, kgain, doc[:, None], doc[None, :])


MESH = pl.DeviceIdType.MESH
ANY = pl.BlockSpec(memory_space=pl.ANY)
VM = pl.BlockSpec(memory_space=pltpu.VMEM)
DMA = pltpu.SemaphoreType.DMA
CHUNK = 32


def flip(index, mask, count):
    result, bit = 0, 1
    while bit < count:
        digit = (index // bit) % 2
        result = result + bit * ((1 - digit) if mask & bit else digit)
        bit *= 2
    return result


def push(src, dst, send, recv, axis, peer):
    return pltpu.make_async_remote_copy(
        src_ref=src,
        dst_ref=dst,
        send_sem=send,
        recv_sem=recv,
        device_id={axis: peer},
        device_id_type=MESH,
    )


def meet(peers):
    barrier = pltpu.get_barrier_semaphore()
    for axis, peer in peers:
        pl.semaphore_signal(barrier, inc=1, device_id={axis: peer}, device_id_type=MESH)
    pl.semaphore_wait(barrier, len(peers))


class Plane:
    def __init__(self, n):
        self.n = n
        self.chips = n // 2
        self.me = lax.axis_index("ctx")
        self.core = self.me % 2
        self.chip = self.me // 2
        self.mate = self.me + 1 - 2 * self.core

    def same(self, s):
        return 2 * flip(self.chip, s, self.chips) + self.core

    def meet(self):
        meet([("ctx", self.same(s)) for s in range(1, self.chips)] + [("ctx", self.mate)])


def far_first(chips):
    return sorted(range(1, chips), key=lambda s: -bin(s).count("1"))


class Gather:
    def __init__(self, plane, src, out, send, recv, local):
        self.plane, self.out, self.send, self.recv = plane, out, send, recv
        self.own = pltpu.make_async_copy(src, out.at[plane.me], local)
        self.far = [
            push(src, out.at[plane.me], send.at[s], recv.at[s], "ctx", plane.same(s))
            for s in far_first(plane.chips)
        ]
        self.near = push(src, out.at[plane.me], send.at[0], recv.at[0], "ctx", plane.mate)

    def start(self):
        for copy in self.far:
            copy.start()
        self.near.start()
        self.own.start()

    def forward(self):
        plane, out = self.plane, self.out
        self.passed = []
        for s in sorted(range(1, plane.chips), key=lambda s: bin(s).count("1")):
            block = out.at[plane.same(s)]
            push(block, block, self.send.at[s], self.recv.at[s], "ctx", plane.mate).wait_recv()
            slot = plane.chips + s
            copy = push(block, block, self.send.at[slot], self.recv.at[slot], "ctx", plane.mate)
            copy.start()
            self.passed.append(copy)

    def finish(self):
        for copy in self.far:
            copy.wait_send()
        self.near.wait_send()
        self.near.wait_recv()
        for copy in self.passed:
            copy.wait_send()
            copy.wait_recv()
        self.own.wait()


def gather_sems(n):
    return [DMA((n,)), DMA((n,)), DMA(())]


def by_rows(rows, body):
    def one(index, carry):
        body(pl.ds(pl.multiple_of(index * CHUNK, CHUNK), CHUNK))
        return carry

    lax.fori_loop(0, rows // CHUNK, one, 0)


class Scatter:
    def __init__(self, plane, part, mine, other, landed, send, recv, local):
        self.plane, self.mine, self.other, self.landed = plane, mine, other, landed
        self.order = far_first(plane.chips) + [0]
        self.loads, self.across, self.far = {}, {}, {}
        mate_core = 1 - plane.core
        for s in self.order:
            block = plane.same(s)
            self.loads[s] = pltpu.make_async_copy(part.at[block], mine.at[s], local.at[s])
            self.across[s] = push(
                part.at[block + mate_core - plane.core],
                other.at[s],
                send.at[s],
                recv.at[s],
                "ctx",
                plane.mate,
            )
            slot = plane.chips + s
            if s:
                self.far[s] = push(
                    mine.at[s], landed.at[s], send.at[slot], recv.at[slot], "ctx", block
                )

    def start(self):
        for s in self.order:
            self.across[s].start()
            self.loads[s].start()

    def run(self):
        rows = self.mine.shape[1]
        mine, other = self.mine, self.other
        for s in self.order:
            self.loads[s].wait()
            self.across[s].wait_recv()
            if s:

                def add(at, s=s):
                    total = mine[s, at, :].astype(F32) + other[s, at, :].astype(F32)
                    mine[s, at, :] = total.astype(BF16)

                by_rows(rows, add)
                self.far[s].start()
        for s in self.order:
            if s:
                self.far[s].wait_recv()

    def total(self, at):
        value = self.mine[0, at, :].astype(F32) + self.other[0, at, :].astype(F32)
        for s in range(1, self.plane.chips):
            value = value + self.landed[s, at, :].astype(F32)
        return value

    def finish(self):
        for s in self.order:
            self.across[s].wait_send()
            if s:
                self.far[s].wait_send()


def scatter_scratch(n, rows, width):
    chips = n // 2
    return [pltpu.VMEM((chips, rows, width), BF16)] * 3 + [DMA((n,)), DMA((n,)), DMA((chips,))]


def comm_call(kernel, ident, name, outs, out_specs, in_specs, scratch, micros, *args):
    return pl.pallas_call(
        kernel,
        out_shape=outs,
        in_specs=in_specs,
        out_specs=out_specs,
        scratch_shapes=scratch,
        compiler_params=pltpu.CompilerParams(
            collective_id=ident, has_side_effects=True, vmem_limit_bytes=VMEM_LIMIT
        ),
        cost_estimate=pl.CostEstimate(
            flops=0, transcendentals=0, bytes_accessed=int(micros * 3.0e6)
        ),
        name=name,
    )(*args)


def swap_all(n, src, out, send, recv, local):
    me = lax.axis_index("ctx")
    own = pltpu.make_async_copy(src.at[me], out.at[me], local)
    own.start()
    copies = []
    for s in range(n - 1, 0, -1):
        peer = flip(me, s, n)
        copies.append(push(src.at[peer], out.at[me], send.at[s], recv.at[s], "ctx", peer))
        copies[-1].start()
    return own, copies


def prep_kernel(n, n_dp, cols_ref, small_ref, out_ref, all_ref, *sems):
    send, recv, local, gsend, grecv, zsend, zrecv = sems
    me, row = lax.axis_index("ctx"), lax.axis_index("dp")
    meet(
        [("ctx", flip(me, s, n)) for s in range(1, n)]
        + [("dp", flip(row, s, n_dp)) for s in range(1, n_dp)]
    )
    all_ref[row, me] = small_ref[...]
    smalls = []
    for s in range(1, n):
        peer = flip(me, s, n)
        smalls.append(push(small_ref, all_ref.at[row, me], gsend.at[s], grecv.at[s], "ctx", peer))
        smalls[-1].start()
    own, copies = swap_all(n, cols_ref, out_ref, send, recv, local)
    for copy in smalls:
        copy.wait_recv()
    planes = []
    for s in range(1, n_dp):
        peer = flip(row, s, n_dp)
        planes.append(push(all_ref.at[row], all_ref.at[row], zsend.at[s], zrecv.at[s], "dp", peer))
        planes[-1].start()
    for copy in copies + planes:
        copy.wait_recv()
    for copy in copies + planes + smalls:
        copy.wait_send()
    own.wait()


def post_kernel(n, n_dp, cols_ref, small_ref, out_ref, sum_ref, first, mid, second, *sems):
    send, recv, local, gsend, grecv, zsend, zrecv = sems
    me, row = lax.axis_index("ctx"), lax.axis_index("dp")
    meet(
        [("ctx", flip(me, s, n)) for s in range(1, n)]
        + [("dp", flip(row, s, n_dp)) for s in range(1, n_dp)]
    )
    smalls = []
    for s in range(1, n):
        peer = flip(me, s, n)
        smalls.append(push(small_ref.at[peer], first.at[s], gsend.at[s], grecv.at[s], "ctx", peer))
        smalls[-1].start()
    own, copies = swap_all(n, cols_ref, out_ref, send, recv, local)
    value = small_ref[me]
    for copy, s in zip(smalls, range(1, n)):
        copy.wait_recv()
        value = value + first[s]
    mid[...] = value
    planes = []
    for s in range(1, n_dp):
        peer = flip(row, s, n_dp)
        planes.append(push(mid.at[peer], second.at[s], zsend.at[s], zrecv.at[s], "dp", peer))
        planes[-1].start()
    value = mid[row]
    for copy, s in zip(planes, range(1, n_dp)):
        copy.wait_recv()
        value = value + second[s]
    sum_ref[...] = value
    for copy in copies:
        copy.wait_recv()
    for copy in copies + planes + smalls:
        copy.wait_send()
    own.wait()


def swap_sems(n, n_dp):
    return [DMA((n,)), DMA((n,)), DMA(()), DMA((n,)), DMA((n,)), DMA((n_dp,)), DMA((n_dp,))]


def prep(n, n_dp, cols, small):
    shape = jax.ShapeDtypeStruct
    return comm_call(
        functools.partial(prep_kernel, n, n_dp),
        0,
        "prep",
        [shape(cols.shape, cols.dtype), shape((n_dp, n) + small.shape, F32)],
        [ANY, VM],
        [ANY, VM],
        swap_sems(n, n_dp),
        8,
        cols,
        small,
    )


def post(n, n_dp, cols, small):
    shape = jax.ShapeDtypeStruct
    tile = small.shape[2:]
    return comm_call(
        functools.partial(post_kernel, n, n_dp),
        1,
        "post",
        [shape(cols.shape, cols.dtype), shape(tile, F32)],
        [ANY, VM],
        [ANY, VM],
        [
            pltpu.VMEM((n, n_dp) + tile, F32),
            pltpu.VMEM((n_dp,) + tile, F32),
            pltpu.VMEM((n_dp,) + tile, F32),
        ]
        + swap_sems(n, n_dp),
        8,
        cols,
        small,
    )


def first_kernel(n, x_ref, gain_ref, grad_ref, info_ref, nall_ref, gall_ref, iall_ref, low, *sems):
    plane = Plane(n)
    plane.meet()
    grads = Gather(plane, grad_ref, gall_ref, *sems[0:3])
    infos = Gather(plane, info_ref, iall_ref, *sems[3:6])
    infos.start()

    def norm(at):
        value = x_ref[at, :].astype(F32)
        low[at, :] = (value * rms_parts(value) * gain_ref[...]).astype(BF16)

    by_rows(x_ref.shape[0], norm)
    normed = Gather(plane, low, nall_ref, *sems[6:9])
    normed.start()
    grads.start()
    infos.forward()
    normed.forward()
    grads.forward()
    for each in (infos, normed, grads):
        each.finish()


def first(n, x, gain, grad, info):
    shape = jax.ShapeDtypeStruct
    many = lambda array, kind: shape((n,) + array.shape, kind)
    return comm_call(
        functools.partial(first_kernel, n),
        2,
        "first",
        [many(x, BF16), many(grad, BF16), many(info, F32)],
        [ANY] * 3,
        [VM] * 4,
        [pltpu.VMEM(x.shape, BF16)] + gather_sems(n) * 3,
        90,
        x,
        gain,
        grad,
        info,
    )


def middle_kernel(n, part_ref, x_ref, gain_ref, after_ref, all_ref, low, *scratch):
    plane = Plane(n)
    plane.meet()
    sums = Scatter(plane, part_ref, *scratch[:6])
    sums.start()
    sums.run()

    def norm(at):
        value = x_ref[at, :].astype(F32) + sums.total(at)
        after_ref[at, :] = value
        low[at, :] = (value * rms_parts(value) * gain_ref[...]).astype(BF16)

    by_rows(x_ref.shape[0], norm)
    normed = Gather(plane, low, all_ref, *scratch[6:])
    normed.start()
    normed.forward()
    sums.finish()
    normed.finish()


def middle(n, part, x, gain):
    shape = jax.ShapeDtypeStruct
    return comm_call(
        functools.partial(middle_kernel, n),
        3,
        "middle",
        [shape(x.shape, F32), shape((n,) + x.shape, BF16)],
        [VM, ANY],
        [ANY, VM, VM],
        [pltpu.VMEM(x.shape, BF16)] + scatter_scratch(n, *x.shape) + gather_sems(n),
        95,
        part,
        x,
        gain,
    )


def turn_kernel(
    n, part_ref, after_ref, grad_ref, gain_ref, mid_ref, fpart_ref, all_ref, low, *scratch
):
    plane = Plane(n)
    plane.meet()
    sums = Scatter(plane, part_ref, *scratch[:6])
    sums.start()
    fpart_ref[...] = jnp.zeros_like(fpart_ref)
    sums.run()

    def norm(at):
        value = after_ref[at, :]
        inv = rms_parts(value)
        unit = value * inv
        grad = sums.total(at)
        fpart_ref[0:1, :] += jnp.sum(grad * unit, axis=0, keepdims=True)
        mid = grad_ref[at, :].astype(F32) + rms_back(grad, unit, inv, gain_ref[...])
        mid_ref[at, :] = mid
        low[at, :] = mid.astype(BF16)

    by_rows(after_ref.shape[0], norm)
    branch = Gather(plane, low, all_ref, *scratch[6:])
    branch.start()
    branch.forward()
    sums.finish()
    branch.finish()


def turn(n, part, after, grad, gain):
    shape = jax.ShapeDtypeStruct
    return comm_call(
        functools.partial(turn_kernel, n),
        4,
        "turn",
        [
            shape(after.shape, F32),
            shape((8, after.shape[1]), F32),
            shape((n,) + after.shape, BF16),
        ],
        [VM, VM, ANY],
        [ANY, VM, VM, VM],
        [pltpu.VMEM(after.shape, BF16)] + scatter_scratch(n, *after.shape) + gather_sems(n),
        95,
        part,
        after,
        grad,
        gain,
    )


def last_kernel(n, part_ref, x_ref, mid_ref, gain_ref, out_ref, apart_ref, *scratch):
    plane = Plane(n)
    plane.meet()
    sums = Scatter(plane, part_ref, *scratch[:6])
    sums.start()
    apart_ref[...] = jnp.zeros_like(apart_ref)
    sums.run()

    def norm(at):
        value = x_ref[at, :].astype(F32)
        inv = rms_parts(value)
        unit = value * inv
        grad = sums.total(at)
        apart_ref[0:1, :] += jnp.sum(grad * unit, axis=0, keepdims=True)
        out_ref[at, :] = mid_ref[at, :] + rms_back(grad, unit, inv, gain_ref[...])

    by_rows(x_ref.shape[0], norm)
    sums.finish()


def last(n, part, x, mid, gain):
    shape = jax.ShapeDtypeStruct
    return comm_call(
        functools.partial(last_kernel, n),
        5,
        "last",
        [shape(mid.shape, F32), shape((8, mid.shape[1]), F32)],
        [VM, VM],
        [ANY, VM, VM, VM],
        scatter_scratch(n, *mid.shape),
        50,
        part,
        x,
        mid,
        gain,
    )


def close_kernel(n, part_ref, after_ref, out_ref, *scratch):
    plane = Plane(n)
    plane.meet()
    sums = Scatter(plane, part_ref, *scratch[:6])
    sums.start()
    sums.run()

    def add(at):
        out_ref[at, :] = (after_ref[at, :] + sums.total(at)).astype(BF16)

    by_rows(after_ref.shape[0], add)
    sums.finish()


def close(n, part, after):
    return comm_call(
        functools.partial(close_kernel, n),
        6,
        "close",
        jax.ShapeDtypeStruct(after.shape, BF16),
        VM,
        [ANY, VM],
        scatter_scratch(n, *after.shape),
        50,
        part,
        after,
    )


def scatter_dp(partial):
    return lax.psum_scatter(partial.astype(BF16), "dp", scatter_dimension=0, tiled=True)


def per_device(
    layer_input,
    doc_ids,
    route_ids,
    route_probs,
    attn_gain,
    ffn_gain,
    query_gain,
    key_gain,
    w_query,
    w_key,
    w_value,
    w_out,
    w_gate,
    w_up,
    w_down,
    out_grad,
):
    tokens, width = layer_input.shape[1:]
    n_dp = lax.axis_size("dp")
    n_ctx = lax.axis_size("ctx")
    ctx_index = lax.axis_index("ctx")
    length = tokens * n_ctx
    heads = HQ // n_ctx
    share = n_ctx // KV
    qw = heads * HD
    both = ("dp", "ctx")
    depth = w_query.shape[0]
    own_e = w_gate.shape[0]

    cut = attn_gain.shape[0]
    hcut = query_gain.shape[0]
    kinds = 2 * (cut + hcut)
    small = jnp.concatenate([attn_gain, ffn_gain, query_gain, key_gain]).astype(F32)
    small = jnp.pad(small, (0, 1024 - kinds)).reshape(8, HD)
    cols = jnp.concatenate(
        [
            w_query.reshape(depth, n_ctx, qw),
            jnp.repeat(w_key.reshape(depth, KV, HD), share, axis=1),
            jnp.repeat(w_value.reshape(depth, KV, HD), share, axis=1),
        ],
        axis=2,
    ).transpose(1, 0, 2)
    cols, small = prep(n_ctx, n_dp, cols, small)
    small = small.reshape(n_dp * n_ctx, 1024)
    gain_attn = small[:, :cut].reshape(1, width)
    gain_ffn = small[:, cut : 2 * cut].reshape(1, width)
    gain_query = small[:, 2 * cut : 2 * cut + hcut].reshape(1, HD)
    gain_key = small[:, 2 * cut + hcut : kinds].reshape(1, HD)
    wqkv = lax.all_gather(cols.reshape(n_ctx * depth, qw + 2 * HD), "dp", axis=0, tiled=True)
    forth = [(c * n_dp + d, d * n_ctx + c) for d in range(n_dp) for c in range(n_ctx)]
    wout = lax.all_gather(lax.ppermute(w_out, both, forth), "dp", axis=0, tiled=True)

    inputs = layer_input.reshape(tokens, width)
    top_own = out_grad.reshape(tokens, width)
    n_experts = own_e * n_ctx
    match = route_ids.reshape(1, tokens, TOP) == jnp.arange(n_experts, dtype=jnp.int32)[:, None, None]
    probs = jnp.sum(jnp.where(match, route_probs.reshape(1, tokens, TOP), 0.0), axis=2)
    info = jnp.concatenate(
        [probs, doc_ids.reshape(1, tokens).astype(F32), jnp.zeros((7, tokens), F32)], axis=0
    )
    normed, top_all, info = first(n_ctx, inputs, gain_attn, top_own, info)
    normed = normed.reshape(length, width)
    top_all = top_all.reshape(length, width)
    doc = info[:, n_experts].reshape(length).astype(jnp.int32)
    my_probs = lax.dynamic_slice_in_dim(info, ctx_index * own_e, own_e, 1)
    my_probs = my_probs.transpose(0, 2, 1).reshape(length, own_e)

    inverse = 1.0 / ROPE_BASE ** (jnp.arange(HD // 2, dtype=F32) * 2.0 / HD)
    angles = jnp.arange(length, dtype=F32)[:, None] * inverse[None, :]
    cosine = jnp.cos(angles)
    sine = jnp.sin(angles)
    cosine = jnp.concatenate([cosine, cosine], axis=1)
    sine = jnp.concatenate([-sine, sine], axis=1)
    qlin, klin, q, k, v, attn, total, part = attn_forward(
        normed, wqkv, wout, cosine, sine, gain_query, gain_key, doc, tokens
    )
    blocks = (n_ctx, tokens, width)
    after, normed2 = middle(n_ctx, part.reshape(blocks), inputs, gain_ffn)
    normed2 = normed2.reshape(length, width)

    moe = 0.0
    row_sum = 0.0
    expert_grads = []
    for e in range(own_e):
        wg = lax.all_gather(w_gate[e], "dp", axis=0, tiled=True)
        wu = lax.all_gather(w_up[e], "dp", axis=0, tiled=True)
        wd = lax.all_gather(w_down[e], "dp", axis=0, tiled=False)
        prob = my_probs[:, e : e + 1]
        gate = dot(normed2, wg)
        up = dot(normed2, wu)
        sig = jax.nn.sigmoid(gate)
        silu = gate * sig
        act = (silu * up).astype(BF16)
        out = jnp.einsum("rf,zfd->rzd", act, wd, preferred_element_type=F32).astype(BF16)
        moe = moe + prob * out.reshape(length, width).astype(F32)
        route_grad = (top_all.astype(F32) * prob).astype(BF16)
        route3 = route_grad.reshape(length, n_dp, width // n_dp)
        act_grad = jnp.einsum("rzd,zfd->rf", route3, wd, preferred_element_type=F32)
        down_grad = jnp.einsum("rf,rzd->zfd", act, route3, preferred_element_type=F32)
        gate_grad = (act_grad * up * sig * (1.0 + gate * (1.0 - sig))).astype(BF16)
        up_grad = (act_grad * silu).astype(BF16)
        row_sum = row_sum + dot(gate_grad, wg, NT) + dot(up_grad, wu, NT)
        raw = (
            dot(normed2, gate_grad, TN).astype(BF16),
            dot(normed2, up_grad, TN).astype(BF16),
            down_grad.astype(BF16),
        )
        raw, normed2, top_all = lax.optimization_barrier((raw, normed2, top_all))
        expert_grads.append((scatter_dp(raw[0]), scatter_dp(raw[1]), scatter_dp(raw[2])[0]))
    mid, ffn_part, branch = turn(
        n_ctx, row_sum.astype(BF16).reshape(blocks), after, top_own, gain_ffn
    )
    branch = branch.reshape(length, width)
    layer_output = close(n_ctx, moe.astype(BF16).reshape(blocks), after)

    dq, dkv, gains = attn_backward(
        branch, wout, attn, total, q, k, v, qlin, klin, cosine, sine, gain_query, gain_key, doc, tokens
    )
    dqkv = jnp.concatenate([dq, dkv], axis=1)
    normed_grad = dot(dqkv, wqkv, NT).astype(BF16).reshape(blocks)
    input_grad, attn_part = last(n_ctx, normed_grad, inputs, mid, gain_attn)

    out_w = scatter_dp(dot(attn, branch, TN))
    out_w = lax.ppermute(out_w, both, [(b, a) for a, b in forth]).astype(F32)
    qkv_w = scatter_dp(dot(normed, dqkv, TN))
    n_all = n_dp * n_ctx
    packed = jnp.concatenate(
        [
            attn_part[0].reshape(n_all, cut),
            ffn_part[0].reshape(n_all, cut),
            gains[0].reshape(n_all, hcut),
            gains[1].reshape(n_all, hcut),
            jnp.zeros((n_all, 1024 - kinds), F32),
        ],
        axis=1,
    )
    packed = packed.reshape(n_dp, n_ctx, 8, HD).transpose(1, 0, 2, 3)
    qkv_w, packed = post(n_ctx, n_dp, qkv_w.reshape(n_ctx, depth, qw + 2 * HD), packed)
    packed = packed.reshape(1024)
    query_w = qkv_w[:, :, :qw].transpose(1, 0, 2).reshape(depth, HQ * HD).astype(F32)
    kv_w = jnp.sum(qkv_w[:, :, qw:].astype(F32).reshape(KV, share, depth, 2 * HD), axis=1)
    key_w = kv_w[:, :, :HD].transpose(1, 0, 2).reshape(depth, KV * HD)
    value_w = kv_w[:, :, HD:].transpose(1, 0, 2).reshape(depth, KV * HD)

    stack = lambda index: jnp.stack([g[index] for g in expert_grads]).astype(F32)
    return (
        layer_output.reshape(1, tokens, width),
        input_grad.reshape(1, tokens, width),
        packed[:cut],
        packed[cut : 2 * cut],
        packed[2 * cut : 2 * cut + hcut],
        packed[2 * cut + hcut : kinds],
        query_w,
        key_w,
        value_w,
        out_w,
        stack(0),
        stack(1),
        stack(2),
    )


def solution(mesh):
    both = ("dp", "ctx")
    seq = P("dp", "ctx", None)
    in_specs = (
        seq,
        P("dp", "ctx"),
        seq,
        seq,
        P(both),
        P(both),
        P(both),
        P(both),
        P(both, None),
        P(both, None),
        P(both, None),
        P(both, None),
        P("ctx", "dp", None),
        P("ctx", "dp", None),
        P("ctx", None, "dp"),
        seq,
    )
    out_specs = (
        seq,
        seq,
        P(both),
        P(both),
        P(both),
        P(both),
        P(both, None),
        P(both, None),
        P(both, None),
        P(both, None),
        P("ctx", "dp", None),
        P("ctx", "dp", None),
        P("ctx", None, "dp"),
    )
    return jax.shard_map(
        per_device, mesh=mesh, in_specs=in_specs, out_specs=out_specs, check_vma=False
    )
```

time: 2280 us -> 1240 us (0.54)
  waiting for transfers between devices: 1360 us -> 137 us
  Pallas kernels: 0 us -> 593 us
  blocking collectives: 199 us -> 0 us
  matrix products: 325 us -> 253 us
  other arithmetic: 113 us -> 44.7 us
  local copies, waits for them, and re-layouts: 214 us -> 175 us
  starting transfers between devices: 46.6 us -> 9.02 us
    reduce_scatter x7 -> x8, waiting for transfers between devices: 881 us -> 93.5 us  [scatter_dp(): lax.psum_scatter(partial.astype(BF16), 'dp', scatter_dimension=0, tiled=T...]
    pallas_call x0 -> x9, Pallas kernels: none -> 593 us  [the longest x7 485 us: comm_call(): pl.pallas_call(kernel, out_shape=outs, in_specs=in_specs, out_specs=out_s...]
    unnamed x3 -> x0, blocking collectives: 199 us -> none
    all_gather x7 -> x8, waiting for transfers between devices: 206 us -> 15.7 us  [the longest x2 15.6 us: per_device(): wg = lax.all_gather(w_gate[e], 'dp', axis=0, tiled=True)]
    all_to_all x4 -> x0, waiting for transfers between devices: 187 us -> none  [the longest x1 92.9 us: per_device(): lax.all_to_all(send_rows.reshape(n_ctx, experts_dev, capacity, width), 'c...]
    convert_element_type x1 -> x9, local copies, waits for them, and re-layouts: 0.05 us -> 146 us  [the longest x4 92.6 us: per_device(): moe = moe + prob * out.reshape(length, width).astype(F32)]
    dot_general x45 -> x21, matrix products: 325 us -> 253 us  [the longest x15 187 us: dot(): lax.dot_general(left, right, (dims, ((), ())), preferred_element_type=F32)]
    ppermute x8 -> x2, waiting for transfers between devices: 79.2 us -> 23.4 us  [the longest x1 23.4 us: per_device(): lax.ppermute(w_out, both, forth)]
  transfers between devices with their start and end apart: 26 -> 18, of which waited for: 18 -> 4; matrix products, arithmetic and copies ran while one was open for 27% -> 33% of each run, Pallas kernels for 0% -> 39%
where the time goes in v1:
time: 1240 us; the launch traced here: 1230 us
  Pallas kernels  593 us (48%)
  matrix products  253 us (20%)
  local copies, waits for them, and re-layouts  175 us (14%)
  waiting for transfers between devices  137 us (11%)
  other arithmetic  44.7 us (4%)
  between operations  14.9 us (1%)
    pallas_call x7, Pallas kernels, comm_call(): pl.pallas_call(kernel, out_shape=outs, in_specs=in_specs, out_specs=out_s...  485 us
    dot_general x15, matrix products, dot(): lax.dot_general(left, right, (dims, ((), ())), preferred_element_type=F32)  187 us
    reduce_scatter x8, waiting for transfers between devices, scatter_dp(): lax.psum_scatter(partial.astype(BF16), 'dp', scatter_dimension=0, tiled=T...  93.5 us
    convert_element_type x4, local copies, waits for them, and re-layouts, per_device(): moe = moe + prob * out.reshape(length, width).astype(F32)  92.6 us
    pallas_call x1, Pallas kernels, attn_backward(): pl.pallas_call(functools.partial(attn_backward_kernel, heads, MOST // row...  65 us
    convert_element_type x3, local copies, waits for them, and re-layouts, per_device(): route_grad = (top_all.astype(F32) * prob).astype(BF16)  51.4 us
    pallas_call x1, Pallas kernels, attn_forward(): pl.pallas_call(functools.partial(attn_forward_kernel, heads, MOST // rows...  42.6 us
    dot_general x2, matrix products, per_device(): act_grad = jnp.einsum('rzd,zfd->rf', route3, wd, preferred_element_type=F32)  25 us
  transfers between devices with their start and end apart: 18, of which 4 were waited for; matrix products, arithmetic and copies ran while one was open for 33% of the time, Pallas kernels for 39%

profile of v1, /device:TPU:14, one launch (start us, length us, event | category | flops | bytes accessed | tf_op | source)
XLA Modules:
  0.0 1226.6 jit_solution(11939404291307281084)
XLA Ops:
  7.3 3.0 collective-permute-start
  10.3 23.4 %collective-permute-done = bf16[128,2048]{1,0:T(8,128)(2,1)S(1)} collective-permute-done((bf16[128,2048]{1,0:T(8,128)(2,1)}, bf16[128,2048]{1,0:T(8,128)(2,1)S(1)}, u32[]{:S(2)}, u32[]{:S(2)}) %collective-permute-start) | collective-permute-done | bytes 524320 | tf_op jit(solution)/shard_map/ppermute | solution.py:864
  38.9 20.1 %prep.1 = (bf16[8,64,768]{2,1,0:T(8,128)(2,1)}, f32[4,8,8,128]{3,2,1,0:T(8,128)}) custom-call(bf16[8,64,768]{2,1,0:T(8,128)(2,1)} %maximum_bitcast_fusion.cols_ref, f32[8,128]{1,0:T(8,128)} %fusion.40.small_ref), custom_call_target="tpu_custom_call" | custom-call | bytes 24000000 | tf_op jit(solution)/shard_map/prep/pallas_call | solution.py:481
  67.4 101.8 %first.1 = (bf16[8,256,2048]{2,1,0:T(8,128)(2,1)}, bf16[8,256,2048]{2,1,0:T(8,128)(2,1)}, f32[8,24,256]{2,1,0:T(8,128)}) custom-call(bf16[256,2048]{1,0:T(8,128)(2,1)} %bitcast.170, f32[1,2048]{1,0:T(1,128)} %reshape.192.gain_ref, bf16[256,2048]{1,0:T(8,128)(2,1)} %bitcast.181, f32[24,256]{1,0:T(8,128)} %maximum_maximum_fusion.info_ref), custom_call_target="tpu_custom_call" | custom-call | bytes 270000000 | tf_op jit(solution)/shard_map/first/pallas_call | solution.py:481
  171.4 3.9 fusion.31
  178.7 19.8 %reshape.219 = f32[2048,4,512]{2,1,0:T(4,128)} reshape(bf16[8,256,2048]{2,1,0:T(8,128)(2,1)} %get-tuple-element.52) | data formatting | bytes 25165824 | tf_op jit(solution)/shard_map/convert_element_type | solution.py:909
  198.5 19.2 %copy.95 = f32[2048,4,512]{0,2,1:T(8,128)} copy(f32[2048,4,512]{2,1,0:T(4,128)} %reshape.219) | data formatting | bytes 33554432 | tf_op jit(solution)/shard_map/convert_element_type | solution.py:909
  219.6 42.6 %attn_forward.1 = (f32[2048,512]{1,0:T(8,128)}, f32[2048,128]{1,0:T(8,128)}, bf16[2048,512]{1,0:T(8,128)(2,1)}, bf16[2048,128]{1,0:T(8,128)(2,1)}, bf16[2048,128...) custom-call(bf16[2048,2048]{1,0:T(8,128)(2,1)} %bitcast.179, ...), custom_call_target="tpu_custom_call" | custom-call | tf_op jit(solution)/shard_map/attn_forward/pallas_call | solution.py:132
  262.2 108.7 %middle.1 = (f32[256,2048]{1,0:T(8,128)}, bf16[8,256,2048]{2,1,0:T(8,128)(2,1)}) custom-call(bf16[8,256,2048]{2,1,0:T(8,128)(2,1)} %bitcast.178, bf16[256,2048]{1,0:T(8,128)(2,1)} %bitcast.171, f32[1,2048]{1,0:T(1,128)} %reshape.200.gain_ref), custom_call_target="tpu_custom_call" | custom-call | bytes 285000000 | tf_op jit(solution)/shard_map/middle/pallas_call | solution.py:481
  370.9 11.7 fusion.23
  382.6 13.2 %fusion.11 = f32[2048,768,1]{1,0,2:T(8,128)} fusion(bf16[4,768,512]{2,1,0:T(8,128)(2,1)} %all-gather.17.cloned.1.call-done, f32[2048,4,512]{0,2,1:T(8,128)} %copy.95, f32[2048]{0:T(1024)S(1)} %bitcast.208), kind=kOutput, calls=%fused_computation.31 | convolution fusion | flops 6450839552 | bytes 26222592 | tf_op jit(solution)/shard_map/rzd,zfd->rf/dot_general | solution.py:911
  395.8 15.9 %fusion.12 = (bf16[2048,768,1]{1,0,2:T(8,128)(2,1)}, bf16[2048,768]{1,0:T(8,128)(2,1)S(1)}, bf16[2048,768]{1,0:T(8,128)(2,1)S(1)}) fusion(f32[2048,768]{1,0:T(8,128)} %fusion.23, f32[2048,768,1]{1,0,2:T(8,128)} %fusion.11, bf16[2048,2048]{1,0:T(8,128)(2,1)} %bitcast.213, bf16[1,2048,768]{2,1,0:T(8,128)(2,1)} %all-gather.21.cloned.1.call-done), kind=kOutput, calls=%fused_computation.32 | convolution fusion | flops 6466043904 | bytes 33554432 | tf_op jit(solution)/shard_map/dot_general | solution.py:25
  413.3 11.4 convolution_convert_fusion.4
  424.7 10.8 convolution_convert_fusion.5
  435.5 12.5 %convert_bitcast_fusion.1 = bf16[4,768,512]{1,2,0:T(8,128)(2,1)} fusion(bf16[2048,768,1]{1,0,2:T(8,128)(2,1)} %get-tuple-element.151, f32[2048,4,512]{0,2,1:T(8,128)} %copy.95, f32[2048]{0:T(1024)S(1)} %bitcast.209), kind=kOutput, calls=%fused_computation.50 | convolution fusion | flops 6452412416 | bytes 23076864 | tf_op jit(solution)/shard_map/rf,rzd->zfd/dot_general | solution.py:912
  448.0 12.4 %fusion.21 = f32[2048,2048]{1,0:T(8,128)} fusion(bf16[2048,768]{1,0:T(8,128)(2,1)} %copy-done.27, bf16[1,2048,768]{2,1,0:T(8,128)(2,1)S(1)} %copy-done.21), kind=kOutput, calls=%fused_computation.41 | convolution fusion | flops 6442450944 | bytes 23068672 | tf_op jit(solution)/shard_map/dot_general | solution.py:25
  460.4 9.7 fusion.25
  470.1 8.3 multiply_convert_fusion
  478.4 12.4 %copy.98 = bf16[2048,2048]{0,1:T(8,128)(2,1)} copy(bf16[2048,2048]{1,0:T(8,128)(2,1)} %multiply_convert_fusion) | data formatting | bytes 16777216 | tf_op jit(solution)/shard_map/convert_element_type | solution.py:909
  490.8 11.8 fusion.52
  502.6 11.7 fusion.15
  514.3 15.6 %all-gather.25.cloned.1.call-done = bf16[1,2048,768]{2,1,0:T(8,128)(2,1)} async-done(((bf16[1,512,768]{2,1,0:T(8,128)(2,1)}), bf16[1,2048,768]{2,1,0:T(8,128)(2,1)}) %all-gather.25.cloned.1.call-update) | async-done | bytes 3145744 | tf_op jit(solution)/shard_map/all_gather | solution.py:898
  529.9 17.7 %fusion.3 = (bf16[2048,768]{1,0:T(8,128)(2,1)S(1)}, bf16[2048,768]{1,0:T(8,128)(2,1)S(1)}, bf16[2048,768,1]{1,0,2:T(8,128)(2,1)}) fusion(f32[2048,768,1]{1,0,2:T(8,128)} %fusion.52, f32[2048,768]{1,0:T(8,128)} %fusion.15, bf16[2048,2048]{1,0:T(8,128)(2,1)} %bitcast.217, bf16[1,2048,768]{2,1,0:T(8,128)(2,1)} %all-gather.25.cloned.1.call-done), kind=kOutput, calls=%fused_computation.12 | convolution fusion | flops 6466043904 | bytes 33554432 | tf_op jit(solution)/shard_map/dot_general | solution.py:25
  547.7 9.8 fusion.17
  557.5 22.4 %add_convert_fusion = bf16[2048,2048]{1,0:T(8,128)(2,1)} fusion(f32[2048,2048]{1,0:T(8,128)} %fusion.17, f32[2048,2048]{1,0:T(8,128)} %fusion.25, f32[2048,2048]{1,0:T(8,128)} %fusion.21, bf16[2048,768]{1,0:T(8,128)(2,1)S(1)} %get-tuple-element.148, bf16[1,2048,768]{2,1,0:T(8,128)(2,1)} %all-gather.27.cloned.1.call-done), kind=kOutput, calls=%fused_computation | convolution fusion | flops 6459228160 | bytes 65011712 | tf_op jit(solution)/shard_map/dot_general | solution.py:25
  579.9 109.1 %turn.1 = (f32[256,2048]{1,0:T(8,128)}, f32[8,2048]{1,0:T(8,128)}, bf16[8,256,2048]{2,1,0:T(8,128)(2,1)}) custom-call(bf16[8,256,2048]{2,1,0:T(8,128)(2,1)} %bitcast.168, f32[256,2048]{1,0:T(8,128)} %get-tuple-element.54.after_ref, bf16[256,2048]{1,0:T(8,128)(2,1)} %bitcast.182, f32[1,2048]{1,0:T(1,128)} %reshape.200.gain_ref), custom_call_target="tpu_custom_call" | custom-call | bytes 285000000 | tf_op jit(solution)/shard_map/turn/pallas_call | solution.py:481
  689.0 9.9 convolution_convert_fusion.6
  699.0 11.6 convert_bitcast_fusion
  710.6 10.4 convolution_convert_fusion.1
  721.0 11.4 convolution_convert_fusion.2
  733.2 65.0 %attn_backward.1 = (bf16[2048,512]{1,0:T(8,128)(2,1)}, bf16[2048,256]{1,0:T(8,128)(2,1)}, f32[8,128]{1,0:T(8,128)}) custom-call(bf16[2048,2048]{1,0:T(8,128)(2,1)} %bitcast.174, bf16[512,2048]{1,0:T(8,128)(2,1)} %all-gather.15.cloned.1.call-done.wout_ref, bf16[2048,512]{1,0:T(8,128)(2,1)} %get-tuple-element.57.attn_ref, ...), custom_call_target="tpu_custom_call" | custom-call | tf_op jit(solution)/shard_map/attn_backward/pallas_call | solution.py:276
  801.8 10.5 convolution_convert_fusion.3
  815.6 8.8 convert_convert_fusion
  824.3 25.6 %copy.97 = f32[2048,4,512]{2,1,0:T(4,128)} copy(f32[2048,4,512]{2,0,1:T(8,128)S(1)} %convert_convert_fusion) | data formatting | bytes 33554432 | tf_op jit(solution)/shard_map/convert_element_type | solution.py:908
  849.9 20.7 %reshape.220 = f32[8,256,2048]{2,1,0:T(8,128)} reshape(f32[2048,4,512]{2,1,0:T(4,128)} %copy.97) | data formatting | bytes 33554432 | tf_op jit(solution)/shard_map/convert_element_type | solution.py:908
  870.7 8.8 convert_convert_fusion.1
  879.5 25.7 %copy.94 = f32[2048,4,512]{2,1,0:T(4,128)} copy(f32[2048,4,512]{2,0,1:T(8,128)S(1)} %convert_convert_fusion.1) | data formatting | bytes 33554432 | tf_op jit(solution)/shard_map/convert_element_type | solution.py:908
  905.1 20.7 %reshape.218 = f32[8,256,2048]{2,1,0:T(8,128)} reshape(f32[2048,4,512]{2,1,0:T(4,128)} %copy.94) | data formatting | bytes 33554432 | tf_op jit(solution)/shard_map/convert_element_type | solution.py:908
  925.8 10.9 convolution_convert_fusion
  936.8 57.5 %last.1 = (f32[256,2048]{1,0:T(8,128)}, f32[8,2048]{1,0:T(8,128)}) custom-call(bf16[8,256,2048]{2,1,0:T(8,128)(2,1)} %bitcast.175, bf16[256,2048]{1,0:T(8,128)(2,1)} %bitcast.172, f32[256,2048]{1,0:T(8,128)} %get-tuple-element.66.mid_ref, f32[1,2048]{1,0:T(1,128)} %reshape.192.gain_ref), custom_call_target="tpu_custom_call" | custom-call | bytes 150000000 | tf_op jit(solution)/shard_map/last/pallas_call | solution.py:481
  994.2 15.2 %add_convert_fusion.1.part_ref = bf16[8,256,2048]{2,1,0:T(8,128)(2,1)} fusion(f32[8,256,2048]{2,1,0:T(8,128)} %reshape.220, f32[8,256,2048]{2,1,0:T(8,128)} %reshape.218, f32[8,256]{1,0:T(8,128)S(1)} %mul.131, f32[8,256]{1,0:T(8,128)S(1)} %mul.123), kind=kLoop, calls=%fused_computation.2 | loop fusion | flops 16777216 | bytes 41959424 | tf_op jit(solution)/shard_map/convert_element_type | solution.py:927
  1009.5 5.4 collective-permute-start.1
  1017.7 63.2 %close.1 = bf16[256,2048]{1,0:T(8,128)(2,1)} custom-call(bf16[8,256,2048]{2,1,0:T(8,128)(2,1)} %add_convert_fusion.1.part_ref, f32[256,2048]{1,0:T(8,128)} %get-tuple-element.54.after_ref), custom_call_target="tpu_custom_call" | custom-call | bytes 150000000 | tf_op jit(solution)/shard_map/close/pallas_call | solution.py:481
  1086.8 24.7 %post.1 = (bf16[8,64,768]{2,1,0:T(8,128)(2,1)}, f32[8,128]{1,0:T(8,128)}) custom-call(bf16[8,64,768]{2,1,0:T(8,128)(2,1)} %bitcast.192, f32[8,4,8,128]{3,2,1,0:T(8,128)} %copy_bitcast_fusion.5.small_ref), custom_call_target="tpu_custom_call" | custom-call | bytes 24000000 | tf_op jit(solution)/shard_map/post/pallas_call | solution.py:481
  1116.1 3.2 maximum_convert_fusion.1
  1120.5 31.0 %reduce-scatter.15.cloned.1.call-done = bf16[512,768]{1,0:T(8,128)(2,1)} async-done(((bf16[2048,768]{1,0:T(8,128)(2,1)}), bf16[512,768]{1,0:T(8,128)(2,1)}) %reduce-scatter.15.cloned.1.call-update) | async-done | bytes 786448 | tf_op jit(solution)/shard_map/reduce_scatter | solution.py:810
  1151.5 62.4 %reduce-scatter.13.cloned.1.call-done = bf16[512,768]{1,0:T(8,128)(2,1)} async-done(((bf16[2048,768]{1,0:T(8,128)(2,1)}), bf16[512,768]{1,0:T(8,128)(2,1)}) %reduce-scatter.13.cloned.1.call-update) | async-done | bytes 786448 | tf_op jit(solution)/shard_map/reduce_scatter | solution.py:810
  1214.0 3.4 maximum_convert_fusion
  (157 shorter events, 47.0 us)
Async XLA Ops:
  7.2 29.8 %copy-start = (bf16[64,512]{1,0:T(8,128)(2,1)S(1)}, bf16[64,512]{1,0:T(8,128)(2,1)}, u32[]{:S(2)}) copy-start(bf16[64,512]{1,0:T(8,128)(2,1)} %param.25) | copy-start | bytes 196612
  7.2 51.9 %copy-start.5 = (bf16[2,512,768]{2,1,0:T(8,128)(2,1)S(1)}, bf16[2,512,768]{2,1,0:T(8,128)(2,1)}, u32[]{:S(2)}) copy-start(bf16[2,512,768]{2,1,0:T(8,128)(2,1)} %param.29) | copy-start | bytes 4718596
  7.2 212.4 %all-gather.15.cloned.1.call-start = ((), (), s32[]{:S(2)}) async-start(), calls=%async_computation.9 | async-start | bytes 2621440 | tf_op jit(solution)/shard_map/all_gather | solution.py:864
  7.3 26.4 %collective-permute-start = (bf16[128,2048]{1,0:T(8,128)(2,1)}, bf16[128,2048]{1,0:T(8,128)(2,1)S(1)}, u32[]{:S(2)}, u32[]{:S(2)}) collective-permute-start(bf16[128,2048]{1,0:T(8,128)(2,1)} %param.27), channel_id=1, source_target_pairs={{0,0},{4,1},{8,2},{12,3},{16,4},{20,5},{24,6},{28,7},{1,8},{5,9},{... | collective-permute-start | bytes 1572872 | tf_op jit(solution)/shard_map/ppermute | solution.py:864
  33.7 0.8 copy-start.10
  34.5 185.2 %all-gather.13.cloned.1.call-start = ((), (), s32[]{:S(2)}) async-start(), calls=%async_computation.8 | async-start | bytes 3932160 | tf_op jit(solution)/shard_map/all_gather | solution.py:862
  38.9 21.5 %copy-start.6 = (bf16[2,768,512]{2,1,0:T(8,128)(2,1)S(1)}, bf16[2,768,512]{2,1,0:T(8,128)(2,1)}, u32[]{:S(2)}) copy-start(bf16[2,768,512]{2,1,0:T(8,128)(2,1)} %param.30) | copy-start | bytes 4718596
  59.0 311.8 %all-gather.23.cloned.1.call-start = ((), (), s32[]{:S(2)}) async-start(), calls=%async_computation.21 | async-start | bytes 3932160 | tf_op jit(solution)/shard_map/all_gather | solution.py:899
  60.3 2.0 copy-start.7
  60.4 322.2 %all-gather.17.cloned.1.call-start = ((), (), s32[]{:S(2)}) async-start(), calls=%async_computation.10 | async-start | bytes 3932160 | tf_op jit(solution)/shard_map/all_gather | solution.py:900
  61.7 4.0 copy-start.12
  61.7 4.9 copy-start.18
  61.7 4.9 copy-start.15
  61.7 4.9 copy-start.16
  61.7 334.0 %all-gather.21.cloned.1.call-start = ((), (), s32[]{:S(2)}) async-start(), calls=%async_computation.20 | async-start | bytes 3932160 | tf_op jit(solution)/shard_map/all_gather | solution.py:898
  63.6 427.2 %all-gather.19.cloned.1.call-start = ((), (), s32[]{:S(2)}) async-start(), calls=%async_computation.11 | async-start | bytes 3932160 | tf_op jit(solution)/shard_map/all_gather | solution.py:900
  64.2 438.4 %all-gather.27.cloned.1.call-start = ((), (), s32[]{:S(2)}) async-start(), calls=%async_computation.23 | async-start | bytes 3932160 | tf_op jit(solution)/shard_map/all_gather | solution.py:899
  64.9 465.0 %all-gather.25.cloned.1.call-start = ((), (), s32[]{:S(2)}) async-start(), calls=%async_computation.22 | async-start | bytes 3932160 | tf_op jit(solution)/shard_map/all_gather | solution.py:898
  65.7 943.8 %reduce-scatter.11.cloned.1.call-start = ((), (), s32[]{:S(2)}) async-start(), calls=%async_computation.13 | async-start | bytes 2621440 | tf_op jit(solution)/shard_map/reduce_scatter | solution.py:810
  170.1 28.4 %copy-start.11 = (s32[8,1,256]{2,1,0:T(1,128)}, s32[8,1,256]{2,1,0:T(1,128)S(1)}, u32[]{:S(2)}) copy-start(s32[8,1,256]{2,1,0:T(1,128)S(1)} %slice_convert_fusion) | copy-start | bytes 24580
  411.6 1.7 copy-start.27
  411.6 13.1 %copy-start.25 = (bf16[2048,768]{1,0:T(8,128)(2,1)}, bf16[2048,768]{1,0:T(8,128)(2,1)S(1)}, u32[]{:S(2)}) copy-start(bf16[2048,768]{1,0:T(8,128)(2,1)S(1)} %get-tuple-element.152) | copy-start | bytes 9437188
  435.5 12.5 %copy-start.21 = (bf16[1,2048,768]{2,1,0:T(8,128)(2,1)S(1)}, bf16[1,2048,768]{2,1,0:T(8,128)(2,1)}, u32[]{:S(2)}) copy-start(bf16[1,2048,768]{2,1,0:T(8,128)(2,1)} %all-gather.23.cloned.1.call-done) | copy-start | bytes 9437188
  448.0 12.4 %copy-start.22 = (bf16[1,2048,768]{2,1,0:T(8,128)(2,1)S(1)}, bf16[1,2048,768]{2,1,0:T(8,128)(2,1)}, u32[]{:S(2)}) copy-start(bf16[1,2048,768]{2,1,0:T(8,128)(2,1)} %all-gather.21.cloned.1.call-done) | copy-start | bytes 9437188
  448.0 12.4 %copy-start.26 = (bf16[2048,768]{1,0:T(8,128)(2,1)S(1)}, bf16[2048,768]{1,0:T(8,128)(2,1)}, u32[]{:S(2)}) copy-start(bf16[2048,768]{1,0:T(8,128)(2,1)} %copy-done.25) | copy-start | bytes 9437188
  529.9 17.7 %copy-start.23 = (bf16[1,2048,768]{2,1,0:T(8,128)(2,1)S(1)}, bf16[1,2048,768]{2,1,0:T(8,128)(2,1)}, u32[]{:S(2)}) copy-start(bf16[1,2048,768]{2,1,0:T(8,128)(2,1)} %all-gather.25.cloned.1.call-done) | copy-start | bytes 9437188
  547.7 9.8 copy-start.24
  699.0 383.9 %reduce-scatter.23.cloned.1.call-start = ((), (), s32[]{:S(2)}) async-start(), calls=%async_computation.19 | async-start | bytes 3932160 | tf_op jit(solution)/shard_map/reduce_scatter | solution.py:810
  732.4 350.4 %reduce-scatter.21.cloned.1.call-start = ((), (), s32[]{:S(2)}) async-start(), calls=%async_computation.18 | async-start | bytes 3932160 | tf_op jit(solution)/shard_map/reduce_scatter | solution.py:810
  733.1 353.6 %reduce-scatter.9.cloned.1.call-start = ((), (), s32[]{:S(2)}) async-start(), calls=%async_computation.12 | async-start | bytes 3932160 | tf_op jit(solution)/shard_map/reduce_scatter | solution.py:810
  798.2 1.9 copy-start.9
  800.1 1.7 copy-start.8
  812.3 303.8 %reduce-scatter.19.cloned.1.call-start = ((), (), s32[]{:S(2)}) async-start(), calls=%async_computation.17 | async-start | bytes 3932160 | tf_op jit(solution)/shard_map/reduce_scatter | solution.py:810
  813.1 1.2 copy-start.14
  813.1 1.3 copy-start.13
  813.1 2.4 copy-start.20
  813.1 303.0 %reduce-scatter.17.cloned.1.call-start = ((), (), s32[]{:S(2)}) async-start(), calls=%async_computation.16 | async-start | bytes 3932160 | tf_op jit(solution)/shard_map/reduce_scatter | solution.py:810
  813.7 337.8 %reduce-scatter.15.cloned.1.call-start = ((), (), s32[]{:S(2)}) async-start(), calls=%async_computation.15 | async-start | bytes 3932160 | tf_op jit(solution)/shard_map/reduce_scatter | solution.py:810
  814.3 399.7 %reduce-scatter.13.cloned.1.call-start = ((), (), s32[]{:S(2)}) async-start(), calls=%async_computation.14 | async-start | bytes 3932160 | tf_op jit(solution)/shard_map/reduce_scatter | solution.py:810
  849.9 20.7 %copy-start.19 = (bf16[4,768,512]{2,1,0:T(8,128)(2,1)S(1)}, bf16[4,768,512]{2,1,0:T(8,128)(2,1)}, u32[]{:S(2)}) copy-start(bf16[4,768,512]{2,1,0:T(8,128)(2,1)} %all-gather.17.cloned.1.call-done) | copy-start | bytes 9437188
  905.1 20.7 %copy-start.3 = (bf16[2048,768]{1,0:T(8,128)(2,1)S(1)}, bf16[2048,768]{1,0:T(8,128)(2,1)}, u32[]{:S(2)}) copy-start(bf16[2048,768]{1,0:T(8,128)(2,1)} %all-gather.13.cloned.1.call-done.wqkv_ref) | copy-start | bytes 9437188
  1009.5 72.3 %collective-permute-start.1 = (bf16[128,2048]{1,0:T(8,128)(2,1)}, bf16[128,2048]{1,0:T(8,128)(2,1)S(1)}, u32[]{:S(2)}, u32[]{:S(2)}) collective-permute-start(bf16[128,2048]{1,0:T(8,128)(2,1)} %reduce-scatter.11.cloned.1.call-done), channel_id=1, source_target_pairs={{0,0},{1,4},{2,8},{3,12},{4,16},{5,20},{6,24},{7,28},{8,1},{9,5},{... | collective-permute-start | bytes 1572872 | tf_op jit(solution)/shard_map/ppermute | solution.py:937
  1113.7 5.6 copy-start.17
  1119.3 98.0 %copy-start.2 = (bf16[256,2048]{1,0:T(8,128)(2,1)S(1)}, bf16[256,2048]{1,0:T(8,128)(2,1)}, u32[]{:S(2)}) copy-start(bf16[256,2048]{1,0:T(8,128)(2,1)} %close.1) | copy-start | bytes 3145732
  1214.0 4.4 copy-start.4
  1217.3 2.3 copy-start.1
Sparse Core Ops, SparseCore 0:
  34.6 48.3 all-gather.14
  84.5 61.9 all-gather.12
  148.7 62.0 all-gather.22
  212.8 62.0 all-gather.16
  276.9 62.0 all-gather.20
  340.4 62.0 all-gather.18
  404.1 62.0 all-gather.26
  467.8 62.0 all-gather.24
  699.1 44.0 reduce-scatter.10
  745.3 59.8 reduce-scatter.22
  807.5 60.3 reduce-scatter.20
  870.0 60.3 reduce-scatter.8
  932.7 60.2 reduce-scatter.18
  995.2 88.9 reduce-scatter.16
  1086.3 65.1 reduce-scatter.14
  1153.7 60.2 reduce-scatter.12

commit v2 on v1

--- a/solution.py
+++ b/solution.py
@@ -7,6 +7,7 @@
 from jax.experimental import pallas as pl
 from jax.experimental.pallas import tpu as pltpu
 from jax.sharding import PartitionSpec as P
+
 
 HQ = 32
 KV = 4
@@ -55,7 +56,6 @@
     back,
     normed_ref,
     wqkv_ref,
-    wout_ref,
     cos_ref,
     sin_ref,
     qgain_ref,
@@ -69,7 +69,6 @@
     v_ref,
     attn_ref,
     total_ref,
-    part_ref,
     acc_ref,
     sum_ref,
 ):
@@ -119,12 +118,11 @@
         totals = jnp.where(lane == head, total, totals)
         attn_ref[:, cols] = (acc_ref[:, cols] / total).astype(BF16)
     total_ref[...] = totals
-    part_ref[...] = dot(attn_ref[...], wout_ref[...]).astype(BF16)
-
-
-def attn_forward(normed, wqkv, wout, cosine, sine, qgain, kgain, doc, rows):
+
+
+def attn_forward(normed, wqkv, cosine, sine, qgain, kgain, doc, rows):
     length, width = normed.shape
-    qw = wout.shape[0]
+    qw = wqkv.shape[1] - 2 * HD
     heads = qw // HD
     blk = lambda cols: pl.BlockSpec((rows, cols), lambda i: (i, 0))
     whole = lambda shape: pl.BlockSpec(shape, lambda i: (0, 0))
@@ -135,7 +133,6 @@
         in_specs=[
             blk(width),
             whole(wqkv.shape),
-            whole(wout.shape),
             blk(HD),
             blk(HD),
             whole((1, HD)),
@@ -151,7 +148,6 @@
             whole((length, HD)),
             blk(qw),
             blk(HD),
-            blk(width),
         ],
         out_shape=[
             shape((length, qw), F32),
@@ -161,12 +157,14 @@
             shape((length, HD), BF16),
             shape((length, qw), BF16),
             shape((length, HD), F32),
-            shape((length, width), BF16),
         ],
         scratch_shapes=[pltpu.VMEM((rows, qw), F32), pltpu.VMEM((rows, qw), F32)],
         compiler_params=pltpu.CompilerParams(vmem_limit_bytes=VMEM_LIMIT),
+        cost_estimate=pl.CostEstimate(
+            flops=35 * 10**9, transcendentals=0, bytes_accessed=30 * 2**20
+        ),
         name="attn_forward",
-    )(normed, wqkv, wout, cosine, sine, qgain, kgain, doc[:, None], doc[None, :])
+    )(normed, wqkv, cosine, sine, qgain, kgain, doc[:, None], doc[None, :])
 
 
 def attn_backward_kernel(
@@ -187,8 +185,7 @@
     kgain_ref,
     docc_ref,
     docr_ref,
-    dq_ref,
-    dkv_ref,
+    dqkv_ref,
     gains_ref,
     dk_ref,
     dv_ref,
@@ -247,7 +244,7 @@
         grad, gain_part = head_backward(
             qlin_ref[:, cols], qgain_ref[...], cosine, sine, dqa_ref[:, cols] * SCALE
         )
-        dq_ref[:, cols] = grad.astype(BF16)
+        dqkv_ref[here, cols] = grad.astype(BF16)
         gains_ref[0:1, :] += gain_part
 
     @pl.when(step == pl.num_programs(0) - 1)
@@ -257,8 +254,9 @@
             grad, gain_part = head_backward(
                 klin_ref[at, :], kgain_ref[...], cos_ref[at, :], sin_ref[at, :], dk_ref[at, :] * SCALE
             )
-            dkv_ref[at, :HD] = grad.astype(BF16)
-            dkv_ref[at, HD:] = dv_ref[at, :].astype(BF16)
+            qw = heads * HD
+            dqkv_ref[at, qw : qw + HD] = grad.astype(BF16)
+            dqkv_ref[at, qw + HD :] = dv_ref[at, :].astype(BF16)
             gains_ref[1:2, :] += gain_part
             return carry
 
@@ -293,10 +291,9 @@
             blk(1),
             whole((1, length)),
         ],
-        out_specs=[blk(qw), whole((length, 2 * HD)), whole((8, HD))],
+        out_specs=[whole((length, qw + 2 * HD)), whole((8, HD))],
         out_shape=[
-            shape((length, qw), BF16),
-            shape((length, 2 * HD), BF16),
+            shape((length, qw + 2 * HD), BF16),
             shape((8, HD), F32),
         ],
         scratch_shapes=[
@@ -305,6 +302,9 @@
             pltpu.VMEM((rows, qw), F32),
         ],
         compiler_params=pltpu.CompilerParams(vmem_limit_bytes=VMEM_LIMIT),
+        cost_estimate=pl.CostEstimate(
+            flops=60 * 10**9, transcendentals=0, bytes_accessed=30 * 2**20
+        ),
         name="attn_backward",
     )(branch, wout, attn, total, q, k, v, qlin, klin, cosine, sine, qgain, kgain, doc[:, None], doc[None, :])
 
@@ -345,7 +345,6 @@
 
 class Plane:
     def __init__(self, n):
-        self.n = n
         self.chips = n // 2
         self.me = lax.axis_index("ctx")
         self.core = self.me % 2
@@ -472,12 +471,82 @@
                 self.far[s].wait_send()
 
 
+class Product:
+    def __init__(self, plane, value, mine, other, landed, given, send, recv):
+        self.plane, self.value = plane, value
+        self.mine, self.other, self.landed, self.given = mine, other, landed, given
+        self.order = far_first(plane.chips) + [0]
+        self.across, self.far = {}, {}
+        for s in self.order:
+            self.across[s] = push(
+                given.at[s], other.at[s], send.at[s], recv.at[s], "ctx", plane.mate
+            )
+            slot = plane.chips + s
+            if s:
+                self.far[s] = push(
+                    mine.at[s], landed.at[s], send.at[slot], recv.at[slot], "ctx", plane.same(s)
+                )
+
+    def start(self):
+        plane = self.plane
+        width = self.mine.shape[2]
+        for s in self.order:
+            block = plane.same(s) + 1 - 2 * plane.core
+
+            def fill(at, s=s, block=block):
+                self.given[s, :, at] = self.value(block, at).astype(BF16)
+
+            by_cols(width, fill)
+            self.across[s].start()
+
+    def run(self):
+        plane, mine, other = self.plane, self.mine, self.other
+        width = mine.shape[2]
+        for s in self.order:
+            block = plane.same(s)
+            self.across[s].wait_recv()
+
+            def fill(at, s=s, block=block):
+                total = self.value(block, at) + other[s, :, at].astype(F32)
+                mine[s, :, at] = total.astype(BF16)
+
+            by_cols(width, fill)
+            if s:
+                self.far[s].start()
+        for s in self.order:
+            if s:
+                self.far[s].wait_recv()
+
+    def total(self, at):
+        value = self.mine[0, at, :].astype(F32)
+        for s in range(1, self.plane.chips):
+            value = value + self.landed[s, at, :].astype(F32)
+        return value
+
+    finish = Scatter.finish
+
+
+def by_cols(width, body):
+    span = 512
+
+    def one(index, carry):
+        body(pl.ds(pl.multiple_of(index * span, span), span))
+        return carry
+
+    lax.fori_loop(0, width // span, one, 0)
+
+
+def product_scratch(n, rows, width):
+    chips = n // 2
+    return [pltpu.VMEM((chips, rows, width), BF16)] * 4 + [DMA((n,)), DMA((n,))]
+
+
 def scatter_scratch(n, rows, width):
     chips = n // 2
     return [pltpu.VMEM((chips, rows, width), BF16)] * 3 + [DMA((n,)), DMA((n,)), DMA((chips,))]
 
 
-def comm_call(kernel, ident, name, outs, out_specs, in_specs, scratch, micros, *args):
+def comm_call(kernel, ident, outs, out_specs, in_specs, scratch, micros, *args):
     return pl.pallas_call(
         kernel,
         out_shape=outs,
@@ -490,7 +559,6 @@
         cost_estimate=pl.CostEstimate(
             flops=0, transcendentals=0, bytes_accessed=int(micros * 3.0e6)
         ),
-        name=name,
     )(*args)
 
 
@@ -578,7 +646,6 @@
     return comm_call(
         functools.partial(prep_kernel, n, n_dp),
         0,
-        "prep",
         [shape(cols.shape, cols.dtype), shape((n_dp, n) + small.shape, F32)],
         [ANY, VM],
         [ANY, VM],
@@ -595,7 +662,6 @@
     return comm_call(
         functools.partial(post_kernel, n, n_dp),
         1,
-        "post",
         [shape(cols.shape, cols.dtype), shape(tile, F32)],
         [ANY, VM],
         [ANY, VM],
@@ -639,7 +705,6 @@
     return comm_call(
         functools.partial(first_kernel, n),
         2,
-        "first",
         [many(x, BF16), many(grad, BF16), many(info, F32)],
         [ANY] * 3,
         [VM] * 4,
@@ -652,10 +717,16 @@
     )
 
 
-def middle_kernel(n, part_ref, x_ref, gain_ref, after_ref, all_ref, low, *scratch):
+def middle_kernel(n, attn_ref, wout_ref, x_ref, gain_ref, after_ref, all_ref, low, *scratch):
     plane = Plane(n)
     plane.meet()
-    sums = Scatter(plane, part_ref, *scratch[:6])
+    rows = x_ref.shape[0]
+
+    def value(block, at):
+        left = attn_ref[pl.ds(pl.multiple_of(block * rows, rows), rows), :]
+        return dot(left, wout_ref[:, at])
+
+    sums = Product(plane, value, *scratch[:6])
     sums.start()
     sums.run()
 
@@ -664,7 +735,7 @@
         after_ref[at, :] = value
         low[at, :] = (value * rms_parts(value) * gain_ref[...]).astype(BF16)
 
-    by_rows(x_ref.shape[0], norm)
+    by_rows(rows, norm)
     normed = Gather(plane, low, all_ref, *scratch[6:])
     normed.start()
     normed.forward()
@@ -672,18 +743,18 @@
     normed.finish()
 
 
-def middle(n, part, x, gain):
+def middle(n, attn, wout, x, gain):
     shape = jax.ShapeDtypeStruct
     return comm_call(
         functools.partial(middle_kernel, n),
         3,
-        "middle",
         [shape(x.shape, F32), shape((n,) + x.shape, BF16)],
         [VM, ANY],
-        [ANY, VM, VM],
-        [pltpu.VMEM(x.shape, BF16)] + scatter_scratch(n, *x.shape) + gather_sems(n),
-        95,
-        part,
+        [VM, VM, VM, VM],
+        [pltpu.VMEM(x.shape, BF16)] + product_scratch(n, *x.shape) + gather_sems(n),
+        105,
+        attn,
+        wout,
         x,
         gain,
     )
@@ -722,7 +793,6 @@
     return comm_call(
         functools.partial(turn_kernel, n),
         4,
-        "turn",
         [
             shape(after.shape, F32),
             shape((8, after.shape[1]), F32),
@@ -739,12 +809,20 @@
     )
 
 
-def last_kernel(n, part_ref, x_ref, mid_ref, gain_ref, out_ref, apart_ref, *scratch):
+def last_kernel(
+    n, grad_ref, wqkv_ref, x_ref, mid_ref, gain_ref, out_ref, apart_ref, *scratch
+):
     plane = Plane(n)
     plane.meet()
-    sums = Scatter(plane, part_ref, *scratch[:6])
+    apart_ref[...] = jnp.zeros_like(apart_ref)
+    rows = x_ref.shape[0]
+
+    def value(block, at):
+        left = grad_ref[pl.ds(pl.multiple_of(block * rows, rows), rows), :]
+        return dot(left, wqkv_ref[at, :], NT)
+
+    sums = Product(plane, value, *scratch[:6])
     sums.start()
-    apart_ref[...] = jnp.zeros_like(apart_ref)
     sums.run()
 
     def norm(at):
@@ -755,22 +833,22 @@
         apart_ref[0:1, :] += jnp.sum(grad * unit, axis=0, keepdims=True)
         out_ref[at, :] = mid_ref[at, :] + rms_back(grad, unit, inv, gain_ref[...])
 
-    by_rows(x_ref.shape[0], norm)
+    by_rows(rows, norm)
     sums.finish()
 
 
-def last(n, part, x, mid, gain):
+def last(n, grad, wqkv, x, mid, gain):
     shape = jax.ShapeDtypeStruct
     return comm_call(
         functools.partial(last_kernel, n),
         5,
-        "last",
         [shape(mid.shape, F32), shape((8, mid.shape[1]), F32)],
         [VM, VM],
-        [ANY, VM, VM, VM],
-        scatter_scratch(n, *mid.shape),
-        50,
-        part,
+        [VM] * 5,
+        product_scratch(n, *mid.shape),
+        60,
+        grad,
+        wqkv,
         x,
         mid,
         gain,
@@ -795,7 +873,6 @@
     return comm_call(
         functools.partial(close_kernel, n),
         6,
-        "close",
         jax.ShapeDtypeStruct(after.shape, BF16),
         VM,
         [ANY, VM],
@@ -804,6 +881,190 @@
         part,
         after,
     )
+
+
+def expert_kernel(chained, plan, z_ref, n2_ref, top_ref, prob_ref, *rest):
+    if chained:
+        moe_in, row_in = rest[:2]
+        rest = rest[2:]
+    sources, rest = rest[: len(plan)], rest[len(plan) :]
+    moe_ref, row_ref, grads_ref, wg_ref, wu_ref, wd_ref = rest[:6]
+    ag_ref, au_ref, ad_ref, stage, wsem, sem = rest[6:]
+    step = pl.program_id(0)
+    rows, width = n2_ref.shape
+    parts, cut, hidden = wd_ref.shape
+    weights = (wg_ref, wu_ref, wd_ref)
+
+    @pl.when(step == 0)
+    def _():
+        z = z_ref[0]
+        for source, (kind, amount, start) in zip(sources, plan):
+            count = source.shape[-2] // cut
+            for k in range(parts) if kind == "all" else [amount]:
+                if kind == "all":
+                    src, owner, wanted = source.at[k], k, None
+                elif kind == "up":
+                    src, owner, wanted = source, z - k, z >= k
+                else:
+                    src, owner, wanted = source, z + k, z + k < parts
+
+                def load(src=src, owner=owner, start=start, count=count):
+                    for piece in range(count):
+                        pltpu.make_async_copy(
+                            src.at[pl.ds(piece * cut, cut), :],
+                            weights[start + piece].at[owner],
+                            wsem.at[start + piece, owner],
+                        ).start()
+
+                if wanted is None:
+                    load()
+                else:
+                    pl.when(wanted)(load)
+        ag_ref[...] = jnp.zeros_like(ag_ref)
+        au_ref[...] = jnp.zeros_like(au_ref)
+        ad_ref[...] = jnp.zeros_like(ad_ref)
+        for index in range(3):
+            for owner in range(parts):
+                block = weights[index].at[owner]
+                pltpu.make_async_copy(block, block, wsem.at[index, owner]).wait()
+
+    n2 = n2_ref[...]
+    prob = prob_ref[...]
+    wg = wg_ref[...].reshape(width, hidden)
+    wu = wu_ref[...].reshape(width, hidden)
+    gate = dot(n2, wg)
+    up = dot(n2, wu)
+    sig = 1.0 / (1.0 + jnp.exp(-gate))
+    silu = gate * sig
+    act = (silu * up).astype(BF16)
+    act_grad = jnp.zeros((rows, hidden), F32)
+    for z in range(parts):
+        cols = slice(z * cut, (z + 1) * cut)
+        out = dot(act, wd_ref[z], NT).astype(BF16).astype(F32) * prob
+        if chained:
+            out = out + moe_in[:, cols].astype(F32)
+        moe_ref[:, cols] = out.astype(BF16)
+        route = (top_ref[:, cols].astype(F32) * prob).astype(BF16)
+        act_grad += dot(route, wd_ref[z])
+        ad_ref[z] += dot(route, act, TN)
+    gate_grad = (act_grad * up * sig * (1.0 + gate * (1.0 - sig))).astype(BF16)
+    up_grad = (act_grad * silu).astype(BF16)
+    row = dot(gate_grad, wg, NT) + dot(up_grad, wu, NT)
+    if chained:
+        row = row + row_in[...].astype(F32)
+    row_ref[...] = row.astype(BF16)
+    ag_ref[...] += dot(n2, gate_grad, TN).reshape(parts, cut, hidden)
+    au_ref[...] += dot(n2, up_grad, TN).reshape(parts, cut, hidden)
+
+    @pl.when(step == pl.num_programs(0) - 1)
+    def _():
+        copies = []
+        pieces = [
+            (acc, place, z) for z in range(parts) for place, acc in enumerate((ag_ref, au_ref, ad_ref))
+        ]
+        for index, (acc, place, z) in enumerate(pieces):
+            slot = index % 2
+            if index >= 2:
+                copies[index - 2].wait()
+            stage[slot] = acc[z].astype(BF16)
+            copies.append(
+                pltpu.make_async_copy(
+                    stage.at[slot], grads_ref.at[z, pl.ds(place * cut, cut), :], sem.at[slot]
+                )
+            )
+            copies[-1].start()
+        copies[-2].wait()
+        copies[-1].wait()
+
+
+def expert(z, n2, top, prob, n_dp, sources, before, rows):
+    length, width = n2.shape
+    cut = width // n_dp
+    hidden = sources[0][0].shape[-1]
+    blk = pl.BlockSpec((rows, width), lambda i: (i, 0))
+    col = pl.BlockSpec((rows, 1), lambda i: (i, 0))
+    shape = jax.ShapeDtypeStruct
+    plan = tuple(entry[1:] for entry in sources)
+    weight = pltpu.VMEM((n_dp, cut, hidden), BF16)
+    total = pltpu.VMEM((n_dp, cut, hidden), F32)
+    return pl.pallas_call(
+        functools.partial(expert_kernel, len(before) > 0, plan),
+        grid=(length // rows,),
+        in_specs=[pl.BlockSpec(memory_space=pltpu.SMEM), blk, blk, col]
+        + [blk] * len(before)
+        + [ANY] * len(sources),
+        out_specs=[blk, blk, ANY],
+        out_shape=[
+            shape((length, width), BF16),
+            shape((length, width), BF16),
+            shape((n_dp, 3 * cut, hidden), BF16),
+        ],
+        scratch_shapes=[weight] * 3
+        + [total] * 3
+        + [pltpu.VMEM((2, cut, hidden), BF16), DMA((3, n_dp)), DMA((2,))],
+        compiler_params=pltpu.CompilerParams(vmem_limit_bytes=VMEM_LIMIT),
+        cost_estimate=pl.CostEstimate(
+            flops=18 * length * width * hidden,
+            transcendentals=length * hidden,
+            bytes_accessed=5 * length * width * 2,
+        ),
+        name="expert",
+    )(z, n2, top, prob, *before, *[entry[0] for entry in sources])
+
+
+def pack_kernel(up_ref, down_ref, out_ref):
+    cut = up_ref.shape[0]
+    out_ref[:cut, :] = up_ref[...]
+    out_ref[cut:, :] = jnp.transpose(down_ref[...].astype(F32)).astype(BF16)
+
+
+def pack(w_up, w_down):
+    cut, hidden = w_up.shape
+    return pl.pallas_call(
+        pack_kernel,
+        in_specs=[VM] * 2,
+        out_specs=VM,
+        out_shape=jax.ShapeDtypeStruct((2 * cut, hidden), BF16),
+        name="pack",
+    )(w_up, w_down)
+
+
+def unpack_kernel(own, *refs):
+    gate_ref, up_ref, down_ref = refs[own:]
+    cut = gate_ref.shape[1]
+    for e in range(own):
+        gate_ref[e] = refs[e][:cut, :].astype(F32)
+        up_ref[e] = refs[e][cut : 2 * cut, :].astype(F32)
+        down_ref[e] = jnp.transpose(refs[e][2 * cut :, :].astype(F32))
+
+
+def unpack(grads):
+    own = len(grads)
+    rows, hidden = grads[0].shape
+    cut = rows // 3
+    shape = jax.ShapeDtypeStruct
+    return pl.pallas_call(
+        functools.partial(unpack_kernel, own),
+        in_specs=[VM] * own,
+        out_specs=[VM] * 3,
+        out_shape=[
+            shape((own, cut, hidden), F32),
+            shape((own, cut, hidden), F32),
+            shape((own, hidden, cut), F32),
+        ],
+        compiler_params=pltpu.CompilerParams(vmem_limit_bytes=VMEM_LIMIT),
+        name="unpack",
+    )(*grads)
+
+
+def line_hop(block_up, block_down, n_dp):
+    up = [(i, i + 1) for i in range(n_dp - 1)]
+    down = [(i + 1, i) for i in range(n_dp - 1)]
+    return lax.ppermute(block_up, "dp", up), lax.ppermute(block_down, "dp", down)
+
+
+def after_of(value, *others):
+    return lax.optimization_barrier((value,) + others)[0]
 
 
 def scatter_dp(partial):
@@ -861,7 +1122,8 @@
     gain_key = small[:, 2 * cut + hcut : kinds].reshape(1, HD)
     wqkv = lax.all_gather(cols.reshape(n_ctx * depth, qw + 2 * HD), "dp", axis=0, tiled=True)
     forth = [(c * n_dp + d, d * n_ctx + c) for d in range(n_dp) for c in range(n_ctx)]
-    wout = lax.all_gather(lax.ppermute(w_out, both, forth), "dp", axis=0, tiled=True)
+    wout = lax.ppermute(after_of(w_out, small), both, forth)
+    wout = lax.all_gather(wout, "dp", axis=0, tiled=True)
 
     inputs = layer_input.reshape(tokens, width)
     top_own = out_grad.reshape(tokens, width)
@@ -884,58 +1146,53 @@
     sine = jnp.sin(angles)
     cosine = jnp.concatenate([cosine, cosine], axis=1)
     sine = jnp.concatenate([-sine, sine], axis=1)
-    qlin, klin, q, k, v, attn, total, part = attn_forward(
-        normed, wqkv, wout, cosine, sine, gain_query, gain_key, doc, tokens
+    qlin, klin, q, k, v, attn, total = attn_forward(
+        normed, wqkv, cosine, sine, gain_query, gain_key, doc, tokens
     )
     blocks = (n_ctx, tokens, width)
-    after, normed2 = middle(n_ctx, part.reshape(blocks), inputs, gain_ffn)
+    after, normed2 = middle(n_ctx, attn, wout, inputs, gain_ffn)
     normed2 = normed2.reshape(length, width)
 
-    moe = 0.0
-    row_sum = 0.0
-    expert_grads = []
+    z = lax.axis_index("dp").astype(jnp.int32).reshape(1)
+    carried, expert_grads = (), []
     for e in range(own_e):
-        wg = lax.all_gather(w_gate[e], "dp", axis=0, tiled=True)
-        wu = lax.all_gather(w_up[e], "dp", axis=0, tiled=True)
-        wd = lax.all_gather(w_down[e], "dp", axis=0, tiled=False)
-        prob = my_probs[:, e : e + 1]
-        gate = dot(normed2, wg)
-        up = dot(normed2, wu)
-        sig = jax.nn.sigmoid(gate)
-        silu = gate * sig
-        act = (silu * up).astype(BF16)
-        out = jnp.einsum("rf,zfd->rzd", act, wd, preferred_element_type=F32).astype(BF16)
-        moe = moe + prob * out.reshape(length, width).astype(F32)
-        route_grad = (top_all.astype(F32) * prob).astype(BF16)
-        route3 = route_grad.reshape(length, n_dp, width // n_dp)
-        act_grad = jnp.einsum("rzd,zfd->rf", route3, wd, preferred_element_type=F32)
-        down_grad = jnp.einsum("rf,rzd->zfd", act, route3, preferred_element_type=F32)
-        gate_grad = (act_grad * up * sig * (1.0 + gate * (1.0 - sig))).astype(BF16)
-        up_grad = (act_grad * silu).astype(BF16)
-        row_sum = row_sum + dot(gate_grad, wg, NT) + dot(up_grad, wu, NT)
-        raw = (
-            dot(normed2, gate_grad, TN).astype(BF16),
-            dot(normed2, up_grad, TN).astype(BF16),
-            down_grad.astype(BF16),
+        pair = pack(w_up[e], w_down[e])
+        if e == 0:
+            one = lax.all_gather(w_gate[e], "dp", axis=0, tiled=False)
+            two = lax.all_gather(pair, "dp", axis=0, tiled=False)
+            sources = [(one, "all", 0, 0), (two, "all", 0, 1)]
+        else:
+            sources = []
+            for block, start in ((w_gate[e], 0), (pair, 1)):
+                sources.append((block, "up", 0, start))
+                up = down = after_of(block, after)
+                for hop in range(1, n_dp):
+                    if hop == 2:
+                        up, down = after_of(up, *carried), after_of(down, *carried)
+                    up, down = line_hop(up, down, n_dp)
+                    sources += [(up, "up", hop, start), (down, "down", hop, start)]
+        moe, rows_grad, grads = expert(
+            z, normed2, top_all, my_probs[:, e : e + 1], n_dp, sources, carried, tokens
         )
-        raw, normed2, top_all = lax.optimization_barrier((raw, normed2, top_all))
-        expert_grads.append((scatter_dp(raw[0]), scatter_dp(raw[1]), scatter_dp(raw[2])[0]))
+        carried = (moe, rows_grad)
+        grads = grads.reshape(3 * width, w_gate.shape[2])
+        expert_grads.append(lax.psum_scatter(grads, "dp", scatter_dimension=0, tiled=True))
     mid, ffn_part, branch = turn(
-        n_ctx, row_sum.astype(BF16).reshape(blocks), after, top_own, gain_ffn
+        n_ctx, rows_grad.reshape(blocks), after, top_own, gain_ffn
     )
     branch = branch.reshape(length, width)
-    layer_output = close(n_ctx, moe.astype(BF16).reshape(blocks), after)
-
-    dq, dkv, gains = attn_backward(
+    layer_output = close(n_ctx, moe.reshape(blocks), after)
+
+    out_w = dot(attn, branch, TN).astype(BF16)
+    out_w = scatter_dp(out_w)
+    dqkv, gains = attn_backward(
         branch, wout, attn, total, q, k, v, qlin, klin, cosine, sine, gain_query, gain_key, doc, tokens
     )
-    dqkv = jnp.concatenate([dq, dkv], axis=1)
-    normed_grad = dot(dqkv, wqkv, NT).astype(BF16).reshape(blocks)
-    input_grad, attn_part = last(n_ctx, normed_grad, inputs, mid, gain_attn)
-
-    out_w = scatter_dp(dot(attn, branch, TN))
+    input_grad, attn_part = last(n_ctx, dqkv, wqkv, inputs, mid, gain_attn)
+
     out_w = lax.ppermute(out_w, both, [(b, a) for a, b in forth]).astype(F32)
-    qkv_w = scatter_dp(dot(normed, dqkv, TN))
+    qkv_w = dot(normed, dqkv, TN).astype(BF16)
+    qkv_w = scatter_dp(qkv_w)
     n_all = n_dp * n_ctx
     packed = jnp.concatenate(
         [
@@ -955,7 +1212,7 @@
     key_w = kv_w[:, :, :HD].transpose(1, 0, 2).reshape(depth, KV * HD)
     value_w = kv_w[:, :, HD:].transpose(1, 0, 2).reshape(depth, KV * HD)
 
-    stack = lambda index: jnp.stack([g[index] for g in expert_grads]).astype(F32)
+    gate_w, up_w, down_w = unpack(expert_grads)
     return (
         layer_output.reshape(1, tokens, width),
         input_grad.reshape(1, tokens, width),
@@ -967,9 +1224,9 @@
         key_w,
         value_w,
         out_w,
-        stack(0),
-        stack(1),
-        stack(2),
+        gate_w,
+        up_w,
+        down_w,
     )
 
 
@@ -1009,6 +1266,7 @@
         P("ctx", "dp", None),
         P("ctx", None, "dp"),
     )
+
     return jax.shard_map(
         per_device, mesh=mesh, in_specs=in_specs, out_specs=out_specs, check_vma=False
     )

time: 1240 us -> 1300 us (1.048)
  waiting for transfers between devices: 137 us -> 406 us
  matrix products: 253 us -> 20.5 us
  Pallas kernels: 593 us -> 762 us
  local copies, waits for them, and re-layouts: 175 us -> 27 us
  starting transfers between devices: 9.02 us -> 46.5 us
  other arithmetic: 44.7 us -> 12.3 us
    reduce_scatter x0 -> x2, waiting for transfers between devices: none -> 196 us  [per_device(): lax.psum_scatter(grads, 'dp', scatter_dimension=0, tiled=True)]
    dot_general x15 -> x2, matrix products: 187 us -> 20.5 us  [dot(): lax.dot_general(left, right, (dims, ((), ())), preferred_element_type=F32)]
    pallas_call x0 -> x5, Pallas kernels: none -> 163 us  [the longest x2 150 us: expert(): pl.pallas_call(functools.partial(expert_kernel, len(before) > 0, plan), g...]
    convert_element_type x7 -> x0, local copies, waits for them, and re-layouts: 144 us -> none  [the longest x4 92.6 us: per_device(): moe = moe + prob * out.reshape(length, width).astype(F32)]
    ppermute x1 -> x13, waiting for transfers between devices: 23.4 us -> 152 us  [the longest x6 53.2 us: line_hop(): lax.ppermute(block_up, 'dp', up)]
    reduce_scatter x8 -> x2, waiting for transfers between devices: 93.5 us -> 0.02 us  [scatter_dp(): lax.psum_scatter(partial.astype(BF16), 'dp', scatter_dimension=0, tiled=T...]
    dot_general x6 -> x0, matrix products: 66.6 us -> none  [the longest x2 25 us: per_device(): act_grad = jnp.einsum('rzd,zfd->rf', route3, wd, preferred_element_type=F32)]
    ppermute x1, waiting for transfers between devices: 0.01 us -> 56.2 us  [per_device(): out_w = lax.ppermute(out_w, both, [(b, a) for a, b in forth]).astype(F32)]
  transfers between devices with their start and end apart: 18 -> 22, of which waited for: 4 -> 8; matrix products, arithmetic and copies ran while one was open for 33% -> 3% of each run, Pallas kernels for 39% -> 43%
where the time goes in v2:
time: 1300 us; the launch traced here: 1290 us
  Pallas kernels  762 us (59%)
  waiting for transfers between devices  406 us (31%)
  starting transfers between devices  46.5 us (4%)
  local copies, waits for them, and re-layouts  27 us (2%)
  matrix products  20.5 us (2%)
  between operations  15 us (1%)
    pallas_call x7, Pallas kernels, comm_call(): pl.pallas_call(kernel, out_shape=outs, in_specs=in_specs, out_specs=out_s...  498 us
    reduce_scatter x2, waiting for transfers between devices, per_device(): lax.psum_scatter(grads, 'dp', scatter_dimension=0, tiled=True)  196 us
    pallas_call x2, Pallas kernels, expert(): pl.pallas_call(functools.partial(expert_kernel, len(before) > 0, plan), g...  150 us
    pallas_call x1, Pallas kernels, attn_backward(): pl.pallas_call(functools.partial(attn_backward_kernel, heads, MOST // row...  65.3 us
    ppermute x1, waiting for transfers between devices, per_device(): out_w = lax.ppermute(out_w, both, [(b, a) for a, b in forth]).astype(F32)  56.2 us
    ppermute x6, waiting for transfers between devices, line_hop(): lax.ppermute(block_up, 'dp', up)  53.2 us
    ppermute x1, waiting for transfers between devices, per_device(): wout = lax.ppermute(after_of(w_out, small), both, forth)  51.6 us
    ppermute x6, waiting for transfers between devices, line_hop(): lax.ppermute(block_down, 'dp', down)  46.9 us
  transfers between devices with their start and end apart: 22, of which 8 were waited for; matrix products, arithmetic and copies ran while one was open for 3% of the time, Pallas kernels for 43%

profile of v2, /device:TPU:14, one launch (start us, length us, event | category | flops | bytes accessed | tf_op | source)
XLA Modules:
  0.0 1289.6 jit_solution(1086614256079430337)
XLA Ops:
  11.7 14.2 %shard_map.255 = (bf16[8,64,768]{2,1,0:T(8,128)(2,1)}, f32[4,8,8,128]{3,2,1,0:T(8,128)}) custom-call(bf16[8,64,768]{2,1,0:T(8,128)(2,1)} %maximum_bitcast_fusion.cols_ref, f32[8,128]{1,0:T(8,128)} %fusion.11.small_ref), custom_call_target="tpu_custom_call" | custom-call | bytes 24000000 | tf_op jit(solution)/shard_map/pallas_call | solution.py:550
  27.1 3.0 collective-permute-start
  30.1 51.6 %collective-permute-done = bf16[128,2048]{1,0:T(8,128)(2,1)} collective-permute-done((bf16[128,2048]{1,0:T(8,128)(2,1)}, bf16[128,2048]{1,0:T(8,128)(2,1)}, u32[]{:S(2)}, u32[]{:S(2)}) %collective-permute-start) | collective-permute-done | bytes 524320 | tf_op jit(solution)/shard_map/ppermute | solution.py:1125
  81.8 1.3 slice_bitcast_fusion.2
  83.1 1.2 slice_bitcast_fusion.1
  85.0 1.2 slice_bitcast_fusion
  86.3 2.8 pack.2
  92.8 104.0 %shard_map.256 = (bf16[8,256,2048]{2,1,0:T(8,128)(2,1)}, bf16[8,256,2048]{2,1,0:T(8,128)(2,1)}, f32[8,24,256]{2,1,0:T(8,128)}) custom-call(bf16[256,2048]{1,0:T(8,128)(2,1)} %bitcast.95, f32[1,2048]{1,0:T(1,128)} %reshape.168.gain_ref, bf16[256,2048]{1,0:T(8,128)(2,1)} %bitcast.100, f32[24,256]{1,0:T(8,128)} %maximum_maximum_fusion.info_ref), custom_call_target="tpu_custom_call" | custom-call | bytes 270000000 | tf_op jit(solution)/shard_map/pallas_call | solution.py:550
  198.8 1.3 copy.69.docc_ref
  200.2 2.8 pack.3.rest_9_
  203.0 3.9 fusion.2
  206.9 1.9 pad_maximum_fusion
  208.8 1.7 fusion.12
  210.5 36.7 %attn_forward.1 = (f32[2048,512]{1,0:T(8,128)}, f32[2048,128]{1,0:T(8,128)}, bf16[2048,512]{1,0:T(8,128)(2,1)}, bf16[2048,128]{1,0:T(8,128)(2,1)}, bf16[2048,128...) custom-call(bf16[2048,2048]{1,0:T(8,128)(2,1)} %bitcast.123, ...), custom_call_target="tpu_custom_call" | custom-call | flops 35000000512 | bytes 31457280 | tf_op jit(solution)/shard_map/attn_forward/pallas_call | solution.py:130
  247.2 113.9 %shard_map.257 = (f32[256,2048]{1,0:T(8,128)}, bf16[8,256,2048]{2,1,0:T(8,128)(2,1)}) custom-call(bf16[2048,512]{1,0:T(8,128)(2,1)} %get-tuple-element.56.attn_ref, bf16[512,2048]{1,0:T(8,128)(2,1)} %all-gather.8.cloned.1.call-done.wout_ref, bf16[256,2048]{1,0:T(8,128)(2,1)} %bitcast.96, f32[1,2048]{1,0:T(1,128)} %reshape.174.gain_ref), custom_call_target="tpu_custom_call" | custom-call | bytes 315000000 | tf_op jit(solution)/shard_map/pallas_call | solution.py:550
  361.1 8.6 collective-permute-start.8
  369.7 2.4 collective-permute-start.7
  372.2 74.4 %expert.2 = (bf16[2048,2048]{1,0:T(8,128)(2,1)}, bf16[2048,2048]{1,0:T(8,128)(2,1)}, bf16[4,1536,768]{2,1,0:T(8,128)(2,1)}) custom-call(s32[1]{0:T(128)} %bitcast.z_ref, bf16[2048,2048]{1,0:T(8,128)(2,1)} %bitcast.127, bf16[2048,2048]{1,0:T(8,128)(2,1)} %bitcast.125, f32[2048,1]{1,0:T(8,128)} %get-tuple-element.99.prob_ref, ...), custom_call_target="tpu_custom_call" | custom-call | flops 57982058496 | bytes 41943040 | tf_op jit(solution)/shard_map/expert/pallas_call | solution.py:990
  446.6 1.9 collective-permute-start.9
  448.6 4.5 collective-permute-start.10
  453.1 1.9 collective-permute-start.2
  455.0 3.9 collective-permute-start.1
  458.9 45.0 %collective-permute-done.2.rest_4_ = bf16[512,768]{1,0:T(8,128)(2,1)S(1)} collective-permute-done((bf16[512,768]{1,0:T(8,128)(2,1)S(1)}, bf16[512,768]{1,0:T(8,128)(2,1)S(1)}, u32[]{:S(2)}, u32[]{:S(2)}) %collective-permute-start.2) | collective-permute-done | bytes 786464 | tf_op jit(solution)/shard_map/ppermute | solution.py:1063
  503.9 1.9 collective-permute-start.3
  505.9 4.0 collective-permute-start.4
  509.9 1.9 collective-permute-start.11
  511.8 4.0 collective-permute-start.12
  515.8 10.4 collective-permute-done.3.rest_5_
  526.2 1.9 collective-permute-start.5
  528.2 4.1 collective-permute-start.6
  532.3 42.7 %collective-permute-done.5.rest_7_ = bf16[512,768]{1,0:T(8,128)(2,1)S(1)} collective-permute-done((bf16[512,768]{1,0:T(8,128)(2,1)S(1)}, bf16[512,768]{1,0:T(8,128)(2,1)S(1)}, u32[]{:S(2)}, u32[]{:S(2)}) %collective-permute-start.5) | collective-permute-done | bytes 786464 | tf_op jit(solution)/shard_map/ppermute | solution.py:1063
  575.1 1.9 collective-permute-done.6.rest_8_
  577.9 1.2 copy-done.22
  579.2 75.8 %expert.3 = (bf16[2048,2048]{1,0:T(8,128)(2,1)}, bf16[2048,2048]{1,0:T(8,128)(2,1)}, bf16[4,1536,768]{2,1,0:T(8,128)(2,1)}) custom-call(s32[1]{0:T(128)} %bitcast.z_ref, bf16[2048,2048]{1,0:T(8,128)(2,1)} %bitcast.128, bf16[2048,2048]{1,0:T(8,128)(2,1)} %bitcast.126, f32[2048,1]{1,0:T(8,128)} %get-tuple-element.100.prob_ref, ...), custom_call_target="tpu_custom_call" | custom-call | flops 57982058496 | bytes 41943040 | tf_op jit(solution)/shard_map/expert/pallas_call | solution.py:990
  655.0 109.9 %shard_map.259 = (f32[256,2048]{1,0:T(8,128)}, f32[8,2048]{1,0:T(8,128)}, bf16[8,256,2048]{2,1,0:T(8,128)(2,1)}) custom-call(bf16[8,256,2048]{2,1,0:T(8,128)(2,1)} %bitcast.98, f32[256,2048]{1,0:T(8,128)} %get-tuple-element.62.after_ref, bf16[256,2048]{1,0:T(8,128)(2,1)} %bitcast.101, f32[1,2048]{1,0:T(1,128)} %reshape.174.gain_ref), custom_call_target="tpu_custom_call" | custom-call | bytes 285000000 | tf_op jit(solution)/shard_map/pallas_call | solution.py:550
  764.9 9.1 convolution_convert_fusion.1
  774.3 65.3 %attn_backward.1 = (bf16[2048,768]{1,0:T(8,128)(2,1)}, f32[8,128]{1,0:T(8,128)}) custom-call(bf16[2048,2048]{1,0:T(8,128)(2,1)} %bitcast.130, bf16[512,2048]{1,0:T(8,128)(2,1)} %all-gather.8.cloned.1.call-done.wout_ref, bf16[2048,512]{1,0:T(8,128)(2,1)} %get-tuple-element.56.attn_ref, f32[2048,128]{1,0:T(8,128)} %get-tuple-element.72.total_ref, ...), custom_call_target="tpu_custom_call" | custom-call | flops 60000002048 | bytes 31457280 | tf_op jit(solution)/shard_map/attn_backward/pallas_call | solution.py:274
  839.5 11.4 convolution_convert_fusion
  852.4 55.4 %shard_map.258 = bf16[256,2048]{1,0:T(8,128)(2,1)} custom-call(bf16[8,256,2048]{2,1,0:T(8,128)(2,1)} %bitcast.99, f32[256,2048]{1,0:T(8,128)} %get-tuple-element.62.after_ref), custom_call_target="tpu_custom_call" | custom-call | bytes 150000000 | tf_op jit(solution)/shard_map/pallas_call | solution.py:550
  907.9 64.1 %shard_map.260 = (f32[256,2048]{1,0:T(8,128)}, f32[8,2048]{1,0:T(8,128)}) custom-call(bf16[2048,768]{1,0:T(8,128)(2,1)} %get-tuple-element.78.grad_ref, bf16[2048,768]{1,0:T(8,128)(2,1)} %all-gather.6.cloned.1.call-done.wqkv_ref, bf16[256,2048]{1,0:T(8,128)(2,1)} %bitcast.97, f32[256,2048]{1,0:T(8,128)} %get-tuple-element.79.mid_ref, ...), custom_call_target="tpu_custom_call" | custom-call | bytes 180000000 | tf_op jit(solution)/shard_map/pallas_call | solution.py:550
  972.0 1.9 collective-permute-start.13
  977.6 56.2 %collective-permute-done.13 = bf16[128,2048]{1,0:T(8,128)(2,1)S(1)} collective-permute-done((bf16[128,2048]{1,0:T(8,128)(2,1)}, bf16[128,2048]{1,0:T(8,128)(2,1)S(1)}, u32[]{:S(2)}, u32[]{:S(2)}) %collective-permute-start.13) | collective-permute-done | bytes 524320 | tf_op jit(solution)/shard_map/ppermute | solution.py:1193
  1034.9 36.4 %shard_map.261 = (bf16[8,64,768]{2,1,0:T(8,128)(2,1)}, f32[8,128]{1,0:T(8,128)}) custom-call(bf16[8,64,768]{2,1,0:T(8,128)(2,1)} %bitcast.107, f32[8,4,8,128]{3,2,1,0:T(8,128)} %copy_bitcast_fusion.5.small_ref), custom_call_target="tpu_custom_call" | custom-call | bytes 24000000 | tf_op jit(solution)/shard_map/pallas_call | solution.py:550
  1073.7 1.2 convert_bitcast_fusion
  1077.1 28.6 %reduce-scatter.9.cloned.1.call-done.refs_0_ = bf16[1536,768]{1,0:T(8,128)(2,1)} async-done(((bf16[6144,768]{1,0:T(8,128)(2,1)}), bf16[1536,768]{1,0:T(8,128)(2,1)}) %reduce-scatter.9.cloned.1.call-update) | async-done | bytes 2359312 | tf_op jit(solution)/shard_map/reduce_scatter | solution.py:1179
  1105.7 167.7 %reduce-scatter.11.cloned.1.call-done.refs_1_ = bf16[1536,768]{1,0:T(8,128)(2,1)} async-done(((bf16[6144,768]{1,0:T(8,128)(2,1)}), bf16[1536,768]{1,0:T(8,128)(2,1)}) %reduce-scatter.11.cloned.1.call-update) | async-done | bytes 2359312 | tf_op jit(solution)/shard_map/reduce_scatter | solution.py:1179
  1273.4 6.8 unpack.1
  1281.2 1.3 copy.100
  (129 shorter events, 25.1 us)
Async XLA Ops:
  7.2 3.8 copy-start.15
  7.2 3.8 copy-start.16
  7.2 3.8 copy-start.17
  7.2 3.8 copy-start.18
  7.2 203.2 %all-gather.6.cloned.1.call-start = ((), (), s32[]{:S(2)}) async-start(), calls=%async_computation.4 | async-start | bytes 3932160 | tf_op jit(solution)/shard_map/all_gather | solution.py:1123
  10.0 71.8 %copy-start.5 = (bf16[2,512,768]{2,1,0:T(8,128)(2,1)S(1)}, bf16[2,512,768]{2,1,0:T(8,128)(2,1)}, u32[]{:S(2)}) copy-start(bf16[2,512,768]{2,1,0:T(8,128)(2,1)} %param.28) | copy-start | bytes 4718596
  26.0 221.2 %all-gather.8.cloned.1.call-start = ((), (), s32[]{:S(2)}) async-start(), calls=%async_computation.5 | async-start | bytes 2621440 | tf_op jit(solution)/shard_map/all_gather | solution.py:1126
  26.0 57.1 %copy-start.6 = (bf16[2,512,768]{2,1,0:T(8,128)(2,1)S(1)}, bf16[2,512,768]{2,1,0:T(8,128)(2,1)}, u32[]{:S(2)}) copy-start(bf16[2,512,768]{2,1,0:T(8,128)(2,1)} %param.29) | copy-start | bytes 4718596
  27.1 54.6 %collective-permute-start = (bf16[128,2048]{1,0:T(8,128)(2,1)}, bf16[128,2048]{1,0:T(8,128)(2,1)}, u32[]{:S(2)}, u32[]{:S(2)}) collective-permute-start(bf16[128,2048]{1,0:T(8,128)(2,1)} %param.27), channel_id=1, source_target_pairs={{0,0},{4,1},{8,2},{12,3},{16,4},{20,5},{24,6},{28,7},{1,8},{5,9},{... | collective-permute-start | bytes 1572872 | tf_op jit(solution)/shard_map/ppermute | solution.py:1125
  81.7 290.4 %all-gather.10.cloned.1.call-start = ((), (), s32[]{:S(2)}) async-start(), calls=%async_computation.6 | async-start | bytes 3932160 | tf_op jit(solution)/shard_map/all_gather | solution.py:1161
  83.0 2.0 copy-start.7
  83.1 289.1 %all-gather.12.cloned.1.call-start = ((), (), s32[]{:S(2)}) async-start(), calls=%async_computation.11 | async-start | bytes 7864320 | tf_op jit(solution)/shard_map/all_gather | solution.py:1162
  86.3 2.9 copy-start.14
  86.3 5.8 copy-start.11
  86.3 5.8 copy-start.12
  89.1 882.8 %reduce-scatter.7.cloned.1.call-start = ((), (), s32[]{:S(2)}) async-start(), calls=%async_computation.8 | async-start | bytes 2621440 | tf_op jit(solution)/shard_map/reduce_scatter | solution.py:1071
  198.8 8.1 copy-start.10
  247.2 114.0 %copy-start.8 = (bf16[1024,768]{1,0:T(8,128)(2,1)S(1)}, bf16[1024,768]{1,0:T(8,128)(2,1)}, u32[]{:S(2)}) copy-start(bf16[1024,768]{1,0:T(8,128)(2,1)} %pack.3.rest_9_) | copy-start | bytes 4718596
  361.1 85.5 %collective-permute-start.8 = (bf16[1024,768]{1,0:T(8,128)(2,1)S(1)}, bf16[1024,768]{1,0:T(8,128)(2,1)}, u32[]{:S(2)}, u32[]{:S(2)}) collective-permute-start(bf16[1024,768]{1,0:T(8,128)(2,1)S(1)} %copy-done.8), channel_id=1, source_target_pairs={{8,0},{16,8},{24,16},{9,1},{17,9},{25,17},{10,2},{18,10},{26,18},{... | collective-permute-start | bytes 4718600 | tf_op jit(solution)/shard_map/ppermute | solution.py:1063
  369.7 76.9 %collective-permute-start.7 = (bf16[1024,768]{1,0:T(8,128)(2,1)S(1)}, bf16[1024,768]{1,0:T(8,128)(2,1)}, u32[]{:S(2)}, u32[]{:S(2)}) collective-permute-start(bf16[1024,768]{1,0:T(8,128)(2,1)S(1)} %copy-done.8), channel_id=1, source_target_pairs={{0,8},{8,16},{16,24},{1,9},{9,17},{17,25},{2,10},{10,18},{18,26},{... | collective-permute-start | bytes 4718600 | tf_op jit(solution)/shard_map/ppermute | solution.py:1063
  372.2 80.9 %copy-start.9 = (bf16[512,768]{1,0:T(8,128)(2,1)S(1)}, bf16[512,768]{1,0:T(8,128)(2,1)}, u32[]{:S(2)}) copy-start(bf16[512,768]{1,0:T(8,128)(2,1)} %get-tuple-element.63.rest_2_) | copy-start | bytes 2359300
  446.6 63.2 %collective-permute-start.9 = (bf16[1024,768]{1,0:T(8,128)(2,1)}, bf16[1024,768]{1,0:T(8,128)(2,1)S(1)}, u32[]{:S(2)}, u32[]{:S(2)}) collective-permute-start(bf16[1024,768]{1,0:T(8,128)(2,1)} %collective-permute-done.7.rest_10_), channel_id=1, source_target_pairs={{0,8},{8,16},{16,24},{1,9},{9,17},{17,25},{2,10},{10,18},{18,26},{... | collective-permute-start | bytes 4718600 | tf_op jit(solution)/shard_map/ppermute | solution.py:1063
  448.6 63.2 %collective-permute-start.10 = (bf16[1024,768]{1,0:T(8,128)(2,1)}, bf16[1024,768]{1,0:T(8,128)(2,1)S(1)}, u32[]{:S(2)}, u32[]{:S(2)}) collective-permute-start(bf16[1024,768]{1,0:T(8,128)(2,1)} %collective-permute-done.8.rest_11_), channel_id=1, source_target_pairs={{8,0},{16,8},{24,16},{9,1},{17,9},{25,17},{10,2},{18,10},{26,18},{... | collective-permute-start | bytes 4718600 | tf_op jit(solution)/shard_map/ppermute | solution.py:1063
  453.1 50.9 %collective-permute-start.2 = (bf16[512,768]{1,0:T(8,128)(2,1)S(1)}, bf16[512,768]{1,0:T(8,128)(2,1)S(1)}, u32[]{:S(2)}, u32[]{:S(2)}) collective-permute-start(bf16[512,768]{1,0:T(8,128)(2,1)S(1)} %copy-done.9), channel_id=1, source_target_pairs={{8,0},{16,8},{24,16},{9,1},{17,9},{25,17},{10,2},{18,10},{26,18},{... | collective-permute-start | bytes 2359304 | tf_op jit(solution)/shard_map/ppermute | solution.py:1063
  455.0 48.9 %collective-permute-start.1 = (bf16[512,768]{1,0:T(8,128)(2,1)S(1)}, bf16[512,768]{1,0:T(8,128)(2,1)S(1)}, u32[]{:S(2)}, u32[]{:S(2)}) collective-permute-start(bf16[512,768]{1,0:T(8,128)(2,1)S(1)} %copy-done.9), channel_id=1, source_target_pairs={{0,8},{8,16},{16,24},{1,9},{9,17},{17,25},{2,10},{10,18},{18,26},{... | collective-permute-start | bytes 2359304 | tf_op jit(solution)/shard_map/ppermute | solution.py:1063
  503.9 75.2 %copy-start.23 = (bf16[512,768]{1,0:T(8,128)(2,1)}, bf16[512,768]{1,0:T(8,128)(2,1)S(1)}, u32[]{:S(2)}) copy-start(bf16[512,768]{1,0:T(8,128)(2,1)S(1)} %collective-permute-done.2.rest_4_) | copy-start | bytes 2359300
  503.9 73.1 %copy-start.24 = (bf16[512,768]{1,0:T(8,128)(2,1)}, bf16[512,768]{1,0:T(8,128)(2,1)S(1)}, u32[]{:S(2)}) copy-start(bf16[512,768]{1,0:T(8,128)(2,1)S(1)} %collective-permute-done.1.rest_3_) | copy-start | bytes 2359300
  503.9 22.3 %collective-permute-start.3 = (bf16[512,768]{1,0:T(8,128)(2,1)S(1)}, bf16[512,768]{1,0:T(8,128)(2,1)S(1)}, u32[]{:S(2)}, u32[]{:S(2)}) collective-permute-start(bf16[512,768]{1,0:T(8,128)(2,1)S(1)} %collective-permute-done.1.rest_3_), channel_id=1, source_target_pairs={{0,8},{8,16},{16,24},{1,9},{9,17},{17,25},{2,10},{10,18},{18,26},{... | collective-permute-start | bytes 2359304 | tf_op jit(solution)/shard_map/ppermute | solution.py:1063
  505.9 22.3 %collective-permute-start.4 = (bf16[512,768]{1,0:T(8,128)(2,1)S(1)}, bf16[512,768]{1,0:T(8,128)(2,1)S(1)}, u32[]{:S(2)}, u32[]{:S(2)}) collective-permute-start(bf16[512,768]{1,0:T(8,128)(2,1)S(1)} %collective-permute-done.2.rest_4_), channel_id=1, source_target_pairs={{8,0},{16,8},{24,16},{9,1},{17,9},{25,17},{10,2},{18,10},{26,18},{... | collective-permute-start | bytes 2359304 | tf_op jit(solution)/shard_map/ppermute | solution.py:1063
  509.8 69.3 %copy-start.19 = (bf16[1024,768]{1,0:T(8,128)(2,1)}, bf16[1024,768]{1,0:T(8,128)(2,1)S(1)}, u32[]{:S(2)}) copy-start(bf16[1024,768]{1,0:T(8,128)(2,1)S(1)} %collective-permute-done.9.rest_12_) | copy-start | bytes 4718596
  509.9 67.1 %collective-permute-start.11 = (bf16[1024,768]{1,0:T(8,128)(2,1)S(1)}, bf16[1024,768]{1,0:T(8,128)(2,1)S(1)}, u32[]{:S(2)}, u32[]{:S(2)}) collective-permute-start(bf16[1024,768]{1,0:T(8,128)(2,1)S(1)} %collective-permute-done.9.rest_12_), channel_id=1, source_target_pairs={{0,8},{8,16},{16,24},{1,9},{9,17},{17,25},{2,10},{10,18},{18,26},{... | collective-permute-start | bytes 4718600 | tf_op jit(solution)/shard_map/ppermute | solution.py:1063
  511.8 65.2 %copy-start.20 = (bf16[1024,768]{1,0:T(8,128)(2,1)}, bf16[1024,768]{1,0:T(8,128)(2,1)S(1)}, u32[]{:S(2)}) copy-start(bf16[1024,768]{1,0:T(8,128)(2,1)S(1)} %collective-permute-done.10.rest_13_) | copy-start | bytes 4718596
  511.8 65.2 %collective-permute-start.12 = (bf16[1024,768]{1,0:T(8,128)(2,1)S(1)}, bf16[1024,768]{1,0:T(8,128)(2,1)S(1)}, u32[]{:S(2)}, u32[]{:S(2)}) collective-permute-start(bf16[1024,768]{1,0:T(8,128)(2,1)S(1)} %collective-permute-done.10.rest_13_), channel_id=1, source_target_pairs={{8,0},{16,8},{24,16},{9,1},{17,9},{25,17},{10,2},{18,10},{26,18},{... | collective-permute-start | bytes 4718600 | tf_op jit(solution)/shard_map/ppermute | solution.py:1063
  526.2 50.8 %copy-start.25 = (bf16[512,768]{1,0:T(8,128)(2,1)}, bf16[512,768]{1,0:T(8,128)(2,1)S(1)}, u32[]{:S(2)}) copy-start(bf16[512,768]{1,0:T(8,128)(2,1)S(1)} %collective-permute-done.3.rest_5_) | copy-start | bytes 2359300
  526.2 48.8 %collective-permute-start.5 = (bf16[512,768]{1,0:T(8,128)(2,1)S(1)}, bf16[512,768]{1,0:T(8,128)(2,1)S(1)}, u32[]{:S(2)}, u32[]{:S(2)}) collective-permute-start(bf16[512,768]{1,0:T(8,128)(2,1)S(1)} %collective-permute-done.3.rest_5_), channel_id=1, source_target_pairs={{0,8},{8,16},{16,24},{1,9},{9,17},{17,25},{2,10},{10,18},{18,26},{... | collective-permute-start | bytes 2359304 | tf_op jit(solution)/shard_map/ppermute | solution.py:1063
  528.2 48.9 %copy-start.26 = (bf16[512,768]{1,0:T(8,128)(2,1)}, bf16[512,768]{1,0:T(8,128)(2,1)S(1)}, u32[]{:S(2)}) copy-start(bf16[512,768]{1,0:T(8,128)(2,1)S(1)} %collective-permute-done.4.rest_6_) | copy-start | bytes 2359300
  528.2 48.8 %collective-permute-start.6 = (bf16[512,768]{1,0:T(8,128)(2,1)S(1)}, bf16[512,768]{1,0:T(8,128)(2,1)S(1)}, u32[]{:S(2)}, u32[]{:S(2)}) collective-permute-start(bf16[512,768]{1,0:T(8,128)(2,1)S(1)} %collective-permute-done.4.rest_6_), channel_id=1, source_target_pairs={{8,0},{16,8},{24,16},{9,1},{17,9},{25,17},{10,2},{18,10},{26,18},{... | collective-permute-start | bytes 2359304 | tf_op jit(solution)/shard_map/ppermute | solution.py:1063
  575.1 2.0 copy-start.27
  577.0 2.2 copy-start.21
  655.0 109.9 %copy-start.3 = (bf16[2048,512]{1,0:T(8,128)(2,1)S(1)}, bf16[2048,512]{1,0:T(8,128)(2,1)}, u32[]{:S(2)}) copy-start(bf16[2048,512]{1,0:T(8,128)(2,1)} %get-tuple-element.56.attn_ref) | copy-start | bytes 6291460
  774.0 260.8 %reduce-scatter.5.cloned.1.call-start = ((), (), s32[]{:S(2)}) async-start(), calls=%async_computation.7 | async-start | bytes 3932160 | tf_op jit(solution)/shard_map/reduce_scatter | solution.py:1071
  850.9 254.8 %reduce-scatter.9.cloned.1.call-start = ((), (), s32[]{:S(2)}) async-start(), calls=%async_computation.9 | async-start | bytes 11796480 | tf_op jit(solution)/shard_map/reduce_scatter | solution.py:1179
  851.7 421.8 %reduce-scatter.11.cloned.1.call-start = ((), (), s32[]{:S(2)}) async-start(), calls=%async_computation.10 | async-start | bytes 11796480 | tf_op jit(solution)/shard_map/reduce_scatter | solution.py:1179
  972.0 61.8 %collective-permute-start.13 = (bf16[128,2048]{1,0:T(8,128)(2,1)}, bf16[128,2048]{1,0:T(8,128)(2,1)S(1)}, u32[]{:S(2)}, u32[]{:S(2)}) collective-permute-start(bf16[128,2048]{1,0:T(8,128)(2,1)} %reduce-scatter.7.cloned.1.call-done), channel_id=1, source_target_pairs={{0,0},{1,4},{2,8},{3,12},{4,16},{5,20},{6,24},{7,28},{8,1},{9,5},{... | collective-permute-start | bytes 1572872 | tf_op jit(solution)/shard_map/ppermute | solution.py:1193
  1072.3 3.6 copy-start.13
  1077.1 203.2 %copy-start.2 = (bf16[256,2048]{1,0:T(8,128)(2,1)S(1)}, bf16[256,2048]{1,0:T(8,128)(2,1)}, u32[]{:S(2)}) copy-start(bf16[256,2048]{1,0:T(8,128)(2,1)} %shard_map.258) | copy-start | bytes 3145732
  1077.1 204.1 %copy-start.4 = (f32[256,2048]{1,0:T(8,128)S(1)}, f32[256,2048]{1,0:T(8,128)}, u32[]{:S(2)}) copy-start(f32[256,2048]{1,0:T(8,128)} %get-tuple-element.80) | copy-start | bytes 6291460
  1280.2 2.3 copy-start.1
  (3 other events, 3.0 us)
Sparse Core Ops, SparseCore 0:
  26.1 78.3 all-gather.5
  106.1 46.4 all-gather.7
  154.1 61.3 all-gather.9
  217.5 113.3 all-gather.11
  774.1 42.1 reduce-scatter.6
  851.1 59.1 reduce-scatter.4
  912.6 193.0 reduce-scatter.8
  1108.1 165.3 reduce-scatter.10

commit v3 on v1

v3 whole, which is shorter than its diff:
```python
import functools
import math

import jax
import jax.numpy as jnp
from jax import lax
from jax.experimental import pallas as pl
from jax.experimental.pallas import tpu as pltpu
from jax.sharding import PartitionSpec as P


HQ = 32
KV = 4
HD = 128
TOP = 8
MOST = 1024
EPS = 1e-06
ROPE_BASE = 1000000.0
F32 = jnp.float32
BF16 = jnp.bfloat16
SCALE = 1.0 / math.sqrt(HD)
VMEM_LIMIT = 60 * 1024 * 1024


def dot(left, right, dims=((1,), (0,))):
    return lax.dot_general(left, right, (dims, ((), ())), preferred_element_type=F32)


NT = ((1,), (1,))
TN = ((0,), (0,))


def rms_parts(values):
    return lax.rsqrt(jnp.mean(values * values, axis=-1, keepdims=True) + EPS)


def rms_back(grad, unit, inv, gain):
    scaled = grad * gain
    return inv * (scaled - unit * jnp.mean(scaled * unit, axis=-1, keepdims=True))


def head_forward(lin, gain, cosine, sine):
    unit = lin * rms_parts(lin) * gain
    return unit * cosine + pltpu.roll(unit, HD // 2, 1) * sine


def head_backward(lin, gain, cosine, sine, rot_grad):
    grad = rot_grad * cosine + pltpu.roll(rot_grad * sine, HD // 2, 1)
    inv = rms_parts(lin)
    unit = lin * inv
    return rms_back(grad, unit, inv, gain), jnp.sum(grad * unit, axis=0, keepdims=True)


MESH = pl.DeviceIdType.MESH
ANY = pl.BlockSpec(memory_space=pl.ANY)
VM = pl.BlockSpec(memory_space=pltpu.VMEM)
DMA = pltpu.SemaphoreType.DMA
CHUNK = 32


def flip(index, mask, count):
    result, bit = 0, 1
    while bit < count:
        digit = (index // bit) % 2
        result = result + bit * ((1 - digit) if mask & bit else digit)
        bit *= 2
    return result


def push(src, dst, send, recv, axis, peer):
    return pltpu.make_async_remote_copy(
        src_ref=src,
        dst_ref=dst,
        send_sem=send,
        recv_sem=recv,
        device_id={axis: peer},
        device_id_type=MESH,
    )


def meet(peers):
    barrier = pltpu.get_barrier_semaphore()
    for axis, peer in peers:
        pl.semaphore_signal(barrier, inc=1, device_id={axis: peer}, device_id_type=MESH)
    pl.semaphore_wait(barrier, len(peers))


class Plane:
    def __init__(self, n):
        self.chips = n // 2
        self.me = lax.axis_index("ctx")
        self.core = self.me % 2
        self.chip = self.me // 2
        self.mate = self.me + 1 - 2 * self.core

    def same(self, s):
        return 2 * flip(self.chip, s, self.chips) + self.core

    def meet(self):
        meet([("ctx", self.same(s)) for s in range(1, self.chips)] + [("ctx", self.mate)])


def far_first(chips):
    return sorted(range(1, chips), key=lambda s: -bin(s).count("1"))


class Gather:
    def __init__(self, plane, src, out, send, recv, local):
        self.plane, self.out, self.send, self.recv = plane, out, send, recv
        self.own = pltpu.make_async_copy(src, out.at[plane.me], local)
        self.far = [
            push(src, out.at[plane.me], send.at[s], recv.at[s], "ctx", plane.same(s))
            for s in far_first(plane.chips)
        ]
        self.near = push(src, out.at[plane.me], send.at[0], recv.at[0], "ctx", plane.mate)

    def start(self):
        for copy in self.far:
            copy.start()
        self.near.start()
        self.own.start()

    def forward(self):
        plane, out = self.plane, self.out
        self.passed = []
        for s in sorted(range(1, plane.chips), key=lambda s: bin(s).count("1")):
            block = out.at[plane.same(s)]
            push(block, block, self.send.at[s], self.recv.at[s], "ctx", plane.mate).wait_recv()
            slot = plane.chips + s
            copy = push(block, block, self.send.at[slot], self.recv.at[slot], "ctx", plane.mate)
            copy.start()
            self.passed.append(copy)

    def finish(self):
        for copy in self.far:
            copy.wait_send()
        self.near.wait_send()
        self.near.wait_recv()
        for copy in self.passed:
            copy.wait_send()
            copy.wait_recv()
        self.own.wait()


def by_rows(rows, body):
    def one(index, carry):
        body(pl.ds(pl.multiple_of(index * CHUNK, CHUNK), CHUNK))
        return carry

    lax.fori_loop(0, rows // CHUNK, one, 0)


class SquareGather:
    def __init__(self, plane, src, out, send, recv, local):
        self.plane, self.out, self.send, self.recv = plane, out, send, recv
        half = src.shape[0] // 2
        self.halves = [pl.ds(0, half), pl.ds(half, half)]
        mine = out.at[plane.me]
        self.own = pltpu.make_async_copy(src, mine, local)
        self.near = push(src, mine, send.at[0], recv.at[0], "ctx", plane.mate)
        self.far = []
        for s, h in ((1, 0), (2, 1), (1, 1), (2, 0)):
            part, slot = self.halves[h], 2 * s + h
            self.far.append(
                push(
                    src.at[part, :],
                    mine.at[part, :],
                    send.at[slot],
                    recv.at[slot],
                    "ctx",
                    plane.same(s),
                )
            )

    def start(self):
        for copy in self.far:
            copy.start()
        self.near.start()
        self.own.start()

    def arrived(self, s, h):
        block = self.out.at[self.plane.same(s)].at[self.halves[h], :]
        slot = 2 * s + h
        push(block, block, self.send.at[slot], self.recv.at[slot], "ctx", self.plane.mate).wait_recv()
        return block

    def forward(self):
        plane = self.plane
        self.passed = []
        for s, h in ((1, 0), (2, 1)):
            block = self.arrived(s, h)
            slot = 6 + h
            copy = push(block, block, self.send.at[slot], self.recv.at[slot], "ctx", plane.same(3 - s))
            copy.start()
            self.far.append(copy)
        for s in (1, 2, 3):
            if s < 3:
                self.arrived(s, 2 - s)
            else:
                self.arrived(3, 0)
                self.arrived(3, 1)
            block, slot = self.out.at[plane.same(s)], 7 + s
            copy = push(block, block, self.send.at[slot], self.recv.at[slot], "ctx", plane.mate)
            copy.start()
            self.passed.append(copy)

    def finish(self):
        for copy in self.far:
            copy.wait_send()
        self.near.wait_send()
        self.near.wait_recv()
        for copy in self.passed:
            copy.wait_send()
            copy.wait_recv()
        self.own.wait()


def gather_of(plane, src, out, send, recv, local):
    kind = SquareGather if plane.chips == 4 else Gather
    return kind(plane, src, out, send, recv, local)


class Spread:
    def __init__(self, plane, mine, landed, send, recv):
        self.plane, self.mine, self.landed = plane, mine, landed
        self.square = plane.chips == 4
        self.order = [3, 1, 2, 0] if self.square else far_first(plane.chips) + [0]
        self.send, self.recv = send, recv
        self.sent = []
        half = mine.shape[1] // 2
        self.halves = [pl.ds(0, half), pl.ds(half, half)]

    def copy(self, s, h, to):
        part, slot = self.halves[h], 2 * s + h
        return push(
            self.mine.at[s].at[part, :],
            self.landed.at[s].at[part, :],
            self.send.at[slot],
            self.recv.at[slot],
            "ctx",
            self.plane.same(to),
        )

    def go(self, s, h, to):
        copy = self.copy(s, h, to)
        copy.start()
        self.sent.append(copy)

    def ready(self, s):
        if self.square:
            if s == 3:
                self.go(3, 0, 1)
                self.go(3, 1, 2)
            elif s == 1:
                self.go(1, 0, 1)
            elif s == 2:
                self.go(2, 1, 2)
        elif s:
            copy = push(
                self.mine.at[s],
                self.landed.at[s],
                self.send.at[s],
                self.recv.at[s],
                "ctx",
                self.plane.same(s),
            )
            copy.start()
            self.sent.append(copy)

    def settle(self):
        mine, landed = self.mine, self.landed
        half = mine.shape[1] // 2
        if not self.square:
            for copy in self.sent:
                copy.wait_recv()
            return
        for s, h in ((2, 0), (1, 1)):
            self.copy(3, h, 1).wait_recv()

            def add(at, s=s, h=h):
                rows = pl.ds(h * half + at.start, CHUNK)
                total = mine[s, rows, :].astype(F32) + landed[3, rows, :].astype(F32)
                mine[s, rows, :] = total.astype(BF16)

            by_rows(half, add)
            self.go(s, h, s)
        for s in (1, 2):
            for h in (0, 1):
                self.copy(s, h, s).wait_recv()

    def total(self, at):
        value = self.mine[0, at, :].astype(F32)
        for s in (1, 2) if self.square else range(1, self.plane.chips):
            value = value + self.landed[s, at, :].astype(F32)
        return value

    def finish(self):
        for copy in self.sent:
            copy.wait_send()


class Scatter:
    def __init__(self, plane, part, mine, other, landed, send, recv, send2, recv2, local):
        self.plane, self.mine, self.other = plane, mine, other
        self.spread = Spread(plane, mine, landed, send2, recv2)
        self.order = self.spread.order
        self.loads, self.across = {}, {}
        for s in self.order:
            block = plane.same(s)
            self.loads[s] = pltpu.make_async_copy(part.at[block], mine.at[s], local.at[s])
            self.across[s] = push(
                part.at[block + 1 - 2 * plane.core],
                other.at[s],
                send.at[s],
                recv.at[s],
                "ctx",
                plane.mate,
            )

    def start(self):
        for s in self.order:
            self.across[s].start()
            self.loads[s].start()

    def run(self):
        mine, other = self.mine, self.other
        for s in self.order:
            self.loads[s].wait()
            self.across[s].wait_recv()

            def add(at, s=s):
                total = mine[s, at, :].astype(F32) + other[s, at, :].astype(F32)
                mine[s, at, :] = total.astype(BF16)

            by_rows(mine.shape[1], add)
            self.spread.ready(s)
        self.spread.settle()

    def total(self, at):
        return self.spread.total(at)

    def finish(self):
        for s in self.order:
            self.across[s].wait_send()
        self.spread.finish()


class Product:
    def __init__(self, plane, value, mine, other, landed, given, send, recv, send2, recv2):
        self.plane, self.value = plane, value
        self.mine, self.other, self.given = mine, other, given
        self.spread = Spread(plane, mine, landed, send2, recv2)
        self.order = self.spread.order
        self.across = {
            s: push(given.at[s], other.at[s], send.at[s], recv.at[s], "ctx", plane.mate)
            for s in self.order
        }

    def start(self):
        plane = self.plane
        for s in self.order:
            block = plane.same(s) + 1 - 2 * plane.core

            def fill(at, s=s, block=block):
                self.given[s, :, at] = self.value(block, at).astype(BF16)

            by_cols(self.mine.shape[2], fill)
            self.across[s].start()

    def run(self):
        plane, mine, other = self.plane, self.mine, self.other
        for s in self.order:
            block = plane.same(s)
            self.across[s].wait_recv()

            def fill(at, s=s, block=block):
                total = self.value(block, at) + other[s, :, at].astype(F32)
                mine[s, :, at] = total.astype(BF16)

            by_cols(mine.shape[2], fill)
            self.spread.ready(s)
        self.spread.settle()

    total = Scatter.total
    finish = Scatter.finish


def by_cols(width, body):
    span = 512

    def one(index, carry):
        body(pl.ds(pl.multiple_of(index * span, span), span))
        return carry

    lax.fori_loop(0, width // span, one, 0)


def gather_sems(n):
    return [DMA((12 if n == 8 else n,)), DMA((12 if n == 8 else n,)), DMA(())]


def scatter_scratch(n, rows, width):
    chips = n // 2
    return (
        [pltpu.VMEM((chips, rows, width), BF16)] * 3
        + [DMA((chips,)), DMA((chips,)), DMA((n,)), DMA((n,))]
        + [DMA((chips,))]
    )


def product_scratch(n, rows, width):
    chips = n // 2
    return [pltpu.VMEM((chips, rows, width), BF16)] * 4 + [
        DMA((chips,)),
        DMA((chips,)),
        DMA((n,)),
        DMA((n,)),
    ]


def comm_call(kernel, ident, outs, out_specs, in_specs, scratch, micros, *args):
    return pl.pallas_call(
        kernel,
        out_shape=outs,
        in_specs=in_specs,
        out_specs=out_specs,
        scratch_shapes=scratch,
        compiler_params=pltpu.CompilerParams(
            collective_id=ident, has_side_effects=True, vmem_limit_bytes=VMEM_LIMIT
        ),
        cost_estimate=pl.CostEstimate(
            flops=0, transcendentals=0, bytes_accessed=int(micros * 3.0e6)
        ),
    )(*args)


def swap_all(n, src, out, send, recv, local):
    me = lax.axis_index("ctx")
    own = pltpu.make_async_copy(src.at[me], out.at[me], local)
    own.start()
    copies = []
    for s in range(n - 1, 0, -1):
        peer = flip(me, s, n)
        copies.append(push(src.at[peer], out.at[me], send.at[s], recv.at[s], "ctx", peer))
        copies[-1].start()
    return own, copies


def prep_kernel(n, n_dp, cols_ref, small_ref, out_ref, all_ref, *sems):
    send, recv, local, gsend, grecv, zsend, zrecv = sems
    me, row = lax.axis_index("ctx"), lax.axis_index("dp")
    meet(
        [("ctx", flip(me, s, n)) for s in range(1, n)]
        + [("dp", flip(row, s, n_dp)) for s in range(1, n_dp)]
    )
    all_ref[row, me] = small_ref[...]
    smalls = []
    for s in range(1, n):
        peer = flip(me, s, n)
        smalls.append(push(small_ref, all_ref.at[row, me], gsend.at[s], grecv.at[s], "ctx", peer))
        smalls[-1].start()
    own, copies = swap_all(n, cols_ref, out_ref, send, recv, local)
    for copy in smalls:
        copy.wait_recv()
    planes = []
    for s in range(1, n_dp):
        peer = flip(row, s, n_dp)
        planes.append(push(all_ref.at[row], all_ref.at[row], zsend.at[s], zrecv.at[s], "dp", peer))
        planes[-1].start()
    for copy in copies + planes:
        copy.wait_recv()
    for copy in copies + planes + smalls:
        copy.wait_send()
    own.wait()


def post_kernel(n, n_dp, cols_ref, small_ref, out_ref, sum_ref, first, mid, second, *sems):
    send, recv, local, gsend, grecv, zsend, zrecv = sems
    me, row = lax.axis_index("ctx"), lax.axis_index("dp")
    meet(
        [("ctx", flip(me, s, n)) for s in range(1, n)]
        + [("dp", flip(row, s, n_dp)) for s in range(1, n_dp)]
    )
    smalls = []
    for s in range(1, n):
        peer = flip(me, s, n)
        smalls.append(push(small_ref.at[peer], first.at[s], gsend.at[s], grecv.at[s], "ctx", peer))
        smalls[-1].start()
    own, copies = swap_all(n, cols_ref, out_ref, send, recv, local)
    value = small_ref[me]
    for copy, s in zip(smalls, range(1, n)):
        copy.wait_recv()
        value = value + first[s]
    mid[...] = value
    planes = []
    for s in range(1, n_dp):
        peer = flip(row, s, n_dp)
        planes.append(push(mid.at[peer], second.at[s], zsend.at[s], zrecv.at[s], "dp", peer))
        planes[-1].start()
    value = mid[row]
    for copy, s in zip(planes, range(1, n_dp)):
        copy.wait_recv()
        value = value + second[s]
    sum_ref[...] = value
    for copy in copies:
        copy.wait_recv()
    for copy in copies + planes + smalls:
        copy.wait_send()
    own.wait()


def swap_sems(n, n_dp):
    return [DMA((n,)), DMA((n,)), DMA(()), DMA((n,)), DMA((n,)), DMA((n_dp,)), DMA((n_dp,))]


def prep(n, n_dp, cols, small):
    shape = jax.ShapeDtypeStruct
    return comm_call(
        functools.partial(prep_kernel, n, n_dp),
        0,
        [shape(cols.shape, cols.dtype), shape((n_dp, n) + small.shape, F32)],
        [ANY, VM],
        [ANY, VM],
        swap_sems(n, n_dp),
        8,
        cols,
        small,
    )


def post(n, n_dp, cols, small):
    shape = jax.ShapeDtypeStruct
    tile = small.shape[2:]
    return comm_call(
        functools.partial(post_kernel, n, n_dp),
        1,
        [shape(cols.shape, cols.dtype), shape(tile, F32)],
        [ANY, VM],
        [ANY, VM],
        [
            pltpu.VMEM((n, n_dp) + tile, F32),
            pltpu.VMEM((n_dp,) + tile, F32),
            pltpu.VMEM((n_dp,) + tile, F32),
        ]
        + swap_sems(n, n_dp),
        8,
        cols,
        small,
    )


def first_kernel(n, x_ref, gain_ref, info_ref, nall_ref, iall_ref, low, *sems):
    plane = Plane(n)
    plane.meet()
    infos = Gather(plane, info_ref, iall_ref, *sems[0:3])
    infos.start()

    def norm(at):
        value = x_ref[at, :].astype(F32)
        low[at, :] = (value * rms_parts(value) * gain_ref[...]).astype(BF16)

    by_rows(x_ref.shape[0], norm)
    normed = gather_of(plane, low, nall_ref, *sems[3:6])
    normed.start()
    infos.forward()
    normed.forward()
    infos.finish()
    normed.finish()


def first(n, x, gain, info):
    shape = jax.ShapeDtypeStruct
    many = lambda array, kind: shape((n,) + array.shape, kind)
    return comm_call(
        functools.partial(first_kernel, n),
        2,
        [many(x, BF16), many(info, F32)],
        [ANY] * 2,
        [VM] * 3,
        [pltpu.VMEM(x.shape, BF16)] + [DMA((n,)), DMA((n,)), DMA(())] + gather_sems(n),
        50,
        x,
        gain,
        info,
    )


def middle_kernel(n, attn_ref, wout_ref, x_ref, gain_ref, after_ref, all_ref, low, *scratch):
    plane = Plane(n)
    plane.meet()
    rows = x_ref.shape[0]

    def value(block, at):
        left = attn_ref[pl.ds(pl.multiple_of(block * rows, rows), rows), :]
        return dot(left, wout_ref[:, at])

    sums = Product(plane, value, *scratch[:8])
    sums.start()
    sums.run()

    def norm(at):
        value = x_ref[at, :].astype(F32) + sums.total(at)
        after_ref[at, :] = value
        low[at, :] = (value * rms_parts(value) * gain_ref[...]).astype(BF16)

    by_rows(rows, norm)
    normed = gather_of(plane, low, all_ref, *scratch[8:])
    normed.start()
    normed.forward()
    sums.finish()
    normed.finish()


def middle(n, attn, wout, x, gain):
    shape = jax.ShapeDtypeStruct
    return comm_call(
        functools.partial(middle_kernel, n),
        3,
        [shape(x.shape, F32), shape((n,) + x.shape, BF16)],
        [VM, ANY],
        [VM, VM, VM, VM],
        [pltpu.VMEM(x.shape, BF16)] + product_scratch(n, *x.shape) + gather_sems(n),
        105,
        attn,
        wout,
        x,
        gain,
    )


def turn_kernel(
    n, part_ref, after_ref, grad_ref, gain_ref, mid_ref, fpart_ref, all_ref, low, *scratch
):
    plane = Plane(n)
    plane.meet()
    sums = Scatter(plane, part_ref, *scratch[:8])
    sums.start()
    fpart_ref[...] = jnp.zeros_like(fpart_ref)
    sums.run()

    def norm(at):
        value = after_ref[at, :]
        inv = rms_parts(value)
        unit = value * inv
        grad = sums.total(at)
        fpart_ref[0:1, :] += jnp.sum(grad * unit, axis=0, keepdims=True)
        mid = grad_ref[at, :].astype(F32) + rms_back(grad, unit, inv, gain_ref[...])
        mid_ref[at, :] = mid
        low[at, :] = mid.astype(BF16)

    by_rows(after_ref.shape[0], norm)
    branch = gather_of(plane, low, all_ref, *scratch[8:])
    branch.start()
    branch.forward()
    sums.finish()
    branch.finish()


def turn(n, part, after, grad, gain):
    shape = jax.ShapeDtypeStruct
    return comm_call(
        functools.partial(turn_kernel, n),
        4,
        [
            shape(after.shape, F32),
            shape((8, after.shape[1]), F32),
            shape((n,) + after.shape, BF16),
        ],
        [VM, VM, ANY],
        [ANY, VM, VM, VM],
        [pltpu.VMEM(after.shape, BF16)] + scatter_scratch(n, *after.shape) + gather_sems(n),
        95,
        part,
        after,
        grad,
        gain,
    )


def last_kernel(
    n, grad_ref, wqkv_ref, x_ref, mid_ref, gain_ref, out_ref, apart_ref, *scratch
):
    plane = Plane(n)
    plane.meet()
    apart_ref[...] = jnp.zeros_like(apart_ref)
    rows = x_ref.shape[0]

    def value(block, at):
        left = grad_ref[pl.ds(pl.multiple_of(block * rows, rows), rows), :]
        return dot(left, wqkv_ref[at, :], NT)

    sums = Product(plane, value, *scratch[:8])
    sums.start()
    sums.run()

    def norm(at):
        value = x_ref[at, :].astype(F32)
        inv = rms_parts(value)
        unit = value * inv
        grad = sums.total(at)
        apart_ref[0:1, :] += jnp.sum(grad * unit, axis=0, keepdims=True)
        out_ref[at, :] = mid_ref[at, :] + rms_back(grad, unit, inv, gain_ref[...])

    by_rows(rows, norm)
    sums.finish()


def last(n, grad, wqkv, x, mid, gain):
    shape = jax.ShapeDtypeStruct
    return comm_call(
        functools.partial(last_kernel, n),
        5,
        [shape(mid.shape, F32), shape((8, mid.shape[1]), F32)],
        [VM, VM],
        [VM] * 5,
        product_scratch(n, *mid.shape),
        60,
        grad,
        wqkv,
        x,
        mid,
        gain,
    )


def close_kernel(n, part_ref, after_ref, out_ref, *scratch):
    plane = Plane(n)
    plane.meet()
    sums = Scatter(plane, part_ref, *scratch[:8])
    sums.start()
    sums.run()

    def add(at):
        out_ref[at, :] = (after_ref[at, :] + sums.total(at)).astype(BF16)

    by_rows(after_ref.shape[0], add)
    sums.finish()


def close(n, part, after):
    return comm_call(
        functools.partial(close_kernel, n),
        6,
        jax.ShapeDtypeStruct(after.shape, BF16),
        VM,
        [ANY, VM],
        scatter_scratch(n, *after.shape),
        50,
        part,
        after,
    )


def attn_forward_kernel(
    n,
    heads,
    back,
    normed_ref,
    wqkv_ref,
    cos_ref,
    sin_ref,
    qgain_ref,
    kgain_ref,
    docc_ref,
    docr_ref,
    grad_ref,
    qlin_ref,
    klin_ref,
    q_ref,
    k_ref,
    v_ref,
    attn_ref,
    total_ref,
    gall_ref,
    acc_ref,
    sum_ref,
    *sems,
):
    step = pl.program_id(0)

    @pl.when(step == 0)
    def _():
        plane = Plane(n)
        plane.meet()
        gather_of(plane, grad_ref, gall_ref, *sems).start()

    rows = normed_ref.shape[0]
    lin = dot(normed_ref[...], wqkv_ref[...])
    here = pl.ds(step * rows, rows)
    cosine = cos_ref[...]
    sine = sin_ref[...]
    qw = heads * HD
    for head in range(heads):
        cols = slice(head * HD, (head + 1) * HD)
        part = lin[:, cols]
        qlin_ref[:, cols] = part
        q_ref[:, cols] = head_forward(part, qgain_ref[...], cosine, sine).astype(BF16)
    key_lin = lin[:, qw : qw + HD]
    klin_ref[...] = key_lin
    k_ref[here, :] = head_forward(key_lin, kgain_ref[...], cosine, sine).astype(BF16)
    v_ref[here, :] = lin[:, qw + HD :].astype(BF16)
    acc_ref[...] = jnp.zeros_like(acc_ref)
    sum_ref[...] = jnp.zeros_like(sum_ref)
    row_pos = step * rows + lax.broadcasted_iota(jnp.int32, (rows, rows), 0)
    col_off = lax.broadcasted_iota(jnp.int32, (rows, rows), 1)

    def one(block, carry):
        at = pl.ds(pl.multiple_of(block * rows, rows), rows)
        key = k_ref[at, :]
        val = v_ref[at, :]
        allowed = (docc_ref[...] == docr_ref[:, at]) & (block * rows + col_off <= row_pos)
        for head in range(heads):
            cols = slice(head * HD, (head + 1) * HD)
            score = dot(q_ref[:, cols], key, NT) * SCALE
            expo = jnp.where(allowed, jnp.exp(score), 0.0)
            folded = expo[:, :HD]
            for piece in range(1, rows // HD):
                folded = folded + expo[:, piece * HD : (piece + 1) * HD]
            sum_ref[:, cols] += folded
            acc_ref[:, cols] += dot(expo.astype(BF16), val)
        return carry

    lax.fori_loop(jnp.maximum(step - back, 0), step + 1, one, 0)
    lane = lax.broadcasted_iota(jnp.int32, (rows, HD), 1)
    totals = jnp.ones((rows, HD), F32)
    for head in range(heads):
        cols = slice(head * HD, (head + 1) * HD)
        total = jnp.sum(sum_ref[:, cols], axis=-1, keepdims=True)
        totals = jnp.where(lane == head, total, totals)
        attn_ref[:, cols] = (acc_ref[:, cols] / total).astype(BF16)
    total_ref[...] = totals

    @pl.when(step == pl.num_programs(0) - 1)
    def _():
        grads = gather_of(Plane(n), grad_ref, gall_ref, *sems)
        grads.forward()
        grads.finish()


def attn_forward(n, normed, wqkv, cosine, sine, qgain, kgain, doc, grad, rows):
    length, width = normed.shape
    qw = wqkv.shape[1] - 2 * HD
    heads = qw // HD
    blk = lambda cols: pl.BlockSpec((rows, cols), lambda i: (i, 0))
    whole = lambda shape: pl.BlockSpec(shape, lambda i: (0, 0))
    shape = jax.ShapeDtypeStruct
    return pl.pallas_call(
        functools.partial(attn_forward_kernel, n, heads, MOST // rows),
        grid=(length // rows,),
        in_specs=[
            blk(width),
            whole(wqkv.shape),
            blk(HD),
            blk(HD),
            whole((1, HD)),
            whole((1, HD)),
            blk(1),
            whole((1, length)),
            whole(grad.shape),
        ],
        out_specs=[
            blk(qw),
            blk(HD),
            blk(qw),
            whole((length, HD)),
            whole((length, HD)),
            blk(qw),
            blk(HD),
            ANY,
        ],
        out_shape=[
            shape((length, qw), F32),
            shape((length, HD), F32),
            shape((length, qw), BF16),
            shape((length, HD), BF16),
            shape((length, HD), BF16),
            shape((length, qw), BF16),
            shape((length, HD), F32),
            shape((n,) + grad.shape, BF16),
        ],
        scratch_shapes=[pltpu.VMEM((rows, qw), F32), pltpu.VMEM((rows, qw), F32)]
        + gather_sems(n),
        compiler_params=pltpu.CompilerParams(
            collective_id=7, has_side_effects=True, vmem_limit_bytes=VMEM_LIMIT
        ),
        cost_estimate=pl.CostEstimate(
            flops=35 * 10**9, transcendentals=0, bytes_accessed=30 * 2**20
        ),
        name="attn_forward",
    )(normed, wqkv, cosine, sine, qgain, kgain, doc[:, None], doc[None, :], grad)


def attn_backward_kernel(
    heads,
    back,
    branch_ref,
    wout_ref,
    attn_ref,
    total_ref,
    q_ref,
    k_ref,
    v_ref,
    qlin_ref,
    klin_ref,
    cos_ref,
    sin_ref,
    qgain_ref,
    kgain_ref,
    docc_ref,
    docr_ref,
    dqkv_ref,
    gains_ref,
    dk_ref,
    dv_ref,
    dqa_ref,
):
    step = pl.program_id(0)
    rows = branch_ref.shape[0]
    here = pl.ds(pl.multiple_of(step * rows, rows), rows)

    @pl.when(step == 0)
    def _():
        gains_ref[...] = jnp.zeros_like(gains_ref)

    dk_ref[here, :] = jnp.zeros((rows, HD), F32)
    dv_ref[here, :] = jnp.zeros((rows, HD), F32)
    dqa_ref[...] = jnp.zeros_like(dqa_ref)
    attn_grad = dot(branch_ref[...], wout_ref[...], NT)
    grads = []
    shifts = []
    for head in range(heads):
        cols = slice(head * HD, (head + 1) * HD)
        part = attn_grad[:, cols]
        inv_total = 1.0 / total_ref[:, head : head + 1]
        delta = jnp.sum(part * attn_ref[:, cols].astype(F32), axis=-1, keepdims=True)
        grads.append((part * inv_total).astype(BF16))
        shifts.append(delta * inv_total)
    row_pos = step * rows + lax.broadcasted_iota(jnp.int32, (rows, rows), 0)
    col_off = lax.broadcasted_iota(jnp.int32, (rows, rows), 1)

    def one(block, carry):
        at = pl.ds(pl.multiple_of(block * rows, rows), rows)
        key = k_ref[at, :]
        val = v_ref[at, :]
        allowed = (docc_ref[...] == docr_ref[:, at]) & (block * rows + col_off <= row_pos)
        dk = jnp.zeros((rows, HD), F32)
        dv = jnp.zeros((rows, HD), F32)
        for head in range(heads):
            cols = slice(head * HD, (head + 1) * HD)
            query = q_ref[:, cols]
            score = dot(query, key, NT) * SCALE
            expo = jnp.where(allowed, jnp.exp(score), 0.0)
            prod = dot(grads[head], val, NT)
            score_grad = (expo * (prod - shifts[head])).astype(BF16)
            dv += dot(expo.astype(BF16), grads[head], TN)
            dk += dot(score_grad, query, TN)
            dqa_ref[:, cols] += dot(score_grad, key)
        dk_ref[at, :] += dk
        dv_ref[at, :] += dv
        return carry

    lax.fori_loop(jnp.maximum(step - back, 0), step + 1, one, 0)
    cosine = cos_ref[here, :]
    sine = sin_ref[here, :]
    for head in range(heads):
        cols = slice(head * HD, (head + 1) * HD)
        grad, gain_part = head_backward(
            qlin_ref[:, cols], qgain_ref[...], cosine, sine, dqa_ref[:, cols] * SCALE
        )
        dqkv_ref[here, cols] = grad.astype(BF16)
        gains_ref[0:1, :] += gain_part

    @pl.when(step == pl.num_programs(0) - 1)
    def _():
        def finish(block, carry):
            at = pl.ds(pl.multiple_of(block * rows, rows), rows)
            grad, gain_part = head_backward(
                klin_ref[at, :], kgain_ref[...], cos_ref[at, :], sin_ref[at, :], dk_ref[at, :] * SCALE
            )
            qw = heads * HD
            dqkv_ref[at, qw : qw + HD] = grad.astype(BF16)
            dqkv_ref[at, qw + HD :] = dv_ref[at, :].astype(BF16)
            gains_ref[1:2, :] += gain_part
            return carry

        lax.fori_loop(0, pl.num_programs(0), finish, 0)


def attn_backward(branch, wout, attn, total, q, k, v, qlin, klin, cosine, sine, qgain, kgain, doc, rows):
    length, width = branch.shape
    qw = wout.shape[0]
    heads = qw // HD
    blk = lambda cols: pl.BlockSpec((rows, cols), lambda i: (i, 0))
    whole = lambda shape: pl.BlockSpec(shape, lambda i: (0, 0))
    shape = jax.ShapeDtypeStruct
    full = whole((length, HD))
    return pl.pallas_call(
        functools.partial(attn_backward_kernel, heads, MOST // rows),
        grid=(length // rows,),
        in_specs=[
            blk(width),
            whole(wout.shape),
            blk(qw),
            blk(HD),
            blk(qw),
            full,
            full,
            blk(qw),
            full,
            full,
            full,
            whole((1, HD)),
            whole((1, HD)),
            blk(1),
            whole((1, length)),
        ],
        out_specs=[whole((length, qw + 2 * HD)), whole((8, HD))],
        out_shape=[
            shape((length, qw + 2 * HD), BF16),
            shape((8, HD), F32),
        ],
        scratch_shapes=[
            pltpu.VMEM((length, HD), F32),
            pltpu.VMEM((length, HD), F32),
            pltpu.VMEM((rows, qw), F32),
        ],
        compiler_params=pltpu.CompilerParams(vmem_limit_bytes=VMEM_LIMIT),
        cost_estimate=pl.CostEstimate(
            flops=60 * 10**9, transcendentals=0, bytes_accessed=30 * 2**20
        ),
        name="attn_backward",
    )(branch, wout, attn, total, q, k, v, qlin, klin, cosine, sine, qgain, kgain, doc[:, None], doc[None, :])


def expert_kernel(chained, plan, z_ref, n2_ref, top_ref, prob_ref, *rest):
    if chained:
        moe_in, row_in = rest[:2]
        rest = rest[2:]
    sources, rest = rest[: len(plan)], rest[len(plan) :]
    moe_ref, row_ref, grads_ref, wg_ref, wu_ref, wd_ref = rest[:6]
    ag_ref, au_ref, ad_ref, stage, wsem, sem = rest[6:]
    step = pl.program_id(0)
    rows, width = n2_ref.shape
    parts, cut, hidden = wd_ref.shape
    weights = (wg_ref, wu_ref, wd_ref)

    @pl.when(step == 0)
    def _():
        z = z_ref[0]
        for source, (kind, amount, start) in zip(sources, plan):
            count = source.shape[-2] // cut
            for k in range(parts) if kind == "all" else [amount]:
                if kind == "all":
                    src, owner, wanted = source.at[k], k, None
                elif kind == "up":
                    src, owner, wanted = source, z - k, z >= k
                else:
                    src, owner, wanted = source, z + k, z + k < parts

                def load(src=src, owner=owner, start=start, count=count):
                    for piece in range(count):
                        pltpu.make_async_copy(
                            src.at[pl.ds(piece * cut, cut), :],
                            weights[start + piece].at[owner],
                            wsem.at[start + piece, owner],
                        ).start()

                if wanted is None:
                    load()
                else:
                    pl.when(wanted)(load)
        ag_ref[...] = jnp.zeros_like(ag_ref)
        au_ref[...] = jnp.zeros_like(au_ref)
        ad_ref[...] = jnp.zeros_like(ad_ref)
        for index in range(3):
            for owner in range(parts):
                block = weights[index].at[owner]
                pltpu.make_async_copy(block, block, wsem.at[index, owner]).wait()

    n2 = n2_ref[...]
    prob = prob_ref[...]
    wg = wg_ref[...].reshape(width, hidden)
    wu = wu_ref[...].reshape(width, hidden)
    gate = dot(n2, wg)
    up = dot(n2, wu)
    sig = 1.0 / (1.0 + jnp.exp(-gate))
    silu = gate * sig
    act = (silu * up).astype(BF16)
    act_grad = jnp.zeros((rows, hidden), F32)
    for z in range(parts):
        cols = slice(z * cut, (z + 1) * cut)
        out = dot(act, wd_ref[z], NT).astype(BF16).astype(F32) * prob
        if chained:
            out = out + moe_in[:, cols].astype(F32)
        moe_ref[:, cols] = out.astype(BF16)
        route = (top_ref[:, cols].astype(F32) * prob).astype(BF16)
        act_grad += dot(route, wd_ref[z])
        ad_ref[z] += dot(route, act, TN)
    gate_grad = (act_grad * up * sig * (1.0 + gate * (1.0 - sig))).astype(BF16)
    up_grad = (act_grad * silu).astype(BF16)
    row = dot(gate_grad, wg, NT) + dot(up_grad, wu, NT)
    if chained:
        row = row + row_in[...].astype(F32)
    row_ref[...] = row.astype(BF16)
    ag_ref[...] += dot(n2, gate_grad, TN).reshape(parts, cut, hidden)
    au_ref[...] += dot(n2, up_grad, TN).reshape(parts, cut, hidden)

    @pl.when(step == pl.num_programs(0) - 1)
    def _():
        copies = []
        pieces = [
            (acc, place, z) for z in range(parts) for place, acc in enumerate((ag_ref, au_ref, ad_ref))
        ]
        for index, (acc, place, z) in enumerate(pieces):
            slot = index % 2
            if index >= 2:
                copies[index - 2].wait()
            stage[slot] = acc[z].astype(BF16)
            copies.append(
                pltpu.make_async_copy(
                    stage.at[slot], grads_ref.at[z, pl.ds(place * cut, cut), :], sem.at[slot]
                )
            )
            copies[-1].start()
        copies[-2].wait()
        copies[-1].wait()


def expert(z, n2, top, prob, n_dp, sources, before, rows):
    length, width = n2.shape
    cut = width // n_dp
    hidden = sources[0][0].shape[-1]
    blk = pl.BlockSpec((rows, width), lambda i: (i, 0))
    col = pl.BlockSpec((rows, 1), lambda i: (i, 0))
    shape = jax.ShapeDtypeStruct
    plan = tuple(entry[1:] for entry in sources)
    weight = pltpu.VMEM((n_dp, cut, hidden), BF16)
    total = pltpu.VMEM((n_dp, cut, hidden), F32)
    return pl.pallas_call(
        functools.partial(expert_kernel, len(before) > 0, plan),
        grid=(length // rows,),
        in_specs=[pl.BlockSpec(memory_space=pltpu.SMEM), blk, blk, col]
        + [blk] * len(before)
        + [ANY] * len(sources),
        out_specs=[blk, blk, ANY],
        out_shape=[
            shape((length, width), BF16),
            shape((length, width), BF16),
            shape((n_dp, 3 * cut, hidden), BF16),
        ],
        scratch_shapes=[weight] * 3
        + [total] * 3
        + [pltpu.VMEM((2, cut, hidden), BF16), DMA((3, n_dp)), DMA((2,))],
        compiler_params=pltpu.CompilerParams(vmem_limit_bytes=VMEM_LIMIT),
        cost_estimate=pl.CostEstimate(
            flops=18 * length * width * hidden,
            transcendentals=length * hidden,
            bytes_accessed=5 * length * width * 2,
        ),
        name="expert",
    )(z, n2, top, prob, *before, *[entry[0] for entry in sources])


def pack_kernel(cuts, gate_ref, up_ref, down_ref, *outs):
    cut = gate_ref.shape[0]
    for (low, high), out in zip(cuts, outs):
        out[:cut, :] = gate_ref[:, low:high]
        out[cut : 2 * cut, :] = up_ref[:, low:high]
        out[2 * cut :, :] = jnp.transpose(down_ref[low:high, :].astype(F32)).astype(BF16)


def pack(cuts, w_gate, w_up, w_down):
    cut = w_gate.shape[0]
    return pl.pallas_call(
        functools.partial(pack_kernel, cuts),
        in_specs=[VM] * 3,
        out_specs=[VM] * len(cuts),
        out_shape=[jax.ShapeDtypeStruct((3 * cut, high - low), BF16) for low, high in cuts],
        name="pack",
    )(w_gate, w_up, w_down)


def unpack_kernel(chunks, *refs):
    gate_ref, up_ref, down_ref = refs[len(chunks) :]
    cut = gate_ref.shape[1]
    for (e, low, high), ref in zip(chunks, refs):
        gate_ref[e, :, low:high] = ref[:cut, :].astype(F32)
        up_ref[e, :, low:high] = ref[cut : 2 * cut, :].astype(F32)
        down_ref[e, low:high, :] = jnp.transpose(ref[2 * cut :, :].astype(F32))


def unpack(own, chunks, grads, hidden):
    cut = grads[0].shape[0] // 3
    shape = jax.ShapeDtypeStruct
    return pl.pallas_call(
        functools.partial(unpack_kernel, chunks),
        in_specs=[VM] * len(grads),
        out_specs=[VM] * 3,
        out_shape=[
            shape((own, cut, hidden), F32),
            shape((own, cut, hidden), F32),
            shape((own, hidden, cut), F32),
        ],
        compiler_params=pltpu.CompilerParams(vmem_limit_bytes=VMEM_LIMIT),
        name="unpack",
    )(*grads)


def line_hop(block_up, block_down, n_dp, hop):
    up = [(i, i + 1) for i in range(hop - 1, n_dp - 1)]
    down = [(i + 1, i) for i in range(n_dp - hop)]
    return lax.ppermute(block_up, "dp", up), lax.ppermute(block_down, "dp", down)


def after_of(value, *others):
    return lax.optimization_barrier((value,) + others)[0]


def scatter_dp(partial):
    return lax.psum_scatter(partial.astype(BF16), "dp", scatter_dimension=0, tiled=True)


def per_device(
    layer_input,
    doc_ids,
    route_ids,
    route_probs,
    attn_gain,
    ffn_gain,
    query_gain,
    key_gain,
    w_query,
    w_key,
    w_value,
    w_out,
    w_gate,
    w_up,
    w_down,
    out_grad,
):
    tokens, width = layer_input.shape[1:]
    n_dp = lax.axis_size("dp")
    n_ctx = lax.axis_size("ctx")
    ctx_index = lax.axis_index("ctx")
    length = tokens * n_ctx
    heads = HQ // n_ctx
    share = n_ctx // KV
    qw = heads * HD
    both = ("dp", "ctx")
    depth = w_query.shape[0]
    own_e = w_gate.shape[0]

    cut = attn_gain.shape[0]
    hcut = query_gain.shape[0]
    kinds = 2 * (cut + hcut)
    small = jnp.concatenate([attn_gain, ffn_gain, query_gain, key_gain]).astype(F32)
    small = jnp.pad(small, (0, 1024 - kinds)).reshape(8, HD)
    cols = jnp.concatenate(
        [
            w_query.reshape(depth, n_ctx, qw),
            jnp.repeat(w_key.reshape(depth, KV, HD), share, axis=1),
            jnp.repeat(w_value.reshape(depth, KV, HD), share, axis=1),
        ],
        axis=2,
    ).transpose(1, 0, 2)
    cols, small = prep(n_ctx, n_dp, cols, small)
    small = small.reshape(n_dp * n_ctx, 1024)
    gain_attn = small[:, :cut].reshape(1, width)
    gain_ffn = small[:, cut : 2 * cut].reshape(1, width)
    gain_query = small[:, 2 * cut : 2 * cut + hcut].reshape(1, HD)
    gain_key = small[:, 2 * cut + hcut : kinds].reshape(1, HD)
    wqkv = lax.all_gather(cols.reshape(n_ctx * depth, qw + 2 * HD), "dp", axis=0, tiled=True)
    forth = [(c * n_dp + d, d * n_ctx + c) for d in range(n_dp) for c in range(n_ctx)]
    wout = lax.ppermute(after_of(w_out, small), both, forth)
    wout = lax.all_gather(wout, "dp", axis=0, tiled=True)

    inputs = layer_input.reshape(tokens, width)
    top_own = out_grad.reshape(tokens, width)
    n_experts = own_e * n_ctx
    match = route_ids.reshape(1, tokens, TOP) == jnp.arange(n_experts, dtype=jnp.int32)[:, None, None]
    probs = jnp.sum(jnp.where(match, route_probs.reshape(1, tokens, TOP), 0.0), axis=2)
    info = jnp.concatenate(
        [probs, doc_ids.reshape(1, tokens).astype(F32), jnp.zeros((7, tokens), F32)], axis=0
    )
    normed, info = first(n_ctx, inputs, gain_attn, info)
    normed = normed.reshape(length, width)
    doc = info[:, n_experts].reshape(length).astype(jnp.int32)
    my_probs = lax.dynamic_slice_in_dim(info, ctx_index * own_e, own_e, 1)
    my_probs = my_probs.transpose(0, 2, 1).reshape(length, own_e)

    inverse = 1.0 / ROPE_BASE ** (jnp.arange(HD // 2, dtype=F32) * 2.0 / HD)
    angles = jnp.arange(length, dtype=F32)[:, None] * inverse[None, :]
    cosine = jnp.cos(angles)
    sine = jnp.sin(angles)
    cosine = jnp.concatenate([cosine, cosine], axis=1)
    sine = jnp.concatenate([-sine, sine], axis=1)
    qlin, klin, q, k, v, attn, total, top_all = attn_forward(
        n_ctx, normed, wqkv, cosine, sine, gain_query, gain_key, doc, top_own, tokens
    )
    top_all = top_all.reshape(length, width)
    blocks = (n_ctx, tokens, width)
    after, normed2 = middle(n_ctx, attn, wout, inputs, gain_ffn)
    normed2 = normed2.reshape(length, width)

    z = lax.axis_index("dp").astype(jnp.int32).reshape(1)
    carried, chunk_grads = (), []
    hidden = w_gate.shape[2]
    chunks = [(0, 0, 256), (0, 256, hidden)] + [(e, 0, hidden) for e in range(1, own_e)]
    for e, low, high in chunks:
        if low == 0:
            cuts = [(f, g) for o, f, g in chunks if o == e]
            packed_e = pack(cuts, w_gate[e], w_up[e], w_down[e])
        block = packed_e[cuts.index((low, high))]
        if e == 0:
            sources = [(lax.all_gather(block, "dp", axis=0, tiled=False), "all", 0, 0)]
        else:
            sources = [(block, "up", 0, 0)]
            up = down = after_of(block, after)
            for hop in range(1, n_dp):
                if hop == 2:
                    up, down = after_of(up, *carried), after_of(down, *carried)
                up, down = line_hop(up, down, n_dp, hop)
                sources += [(up, "up", hop, 0), (down, "down", hop, 0)]
        moe, rows_grad, grads = expert(
            z, normed2, top_all, my_probs[:, e : e + 1], n_dp, sources, carried, tokens
        )
        carried = (moe, rows_grad)
        grads = grads.reshape(3 * width, high - low)
        chunk_grads.append(lax.psum_scatter(grads, "dp", scatter_dimension=0, tiled=True))
    mid, ffn_part, branch = turn(
        n_ctx, rows_grad.reshape(blocks), after, top_own, gain_ffn
    )
    branch = branch.reshape(length, width)

    out_w = dot(attn, branch, TN).astype(BF16)
    out_w = scatter_dp(out_w)
    dqkv, gains = attn_backward(
        branch, wout, attn, total, q, k, v, qlin, klin, cosine, sine, gain_query, gain_key, doc, tokens
    )
    input_grad, attn_part = last(n_ctx, dqkv, wqkv, inputs, mid, gain_attn)
    moe = after_of(moe, attn_part)
    layer_output = close(n_ctx, moe.reshape(blocks), after)

    out_w = lax.ppermute(out_w, both, [(b, a) for a, b in forth]).astype(F32)
    qkv_w = dot(normed, dqkv, TN).astype(BF16)
    qkv_w = scatter_dp(qkv_w)
    n_all = n_dp * n_ctx
    packed = jnp.concatenate(
        [
            attn_part[0].reshape(n_all, cut),
            ffn_part[0].reshape(n_all, cut),
            gains[0].reshape(n_all, hcut),
            gains[1].reshape(n_all, hcut),
            jnp.zeros((n_all, 1024 - kinds), F32),
        ],
        axis=1,
    )
    packed = packed.reshape(n_dp, n_ctx, 8, HD).transpose(1, 0, 2, 3)
    qkv_w, packed = post(n_ctx, n_dp, qkv_w.reshape(n_ctx, depth, qw + 2 * HD), packed)
    packed = packed.reshape(1024)
    query_w = qkv_w[:, :, :qw].transpose(1, 0, 2).reshape(depth, HQ * HD).astype(F32)
    kv_w = jnp.sum(qkv_w[:, :, qw:].astype(F32).reshape(KV, share, depth, 2 * HD), axis=1)
    key_w = kv_w[:, :, :HD].transpose(1, 0, 2).reshape(depth, KV * HD)
    value_w = kv_w[:, :, HD:].transpose(1, 0, 2).reshape(depth, KV * HD)

    gate_w, up_w, down_w = unpack(own_e, chunks, chunk_grads, hidden)
    return (
        layer_output.reshape(1, tokens, width),
        input_grad.reshape(1, tokens, width),
        packed[:cut],
        packed[cut : 2 * cut],
        packed[2 * cut : 2 * cut + hcut],
        packed[2 * cut + hcut : kinds],
        query_w,
        key_w,
        value_w,
        out_w,
        gate_w,
        up_w,
        down_w,
    )


def solution(mesh):
    both = ("dp", "ctx")
    seq = P("dp", "ctx", None)
    in_specs = (
        seq,
        P("dp", "ctx"),
        seq,
        seq,
        P(both),
        P(both),
        P(both),
        P(both),
        P(both, None),
        P(both, None),
        P(both, None),
        P(both, None),
        P("ctx", "dp", None),
        P("ctx", "dp", None),
        P("ctx", None, "dp"),
        seq,
    )
    out_specs = (
        seq,
        seq,
        P(both),
        P(both),
        P(both),
        P(both),
        P(both, None),
        P(both, None),
        P(both, None),
        P(both, None),
        P("ctx", "dp", None),
        P("ctx", "dp", None),
        P("ctx", None, "dp"),
    )

    return jax.shard_map(
        per_device, mesh=mesh, in_specs=in_specs, out_specs=out_specs, check_vma=False
    )
```

time: 1240 us -> 1230 us (level)
  waiting for transfers between devices: 137 us -> 464 us
  matrix products: 253 us -> 20.5 us
  local copies, waits for them, and re-layouts: 175 us -> 25.4 us
  Pallas kernels: 593 us -> 650 us
  other arithmetic: 44.7 us -> 12.3 us
  starting transfers between devices: 9.02 us -> 34.1 us
    reduce_scatter x0 -> x3, waiting for transfers between devices: none -> 255 us  [per_device(): lax.psum_scatter(grads, 'dp', scatter_dimension=0, tiled=True)]
    pallas_call x1 -> x7, Pallas kernels: 42.6 us -> 232 us  [the longest x3 163 us: expert(): pl.pallas_call(functools.partial(expert_kernel, len(before) > 0, plan), g...]
    dot_general x15 -> x2, matrix products: 187 us -> 20.5 us  [dot(): lax.dot_general(left, right, (dims, ((), ())), preferred_element_type=F32)]
    convert_element_type x7 -> x0, local copies, waits for them, and re-layouts: 144 us -> none  [the longest x4 92.6 us: per_device(): moe = moe + prob * out.reshape(length, width).astype(F32)]
    pallas_call x7, Pallas kernels: 485 us -> 353 us  [comm_call(): pl.pallas_call(kernel, out_shape=outs, in_specs=in_specs, out_specs=out_s...]
    ppermute x1 -> x7, waiting for transfers between devices: 23.4 us -> 151 us  [the longest x3 51.8 us: line_hop(): lax.ppermute(block_down, 'dp', down)]
    reduce_scatter x8 -> x2, waiting for transfers between devices: 93.5 us -> 0.02 us  [scatter_dp(): lax.psum_scatter(partial.astype(BF16), 'dp', scatter_dimension=0, tiled=T...]
    dot_general x6 -> x0, matrix products: 66.6 us -> none  [the longest x2 25 us: per_device(): act_grad = jnp.einsum('rzd,zfd->rf', route3, wd, preferred_element_type=F32)]
  transfers between devices with their start and end apart: 18 -> 17, of which waited for: 4 -> 8; matrix products, arithmetic and copies ran while one was open for 33% -> 3% of each run, Pallas kernels for 39% -> 38%
where the time goes in v3:
time: 1230 us; the launch traced here: 1220 us
  Pallas kernels  650 us (53%)
  waiting for transfers between devices  464 us (38%)
  starting transfers between devices  34.1 us (3%)
  local copies, waits for them, and re-layouts  25.4 us (2%)
  matrix products  20.5 us (2%)
  between operations  14.6 us (1%)
  other arithmetic  12.3 us (1%)
    pallas_call x7, Pallas kernels, comm_call(): pl.pallas_call(kernel, out_shape=outs, in_specs=in_specs, out_specs=out_s...  353 us
    reduce_scatter x3, waiting for transfers between devices, per_device(): lax.psum_scatter(grads, 'dp', scatter_dimension=0, tiled=True)  255 us
    pallas_call x3, Pallas kernels, expert(): pl.pallas_call(functools.partial(expert_kernel, len(before) > 0, plan), g...  163 us
    pallas_call x1, Pallas kernels, attn_backward(): pl.pallas_call(functools.partial(attn_backward_kernel, heads, MOST // row...  65 us
    pallas_call x1, Pallas kernels, attn_forward(): pl.pallas_call(functools.partial(attn_forward_kernel, n, heads, MOST // r...  55.4 us
    ppermute x3, waiting for transfers between devices, line_hop(): lax.ppermute(block_down, 'dp', down)  51.8 us
    ppermute x1, waiting for transfers between devices, per_device(): wout = lax.ppermute(after_of(w_out, small), both, forth)  51.6 us
    ppermute x3, waiting for transfers between devices, line_hop(): lax.ppermute(block_up, 'dp', up)  47.9 us
  transfers between devices with their start and end apart: 17, of which 8 were waited for; matrix products, arithmetic and copies ran while one was open for 3% of the time, Pallas kernels for 38%

profile of v3, /device:TPU:14, one launch (start us, length us, event | category | flops | bytes accessed | tf_op | source)
XLA Modules:
  0.0 1221.2 jit_solution(14677790835358656842)
XLA Ops:
  8.9 1.1 copy.93
  10.0 1.0 maximum_bitcast_fusion.cols_ref
  11.7 14.2 %shard_map.255 = (bf16[8,64,768]{2,1,0:T(8,128)(2,1)}, f32[4,8,8,128]{3,2,1,0:T(8,128)}) custom-call(bf16[8,64,768]{2,1,0:T(8,128)(2,1)} %maximum_bitcast_fusion.cols_ref, f32[8,128]{1,0:T(8,128)} %fusion.11.small_ref), custom_call_target="tpu_custom_call" | custom-call | bytes 24000000 | tf_op jit(solution)/shard_map/pallas_call | solution.py:422
  26.0 0.9 copy.94
  27.0 3.0 collective-permute-start
  29.9 51.6 %collective-permute-done = bf16[128,2048]{1,0:T(8,128)(2,1)} collective-permute-done((bf16[128,2048]{1,0:T(8,128)(2,1)}, bf16[128,2048]{1,0:T(8,128)(2,1)}, u32[]{:S(2)}, u32[]{:S(2)}) %collective-permute-start) | collective-permute-done | bytes 524320 | tf_op jit(solution)/shard_map/ppermute | solution.py:1274
  81.6 1.2 slice_bitcast_fusion
  83.6 1.7 slice_bitcast_fusion.1
  85.3 3.3 pack.2
  92.8 45.3 %shard_map.256 = (bf16[8,256,2048]{2,1,0:T(8,128)(2,1)}, f32[8,24,256]{2,1,0:T(8,128)}) custom-call(bf16[256,2048]{1,0:T(8,128)(2,1)} %bitcast.98, f32[1,2048]{1,0:T(1,128)} %reshape.171.gain_ref, f32[24,256]{1,0:T(8,128)} %maximum_maximum_fusion.info_ref), custom_call_target="tpu_custom_call" | custom-call | bytes 150000000 | tf_op jit(solution)/shard_map/pallas_call | solution.py:422
  140.2 1.3 copy.69.docc_ref
  141.5 3.4 pack.3.rest_2_
  144.9 3.9 fusion.2
  148.8 1.9 pad_maximum_fusion
  150.8 1.6 fusion.12
  152.4 55.4 %attn_forward.1 = (f32[2048,512]{1,0:T(8,128)}, f32[2048,128]{1,0:T(8,128)}, bf16[2048,512]{1,0:T(8,128)(2,1)}, bf16[2048,128]{1,0:T(8,128)(2,1)}, bf16[2048,128...) custom-call(bf16[2048,2048]{1,0:T(8,128)(2,1)} %bitcast.128, ...), custom_call_target="tpu_custom_call" | custom-call | flops 35000000512 | bytes 31457280 | tf_op jit(solution)/shard_map/attn_forward/pallas_call | solution.py:847
  207.8 87.1 %shard_map.257 = (f32[256,2048]{1,0:T(8,128)}, bf16[8,256,2048]{2,1,0:T(8,128)(2,1)}) custom-call(bf16[2048,512]{1,0:T(8,128)(2,1)} %get-tuple-element.59.attn_ref, bf16[512,2048]{1,0:T(8,128)(2,1)} %all-gather.9.cloned.1.call-done.wout_ref, bf16[256,2048]{1,0:T(8,128)(2,1)} %bitcast.99, f32[1,2048]{1,0:T(1,128)} %reshape.177.gain_ref), custom_call_target="tpu_custom_call" | custom-call | bytes 315000000 | tf_op jit(solution)/shard_map/pallas_call | solution.py:422
  294.9 9.0 collective-permute-start.2
  303.9 2.4 collective-permute-start.1
  306.3 32.2 %expert.3 = (bf16[2048,2048]{1,0:T(8,128)(2,1)}, bf16[2048,2048]{1,0:T(8,128)(2,1)}, bf16[4,1536,256]{2,1,0:T(8,128)(2,1)}) custom-call(s32[1]{0:T(128)} %bitcast.z_ref, bf16[2048,2048]{1,0:T(8,128)(2,1)} %bitcast.130, bf16[2048,2048]{1,0:T(8,128)(2,1)} %bitcast.137, f32[2048,1]{1,0:T(8,128)} %get-tuple-element.105.prob_ref, bf16[4,1536,256]{2,1,0:T(8,128)(2,1)} %bitcast.136), custom_call_target="tpu_custom_call" | custom-call | flops 19327352832 | bytes 41943040 | tf_op jit(solution)/shard_map/expert/pallas_call | solution.py:1139
  338.5 16.6 %all-gather.13.cloned.1.call-done = bf16[6144,512]{1,0:T(8,128)(2,1)} async-done(((bf16[1536,512]{1,0:T(8,128)(2,1)}), bf16[6144,512]{1,0:T(8,128)(2,1)}) %all-gather.13.cloned.1.call-update) | async-done | bytes 6291472 | tf_op jit(solution)/shard_map/all_gather | solution.py:1315
  355.1 55.2 %expert.4 = (bf16[2048,2048]{1,0:T(8,128)(2,1)}, bf16[2048,2048]{1,0:T(8,128)(2,1)}, bf16[4,1536,512]{2,1,0:T(8,128)(2,1)}) custom-call(s32[1]{0:T(128)} %bitcast.z_ref, bf16[2048,2048]{1,0:T(8,128)(2,1)} %bitcast.131, bf16[2048,2048]{1,0:T(8,128)(2,1)} %bitcast.138, f32[2048,1]{1,0:T(8,128)} %get-tuple-element.105.prob_ref, ...), custom_call_target="tpu_custom_call" | custom-call | flops 38654705664 | bytes 41943040 | tf_op jit(solution)/shard_map/expert/pallas_call | solution.py:1139
  410.3 10.7 collective-permute-start.3
  421.0 1.9 collective-permute-start.4
  423.0 47.9 %collective-permute-done.3.rest_5_ = bf16[1536,768]{1,0:T(8,128)(2,1)S(1)} collective-permute-done((bf16[1536,768]{1,0:T(8,128)(2,1)}, bf16[1536,768]{1,0:T(8,128)(2,1)S(1)}, u32[]{:S(2)}, u32[]{:S(2)}) %collective-permute-start.3) | collective-permute-done | bytes 2359328 | tf_op jit(solution)/shard_map/ppermute | solution.py:1212
  471.7 3.3 collective-permute-done.4.rest_6_
  475.0 2.5 collective-permute-start.6
  477.6 48.4 %collective-permute-done.6.rest_8_ = bf16[1536,768]{1,0:T(8,128)(2,1)S(1)} collective-permute-done((bf16[1536,768]{1,0:T(8,128)(2,1)S(1)}, bf16[1536,768]{1,0:T(8,128)(2,1)S(1)}, u32[]{:S(2)}, u32[]{:S(2)}) %collective-permute-start.6) | collective-permute-done | bytes 2359328 | tf_op jit(solution)/shard_map/ppermute | solution.py:1212
  526.0 1.4 copy-done.21
  527.4 75.8 %expert.5 = (bf16[2048,2048]{1,0:T(8,128)(2,1)}, bf16[2048,2048]{1,0:T(8,128)(2,1)}, bf16[4,1536,768]{2,1,0:T(8,128)(2,1)}) custom-call(s32[1]{0:T(128)} %bitcast.z_ref, bf16[2048,2048]{1,0:T(8,128)(2,1)} %bitcast.132, bf16[2048,2048]{1,0:T(8,128)(2,1)} %bitcast.139, f32[2048,1]{1,0:T(8,128)} %get-tuple-element.106.prob_ref, ...), custom_call_target="tpu_custom_call" | custom-call | flops 57982058496 | bytes 41943040 | tf_op jit(solution)/shard_map/expert/pallas_call | solution.py:1139
  603.3 83.3 %shard_map.258 = (f32[256,2048]{1,0:T(8,128)}, f32[8,2048]{1,0:T(8,128)}, bf16[8,256,2048]{2,1,0:T(8,128)(2,1)}) custom-call(bf16[8,256,2048]{2,1,0:T(8,128)(2,1)} %bitcast.101, f32[256,2048]{1,0:T(8,128)} %get-tuple-element.69.after_ref, bf16[256,2048]{1,0:T(8,128)(2,1)} %bitcast.109, f32[1,2048]{1,0:T(1,128)} %reshape.177.gain_ref), custom_call_target="tpu_custom_call" | custom-call | bytes 285000000 | tf_op jit(solution)/shard_map/pallas_call | solution.py:422
  686.6 9.1 convolution_convert_fusion.1
  696.0 65.0 %attn_backward.1 = (bf16[2048,768]{1,0:T(8,128)(2,1)}, f32[8,128]{1,0:T(8,128)}) custom-call(bf16[2048,2048]{1,0:T(8,128)(2,1)} %bitcast.134, bf16[512,2048]{1,0:T(8,128)(2,1)} %all-gather.9.cloned.1.call-done.wout_ref, bf16[2048,512]{1,0:T(8,128)(2,1)} %get-tuple-element.59.attn_ref, f32[2048,128]{1,0:T(8,128)} %get-tuple-element.76.total_ref, ...), custom_call_target="tpu_custom_call" | custom-call | flops 60000002048 | bytes 31457280 | tf_op jit(solution)/shard_map/attn_backward/pallas_call | solution.py:997
  761.0 11.4 convolution_convert_fusion
  774.6 52.5 %shard_map.259 = (f32[256,2048]{1,0:T(8,128)}, f32[8,2048]{1,0:T(8,128)}) custom-call(bf16[2048,768]{1,0:T(8,128)(2,1)} %get-tuple-element.82.grad_ref, bf16[2048,768]{1,0:T(8,128)(2,1)} %all-gather.7.cloned.1.call-done.wqkv_ref, bf16[256,2048]{1,0:T(8,128)(2,1)} %bitcast.100, f32[256,2048]{1,0:T(8,128)} %get-tuple-element.83.mid_ref, ...), custom_call_target="tpu_custom_call" | custom-call | bytes 180000000 | tf_op jit(solution)/shard_map/pallas_call | solution.py:422
  827.2 44.0 %shard_map.260 = bf16[256,2048]{1,0:T(8,128)(2,1)} custom-call(bf16[8,256,2048]{2,1,0:T(8,128)(2,1)} %bitcast.102, f32[256,2048]{1,0:T(8,128)} %get-tuple-element.69.after_ref), custom_call_target="tpu_custom_call" | custom-call | bytes 150000000 | tf_op jit(solution)/shard_map/pallas_call | solution.py:422
  871.2 3.2 collective-permute-start.7
  878.2 39.1 %collective-permute-done.7 = bf16[128,2048]{1,0:T(8,128)(2,1)S(1)} collective-permute-done((bf16[128,2048]{1,0:T(8,128)(2,1)}, bf16[128,2048]{1,0:T(8,128)(2,1)S(1)}, u32[]{:S(2)}, u32[]{:S(2)}) %collective-permute-start.7) | collective-permute-done | bytes 524320 | tf_op jit(solution)/shard_map/ppermute | solution.py:1344
  917.3 1.1 convert_element_type.57
  918.4 26.6 %shard_map.261 = (bf16[8,64,768]{2,1,0:T(8,128)(2,1)}, f32[8,128]{1,0:T(8,128)}) custom-call(bf16[8,64,768]{2,1,0:T(8,128)(2,1)} %bitcast.112, f32[8,4,8,128]{3,2,1,0:T(8,128)} %copy_bitcast_fusion.5.small_ref), custom_call_target="tpu_custom_call" | custom-call | bytes 24000000 | tf_op jit(solution)/shard_map/pallas_call | solution.py:422
  945.0 1.0 convert_reduce_fusion
  947.4 1.2 convert_bitcast_fusion
  948.6 1.1 copy.79
  950.8 90.8 %reduce-scatter.12.cloned.1.call-done.refs_1_ = bf16[1536,512]{1,0:T(8,128)(2,1)} async-done(((bf16[6144,512]{1,0:T(8,128)(2,1)}), bf16[1536,512]{1,0:T(8,128)(2,1)}) %reduce-scatter.12.cloned.1.call-update) | async-done | bytes 1572880 | tf_op jit(solution)/shard_map/reduce_scatter | solution.py:1329
  1041.6 163.8 %reduce-scatter.14.cloned.1.call-done.refs_2_ = bf16[1536,768]{1,0:T(8,128)(2,1)} async-done(((bf16[6144,768]{1,0:T(8,128)(2,1)}), bf16[1536,768]{1,0:T(8,128)(2,1)}) %reduce-scatter.14.cloned.1.call-update) | async-done | bytes 2359312 | tf_op jit(solution)/shard_map/reduce_scatter | solution.py:1329
  1205.4 6.8 unpack.1
  1212.2 1.0 copy.99
  1213.2 1.3 copy.100
  (106 shorter events, 19.0 us)
Async XLA Ops:
  7.2 0.8 copy-start
  7.2 3.8 copy-start.14
  7.2 3.8 copy-start.15
  7.2 3.8 copy-start.16
  7.2 3.8 copy-start.17
  7.2 74.4 %copy-start.6 = (bf16[2,768,512]{2,1,0:T(8,128)(2,1)S(1)}, bf16[2,768,512]{2,1,0:T(8,128)(2,1)}, u32[]{:S(2)}) copy-start(bf16[2,768,512]{2,1,0:T(8,128)(2,1)} %param.30) | copy-start | bytes 4718596
  7.2 145.2 %all-gather.7.cloned.1.call-start = ((), (), s32[]{:S(2)}) async-start(), calls=%async_computation.5 | async-start | bytes 3932160 | tf_op jit(solution)/shard_map/all_gather | solution.py:1272
  11.0 71.9 %copy-start.7 = (bf16[2,512,768]{2,1,0:T(8,128)(2,1)S(1)}, bf16[2,512,768]{2,1,0:T(8,128)(2,1)}, u32[]{:S(2)}) copy-start(bf16[2,512,768]{2,1,0:T(8,128)(2,1)} %param.29) | copy-start | bytes 4718596
  26.0 181.8 %all-gather.9.cloned.1.call-start = ((), (), s32[]{:S(2)}) async-start(), calls=%async_computation.6 | async-start | bytes 2621440 | tf_op jit(solution)/shard_map/all_gather | solution.py:1275
  27.0 54.6 %collective-permute-start = (bf16[128,2048]{1,0:T(8,128)(2,1)}, bf16[128,2048]{1,0:T(8,128)(2,1)}, u32[]{:S(2)}, u32[]{:S(2)}) collective-permute-start(bf16[128,2048]{1,0:T(8,128)(2,1)} %param.27), channel_id=1, source_target_pairs={{0,0},{4,1},{8,2},{12,3},{16,4},{20,5},{24,6},{28,7},{1,8},{5,9},{... | collective-permute-start | bytes 1572872 | tf_op jit(solution)/shard_map/ppermute | solution.py:1274
  81.6 224.8 %all-gather.11.cloned.1.call-start = ((), (), s32[]{:S(2)}) async-start(), calls=%async_computation.12 | async-start | bytes 3932160 | tf_op jit(solution)/shard_map/all_gather | solution.py:1315
  81.6 2.0 copy-start.8
  85.3 4.0 copy-start.13
  85.3 6.8 copy-start.10
  85.3 6.8 copy-start.11
  88.6 266.5 %all-gather.13.cloned.1.call-start = ((), (), s32[]{:S(2)}) async-start(), calls=%async_computation.13 | async-start | bytes 7864320 | tf_op jit(solution)/shard_map/all_gather | solution.py:1315
  89.2 782.0 %reduce-scatter.8.cloned.1.call-start = ((), (), s32[]{:S(2)}) async-start(), calls=%async_computation.8 | async-start | bytes 2621440 | tf_op jit(solution)/shard_map/reduce_scatter | solution.py:1220
  140.2 8.6 copy-start.9
  207.8 87.1 %copy-start.3 = (bf16[1536,768]{1,0:T(8,128)(2,1)S(1)}, bf16[1536,768]{1,0:T(8,128)(2,1)}, u32[]{:S(2)}) copy-start(bf16[1536,768]{1,0:T(8,128)(2,1)} %pack.3.rest_2_) | copy-start | bytes 7077892
  294.9 115.4 %collective-permute-start.2 = (bf16[1536,768]{1,0:T(8,128)(2,1)S(1)}, bf16[1536,768]{1,0:T(8,128)(2,1)}, u32[]{:S(2)}, u32[]{:S(2)}) collective-permute-start(bf16[1536,768]{1,0:T(8,128)(2,1)S(1)} %copy-done.3), channel_id=1, source_target_pairs={{8,0},{16,8},{24,16},{9,1},{17,9},{25,17},{10,2},{18,10},{26,18},{... | collective-permute-start | bytes 7077896 | tf_op jit(solution)/shard_map/ppermute | solution.py:1212
  303.9 106.4 %collective-permute-start.1 = (bf16[1536,768]{1,0:T(8,128)(2,1)S(1)}, bf16[1536,768]{1,0:T(8,128)(2,1)}, u32[]{:S(2)}, u32[]{:S(2)}) collective-permute-start(bf16[1536,768]{1,0:T(8,128)(2,1)S(1)} %copy-done.3), channel_id=1, source_target_pairs={{0,8},{8,16},{16,24},{1,9},{9,17},{17,25},{2,10},{10,18},{18,26},{... | collective-permute-start | bytes 7077896 | tf_op jit(solution)/shard_map/ppermute | solution.py:1212
  410.3 60.5 %collective-permute-start.3 = (bf16[1536,768]{1,0:T(8,128)(2,1)}, bf16[1536,768]{1,0:T(8,128)(2,1)S(1)}, u32[]{:S(2)}, u32[]{:S(2)}) collective-permute-start(bf16[1536,768]{1,0:T(8,128)(2,1)} %collective-permute-done.1.rest_3_), channel_id=1, source_target_pairs={{8,16},{16,24},{9,17},{17,25},{10,18},{18,26},{11,19},{19,27},{12,... | collective-permute-start | bytes 7077896 | tf_op jit(solution)/shard_map/ppermute | solution.py:1212
  421.0 54.0 %collective-permute-start.4 = (bf16[1536,768]{1,0:T(8,128)(2,1)}, bf16[1536,768]{1,0:T(8,128)(2,1)S(1)}, u32[]{:S(2)}, u32[]{:S(2)}) collective-permute-start(bf16[1536,768]{1,0:T(8,128)(2,1)} %collective-permute-done.2.rest_4_), channel_id=1, source_target_pairs={{8,0},{16,8},{9,1},{17,9},{10,2},{18,10},{11,3},{19,11},{12,4},{20... | collective-permute-start | bytes 7077896 | tf_op jit(solution)/shard_map/ppermute | solution.py:1212
  470.8 56.6 %copy-start.18 = (bf16[1536,768]{1,0:T(8,128)(2,1)}, bf16[1536,768]{1,0:T(8,128)(2,1)S(1)}, u32[]{:S(2)}) copy-start(bf16[1536,768]{1,0:T(8,128)(2,1)S(1)} %collective-permute-done.3.rest_5_) | copy-start | bytes 7077892
  470.9 6.7 collective-permute-start.5
  475.0 2.5 copy-start.19
  475.0 51.0 %collective-permute-start.6 = (bf16[1536,768]{1,0:T(8,128)(2,1)S(1)}, bf16[1536,768]{1,0:T(8,128)(2,1)S(1)}, u32[]{:S(2)}, u32[]{:S(2)}) collective-permute-start(bf16[1536,768]{1,0:T(8,128)(2,1)S(1)} %collective-permute-done.4.rest_6_), channel_id=1, source_target_pairs={{8,0},{9,1},{10,2},{11,3},{12,4},{13,5},{14,6},{15,7}} | collective-permute-start | bytes 7077896 | tf_op jit(solution)/shard_map/ppermute | solution.py:1212
  477.5 48.4 %copy-start.20 = (bf16[1536,768]{1,0:T(8,128)(2,1)}, bf16[1536,768]{1,0:T(8,128)(2,1)S(1)}, u32[]{:S(2)}) copy-start(bf16[1536,768]{1,0:T(8,128)(2,1)S(1)} %collective-permute-done.5.rest_7_) | copy-start | bytes 7077892
  526.0 1.5 copy-start.21
  603.2 83.4 %copy-start.4 = (bf16[2048,512]{1,0:T(8,128)(2,1)S(1)}, bf16[2048,512]{1,0:T(8,128)(2,1)}, u32[]{:S(2)}) copy-start(bf16[2048,512]{1,0:T(8,128)(2,1)} %get-tuple-element.59.attn_ref) | copy-start | bytes 6291460
  695.7 222.6 %reduce-scatter.6.cloned.1.call-start = ((), (), s32[]{:S(2)}) async-start(), calls=%async_computation.7 | async-start | bytes 3932160 | tf_op jit(solution)/shard_map/reduce_scatter | solution.py:1220
  772.4 178.4 %reduce-scatter.10.cloned.1.call-start = ((), (), s32[]{:S(2)}) async-start(), calls=%async_computation.9 | async-start | bytes 3932160 | tf_op jit(solution)/shard_map/reduce_scatter | solution.py:1329
  773.2 268.4 %reduce-scatter.12.cloned.1.call-start = ((), (), s32[]{:S(2)}) async-start(), calls=%async_computation.10 | async-start | bytes 7864320 | tf_op jit(solution)/shard_map/reduce_scatter | solution.py:1329
  773.9 431.5 %reduce-scatter.14.cloned.1.call-start = ((), (), s32[]{:S(2)}) async-start(), calls=%async_computation.11 | async-start | bytes 11796480 | tf_op jit(solution)/shard_map/reduce_scatter | solution.py:1329
  871.2 46.1 %collective-permute-start.7 = (bf16[128,2048]{1,0:T(8,128)(2,1)}, bf16[128,2048]{1,0:T(8,128)(2,1)S(1)}, u32[]{:S(2)}, u32[]{:S(2)}) collective-permute-start(bf16[128,2048]{1,0:T(8,128)(2,1)} %reduce-scatter.8.cloned.1.call-done), channel_id=1, source_target_pairs={{0,0},{1,4},{2,8},{3,12},{4,16},{5,20},{6,24},{7,28},{8,1},{9,5},{... | collective-permute-start | bytes 1572872 | tf_op jit(solution)/shard_map/ppermute | solution.py:1344
  945.0 4.6 copy-start.12
  948.6 263.6 %copy-start.2 = (bf16[256,2048]{1,0:T(8,128)(2,1)S(1)}, bf16[256,2048]{1,0:T(8,128)(2,1)}, u32[]{:S(2)}) copy-start(bf16[256,2048]{1,0:T(8,128)(2,1)} %shard_map.260) | copy-start | bytes 3145732
  950.8 262.3 %copy-start.5 = (f32[256,2048]{1,0:T(8,128)S(1)}, f32[256,2048]{1,0:T(8,128)}, u32[]{:S(2)}) copy-start(f32[256,2048]{1,0:T(8,128)} %get-tuple-element.86) | copy-start | bytes 6291460
  1212.2 2.3 copy-start.1
Sparse Core Ops, SparseCore 0:
  26.1 78.2 all-gather.6
  105.9 46.4 all-gather.8
  154.0 61.4 all-gather.10
  217.5 137.6 all-gather.12
  695.9 43.1 reduce-scatter.7
  772.5 60.3 reduce-scatter.5
  835.8 77.9 reduce-scatter.9
  916.2 125.4 reduce-scatter.11
  1044.0 161.3 reduce-scatter.13

commit v4 on v3

--- a/solution.py
+++ b/solution.py
@@ -474,8 +474,8 @@
     own.wait()
 
 
-def post_kernel(n, n_dp, cols_ref, small_ref, out_ref, sum_ref, first, mid, second, *sems):
-    send, recv, local, gsend, grecv, zsend, zrecv = sems
+def gains_kernel(n, n_dp, small_ref, sum_ref, landed, mid, second, *sems):
+    gsend, grecv, zsend, zrecv = sems
     me, row = lax.axis_index("ctx"), lax.axis_index("dp")
     meet(
         [("ctx", flip(me, s, n)) for s in range(1, n)]
@@ -484,13 +484,12 @@
     smalls = []
     for s in range(1, n):
         peer = flip(me, s, n)
-        smalls.append(push(small_ref.at[peer], first.at[s], gsend.at[s], grecv.at[s], "ctx", peer))
+        smalls.append(push(small_ref.at[peer], landed.at[s], gsend.at[s], grecv.at[s], "ctx", peer))
         smalls[-1].start()
-    own, copies = swap_all(n, cols_ref, out_ref, send, recv, local)
     value = small_ref[me]
     for copy, s in zip(smalls, range(1, n)):
         copy.wait_recv()
-        value = value + first[s]
+        value = value + landed[s]
     mid[...] = value
     planes = []
     for s in range(1, n_dp):
@@ -502,11 +501,29 @@
         copy.wait_recv()
         value = value + second[s]
     sum_ref[...] = value
+    for copy in planes + smalls:
+        copy.wait_send()
+
+
+def post_kernel(n, src_ref, query_ref, key_ref, value_ref, blocks, send, recv, local):
+    me = lax.axis_index("ctx")
+    meet([("ctx", flip(me, s, n)) for s in range(1, n)])
+    own, copies = swap_all(n, src_ref, blocks, send, recv, local)
     for copy in copies:
         copy.wait_recv()
-    for copy in copies + planes + smalls:
+    own.wait()
+    share = n // KV
+    qw = HQ * HD // n
+    for c in range(n):
+        query_ref[:, c * qw : (c + 1) * qw] = blocks[c, :, :qw].astype(F32)
+    for g in range(KV):
+        for out, at in ((key_ref, qw), (value_ref, qw + HD)):
+            total = blocks[g * share, :, at : at + HD].astype(F32)
+            for c in range(1, share):
+                total = total + blocks[g * share + c, :, at : at + HD].astype(F32)
+            out[:, g * HD : (g + 1) * HD] = total
+    for copy in copies:
         copy.wait_send()
-    own.wait()
 
 
 def swap_sems(n, n_dp):
@@ -528,24 +545,44 @@
     )
 
 
-def post(n, n_dp, cols, small):
-    shape = jax.ShapeDtypeStruct
+def gains_sum(n, n_dp, small):
     tile = small.shape[2:]
     return comm_call(
-        functools.partial(post_kernel, n, n_dp),
-        1,
-        [shape(cols.shape, cols.dtype), shape(tile, F32)],
-        [ANY, VM],
-        [ANY, VM],
+        functools.partial(gains_kernel, n, n_dp),
+        8,
+        jax.ShapeDtypeStruct(tile, F32),
+        VM,
+        [VM],
         [
             pltpu.VMEM((n, n_dp) + tile, F32),
             pltpu.VMEM((n_dp,) + tile, F32),
             pltpu.VMEM((n_dp,) + tile, F32),
-        ]
-        + swap_sems(n, n_dp),
-        8,
+            DMA((n,)),
+            DMA((n,)),
+            DMA((n_dp,)),
+            DMA((n_dp,)),
+        ],
+        10,
+        small,
+    )
+
+
+def post(n, cols):
+    shape = jax.ShapeDtypeStruct
+    depth = cols.shape[1]
+    return comm_call(
+        functools.partial(post_kernel, n),
+        1,
+        [
+            shape((depth, HQ * HD), F32),
+            shape((depth, KV * HD), F32),
+            shape((depth, KV * HD), F32),
+        ],
+        [VM] * 3,
+        [VM],
+        [pltpu.VMEM(cols.shape, BF16), DMA((n,)), DMA((n,)), DMA(())],
+        10,
         cols,
-        small,
     )
 
 
@@ -1032,7 +1069,9 @@
     )(branch, wout, attn, total, q, k, v, qlin, klin, cosine, sine, qgain, kgain, doc[:, None], doc[None, :])
 
 
-def expert_kernel(chained, plan, z_ref, n2_ref, top_ref, prob_ref, *rest):
+def expert_kernel(chained, low, aliased, plan, z_ref, n2_ref, top_ref, prob_ref, *rest):
+    if aliased:
+        rest = rest[1:]
     if chained:
         moe_in, row_in = rest[:2]
         rest = rest[2:]
@@ -1118,7 +1157,9 @@
             stage[slot] = acc[z].astype(BF16)
             copies.append(
                 pltpu.make_async_copy(
-                    stage.at[slot], grads_ref.at[z, pl.ds(place * cut, cut), :], sem.at[slot]
+                    stage.at[slot],
+                    grads_ref.at[z, pl.ds(place * cut, cut), pl.ds(low, acc.shape[2])],
+                    sem.at[slot],
                 )
             )
             copies[-1].start()
@@ -1126,7 +1167,7 @@
         copies[-1].wait()
 
 
-def expert(z, n2, top, prob, n_dp, sources, before, rows):
+def expert(z, n2, top, prob, n_dp, sources, before, rows, low, full, grads):
     length, width = n2.shape
     cut = width // n_dp
     hidden = sources[0][0].shape[-1]
@@ -1137,17 +1178,19 @@
     weight = pltpu.VMEM((n_dp, cut, hidden), BF16)
     total = pltpu.VMEM((n_dp, cut, hidden), F32)
     return pl.pallas_call(
-        functools.partial(expert_kernel, len(before) > 0, plan),
+        functools.partial(expert_kernel, len(before) > 0, low, len(grads) > 0, plan),
         grid=(length // rows,),
         in_specs=[pl.BlockSpec(memory_space=pltpu.SMEM), blk, blk, col]
+        + [ANY] * len(grads)
         + [blk] * len(before)
         + [ANY] * len(sources),
         out_specs=[blk, blk, ANY],
         out_shape=[
             shape((length, width), BF16),
             shape((length, width), BF16),
-            shape((n_dp, 3 * cut, hidden), BF16),
+            shape((n_dp, 3 * cut, full), BF16),
         ],
+        input_output_aliases={4: 2} if grads else {},
         scratch_shapes=[weight] * 3
         + [total] * 3
         + [pltpu.VMEM((2, cut, hidden), BF16), DMA((3, n_dp)), DMA((2,))],
@@ -1158,7 +1201,7 @@
             bytes_accessed=5 * length * width * 2,
         ),
         name="expert",
-    )(z, n2, top, prob, *before, *[entry[0] for entry in sources])
+    )(z, n2, top, prob, *grads, *before, *[entry[0] for entry in sources])
 
 
 def pack_kernel(cuts, gate_ref, up_ref, down_ref, *outs):
@@ -1210,6 +1253,18 @@
     up = [(i, i + 1) for i in range(hop - 1, n_dp - 1)]
     down = [(i + 1, i) for i in range(n_dp - hop)]
     return lax.ppermute(block_up, "dp", up), lax.ppermute(block_down, "dp", down)
+
+
+def reduce_hop(grads, got, n_dp, hop):
+    place = lax.axis_index("dp")
+    reach = n_dp - hop
+    spots = (jnp.minimum(place + reach, n_dp - 1), jnp.maximum(place - reach, 0))
+    blocks = [lax.dynamic_index_in_dim(grads, spot, 0, False) for spot in spots]
+    if got is not None:
+        blocks = [(b.astype(F32) + g.astype(F32)).astype(BF16) for b, g in zip(blocks, got)]
+    up = [(i, i + 1) for i in range(hop)]
+    down = [(i, i - 1) for i in range(n_dp - hop, n_dp)]
+    return lax.ppermute(blocks[0], "dp", up), lax.ppermute(blocks[1], "dp", down)
 
 
 def after_of(value, *others):
@@ -1303,30 +1358,53 @@
     normed2 = normed2.reshape(length, width)
 
     z = lax.axis_index("dp").astype(jnp.int32).reshape(1)
-    carried, chunk_grads = (), []
     hidden = w_gate.shape[2]
-    chunks = [(0, 0, 256), (0, 256, hidden)] + [(e, 0, hidden) for e in range(1, own_e)]
-    for e, low, high in chunks:
-        if low == 0:
-            cuts = [(f, g) for o, f, g in chunks if o == e]
-            packed_e = pack(cuts, w_gate[e], w_up[e], w_down[e])
-        block = packed_e[cuts.index((low, high))]
-        if e == 0:
-            sources = [(lax.all_gather(block, "dp", axis=0, tiled=False), "all", 0, 0)]
+
+    def run(e, sources, carried, low, grads):
+        moe, rows_grad, grads = expert(
+            z,
+            normed2,
+            top_all,
+            my_probs[:, e : e + 1],
+            n_dp,
+            sources,
+            carried,
+            tokens,
+            low,
+            hidden,
+            grads,
+        )
+        return (moe, rows_grad), grads
+
+    cuts = [(0, 256), (256, hidden)]
+    blocks0 = pack(cuts, w_gate[0], w_up[0], w_down[0])
+    carried, grads0 = (), ()
+    for index, (low, high) in enumerate(cuts):
+        full = lax.all_gather(blocks0[index], "dp", axis=0, tiled=False)
+        if index == 1:
+            (block1,) = pack([(0, hidden)], w_gate[1], w_up[1], w_down[1])
+            sources1 = [(block1, "up", 0, 0)]
+            up = down = after_of(block1, full)
+            up, down = line_hop(up, down, n_dp, 1)
+            sources1 += [(up, "up", 1, 0), (down, "down", 1, 0)]
+        carried, grads = run(0, [(full, "all", 0, 0)], carried, low, grads0)
+        grads0 = (grads,)
+    got = None
+    for hop in range(2, n_dp + 1):
+        if hop == 2:
+            up, down, grads = lax.optimization_barrier((up, down, grads))
         else:
-            sources = [(block, "up", 0, 0)]
-            up = down = after_of(block, after)
-            for hop in range(1, n_dp):
-                if hop == 2:
-                    up, down = after_of(up, *carried), after_of(down, *carried)
-                up, down = line_hop(up, down, n_dp, hop)
-                sources += [(up, "up", hop, 0), (down, "down", hop, 0)]
-        moe, rows_grad, grads = expert(
-            z, normed2, top_all, my_probs[:, e : e + 1], n_dp, sources, carried, tokens
-        )
-        carried = (moe, rows_grad)
-        grads = grads.reshape(3 * width, high - low)
-        chunk_grads.append(lax.psum_scatter(grads, "dp", scatter_dimension=0, tiled=True))
+            up, down, got = lax.optimization_barrier((up, down, got))
+        if hop < n_dp:
+            up, down = line_hop(up, down, n_dp, hop)
+            sources1 += [(up, "up", hop, 0), (down, "down", hop, 0)]
+        got = reduce_hop(grads, got, n_dp, hop - 1)
+    (moe, rows_grad), grads1 = run(1, sources1, carried, 0, ())
+    own0 = lax.dynamic_index_in_dim(grads, lax.axis_index("dp"), 0, False).astype(F32)
+    done1 = lax.psum_scatter(
+        grads1.reshape(3 * width, hidden), "dp", scatter_dimension=0, tiled=True
+    )
+    done0 = own0 + got[0].astype(F32) + got[1].astype(F32)
     mid, ffn_part, branch = turn(
         n_ctx, rows_grad.reshape(blocks), after, top_own, gain_ffn
     )
@@ -1341,7 +1419,8 @@
     moe = after_of(moe, attn_part)
     layer_output = close(n_ctx, moe.reshape(blocks), after)
 
-    out_w = lax.ppermute(out_w, both, [(b, a) for a, b in forth]).astype(F32)
+    out_w = lax.ppermute(out_w, both, [(b, a) for a, b in forth])
+    out_w = out_w.astype(F32)
     qkv_w = dot(normed, dqkv, TN).astype(BF16)
     qkv_w = scatter_dp(qkv_w)
     n_all = n_dp * n_ctx
@@ -1356,14 +1435,10 @@
         axis=1,
     )
     packed = packed.reshape(n_dp, n_ctx, 8, HD).transpose(1, 0, 2, 3)
-    qkv_w, packed = post(n_ctx, n_dp, qkv_w.reshape(n_ctx, depth, qw + 2 * HD), packed)
-    packed = packed.reshape(1024)
-    query_w = qkv_w[:, :, :qw].transpose(1, 0, 2).reshape(depth, HQ * HD).astype(F32)
-    kv_w = jnp.sum(qkv_w[:, :, qw:].astype(F32).reshape(KV, share, depth, 2 * HD), axis=1)
-    key_w = kv_w[:, :, :HD].transpose(1, 0, 2).reshape(depth, KV * HD)
-    value_w = kv_w[:, :, HD:].transpose(1, 0, 2).reshape(depth, KV * HD)
-
-    gate_w, up_w, down_w = unpack(own_e, chunks, chunk_grads, hidden)
+    packed = gains_sum(n_ctx, n_dp, after_of(packed, layer_output)).reshape(1024)
+    query_w, key_w, value_w = post(n_ctx, qkv_w.reshape(n_ctx, depth, qw + 2 * HD))
+
+    gate_w, up_w, down_w = unpack(own_e, [(0, 0, hidden), (1, 0, hidden)], [done0, done1], hidden)
     return (
         layer_output.reshape(1, tokens, width),
         input_grad.reshape(1, tokens, width),

time: 1230 us -> 1150 us (0.935)
  waiting for transfers between devices: 464 us -> 309 us
  Pallas kernels: 650 us -> 691 us
  other arithmetic: 12.3 us -> 28.8 us
    reduce_scatter x3 -> x1, waiting for transfers between devices: 255 us -> 0.02 us  [per_device(): lax.psum_scatter(grads1.reshape(3 * width, hidden), 'dp', scatter_dimensi...]
    ppermute x1 -> x7, waiting for transfers between devices: 39.1 us -> 198 us  [the longest x3 144 us: reduce_hop(): lax.ppermute(blocks[0], 'dp', up)]
    ppermute x3, waiting for transfers between devices: 47.9 us -> 0.9 us  [line_hop(): lax.ppermute(block_up, 'dp', up)]
    pallas_call x7 -> x8, Pallas kernels: 353 us -> 392 us  [comm_call(): pl.pallas_call(kernel, out_shape=outs, in_specs=in_specs, out_specs=out_s...]
    ppermute x1 -> x7, starting transfers between devices: 3.25 us -> 17.3 us  [the longest x3 7.26 us: reduce_hop(): lax.ppermute(blocks[1], 'dp', down)]
    all_gather x2, waiting for transfers between devices: 16.6 us -> 3.3 us  [per_device(): full = lax.all_gather(blocks0[index], 'dp', axis=0, tiled=False)]
    convert_element_type x1 -> x3, other arithmetic: 1.07 us -> 13.8 us  [the longest x2 12.7 us: reduce_hop(): (b.astype(F32) + g.astype(F32)).astype(BF16)]
  transfers between devices with their start and end apart: 17 -> 21, of which waited for: 8 -> 8; matrix products, arithmetic and copies ran while one was open for 3% -> 5% of each run, Pallas kernels for 38% -> 45%
where the time goes in v4:
time: 1150 us; the launch traced here: 1140 us
  Pallas kernels  691 us (60%)
  waiting for transfers between devices  309 us (27%)
  starting transfers between devices  39.2 us (3%)
  local copies, waits for them, and re-layouts  32.2 us (3%)
  other arithmetic  28.8 us (3%)
  matrix products  21.3 us (2%)
  between operations  14.9 us (1%)
    pallas_call x8, Pallas kernels, comm_call(): pl.pallas_call(kernel, out_shape=outs, in_specs=in_specs, out_specs=out_s...  392 us
    pallas_call x3, Pallas kernels, expert(): pl.pallas_call(functools.partial(expert_kernel, len(before) > 0, low, len...  164 us
    ppermute x3, waiting for transfers between devices, reduce_hop(): lax.ppermute(blocks[0], 'dp', up)  144 us
    pallas_call x1, Pallas kernels, attn_backward(): pl.pallas_call(functools.partial(attn_backward_kernel, heads, MOST // row...  65.3 us
    pallas_call x1, Pallas kernels, attn_forward(): pl.pallas_call(functools.partial(attn_forward_kernel, n, heads, MOST // r...  55.3 us
    ppermute x1, waiting for transfers between devices, per_device(): out_w = lax.ppermute(out_w, both, [(b, a) for a, b in forth])  53.8 us
    ppermute x3, waiting for transfers between devices, line_hop(): lax.ppermute(block_down, 'dp', down)  53.6 us
    ppermute x1, waiting for transfers between devices, per_device(): wout = lax.ppermute(after_of(w_out, small), both, forth)  51.6 us
  transfers between devices with their start and end apart: 21, of which 8 were waited for; matrix products, arithmetic and copies ran while one was open for 5% of the time, Pallas kernels for 45%

profile of v4, /device:TPU:14, one launch (start us, length us, event | category | flops | bytes accessed | tf_op | source)
XLA Modules:
  0.0 1136.1 jit_solution(11875598718046265576)
XLA Ops:
  11.1 14.2 %shard_map.255 = (bf16[8,64,768]{2,1,0:T(8,128)(2,1)}, f32[4,8,8,128]{3,2,1,0:T(8,128)}) custom-call(bf16[8,64,768]{2,1,0:T(8,128)(2,1)} %maximum_bitcast_fusion.cols_ref, f32[8,128]{1,0:T(8,128)} %fusion.16.small_ref), custom_call_target="tpu_custom_call" | custom-call | bytes 24000000 | tf_op jit(solution)/shard_map/pallas_call | solution.py:422
  26.5 3.0 collective-permute-start
  29.4 51.6 %collective-permute-done = bf16[128,2048]{1,0:T(8,128)(2,1)} collective-permute-done((bf16[128,2048]{1,0:T(8,128)(2,1)}, bf16[128,2048]{1,0:T(8,128)(2,1)}, u32[]{:S(2)}, u32[]{:S(2)}) %collective-permute-start) | collective-permute-done | bytes 524320 | tf_op jit(solution)/shard_map/ppermute | solution.py:1329
  83.1 1.7 slice_bitcast_fusion.1
  84.8 3.3 pack.2
  90.3 45.3 %shard_map.256 = (bf16[8,256,2048]{2,1,0:T(8,128)(2,1)}, f32[8,24,256]{2,1,0:T(8,128)}) custom-call(bf16[256,2048]{1,0:T(8,128)(2,1)} %bitcast.96, f32[1,2048]{1,0:T(1,128)} %reshape.160.gain_ref, f32[24,256]{1,0:T(8,128)} %maximum_maximum_fusion.info_ref), custom_call_target="tpu_custom_call" | custom-call | bytes 150000000 | tf_op jit(solution)/shard_map/pallas_call | solution.py:422
  136.5 1.3 copy.47.docc_ref
  141.0 3.4 pack.3.rest_2_
  144.4 3.9 fusion.7
  148.3 1.9 pad_maximum_fusion
  150.2 1.7 fusion.17
  151.9 55.3 %attn_forward.1 = (f32[2048,512]{1,0:T(8,128)}, f32[2048,128]{1,0:T(8,128)}, bf16[2048,512]{1,0:T(8,128)(2,1)}, bf16[2048,128]{1,0:T(8,128)(2,1)}, bf16[2048,128...) custom-call(bf16[2048,2048]{1,0:T(8,128)(2,1)} %bitcast.121, ...), custom_call_target="tpu_custom_call" | custom-call | flops 35000000512 | bytes 31457280 | tf_op jit(solution)/shard_map/attn_forward/pallas_call | solution.py:884
  207.3 86.8 %shard_map.257 = (f32[256,2048]{1,0:T(8,128)}, bf16[8,256,2048]{2,1,0:T(8,128)(2,1)}) custom-call(bf16[2048,512]{1,0:T(8,128)(2,1)} %get-tuple-element.68.attn_ref, bf16[512,2048]{1,0:T(8,128)(2,1)} %all-gather.9.cloned.1.call-done.wout_ref, bf16[256,2048]{1,0:T(8,128)(2,1)} %bitcast.97, f32[1,2048]{1,0:T(1,128)} %reshape.166.gain_ref), custom_call_target="tpu_custom_call" | custom-call | bytes 315000000 | tf_op jit(solution)/shard_map/pallas_call | solution.py:422
  294.2 32.9 %expert.3 = (bf16[2048,2048]{1,0:T(8,128)(2,1)}, bf16[2048,2048]{1,0:T(8,128)(2,1)}, bf16[4,1536,768]{2,1,0:T(8,128)(2,1)}) custom-call(s32[1]{0:T(128)} %bitcast.z_ref, bf16[2048,2048]{1,0:T(8,128)(2,1)} %bitcast.123, bf16[2048,2048]{1,0:T(8,128)(2,1)} %bitcast.130, f32[2048,1]{1,0:T(8,128)} %get-tuple-element.129.prob_ref, bf16[4,1536,256]{2,1,0:T(8,128)(2,1)} %bitcast.129), custom_call_target="tpu_custom_call" | custom-call | flops 19327352832 | bytes 41943040 | tf_op jit(solution)/shard_map/expert/pallas_call | solution.py:1180
  327.1 3.3 all-gather.13.cloned.1.call-done
  330.4 4.3 collective-permute-start.1
  334.7 4.1 collective-permute-start.2
  338.8 55.4 %expert.4 = (bf16[2048,2048]{1,0:T(8,128)(2,1)}, bf16[2048,2048]{1,0:T(8,128)(2,1)}, bf16[4,1536,768]{2,1,0:T(8,128)(2,1)}) custom-call(s32[1]{0:T(128)} %bitcast.z_ref, bf16[2048,2048]{1,0:T(8,128)(2,1)} %bitcast.124, bf16[2048,2048]{1,0:T(8,128)(2,1)} %bitcast.131, f32[2048,1]{1,0:T(8,128)} %get-tuple-element.129.prob_ref, ...), custom_call_target="tpu_custom_call", output_to_operand_aliasing={{2}: (4, {})} | custom-call | flops 38654705664 | bytes 41943040 | tf_op jit(solution)/shard_map/expert/pallas_call | solution.py:1180
  394.3 2.7 dynamic-slice_bitcast_fusion
  398.3 2.1 collective-permute-start.6
  400.4 1.4 collective-permute-start.3
  401.8 4.1 collective-permute-start.4
  405.9 46.2 %collective-permute-done.5 = bf16[1536,768]{1,0:T(8,128)(2,1)S(1)} collective-permute-done((bf16[1536,768]{1,0:T(8,128)(2,1)S(1)}, bf16[1536,768]{1,0:T(8,128)(2,1)S(1)}, u32[]{:S(2)}, u32[]{:S(2)}) %collective-permute-start.5) | collective-permute-done | bytes 2359328 | tf_op jit(solution)/shard_map/ppermute | solution.py:1267
  453.0 4.2 collective-permute-done.4.rest_6_
  458.0 3.9 collective-permute-start.8
  461.9 49.4 %collective-permute-done.8.rest_8_ = bf16[1536,768]{1,0:T(8,128)(2,1)S(1)} collective-permute-done((bf16[1536,768]{1,0:T(8,128)(2,1)S(1)}, bf16[1536,768]{1,0:T(8,128)(2,1)S(1)}, u32[]{:S(2)}, u32[]{:S(2)}) %collective-permute-start.8) | collective-permute-done | bytes 2359328 | tf_op jit(solution)/shard_map/ppermute | solution.py:1255
  511.4 1.6 copy-done.23
  513.0 76.0 %expert.5 = (bf16[2048,2048]{1,0:T(8,128)(2,1)}, bf16[2048,2048]{1,0:T(8,128)(2,1)}, bf16[4,1536,768]{2,1,0:T(8,128)(2,1)}) custom-call(s32[1]{0:T(128)} %bitcast.z_ref, bf16[2048,2048]{1,0:T(8,128)(2,1)} %bitcast.125, bf16[2048,2048]{1,0:T(8,128)(2,1)} %bitcast.132, f32[2048,1]{1,0:T(8,128)} %get-tuple-element.130.prob_ref, ...), custom_call_target="tpu_custom_call" | custom-call | flops 57982058496 | bytes 41943040 | tf_op jit(solution)/shard_map/expert/pallas_call | solution.py:1180
  588.9 83.8 %shard_map.258 = (f32[256,2048]{1,0:T(8,128)}, f32[8,2048]{1,0:T(8,128)}, bf16[8,256,2048]{2,1,0:T(8,128)(2,1)}) custom-call(bf16[8,256,2048]{2,1,0:T(8,128)(2,1)} %bitcast.99, f32[256,2048]{1,0:T(8,128)} %get-tuple-element.88.after_ref, bf16[256,2048]{1,0:T(8,128)(2,1)} %bitcast.105, f32[1,2048]{1,0:T(1,128)} %reshape.166.gain_ref), custom_call_target="tpu_custom_call" | custom-call | bytes 285000000 | tf_op jit(solution)/shard_map/pallas_call | solution.py:422
  672.8 9.9 convolution_convert_fusion.1
  682.7 65.3 %attn_backward.1 = (bf16[2048,768]{1,0:T(8,128)(2,1)}, f32[8,128]{1,0:T(8,128)}) custom-call(bf16[2048,2048]{1,0:T(8,128)(2,1)} %bitcast.127, bf16[512,2048]{1,0:T(8,128)(2,1)} %all-gather.9.cloned.1.call-done.wout_ref, bf16[2048,512]{1,0:T(8,128)(2,1)} %get-tuple-element.68.attn_ref, f32[2048,128]{1,0:T(8,128)} %get-tuple-element.90.total_ref, ...), custom_call_target="tpu_custom_call" | custom-call | flops 60000002048 | bytes 31457280 | tf_op jit(solution)/shard_map/attn_backward/pallas_call | solution.py:1034
  748.0 11.4 %convolution_convert_fusion = bf16[2048,768]{1,0:T(8,128)(2,1)} fusion(bf16[2048,2048]{1,0:T(8,128)(2,1)} %bitcast.122, bf16[2048,768]{1,0:T(8,128)(2,1)} %get-tuple-element.96.grad_ref), kind=kOutput, calls=%fused_computation.10 | convolution fusion | flops 6444023808 | bytes 14680064 | tf_op jit(solution)/shard_map/dot_general | solution.py:26
  760.1 6.4 fusion.1
  766.6 2.1 collective-permute-start.10
  770.0 98.1 %collective-permute-done.10 = bf16[1536,768]{1,0:T(8,128)(2,1)S(1)} collective-permute-done((bf16[1536,768]{1,0:T(8,128)(2,1)}, bf16[1536,768]{1,0:T(8,128)(2,1)S(1)}, u32[]{:S(2)}, u32[]{:S(2)}) %collective-permute-start.10) | collective-permute-done | bytes 2359328 | tf_op jit(solution)/shard_map/ppermute | solution.py:1267
  868.1 1.4 copy-done.3
  869.5 6.3 fusion.3
  875.8 3.3 collective-permute-start.12
  879.1 3.9 collective-permute-start.13
  883.0 51.4 %shard_map.259 = (f32[256,2048]{1,0:T(8,128)}, f32[8,2048]{1,0:T(8,128)}) custom-call(bf16[2048,768]{1,0:T(8,128)(2,1)} %get-tuple-element.96.grad_ref, bf16[2048,768]{1,0:T(8,128)(2,1)} %all-gather.7.cloned.1.call-done.wqkv_ref, bf16[256,2048]{1,0:T(8,128)(2,1)} %bitcast.98, f32[256,2048]{1,0:T(8,128)} %get-tuple-element.97.mid_ref, ...), custom_call_target="tpu_custom_call" | custom-call | bytes 180000000 | tf_op jit(solution)/shard_map/pallas_call | solution.py:422
  937.3 42.2 %shard_map.260 = bf16[256,2048]{1,0:T(8,128)(2,1)} custom-call(bf16[8,256,2048]{2,1,0:T(8,128)(2,1)} %bitcast.100, f32[256,2048]{1,0:T(8,128)} %get-tuple-element.88.after_ref), custom_call_target="tpu_custom_call" | custom-call | bytes 150000000 | tf_op jit(solution)/shard_map/pallas_call | solution.py:422
  980.4 44.3 %shard_map.261 = f32[8,128]{1,0:T(8,128)} custom-call(f32[8,4,8,128]{3,2,1,0:T(8,128)} %copy_bitcast_fusion.3.small_ref), custom_call_target="tpu_custom_call" | custom-call | bytes 30000000 | tf_op jit(solution)/shard_map/pallas_call | solution.py:422
  1024.7 1.3 fusion.21
  1027.4 3.3 collective-permute-start.9
  1030.7 6.0 fusion.4.refs_0_
  1036.7 53.8 %collective-permute-done.9 = bf16[128,2048]{1,0:T(8,128)(2,1)S(1)} collective-permute-done((bf16[128,2048]{1,0:T(8,128)(2,1)}, bf16[128,2048]{1,0:T(8,128)(2,1)S(1)}, u32[]{:S(2)}, u32[]{:S(2)}) %collective-permute-start.9) | collective-permute-done | bytes 524320 | tf_op jit(solution)/shard_map/ppermute | solution.py:1422
  1091.6 23.5 %shard_map.262 = (f32[64,4096]{1,0:T(8,128)}, f32[64,512]{1,0:T(8,128)}, f32[64,512]{1,0:T(8,128)}) custom-call(bf16[8,64,768]{2,1,0:T(8,128)(2,1)} %bitcast.106), custom_call_target="tpu_custom_call" | custom-call | bytes 30000000 | tf_op jit(solution)/shard_map/pallas_call | solution.py:422
  1115.1 7.8 unpack.1
  (118 shorter events, 30.6 us)
Async XLA Ops:
  7.2 1.2 copy-start
  7.2 3.2 copy-start.19
  7.2 3.2 copy-start.18
  7.2 3.2 copy-start.17
  7.2 3.2 copy-start.16
  7.2 144.7 %all-gather.7.cloned.1.call-start = ((), (), s32[]{:S(2)}) async-start(), calls=%async_computation.3 | async-start | bytes 3932160 | tf_op jit(solution)/shard_map/all_gather | solution.py:1327
  8.4 72.7 %copy-start.6 = (bf16[2,768,512]{2,1,0:T(8,128)(2,1)S(1)}, bf16[2,768,512]{2,1,0:T(8,128)(2,1)}, u32[]{:S(2)}) copy-start(bf16[2,768,512]{2,1,0:T(8,128)(2,1)} %param.30) | copy-start | bytes 4718596
  25.3 57.1 %copy-start.7 = (bf16[2,512,768]{2,1,0:T(8,128)(2,1)S(1)}, bf16[2,512,768]{2,1,0:T(8,128)(2,1)}, u32[]{:S(2)}) copy-start(bf16[2,512,768]{2,1,0:T(8,128)(2,1)} %param.29) | copy-start | bytes 4718596
  25.4 181.9 %all-gather.9.cloned.1.call-start = ((), (), s32[]{:S(2)}) async-start(), calls=%async_computation.4 | async-start | bytes 2621440 | tf_op jit(solution)/shard_map/all_gather | solution.py:1330
  26.5 54.6 %collective-permute-start = (bf16[128,2048]{1,0:T(8,128)(2,1)}, bf16[128,2048]{1,0:T(8,128)(2,1)}, u32[]{:S(2)}, u32[]{:S(2)}) collective-permute-start(bf16[128,2048]{1,0:T(8,128)(2,1)} %param.27), channel_id=1, source_target_pairs={{0,0},{4,1},{8,2},{12,3},{16,4},{20,5},{24,6},{28,7},{1,8},{5,9},{... | collective-permute-start | bytes 1572872 | tf_op jit(solution)/shard_map/ppermute | solution.py:1329
  81.1 213.1 %all-gather.11.cloned.1.call-start = ((), (), s32[]{:S(2)}) async-start(), calls=%async_computation.8 | async-start | bytes 3932160 | tf_op jit(solution)/shard_map/all_gather | solution.py:1383
  81.1 2.0 copy-start.8
  84.8 4.7 copy-start.15
  84.8 4.8 copy-start.13
  84.8 4.8 copy-start.14
  88.1 242.2 %all-gather.13.cloned.1.call-start = ((), (), s32[]{:S(2)}) async-start(), calls=%async_computation.9 | async-start | bytes 7864320 | tf_op jit(solution)/shard_map/all_gather | solution.py:1383
  88.7 938.6 %reduce-scatter.6.cloned.1.call-start = ((), (), s32[]{:S(2)}) async-start(), calls=%async_computation.6 | async-start | bytes 2621440 | tf_op jit(solution)/shard_map/reduce_scatter | solution.py:1275
  136.5 7.9 copy-start.12
  294.1 36.2 %copy-start.4 = (bf16[1536,768]{1,0:T(8,128)(2,1)S(1)}, bf16[1536,768]{1,0:T(8,128)(2,1)}, u32[]{:S(2)}) copy-start(bf16[1536,768]{1,0:T(8,128)(2,1)} %pack.3.rest_2_) | copy-start | bytes 7077892
  330.4 63.9 %collective-permute-start.1 = (bf16[1536,768]{1,0:T(8,128)(2,1)S(1)}, bf16[1536,768]{1,0:T(8,128)(2,1)}, u32[]{:S(2)}, u32[]{:S(2)}) collective-permute-start(bf16[1536,768]{1,0:T(8,128)(2,1)S(1)} %copy-done.4), channel_id=1, source_target_pairs={{0,8},{8,16},{16,24},{1,9},{9,17},{17,25},{2,10},{10,18},{18,26},{... | collective-permute-start | bytes 7077896 | tf_op jit(solution)/shard_map/ppermute | solution.py:1255
  334.7 59.6 %collective-permute-start.2 = (bf16[1536,768]{1,0:T(8,128)(2,1)S(1)}, bf16[1536,768]{1,0:T(8,128)(2,1)}, u32[]{:S(2)}, u32[]{:S(2)}) collective-permute-start(bf16[1536,768]{1,0:T(8,128)(2,1)S(1)} %copy-done.4), channel_id=1, source_target_pairs={{8,0},{16,8},{24,16},{9,1},{17,9},{25,17},{10,2},{18,10},{26,18},{... | collective-permute-start | bytes 7077896 | tf_op jit(solution)/shard_map/ppermute | solution.py:1255
  397.0 55.1 %collective-permute-start.5 = (bf16[1536,768]{1,0:T(8,128)(2,1)S(1)}, bf16[1536,768]{1,0:T(8,128)(2,1)S(1)}, u32[]{:S(2)}, u32[]{:S(2)}) collective-permute-start(bf16[1536,768]{1,0:T(8,128)(2,1)S(1)} %get-tuple-element.122), channel_id=1, source_target_pairs={{0,8},{1,9},{2,10},{3,11},{4,12},{5,13},{6,14},{7,15}} | collective-permute-start | bytes 7077896 | tf_op jit(solution)/shard_map/ppermute | solution.py:1267
  398.3 53.8 %collective-permute-start.6 = (bf16[1536,768]{1,0:T(8,128)(2,1)S(1)}, bf16[1536,768]{1,0:T(8,128)(2,1)}, u32[]{:S(2)}, u32[]{:S(2)}) collective-permute-start(bf16[1536,768]{1,0:T(8,128)(2,1)S(1)} %get-tuple-element.121), channel_id=1, source_target_pairs={{24,16},{25,17},{26,18},{27,19},{28,20},{29,21},{30,22},{31,23}} | collective-permute-start | bytes 7077896 | tf_op jit(solution)/shard_map/ppermute | solution.py:1267
  400.4 52.6 %collective-permute-start.3 = (bf16[1536,768]{1,0:T(8,128)(2,1)}, bf16[1536,768]{1,0:T(8,128)(2,1)S(1)}, u32[]{:S(2)}, u32[]{:S(2)}) collective-permute-start(bf16[1536,768]{1,0:T(8,128)(2,1)} %collective-permute-done.1.rest_3_), channel_id=1, source_target_pairs={{8,16},{16,24},{9,17},{17,25},{10,18},{18,26},{11,19},{19,27},{12,... | collective-permute-start | bytes 7077896 | tf_op jit(solution)/shard_map/ppermute | solution.py:1255
  401.8 55.4 %collective-permute-start.4 = (bf16[1536,768]{1,0:T(8,128)(2,1)}, bf16[1536,768]{1,0:T(8,128)(2,1)S(1)}, u32[]{:S(2)}, u32[]{:S(2)}) collective-permute-start(bf16[1536,768]{1,0:T(8,128)(2,1)} %collective-permute-done.2.rest_4_), channel_id=1, source_target_pairs={{8,0},{16,8},{9,1},{17,9},{10,2},{18,10},{11,3},{19,11},{12,4},{20... | collective-permute-start | bytes 7077896 | tf_op jit(solution)/shard_map/ppermute | solution.py:1255
  453.0 4.2 copy-start.20
  457.2 4.8 copy-start.21
  457.2 4.8 collective-permute-start.7
  458.0 53.4 %collective-permute-start.8 = (bf16[1536,768]{1,0:T(8,128)(2,1)S(1)}, bf16[1536,768]{1,0:T(8,128)(2,1)S(1)}, u32[]{:S(2)}, u32[]{:S(2)}) collective-permute-start(bf16[1536,768]{1,0:T(8,128)(2,1)S(1)} %collective-permute-done.4.rest_6_), channel_id=1, source_target_pairs={{8,0},{9,1},{10,2},{11,3},{12,4},{13,5},{14,6},{15,7}} | collective-permute-start | bytes 7077896 | tf_op jit(solution)/shard_map/ppermute | solution.py:1255
  461.9 49.4 %copy-start.22 = (bf16[1536,768]{1,0:T(8,128)(2,1)}, bf16[1536,768]{1,0:T(8,128)(2,1)S(1)}, u32[]{:S(2)}) copy-start(bf16[1536,768]{1,0:T(8,128)(2,1)S(1)} %collective-permute-done.7.rest_7_) | copy-start | bytes 7077892
  511.4 1.6 copy-start.23
  682.7 408.9 %reduce-scatter.4.cloned.1.call-start = ((), (), s32[]{:S(2)}) async-start(), calls=%async_computation.5 | async-start | bytes 3932160 | tf_op jit(solution)/shard_map/reduce_scatter | solution.py:1275
  759.4 355.7 %reduce-scatter.8.cloned.1.call-start = ((), (), s32[]{:S(2)}) async-start(), calls=%async_computation.7 | async-start | bytes 11796480 | tf_op jit(solution)/shard_map/reduce_scatter | solution.py:1404
  766.6 101.5 %collective-permute-start.10 = (bf16[1536,768]{1,0:T(8,128)(2,1)}, bf16[1536,768]{1,0:T(8,128)(2,1)S(1)}, u32[]{:S(2)}, u32[]{:S(2)}) collective-permute-start(bf16[1536,768]{1,0:T(8,128)(2,1)} %get-tuple-element.120), channel_id=1, source_target_pairs={{0,8},{8,16},{1,9},{9,17},{2,10},{10,18},{3,11},{11,19},{4,12},{12... | collective-permute-start | bytes 7077896 | tf_op jit(solution)/shard_map/ppermute | solution.py:1267
  768.6 100.9 %collective-permute-start.11 = (bf16[1536,768]{1,0:T(8,128)(2,1)}, bf16[1536,768]{1,0:T(8,128)(2,1)}, u32[]{:S(2)}, u32[]{:S(2)}) collective-permute-start(bf16[1536,768]{1,0:T(8,128)(2,1)} %get-tuple-element.119), channel_id=1, source_target_pairs={{16,8},{24,16},{17,9},{25,17},{18,10},{26,18},{19,11},{27,19},{20,... | collective-permute-start | bytes 7077896 | tf_op jit(solution)/shard_map/ppermute | solution.py:1267
  868.1 1.4 copy-start.3
  875.8 154.8 %collective-permute-start.12 = (bf16[1536,768]{1,0:T(8,128)(2,1)}, bf16[1536,768]{1,0:T(8,128)(2,1)}, u32[]{:S(2)}, u32[]{:S(2)}) collective-permute-start(bf16[1536,768]{1,0:T(8,128)(2,1)} %get-tuple-element.117), channel_id=1, source_target_pairs={{0,8},{8,16},{16,24},{1,9},{9,17},{17,25},{2,10},{10,18},{18,26},{... | collective-permute-start | bytes 7077896 | tf_op jit(solution)/shard_map/ppermute | solution.py:1267
  879.1 151.5 %collective-permute-start.13 = (bf16[1536,768]{1,0:T(8,128)(2,1)S(1)}, bf16[1536,768]{1,0:T(8,128)(2,1)}, u32[]{:S(2)}, u32[]{:S(2)}) collective-permute-start(bf16[1536,768]{1,0:T(8,128)(2,1)S(1)} %get-tuple-element.118), channel_id=1, source_target_pairs={{8,0},{16,8},{24,16},{9,1},{17,9},{25,17},{10,2},{18,10},{26,18},{... | collective-permute-start | bytes 7077896 | tf_op jit(solution)/shard_map/ppermute | solution.py:1267
  1027.4 63.1 %collective-permute-start.9 = (bf16[128,2048]{1,0:T(8,128)(2,1)}, bf16[128,2048]{1,0:T(8,128)(2,1)S(1)}, u32[]{:S(2)}, u32[]{:S(2)}) collective-permute-start(bf16[128,2048]{1,0:T(8,128)(2,1)} %reduce-scatter.6.cloned.1.call-done), channel_id=1, source_target_pairs={{0,0},{1,4},{2,8},{3,12},{4,16},{5,20},{6,24},{7,28},{8,1},{9,5},{... | collective-permute-start | bytes 1572872 | tf_op jit(solution)/shard_map/ppermute | solution.py:1422
  1115.1 7.8 copy-start.2
  1122.9 2.0 copy-start.5
  1124.9 1.9 copy-start.9
  1124.9 2.9 copy-start.11
  1124.9 3.6 copy-start.10
  1124.9 4.2 copy-start.1
Sparse Core Ops, SparseCore 0:
  25.5 78.3 all-gather.6
  105.4 46.4 all-gather.8
  153.5 61.3 all-gather.10
  216.9 113.4 all-gather.12
  682.8 43.0 reduce-scatter.5
  759.5 101.3 reduce-scatter.3
  863.2 247.7 reduce-scatter.7

commit v5 on v4

--- a/solution.py
+++ b/solution.py
@@ -19,6 +19,7 @@
 F32 = jnp.float32
 BF16 = jnp.bfloat16
 SCALE = 1.0 / math.sqrt(HD)
+SCALE2 = SCALE / math.log(2.0)
 VMEM_LIMIT = 60 * 1024 * 1024
 
 
@@ -267,10 +268,12 @@
             copy.start()
             self.sent.append(copy)
 
-    def settle(self):
+    def settle(self, extra=None):
         mine, landed = self.mine, self.landed
         half = mine.shape[1] // 2
         if not self.square:
+            if extra is not None:
+                extra()
             for copy in self.sent:
                 copy.wait_recv()
             return
@@ -284,6 +287,8 @@
 
             by_rows(half, add)
             self.go(s, h, s)
+        if extra is not None:
+            extra()
         for s in (1, 2):
             for h in (0, 1):
                 self.copy(s, h, s).wait_recv()
@@ -322,7 +327,7 @@
             self.across[s].start()
             self.loads[s].start()
 
-    def run(self):
+    def run(self, extra=None):
         mine, other = self.mine, self.other
         for s in self.order:
             self.loads[s].wait()
@@ -334,6 +339,8 @@
 
             by_rows(mine.shape[1], add)
             self.spread.ready(s)
+        if extra is not None:
+            extra()
         self.spread.settle()
 
     def total(self, at):
@@ -367,7 +374,7 @@
             by_cols(self.mine.shape[2], fill)
             self.across[s].start()
 
-    def run(self):
+    def run(self, extra=None):
         plane, mine, other = self.plane, self.mine, self.other
         for s in self.order:
             block = plane.same(s)
@@ -379,7 +386,7 @@
 
             by_cols(mine.shape[2], fill)
             self.spread.ready(s)
-        self.spread.settle()
+        self.spread.settle(extra)
 
     total = Scatter.total
     finish = Scatter.finish
@@ -444,6 +451,39 @@
         copies.append(push(src.at[peer], out.at[me], send.at[s], recv.at[s], "ctx", peer))
         copies[-1].start()
     return own, copies
+
+
+class RowSwap:
+    def __init__(self, n, n_dp, src, dst, send, recv, spread):
+        self.me = lax.axis_index("ctx")
+        self.dst, self.send, self.recv, self.n_dp = dst, send, recv, n_dp
+        self.entries = []
+        for k in range(n_dp):
+            flat = self.me * n_dp + k if spread else k * n + self.me
+            peer = flat % n if spread else flat // n_dp
+            slot = flat // n if spread else flat % n_dp
+            far = push(src.at[k], dst.at[slot], send.at[k], recv.at[slot], "ctx", peer)
+            near = pltpu.make_async_copy(src.at[k], dst.at[slot], recv.at[slot])
+            self.entries.append((peer, far, near))
+
+    def start(self):
+        for peer, far, near in self.entries:
+            pl.when(peer != self.me)(far.start)
+            pl.when(peer == self.me)(near.start)
+
+    def arrive(self):
+        for slot in range(self.n_dp):
+            block = self.dst.at[slot]
+            pltpu.make_async_copy(block, block, self.recv.at[slot]).wait()
+
+    def finish(self):
+        for peer, far, near in self.entries:
+            pl.when(peer != self.me)(far.wait_send)
+
+
+def meet_all(n):
+    me = lax.axis_index("ctx")
+    meet([("ctx", flip(me, s, n)) for s in range(1, n)])
 
 
 def prep_kernel(n, n_dp, cols_ref, small_ref, out_ref, all_ref, *sems):
@@ -474,35 +514,39 @@
     own.wait()
 
 
-def gains_kernel(n, n_dp, small_ref, sum_ref, landed, mid, second, *sems):
-    gsend, grecv, zsend, zrecv = sems
-    me, row = lax.axis_index("ctx"), lax.axis_index("dp")
-    meet(
-        [("ctx", flip(me, s, n)) for s in range(1, n)]
-        + [("dp", flip(row, s, n_dp)) for s in range(1, n_dp)]
-    )
-    smalls = []
-    for s in range(1, n):
-        peer = flip(me, s, n)
-        smalls.append(push(small_ref.at[peer], landed.at[s], gsend.at[s], grecv.at[s], "ctx", peer))
-        smalls[-1].start()
-    value = small_ref[me]
-    for copy, s in zip(smalls, range(1, n)):
-        copy.wait_recv()
-        value = value + landed[s]
-    mid[...] = value
-    planes = []
-    for s in range(1, n_dp):
-        peer = flip(row, s, n_dp)
-        planes.append(push(mid.at[peer], second.at[s], zsend.at[s], zrecv.at[s], "dp", peer))
-        planes[-1].start()
-    value = mid[row]
-    for copy, s in zip(planes, range(1, n_dp)):
-        copy.wait_recv()
-        value = value + second[s]
-    sum_ref[...] = value
-    for copy in planes + smalls:
-        copy.wait_send()
+class Gains:
+    def __init__(self, n, n_dp, small, landed, mid, second, gsend, grecv, zsend, zrecv):
+        self.me, self.row = lax.axis_index("ctx"), lax.axis_index("dp")
+        self.small, self.landed, self.mid, self.second = small, landed, mid, second
+        self.near, self.far = [], []
+        for s in range(1, n):
+            peer = flip(self.me, s, n)
+            self.near.append(push(small.at[peer], landed.at[s], gsend.at[s], grecv.at[s], "ctx", peer))
+        for s in range(1, n_dp):
+            peer = flip(self.row, s, n_dp)
+            self.far.append(push(mid.at[peer], second.at[s], zsend.at[s], zrecv.at[s], "dp", peer))
+
+    def start(self):
+        for copy in self.near:
+            copy.start()
+
+    def middle(self):
+        value = self.small[self.me]
+        for s, copy in enumerate(self.near, 1):
+            copy.wait_recv()
+            value = value + self.landed[s]
+        self.mid[...] = value
+        for copy in self.far:
+            copy.start()
+
+    def finish(self):
+        value = self.mid[self.row]
+        for s, copy in enumerate(self.far, 1):
+            copy.wait_recv()
+            value = value + self.second[s]
+        for copy in self.near + self.far:
+            copy.wait_send()
+        return value
 
 
 def post_kernel(n, src_ref, query_ref, key_ref, value_ref, blocks, send, recv, local):
@@ -545,28 +589,6 @@
     )
 
 
-def gains_sum(n, n_dp, small):
-    tile = small.shape[2:]
-    return comm_call(
-        functools.partial(gains_kernel, n, n_dp),
-        8,
-        jax.ShapeDtypeStruct(tile, F32),
-        VM,
-        [VM],
-        [
-            pltpu.VMEM((n, n_dp) + tile, F32),
-            pltpu.VMEM((n_dp,) + tile, F32),
-            pltpu.VMEM((n_dp,) + tile, F32),
-            DMA((n,)),
-            DMA((n,)),
-            DMA((n_dp,)),
-            DMA((n_dp,)),
-        ],
-        10,
-        small,
-    )
-
-
 def post(n, cols):
     shape = jax.ShapeDtypeStruct
     depth = cols.shape[1]
@@ -622,14 +644,24 @@
     )
 
 
-def middle_kernel(n, attn_ref, wout_ref, x_ref, gain_ref, after_ref, all_ref, low, *scratch):
+def middle_kernel(
+    n, n_dp, attn_ref, rows_ref, x_ref, gain_ref, after_ref, all_ref, wout_ref, low, *scratch
+):
+    meet_all(n)
     plane = Plane(n)
-    plane.meet()
+    swap = RowSwap(n, n_dp, rows_ref, wout_ref, *scratch[:2], False)
+    swap.start()
+    scratch = scratch[2:]
     rows = x_ref.shape[0]
+    deep = wout_ref.shape[1]
+    swap.arrive()
 
     def value(block, at):
-        left = attn_ref[pl.ds(pl.multiple_of(block * rows, rows), rows), :]
-        return dot(left, wout_ref[:, at])
+        here = pl.ds(pl.multiple_of(block * rows, rows), rows)
+        total = dot(attn_ref[here, :deep], wout_ref[0, :, at])
+        for k in range(1, n_dp):
+            total = total + dot(attn_ref[here, k * deep : (k + 1) * deep], wout_ref[k, :, at])
+        return total
 
     sums = Product(plane, value, *scratch[:8])
     sums.start()
@@ -646,20 +678,23 @@
     normed.forward()
     sums.finish()
     normed.finish()
-
-
-def middle(n, attn, wout, x, gain):
+    swap.finish()
+
+
+def middle(n, n_dp, attn, wrows, x, gain):
     shape = jax.ShapeDtypeStruct
     return comm_call(
-        functools.partial(middle_kernel, n),
+        functools.partial(middle_kernel, n, n_dp),
         3,
-        [shape(x.shape, F32), shape((n,) + x.shape, BF16)],
-        [VM, ANY],
-        [VM, VM, VM, VM],
-        [pltpu.VMEM(x.shape, BF16)] + product_scratch(n, *x.shape) + gather_sems(n),
+        [shape(x.shape, F32), shape((n,) + x.shape, BF16), shape(wrows.shape, BF16)],
+        [VM, ANY, VM],
+        [VM, ANY, VM, VM],
+        [pltpu.VMEM(x.shape, BF16), DMA((n_dp,)), DMA((n_dp,))]
+        + product_scratch(n, *x.shape)
+        + gather_sems(n),
         105,
         attn,
-        wout,
+        wrows,
         x,
         gain,
     )
@@ -715,8 +750,18 @@
 
 
 def last_kernel(
-    n, grad_ref, wqkv_ref, x_ref, mid_ref, gain_ref, out_ref, apart_ref, *scratch
+    n,
+    grad_ref,
+    wqkv_ref,
+    x_ref,
+    mid_ref,
+    gain_ref,
+    *rest,
 ):
+    fused = n == 8
+    normed_ref, rest = (rest[0], rest[1:]) if fused else (None, rest)
+    out_ref, apart_ref, rest = rest[0], rest[1], rest[2:]
+    wgrad_ref, scratch = (rest[0], rest[1:]) if fused else (None, rest)
     plane = Plane(n)
     plane.meet()
     apart_ref[...] = jnp.zeros_like(apart_ref)
@@ -728,7 +773,14 @@
 
     sums = Product(plane, value, *scratch[:8])
     sums.start()
-    sums.run()
+
+    def weights():
+        def fill(at):
+            wgrad_ref[at, :] = dot(normed_ref[:, at], grad_ref[...], TN).astype(BF16)
+
+        by_cols(normed_ref.shape[1], fill)
+
+    sums.run(weights if fused else None)
 
     def norm(at):
         value = x_ref[at, :].astype(F32)
@@ -742,14 +794,17 @@
     sums.finish()
 
 
-def last(n, grad, wqkv, x, mid, gain):
+def last(n, grad, wqkv, x, mid, gain, normed):
     shape = jax.ShapeDtypeStruct
-    return comm_call(
+    outs = [shape(mid.shape, F32), shape((8, mid.shape[1]), F32)]
+    more = [normed] if n == 8 else []
+    outs += [shape(wqkv.shape, BF16) for _ in more]
+    got = comm_call(
         functools.partial(last_kernel, n),
         5,
-        [shape(mid.shape, F32), shape((8, mid.shape[1]), F32)],
-        [VM, VM],
-        [VM] * 5,
+        outs,
+        [VM] * len(outs),
+        [VM] * (5 + len(more)),
         product_scratch(n, *mid.shape),
         60,
         grad,
@@ -757,34 +812,54 @@
         x,
         mid,
         gain,
-    )
-
-
-def close_kernel(n, part_ref, after_ref, out_ref, *scratch):
+        *more,
+    )
+    return got if more else (*got, dot(normed, grad, TN).astype(BF16))
+
+
+def close_kernel(n, n_dp, part_ref, after_ref, small_ref, out_ref, sum_ref, *scratch):
+    meet(
+        [("ctx", flip(lax.axis_index("ctx"), s, n)) for s in range(1, n)]
+        + [("dp", flip(lax.axis_index("dp"), s, n_dp)) for s in range(1, n_dp)]
+    )
     plane = Plane(n)
-    plane.meet()
     sums = Scatter(plane, part_ref, *scratch[:8])
     sums.start()
-    sums.run()
+    gains = Gains(n, n_dp, small_ref, *scratch[8:])
+    gains.start()
+    sums.run(gains.middle)
 
     def add(at):
         out_ref[at, :] = (after_ref[at, :] + sums.total(at)).astype(BF16)
 
     by_rows(after_ref.shape[0], add)
     sums.finish()
-
-
-def close(n, part, after):
+    sum_ref[...] = gains.finish()
+
+
+def close(n, n_dp, part, after, small):
+    shape = jax.ShapeDtypeStruct
+    tile = small.shape[2:]
     return comm_call(
-        functools.partial(close_kernel, n),
+        functools.partial(close_kernel, n, n_dp),
         6,
-        jax.ShapeDtypeStruct(after.shape, BF16),
-        VM,
-        [ANY, VM],
-        scatter_scratch(n, *after.shape),
+        [shape(after.shape, BF16), shape(tile, F32)],
+        [VM, VM],
+        [ANY, VM, VM],
+        scatter_scratch(n, *after.shape)
+        + [
+            pltpu.VMEM((n, n_dp) + tile, F32),
+            pltpu.VMEM((n_dp,) + tile, F32),
+            pltpu.VMEM((n_dp,) + tile, F32),
+            DMA((n,)),
+            DMA((n,)),
+            DMA((n_dp,)),
+            DMA((n_dp,)),
+        ],
         50,
         part,
         after,
+        small,
     )
 
 
@@ -848,8 +923,8 @@
         allowed = (docc_ref[...] == docr_ref[:, at]) & (block * rows + col_off <= row_pos)
         for head in range(heads):
             cols = slice(head * HD, (head + 1) * HD)
-            score = dot(q_ref[:, cols], key, NT) * SCALE
-            expo = jnp.where(allowed, jnp.exp(score), 0.0)
+            score = dot(q_ref[:, cols], key, NT) * SCALE2
+            expo = jnp.where(allowed, jnp.exp2(score), 0.0)
             folded = expo[:, :HD]
             for piece in range(1, rows // HD):
                 folded = folded + expo[:, piece * HD : (piece + 1) * HD]
@@ -928,6 +1003,8 @@
 
 
 def attn_backward_kernel(
+    n,
+    n_dp,
     heads,
     back,
     branch_ref,
@@ -945,13 +1022,28 @@
     kgain_ref,
     docc_ref,
     docr_ref,
+    wgrad_ref,
     dqkv_ref,
     gains_ref,
+    swapped_ref,
     dk_ref,
     dv_ref,
     dqa_ref,
+    *sems,
 ):
     step = pl.program_id(0)
+
+    @pl.when(step == 0)
+    def _():
+        meet_all(n)
+        RowSwap(n, n_dp, wgrad_ref, swapped_ref, *sems, True).start()
+
+    @pl.when(step == pl.num_programs(0) - 1)
+    def _():
+        swap = RowSwap(n, n_dp, wgrad_ref, swapped_ref, *sems, True)
+        swap.arrive()
+        swap.finish()
+
     rows = branch_ref.shape[0]
     here = pl.ds(pl.multiple_of(step * rows, rows), rows)
 
@@ -985,8 +1077,8 @@
         for head in range(heads):
             cols = slice(head * HD, (head + 1) * HD)
             query = q_ref[:, cols]
-            score = dot(query, key, NT) * SCALE
-            expo = jnp.where(allowed, jnp.exp(score), 0.0)
+            score = dot(query, key, NT) * SCALE2
+            expo = jnp.where(allowed, jnp.exp2(score), 0.0)
             prod = dot(grads[head], val, NT)
             score_grad = (expo * (prod - shifts[head])).astype(BF16)
             dv += dot(expo.astype(BF16), grads[head], TN)
@@ -1023,7 +1115,7 @@
         lax.fori_loop(0, pl.num_programs(0), finish, 0)
 
 
-def attn_backward(branch, wout, attn, total, q, k, v, qlin, klin, cosine, sine, qgain, kgain, doc, rows):
+def attn_backward(n, n_dp, wgrad, branch, wout, attn, total, q, k, v, qlin, klin, cosine, sine, qgain, kgain, doc, rows):
     length, width = branch.shape
     qw = wout.shape[0]
     heads = qw // HD
@@ -1032,7 +1124,7 @@
     shape = jax.ShapeDtypeStruct
     full = whole((length, HD))
     return pl.pallas_call(
-        functools.partial(attn_backward_kernel, heads, MOST // rows),
+        functools.partial(attn_backward_kernel, n, n_dp, heads, MOST // rows),
         grid=(length // rows,),
         in_specs=[
             blk(width),
@@ -1050,23 +1142,29 @@
             whole((1, HD)),
             blk(1),
             whole((1, length)),
+            ANY,
         ],
-        out_specs=[whole((length, qw + 2 * HD)), whole((8, HD))],
+        out_specs=[whole((length, qw + 2 * HD)), whole((8, HD)), ANY],
         out_shape=[
             shape((length, qw + 2 * HD), BF16),
             shape((8, HD), F32),
+            shape(wgrad.shape, BF16),
         ],
         scratch_shapes=[
             pltpu.VMEM((length, HD), F32),
             pltpu.VMEM((length, HD), F32),
             pltpu.VMEM((rows, qw), F32),
+            DMA((n_dp,)),
+            DMA((n_dp,)),
         ],
-        compiler_params=pltpu.CompilerParams(vmem_limit_bytes=VMEM_LIMIT),
+        compiler_params=pltpu.CompilerParams(
+            collective_id=9, has_side_effects=True, vmem_limit_bytes=VMEM_LIMIT
+        ),
         cost_estimate=pl.CostEstimate(
             flops=60 * 10**9, transcendentals=0, bytes_accessed=30 * 2**20
         ),
         name="attn_backward",
-    )(branch, wout, attn, total, q, k, v, qlin, klin, cosine, sine, qgain, kgain, doc[:, None], doc[None, :])
+    )(branch, wout, attn, total, q, k, v, qlin, klin, cosine, sine, qgain, kgain, doc[:, None], doc[None, :], wgrad)
 
 
 def expert_kernel(chained, low, aliased, plan, z_ref, n2_ref, top_ref, prob_ref, *rest):
@@ -1223,30 +1321,41 @@
     )(w_gate, w_up, w_down)
 
 
-def unpack_kernel(chunks, *refs):
-    gate_ref, up_ref, down_ref = refs[len(chunks) :]
-    cut = gate_ref.shape[1]
-    for (e, low, high), ref in zip(chunks, refs):
-        gate_ref[e, :, low:high] = ref[:cut, :].astype(F32)
-        up_ref[e, :, low:high] = ref[cut : 2 * cut, :].astype(F32)
-        down_ref[e, low:high, :] = jnp.transpose(ref[2 * cut :, :].astype(F32))
-
-
-def unpack(own, chunks, grads, hidden):
-    cut = grads[0].shape[0] // 3
+def unpack_kernel(z_ref, one_ref, all_ref, up_ref, down_ref, dg_ref, du_ref, dd_ref, own, sem):
+    copy = pltpu.make_async_copy(all_ref.at[z_ref[0]], own, sem)
+    copy.start()
+    cut = dg_ref.shape[1]
+    piece = [slice(k * cut, (k + 1) * cut) for k in range(3)]
+    dg_ref[1] = one_ref[piece[0], :].astype(F32)
+    du_ref[1] = one_ref[piece[1], :].astype(F32)
+    dd_ref[1] = jnp.transpose(one_ref[piece[2], :].astype(F32))
+    copy.wait()
+
+    def total(at):
+        return own[at, :].astype(F32) + up_ref[at, :].astype(F32) + down_ref[at, :].astype(F32)
+
+    dg_ref[0] = total(piece[0])
+    du_ref[0] = total(piece[1])
+    dd_ref[0] = jnp.transpose(total(piece[2]))
+
+
+def unpack(z, one, grads, got):
+    rows, hidden = one.shape
+    cut = rows // 3
     shape = jax.ShapeDtypeStruct
     return pl.pallas_call(
-        functools.partial(unpack_kernel, chunks),
-        in_specs=[VM] * len(grads),
+        unpack_kernel,
+        in_specs=[pl.BlockSpec(memory_space=pltpu.SMEM), VM, ANY, VM, VM],
         out_specs=[VM] * 3,
         out_shape=[
-            shape((own, cut, hidden), F32),
-            shape((own, cut, hidden), F32),
-            shape((own, hidden, cut), F32),
+            shape((2, cut, hidden), F32),
+            shape((2, cut, hidden), F32),
+            shape((2, hidden, cut), F32),
         ],
+        scratch_shapes=[pltpu.VMEM((rows, hidden), BF16), DMA(())],
         compiler_params=pltpu.CompilerParams(vmem_limit_bytes=VMEM_LIMIT),
         name="unpack",
-    )(*grads)
+    )(z, one, grads, *got)
 
 
 def line_hop(block_up, block_down, n_dp, hop):
@@ -1269,10 +1378,6 @@
 
 def after_of(value, *others):
     return lax.optimization_barrier((value,) + others)[0]
-
-
-def scatter_dp(partial):
-    return lax.psum_scatter(partial.astype(BF16), "dp", scatter_dimension=0, tiled=True)
 
 
 def per_device(
@@ -1301,7 +1406,6 @@
     heads = HQ // n_ctx
     share = n_ctx // KV
     qw = heads * HD
-    both = ("dp", "ctx")
     depth = w_query.shape[0]
     own_e = w_gate.shape[0]
 
@@ -1325,9 +1429,7 @@
     gain_query = small[:, 2 * cut : 2 * cut + hcut].reshape(1, HD)
     gain_key = small[:, 2 * cut + hcut : kinds].reshape(1, HD)
     wqkv = lax.all_gather(cols.reshape(n_ctx * depth, qw + 2 * HD), "dp", axis=0, tiled=True)
-    forth = [(c * n_dp + d, d * n_ctx + c) for d in range(n_dp) for c in range(n_ctx)]
-    wout = lax.ppermute(after_of(w_out, small), both, forth)
-    wout = lax.all_gather(wout, "dp", axis=0, tiled=True)
+    wrows = lax.all_gather(after_of(w_out, small), "dp", axis=0, tiled=False)
 
     inputs = layer_input.reshape(tokens, width)
     top_own = out_grad.reshape(tokens, width)
@@ -1354,7 +1456,8 @@
     )
     top_all = top_all.reshape(length, width)
     blocks = (n_ctx, tokens, width)
-    after, normed2 = middle(n_ctx, attn, wout, inputs, gain_ffn)
+    after, normed2, wout = middle(n_ctx, n_dp, attn, wrows, inputs, gain_ffn)
+    wout = wout.reshape(qw, width)
     normed2 = normed2.reshape(length, width)
 
     z = lax.axis_index("dp").astype(jnp.int32).reshape(1)
@@ -1400,29 +1503,39 @@
             sources1 += [(up, "up", hop, 0), (down, "down", hop, 0)]
         got = reduce_hop(grads, got, n_dp, hop - 1)
     (moe, rows_grad), grads1 = run(1, sources1, carried, 0, ())
-    own0 = lax.dynamic_index_in_dim(grads, lax.axis_index("dp"), 0, False).astype(F32)
     done1 = lax.psum_scatter(
         grads1.reshape(3 * width, hidden), "dp", scatter_dimension=0, tiled=True
     )
-    done0 = own0 + got[0].astype(F32) + got[1].astype(F32)
     mid, ffn_part, branch = turn(
         n_ctx, rows_grad.reshape(blocks), after, top_own, gain_ffn
     )
     branch = branch.reshape(length, width)
 
-    out_w = dot(attn, branch, TN).astype(BF16)
-    out_w = scatter_dp(out_w)
-    dqkv, gains = attn_backward(
-        branch, wout, attn, total, q, k, v, qlin, klin, cosine, sine, gain_query, gain_key, doc, tokens
-    )
-    input_grad, attn_part = last(n_ctx, dqkv, wqkv, inputs, mid, gain_attn)
-    moe = after_of(moe, attn_part)
-    layer_output = close(n_ctx, moe.reshape(blocks), after)
-
-    out_w = lax.ppermute(out_w, both, [(b, a) for a, b in forth])
+    out_w = dot(attn, branch, TN).astype(BF16).reshape(n_dp, qw // n_dp, width)
+    dqkv, gains, out_w = attn_backward(
+        n_ctx,
+        n_dp,
+        out_w,
+        branch,
+        wout,
+        attn,
+        total,
+        q,
+        k,
+        v,
+        qlin,
+        klin,
+        cosine,
+        sine,
+        gain_query,
+        gain_key,
+        doc,
+        tokens,
+    )
+    out_w = lax.psum_scatter(out_w.reshape(qw, width), "dp", scatter_dimension=0, tiled=True)
     out_w = out_w.astype(F32)
-    qkv_w = dot(normed, dqkv, TN).astype(BF16)
-    qkv_w = scatter_dp(qkv_w)
+    input_grad, attn_part, qkv_w = last(n_ctx, dqkv, wqkv, inputs, mid, gain_attn, normed)
+    qkv_w = lax.psum_scatter(qkv_w, "dp", scatter_dimension=0, tiled=True)
     n_all = n_dp * n_ctx
     packed = jnp.concatenate(
         [
@@ -1435,10 +1548,10 @@
         axis=1,
     )
     packed = packed.reshape(n_dp, n_ctx, 8, HD).transpose(1, 0, 2, 3)
-    packed = gains_sum(n_ctx, n_dp, after_of(packed, layer_output)).reshape(1024)
+    layer_output, packed = close(n_ctx, n_dp, moe.reshape(blocks), after, packed)
+    packed = packed.reshape(1024)
     query_w, key_w, value_w = post(n_ctx, qkv_w.reshape(n_ctx, depth, qw + 2 * HD))
-
-    gate_w, up_w, down_w = unpack(own_e, [(0, 0, hidden), (1, 0, hidden)], [done0, done1], hidden)
+    gate_w, up_w, down_w = unpack(z, done1, grads, got)
     return (
         layer_output.reshape(1, tokens, width),
         input_grad.reshape(1, tokens, width),

time: 1150 us -> 1140 us (level)
  Pallas kernels: 691 us -> 767 us
  waiting for transfers between devices: 309 us -> 254 us
    ppermute x2 -> x0, waiting for transfers between devices: 105 us -> none  [the longest x1 53.8 us: per_device(): out_w = lax.ppermute(out_w, both, [(b, a) for a, b in forth])]
    pallas_call x8 -> x7, Pallas kernels: 392 us -> 465 us  [comm_call(): pl.pallas_call(kernel, out_shape=outs, in_specs=in_specs, out_specs=out_s...]
    reduce_scatter x1, waiting for transfers between devices: 0.02 us -> 38.3 us  [per_device(): lax.psum_scatter(grads1.reshape(3 * width, hidden), 'dp', scatter_dimensi...]
    all_gather x2, waiting for transfers between devices: 3.3 us -> 14.8 us  [per_device(): full = lax.all_gather(blocks0[index], 'dp', axis=0, tiled=False)]
  transfers between devices with their start and end apart: 21 -> 19, of which waited for: 8 -> 8; matrix products, arithmetic and copies ran while one was open for 5% -> 4% of each run, Pallas kernels for 45% -> 46%
where the time goes in v5:
time: 1140 us; the launch traced here: 1130 us
  Pallas kernels  767 us (67%)
  waiting for transfers between devices  254 us (22%)
  starting transfers between devices  31.3 us (3%)
  local copies, waits for them, and re-layouts  30.8 us (3%)
  other arithmetic  23.9 us (2%)
  between operations  14.9 us (1%)
    pallas_call x7, Pallas kernels, comm_call(): pl.pallas_call(kernel, out_shape=outs, in_specs=in_specs, out_specs=out_s...  465 us
    pallas_call x3, Pallas kernels, expert(): pl.pallas_call(functools.partial(expert_kernel, len(before) > 0, low, len...  164 us
    ppermute x3, waiting for transfers between devices, reduce_hop(): lax.ppermute(blocks[0], 'dp', up)  144 us
    pallas_call x1, Pallas kernels, attn_backward(): pl.pallas_call(functools.partial(attn_backward_kernel, n, n_dp, heads, MO...  67 us
    pallas_call x1, Pallas kernels, attn_forward(): pl.pallas_call(functools.partial(attn_forward_kernel, n, heads, MOST // r...  55.2 us
    ppermute x3, waiting for transfers between devices, line_hop(): lax.ppermute(block_down, 'dp', down)  53.3 us
    reduce_scatter x1, waiting for transfers between devices, per_device(): lax.psum_scatter(grads1.reshape(3 * width, hidden), 'dp', scatter_dimensi...  38.3 us
  transfers between devices with their start and end apart: 19, of which 8 were waited for; matrix products, arithmetic and copies ran while one was open for 4% of the time, Pallas kernels for 46%

profile of v5, /device:TPU:14, one launch (start us, length us, event | category | flops | bytes accessed | tf_op | source)
XLA Modules:
  0.0 1131.6 jit_solution(12641389417204623565)
XLA Ops:
  7.3 1.1 copy.63
  11.1 14.2 %shard_map.255 = (bf16[8,64,768]{2,1,0:T(8,128)(2,1)}, f32[4,8,8,128]{3,2,1,0:T(8,128)}) custom-call(bf16[8,64,768]{2,1,0:T(8,128)(2,1)} %maximum_bitcast_fusion.cols_ref, f32[8,128]{1,0:T(8,128)} %fusion.15.small_ref), custom_call_target="tpu_custom_call" | custom-call | bytes 24000000 | tf_op jit(solution)/shard_map/pallas_call | solution.py:429
  26.5 1.2 slice_bitcast_fusion
  28.6 1.7 slice_bitcast_fusion.1
  30.3 3.3 pack.2
  35.8 43.0 %shard_map.256 = (bf16[8,256,2048]{2,1,0:T(8,128)(2,1)}, f32[8,24,256]{2,1,0:T(8,128)}) custom-call(bf16[256,2048]{1,0:T(8,128)(2,1)} %bitcast.93, f32[1,2048]{1,0:T(1,128)} %reshape.167.gain_ref, f32[24,256]{1,0:T(8,128)} %maximum_maximum_fusion.info_ref), custom_call_target="tpu_custom_call" | custom-call | bytes 150000000 | tf_op jit(solution)/shard_map/pallas_call | solution.py:429
  79.7 1.3 copy.47.docc_ref
  84.2 3.3 pack.3.rest_2_
  87.6 3.9 fusion.6
  91.5 1.9 pad_maximum_fusion
  93.4 1.7 fusion.16
  95.1 55.2 %attn_forward.1 = (f32[2048,512]{1,0:T(8,128)}, f32[2048,128]{1,0:T(8,128)}, bf16[2048,512]{1,0:T(8,128)(2,1)}, bf16[2048,128]{1,0:T(8,128)(2,1)}, bf16[2048,128...) custom-call(bf16[2048,2048]{1,0:T(8,128)(2,1)} %bitcast.99, ...), custom_call_target="tpu_custom_call" | custom-call | flops 35000000512 | bytes 31457280 | tf_op jit(solution)/shard_map/attn_forward/pallas_call | solution.py:959
  150.3 114.5 %shard_map.257 = (f32[256,2048]{1,0:T(8,128)}, bf16[8,256,2048]{2,1,0:T(8,128)(2,1)}, bf16[4,128,2048]{2,1,0:T(8,128)(2,1)}) custom-call(bf16[2048,512]{1,0:T(8,128)(2,1)} %get-tuple-element.71.attn_ref, bf16[4,128,2048]{2,1,0:T(8,128)(2,1)} %bitcast.102, bf16[256,2048]{1,0:T(8,128)(2,1)} %bitcast.94, f32[1,2048]{1,0:T(1,128)} %reshape.173.gain_ref), custom_call_target="tpu_custom_call" | custom-call | bytes 315000000 | tf_op jit(solution)/shard_map/pallas_call | solution.py:429
  264.9 32.9 %expert.3 = (bf16[2048,2048]{1,0:T(8,128)(2,1)}, bf16[2048,2048]{1,0:T(8,128)(2,1)}, bf16[4,1536,768]{2,1,0:T(8,128)(2,1)}) custom-call(s32[1]{0:T(128)} %bitcast.z_ref, bf16[2048,2048]{1,0:T(8,128)(2,1)} %bitcast.124, bf16[2048,2048]{1,0:T(8,128)(2,1)} %bitcast.132, f32[2048,1]{1,0:T(8,128)} %get-tuple-element.135.prob_ref, bf16[4,1536,256]{2,1,0:T(8,128)(2,1)} %bitcast.130), custom_call_target="tpu_custom_call" | custom-call | flops 19327352832 | bytes 41943040 | tf_op jit(solution)/shard_map/expert/pallas_call | solution.py:1278
  297.8 14.8 %all-gather.14.cloned.1.call-done = bf16[6144,512]{1,0:T(8,128)(2,1)} async-done(((bf16[1536,512]{1,0:T(8,128)(2,1)}), bf16[6144,512]{1,0:T(8,128)(2,1)}) %all-gather.14.cloned.1.call-update) | async-done | bytes 6291472 | tf_op jit(solution)/shard_map/all_gather | solution.py:1486
  312.6 4.3 collective-permute-start
  317.0 3.6 collective-permute-start.1
  320.5 55.3 %expert.4 = (bf16[2048,2048]{1,0:T(8,128)(2,1)}, bf16[2048,2048]{1,0:T(8,128)(2,1)}, bf16[4,1536,768]{2,1,0:T(8,128)(2,1)}) custom-call(s32[1]{0:T(128)} %bitcast.z_ref, bf16[2048,2048]{1,0:T(8,128)(2,1)} %bitcast.125, bf16[2048,2048]{1,0:T(8,128)(2,1)} %bitcast.133, f32[2048,1]{1,0:T(8,128)} %get-tuple-element.135.prob_ref, ...), custom_call_target="tpu_custom_call", output_to_operand_aliasing={{2}: (4, {})} | custom-call | flops 38654705664 | bytes 41943040 | tf_op jit(solution)/shard_map/expert/pallas_call | solution.py:1278
  375.9 2.7 dynamic-slice_bitcast_fusion
  378.6 1.3 collective-permute-start.4
  379.9 2.1 collective-permute-start.5
  382.0 1.4 collective-permute-start.2
  383.4 4.1 collective-permute-start.3
  387.5 45.8 %collective-permute-done.4 = bf16[1536,768]{1,0:T(8,128)(2,1)S(1)} collective-permute-done((bf16[1536,768]{1,0:T(8,128)(2,1)S(1)}, bf16[1536,768]{1,0:T(8,128)(2,1)S(1)}, u32[]{:S(2)}, u32[]{:S(2)}) %collective-permute-start.4) | collective-permute-done | bytes 2359328 | tf_op jit(solution)/shard_map/ppermute | solution.py:1376
  434.2 4.3 collective-permute-done.3.rest_6_
  439.3 3.8 collective-permute-start.7
  443.1 49.0 %collective-permute-done.7.rest_8_ = bf16[1536,768]{1,0:T(8,128)(2,1)S(1)} collective-permute-done((bf16[1536,768]{1,0:T(8,128)(2,1)S(1)}, bf16[1536,768]{1,0:T(8,128)(2,1)S(1)}, u32[]{:S(2)}, u32[]{:S(2)}) %collective-permute-start.7) | collective-permute-done | bytes 2359328 | tf_op jit(solution)/shard_map/ppermute | solution.py:1364
  492.2 1.6 copy-done.23
  493.8 76.0 %expert.5 = (bf16[2048,2048]{1,0:T(8,128)(2,1)}, bf16[2048,2048]{1,0:T(8,128)(2,1)}, bf16[4,1536,768]{2,1,0:T(8,128)(2,1)}) custom-call(s32[1]{0:T(128)} %bitcast.z_ref, bf16[2048,2048]{1,0:T(8,128)(2,1)} %bitcast.126, bf16[2048,2048]{1,0:T(8,128)(2,1)} %bitcast.134, f32[2048,1]{1,0:T(8,128)} %get-tuple-element.136.prob_ref, ...), custom_call_target="tpu_custom_call" | custom-call | flops 57982058496 | bytes 41943040 | tf_op jit(solution)/shard_map/expert/pallas_call | solution.py:1278
  569.7 84.0 %shard_map.258 = (f32[256,2048]{1,0:T(8,128)}, f32[8,2048]{1,0:T(8,128)}, bf16[8,256,2048]{2,1,0:T(8,128)(2,1)}) custom-call(bf16[8,256,2048]{2,1,0:T(8,128)(2,1)} %bitcast.98, f32[256,2048]{1,0:T(8,128)} %get-tuple-element.90.after_ref, bf16[256,2048]{1,0:T(8,128)(2,1)} %bitcast.107, f32[1,2048]{1,0:T(1,128)} %reshape.173.gain_ref), custom_call_target="tpu_custom_call" | custom-call | bytes 285000000 | tf_op jit(solution)/shard_map/pallas_call | solution.py:429
  653.7 9.9 convolution_convert_fusion
  663.6 67.0 %attn_backward.1 = (bf16[2048,768]{1,0:T(8,128)(2,1)}, f32[8,128]{1,0:T(8,128)}, bf16[4,128,2048]{2,1,0:T(8,128)(2,1)}) custom-call(bf16[2048,2048]{1,0:T(8,128)(2,1)} %bitcast.128, bf16[512,2048]{1,0:T(8,128)(2,1)} %bitcast.131, bf16[2048,512]{1,0:T(8,128)(2,1)} %get-tuple-element.71.attn_ref, f32[2048,128]{1,0:T(8,128)} %get-tuple-element.94.total_ref, ...), custom_call_target="tpu_custom_call" | custom-call | flops 60000002048 | bytes 31457280 | tf_op jit(solution)/shard_map/attn_backward/pallas_call | solution.py:1126
  730.7 55.4 %shard_map.259 = (f32[256,2048]{1,0:T(8,128)}, f32[8,2048]{1,0:T(8,128)}, bf16[2048,768]{1,0:T(8,128)(2,1)}) custom-call(bf16[2048,768]{1,0:T(8,128)(2,1)} %get-tuple-element.100.grad_ref, bf16[2048,768]{1,0:T(8,128)(2,1)} %all-gather.8.cloned.1.call-done.wqkv_ref, bf16[256,2048]{1,0:T(8,128)(2,1)} %bitcast.95, f32[256,2048]{1,0:T(8,128)} %get-tuple-element.101.mid_ref, ...), custom_call_target="tpu_custom_call" | custom-call | bytes 180000000 | tf_op jit(solution)/shard_map/pallas_call | solution.py:429
  786.8 6.4 fusion.1
  793.2 2.2 collective-permute-start.8
  795.4 1.3 collective-permute-start.9
  796.7 98.4 %collective-permute-done.8 = bf16[1536,768]{1,0:T(8,128)(2,1)S(1)} collective-permute-done((bf16[1536,768]{1,0:T(8,128)(2,1)}, bf16[1536,768]{1,0:T(8,128)(2,1)S(1)}, u32[]{:S(2)}, u32[]{:S(2)}) %collective-permute-start.8) | collective-permute-done | bytes 2359328 | tf_op jit(solution)/shard_map/ppermute | solution.py:1376
  896.1 6.4 fusion
  902.5 3.4 collective-permute-start.10
  905.9 2.6 collective-permute-start.11
  912.1 139.6 %shard_map.260 = (bf16[256,2048]{1,0:T(8,128)(2,1)}, f32[8,128]{1,0:T(8,128)}) custom-call(bf16[8,256,2048]{2,1,0:T(8,128)(2,1)} %bitcast.101, f32[256,2048]{1,0:T(8,128)} %get-tuple-element.90.after_ref, f32[8,4,8,128]{3,2,1,0:T(8,128)} %copy_bitcast_fusion.3.small_ref), custom_call_target="tpu_custom_call" | custom-call | bytes 150000000 | tf_op jit(solution)/shard_map/pallas_call | solution.py:429
  1051.8 1.3 fusion.20
  1053.1 1.3 fusion.19
  1054.5 2.1 convert_element_type.88
  1056.6 14.1 %shard_map.261 = (f32[64,4096]{1,0:T(8,128)}, f32[64,512]{1,0:T(8,128)}, f32[64,512]{1,0:T(8,128)}) custom-call(bf16[8,64,768]{2,1,0:T(8,128)(2,1)} %bitcast.110), custom_call_target="tpu_custom_call" | custom-call | bytes 30000000 | tf_op jit(solution)/shard_map/pallas_call | solution.py:429
  1070.7 38.3 %reduce-scatter.8.cloned.1.call-done.one_ref = bf16[1536,768]{1,0:T(8,128)(2,1)} async-done(((bf16[6144,768]{1,0:T(8,128)(2,1)}), bf16[1536,768]{1,0:T(8,128)(2,1)}) %reduce-scatter.8.cloned.1.call-update) | async-done | bytes 2359312 | tf_op jit(solution)/shard_map/reduce_scatter | solution.py:1506
  1109.0 9.4 unpack.1
  1120.4 1.3 copy.72
  (111 shorter events, 23.0 us)
Async XLA Ops:
  7.2 1.2 copy-start
  7.2 3.2 copy-start.19
  7.2 3.2 copy-start.18
  7.2 3.2 copy-start.17
  7.2 3.2 copy-start.16
  7.2 87.9 %all-gather.8.cloned.1.call-start = ((), (), s32[]{:S(2)}) async-start(), calls=%async_computation.3 | async-start | bytes 3932160 | tf_op jit(solution)/shard_map/all_gather | solution.py:1431
  8.4 18.1 %copy-start.5 = (bf16[2,768,512]{2,1,0:T(8,128)(2,1)S(1)}, bf16[2,768,512]{2,1,0:T(8,128)(2,1)}, u32[]{:S(2)}) copy-start(bf16[2,768,512]{2,1,0:T(8,128)(2,1)} %param.30) | copy-start | bytes 4718596
  25.3 2.5 copy-start.6
  25.4 125.0 %all-gather.10.cloned.1.call-start = ((), (), s32[]{:S(2)}) async-start(), calls=%async_computation.7 | async-start | bytes 2621440 | tf_op jit(solution)/shard_map/all_gather | solution.py:1432
  26.5 238.4 %all-gather.12.cloned.1.call-start = ((), (), s32[]{:S(2)}) async-start(), calls=%async_computation.8 | async-start | bytes 3932160 | tf_op jit(solution)/shard_map/all_gather | solution.py:1486
  26.5 2.0 copy-start.7
  30.3 4.7 copy-start.15
  30.3 4.8 copy-start.13
  30.3 4.8 copy-start.14
  33.6 279.0 %all-gather.14.cloned.1.call-start = ((), (), s32[]{:S(2)}) async-start(), calls=%async_computation.9 | async-start | bytes 7864320 | tf_op jit(solution)/shard_map/all_gather | solution.py:1486
  34.2 1020.3 %reduce-scatter.6.cloned.1.call-start = ((), (), s32[]{:S(2)}) async-start(), calls=%async_computation.5 | async-start | bytes 2621440 | tf_op jit(solution)/shard_map/reduce_scatter | solution.py:1535
  79.7 7.9 copy-start.12
  264.9 47.7 %copy-start.3 = (bf16[1536,768]{1,0:T(8,128)(2,1)S(1)}, bf16[1536,768]{1,0:T(8,128)(2,1)}, u32[]{:S(2)}) copy-start(bf16[1536,768]{1,0:T(8,128)(2,1)} %pack.3.rest_2_) | copy-start | bytes 7077892
  312.6 63.2 %collective-permute-start = (bf16[1536,768]{1,0:T(8,128)(2,1)S(1)}, bf16[1536,768]{1,0:T(8,128)(2,1)}, u32[]{:S(2)}, u32[]{:S(2)}) collective-permute-start(bf16[1536,768]{1,0:T(8,128)(2,1)S(1)} %copy-done.3), channel_id=1, source_target_pairs={{0,8},{8,16},{16,24},{1,9},{9,17},{17,25},{2,10},{10,18},{18,26},{... | collective-permute-start | bytes 7077896 | tf_op jit(solution)/shard_map/ppermute | solution.py:1364
  317.0 58.9 %collective-permute-start.1 = (bf16[1536,768]{1,0:T(8,128)(2,1)S(1)}, bf16[1536,768]{1,0:T(8,128)(2,1)}, u32[]{:S(2)}, u32[]{:S(2)}) collective-permute-start(bf16[1536,768]{1,0:T(8,128)(2,1)S(1)} %copy-done.3), channel_id=1, source_target_pairs={{8,0},{16,8},{24,16},{9,1},{17,9},{25,17},{10,2},{18,10},{26,18},{... | collective-permute-start | bytes 7077896 | tf_op jit(solution)/shard_map/ppermute | solution.py:1364
  378.6 54.7 %collective-permute-start.4 = (bf16[1536,768]{1,0:T(8,128)(2,1)S(1)}, bf16[1536,768]{1,0:T(8,128)(2,1)S(1)}, u32[]{:S(2)}, u32[]{:S(2)}) collective-permute-start(bf16[1536,768]{1,0:T(8,128)(2,1)S(1)} %get-tuple-element.128), channel_id=1, source_target_pairs={{0,8},{1,9},{2,10},{3,11},{4,12},{5,13},{6,14},{7,15}} | collective-permute-start | bytes 7077896 | tf_op jit(solution)/shard_map/ppermute | solution.py:1376
  379.9 53.4 %collective-permute-start.5 = (bf16[1536,768]{1,0:T(8,128)(2,1)S(1)}, bf16[1536,768]{1,0:T(8,128)(2,1)}, u32[]{:S(2)}, u32[]{:S(2)}) collective-permute-start(bf16[1536,768]{1,0:T(8,128)(2,1)S(1)} %get-tuple-element.127), channel_id=1, source_target_pairs={{24,16},{25,17},{26,18},{27,19},{28,20},{29,21},{30,22},{31,23}} | collective-permute-start | bytes 7077896 | tf_op jit(solution)/shard_map/ppermute | solution.py:1376
  382.0 52.2 %collective-permute-start.2 = (bf16[1536,768]{1,0:T(8,128)(2,1)}, bf16[1536,768]{1,0:T(8,128)(2,1)S(1)}, u32[]{:S(2)}, u32[]{:S(2)}) collective-permute-start(bf16[1536,768]{1,0:T(8,128)(2,1)} %collective-permute-done.rest_3_), channel_id=1, source_target_pairs={{8,16},{16,24},{9,17},{17,25},{10,18},{18,26},{11,19},{19,27},{12,... | collective-permute-start | bytes 7077896 | tf_op jit(solution)/shard_map/ppermute | solution.py:1364
  383.4 55.1 %collective-permute-start.3 = (bf16[1536,768]{1,0:T(8,128)(2,1)}, bf16[1536,768]{1,0:T(8,128)(2,1)S(1)}, u32[]{:S(2)}, u32[]{:S(2)}) collective-permute-start(bf16[1536,768]{1,0:T(8,128)(2,1)} %collective-permute-done.1.rest_4_), channel_id=1, source_target_pairs={{8,0},{16,8},{9,1},{17,9},{10,2},{18,10},{11,3},{19,11},{12,4},{20... | collective-permute-start | bytes 7077896 | tf_op jit(solution)/shard_map/ppermute | solution.py:1364
  434.2 4.3 copy-start.20
  438.5 4.7 copy-start.21
  438.5 4.7 collective-permute-start.6
  439.3 52.9 %collective-permute-start.7 = (bf16[1536,768]{1,0:T(8,128)(2,1)S(1)}, bf16[1536,768]{1,0:T(8,128)(2,1)S(1)}, u32[]{:S(2)}, u32[]{:S(2)}) collective-permute-start(bf16[1536,768]{1,0:T(8,128)(2,1)S(1)} %collective-permute-done.3.rest_6_), channel_id=1, source_target_pairs={{8,0},{9,1},{10,2},{11,3},{12,4},{13,5},{14,6},{15,7}} | collective-permute-start | bytes 7077896 | tf_op jit(solution)/shard_map/ppermute | solution.py:1364
  443.1 49.0 %copy-start.22 = (bf16[1536,768]{1,0:T(8,128)(2,1)}, bf16[1536,768]{1,0:T(8,128)(2,1)S(1)}, u32[]{:S(2)}) copy-start(bf16[1536,768]{1,0:T(8,128)(2,1)S(1)} %collective-permute-done.6.rest_7_) | copy-start | bytes 7077892
  492.2 1.6 copy-start.23
  730.6 325.9 %reduce-scatter.4.cloned.1.call-start = ((), (), s32[]{:S(2)}) async-start(), calls=%async_computation.4 | async-start | bytes 3932160 | tf_op jit(solution)/shard_map/reduce_scatter | solution.py:1538
  786.1 323.0 %reduce-scatter.8.cloned.1.call-start = ((), (), s32[]{:S(2)}) async-start(), calls=%async_computation.6 | async-start | bytes 11796480 | tf_op jit(solution)/shard_map/reduce_scatter | solution.py:1506
  793.2 101.8 %collective-permute-start.8 = (bf16[1536,768]{1,0:T(8,128)(2,1)}, bf16[1536,768]{1,0:T(8,128)(2,1)S(1)}, u32[]{:S(2)}, u32[]{:S(2)}) collective-permute-start(bf16[1536,768]{1,0:T(8,128)(2,1)} %get-tuple-element.126), channel_id=1, source_target_pairs={{0,8},{8,16},{1,9},{9,17},{2,10},{10,18},{3,11},{11,19},{4,12},{12... | collective-permute-start | bytes 7077896 | tf_op jit(solution)/shard_map/ppermute | solution.py:1376
  795.4 100.7 %collective-permute-start.9 = (bf16[1536,768]{1,0:T(8,128)(2,1)}, bf16[1536,768]{1,0:T(8,128)(2,1)}, u32[]{:S(2)}, u32[]{:S(2)}) collective-permute-start(bf16[1536,768]{1,0:T(8,128)(2,1)} %get-tuple-element.125), channel_id=1, source_target_pairs={{16,8},{24,16},{17,9},{25,17},{18,10},{26,18},{19,11},{27,19},{20,... | collective-permute-start | bytes 7077896 | tf_op jit(solution)/shard_map/ppermute | solution.py:1376
  902.5 168.2 %collective-permute-start.10 = (bf16[1536,768]{1,0:T(8,128)(2,1)}, bf16[1536,768]{1,0:T(8,128)(2,1)S(1)}, u32[]{:S(2)}, u32[]{:S(2)}) collective-permute-start(bf16[1536,768]{1,0:T(8,128)(2,1)} %get-tuple-element.124), channel_id=1, source_target_pairs={{0,8},{8,16},{16,24},{1,9},{9,17},{17,25},{2,10},{10,18},{18,26},{... | collective-permute-start | bytes 7077896 | tf_op jit(solution)/shard_map/ppermute | solution.py:1376
  905.9 164.8 %collective-permute-start.11 = (bf16[1536,768]{1,0:T(8,128)(2,1)}, bf16[1536,768]{1,0:T(8,128)(2,1)}, u32[]{:S(2)}, u32[]{:S(2)}) collective-permute-start(bf16[1536,768]{1,0:T(8,128)(2,1)} %get-tuple-element.123), channel_id=1, source_target_pairs={{8,0},{16,8},{24,16},{9,1},{17,9},{25,17},{10,2},{18,10},{26,18},{... | collective-permute-start | bytes 7077896 | tf_op jit(solution)/shard_map/ppermute | solution.py:1376
  1070.6 47.8 %copy-start.8 = (bf16[256,2048]{1,0:T(8,128)(2,1)S(1)}, bf16[256,2048]{1,0:T(8,128)(2,1)}, u32[]{:S(2)}) copy-start(bf16[256,2048]{1,0:T(8,128)(2,1)} %get-tuple-element.105) | copy-start | bytes 3145732
  1070.7 38.4 %copy-start.2 = (bf16[1536,768]{1,0:T(8,128)(2,1)}, bf16[1536,768]{1,0:T(8,128)(2,1)S(1)}, u32[]{:S(2)}) copy-start(bf16[1536,768]{1,0:T(8,128)(2,1)S(1)} %collective-permute-done.10.up_ref) | copy-start | bytes 7077892
  1118.4 2.0 copy-start.4
  1120.4 1.9 copy-start.9
  1120.4 2.9 copy-start.11
  1120.4 3.6 copy-start.10
  1120.4 4.2 copy-start.1
Sparse Core Ops, SparseCore 0:
  25.5 61.8 all-gather.7
  88.9 45.2 all-gather.9
  135.8 61.3 all-gather.11
  199.2 113.3 all-gather.13
  730.8 43.4 reduce-scatter.5
  786.2 102.4 reduce-scatter.3
  891.0 217.9 reduce-scatter.7

commit v6 on v5

--- a/solution.py
+++ b/solution.py
@@ -608,7 +608,9 @@
     )
 
 
-def first_kernel(n, x_ref, gain_ref, info_ref, nall_ref, iall_ref, low, *sems):
+def first_kernel(
+    n, x_ref, gain_ref, info_ref, grad_ref, nall_ref, iall_ref, gall_ref, low, *sems
+):
     plane = Plane(n)
     plane.meet()
     infos = Gather(plane, info_ref, iall_ref, *sems[0:3])
@@ -621,47 +623,47 @@
     by_rows(x_ref.shape[0], norm)
     normed = gather_of(plane, low, nall_ref, *sems[3:6])
     normed.start()
+    grads = gather_of(plane, grad_ref, gall_ref, *sems[6:9])
+    grads.start()
     infos.forward()
     normed.forward()
+    grads.forward()
     infos.finish()
     normed.finish()
-
-
-def first(n, x, gain, info):
+    grads.finish()
+
+
+def first(n, x, gain, info, grad):
     shape = jax.ShapeDtypeStruct
     many = lambda array, kind: shape((n,) + array.shape, kind)
     return comm_call(
         functools.partial(first_kernel, n),
         2,
-        [many(x, BF16), many(info, F32)],
-        [ANY] * 2,
-        [VM] * 3,
-        [pltpu.VMEM(x.shape, BF16)] + [DMA((n,)), DMA((n,)), DMA(())] + gather_sems(n),
-        50,
+        [many(x, BF16), many(info, F32), many(grad, BF16)],
+        [ANY] * 3,
+        [VM] * 4,
+        [pltpu.VMEM(x.shape, BF16)]
+        + [DMA((n,)), DMA((n,)), DMA(())]
+        + gather_sems(n)
+        + gather_sems(n),
+        90,
         x,
         gain,
         info,
+        grad,
     )
 
 
 def middle_kernel(
-    n, n_dp, attn_ref, rows_ref, x_ref, gain_ref, after_ref, all_ref, wout_ref, low, *scratch
+    n, attn_ref, wout_ref, x_ref, gain_ref, after_ref, all_ref, low, *scratch
 ):
-    meet_all(n)
     plane = Plane(n)
-    swap = RowSwap(n, n_dp, rows_ref, wout_ref, *scratch[:2], False)
-    swap.start()
-    scratch = scratch[2:]
+    plane.meet()
     rows = x_ref.shape[0]
-    deep = wout_ref.shape[1]
-    swap.arrive()
 
     def value(block, at):
-        here = pl.ds(pl.multiple_of(block * rows, rows), rows)
-        total = dot(attn_ref[here, :deep], wout_ref[0, :, at])
-        for k in range(1, n_dp):
-            total = total + dot(attn_ref[here, k * deep : (k + 1) * deep], wout_ref[k, :, at])
-        return total
+        left = attn_ref[pl.ds(pl.multiple_of(block * rows, rows), rows), :]
+        return dot(left, wout_ref[:, at])
 
     sums = Product(plane, value, *scratch[:8])
     sums.start()
@@ -678,23 +680,22 @@
     normed.forward()
     sums.finish()
     normed.finish()
-    swap.finish()
-
-
-def middle(n, n_dp, attn, wrows, x, gain):
+
+
+def middle(n, attn, wout, x, gain):
     shape = jax.ShapeDtypeStruct
     return comm_call(
-        functools.partial(middle_kernel, n, n_dp),
+        functools.partial(middle_kernel, n),
         3,
-        [shape(x.shape, F32), shape((n,) + x.shape, BF16), shape(wrows.shape, BF16)],
-        [VM, ANY, VM],
-        [VM, ANY, VM, VM],
-        [pltpu.VMEM(x.shape, BF16), DMA((n_dp,)), DMA((n_dp,))]
+        [shape(x.shape, F32), shape((n,) + x.shape, BF16)],
+        [VM, ANY],
+        [VM, VM, VM, VM],
+        [pltpu.VMEM(x.shape, BF16)]
         + product_scratch(n, *x.shape)
         + gather_sems(n),
         105,
         attn,
-        wrows,
+        wout,
         x,
         gain,
     )
@@ -865,6 +866,7 @@
 
 def attn_forward_kernel(
     n,
+    n_dp,
     heads,
     back,
     normed_ref,
@@ -875,7 +877,7 @@
     kgain_ref,
     docc_ref,
     docr_ref,
-    grad_ref,
+    rows_ref,
     qlin_ref,
     klin_ref,
     q_ref,
@@ -883,7 +885,7 @@
     v_ref,
     attn_ref,
     total_ref,
-    gall_ref,
+    wout_ref,
     acc_ref,
     sum_ref,
     *sems,
@@ -892,9 +894,8 @@
 
     @pl.when(step == 0)
     def _():
-        plane = Plane(n)
-        plane.meet()
-        gather_of(plane, grad_ref, gall_ref, *sems).start()
+        meet_all(n)
+        RowSwap(n, n_dp, rows_ref, wout_ref, *sems, False).start()
 
     rows = normed_ref.shape[0]
     lin = dot(normed_ref[...], wqkv_ref[...])
@@ -944,12 +945,12 @@
 
     @pl.when(step == pl.num_programs(0) - 1)
     def _():
-        grads = gather_of(Plane(n), grad_ref, gall_ref, *sems)
-        grads.forward()
-        grads.finish()
-
-
-def attn_forward(n, normed, wqkv, cosine, sine, qgain, kgain, doc, grad, rows):
+        swap = RowSwap(n, n_dp, rows_ref, wout_ref, *sems, False)
+        swap.arrive()
+        swap.finish()
+
+
+def attn_forward(n, n_dp, normed, wqkv, cosine, sine, qgain, kgain, doc, wrows, rows):
     length, width = normed.shape
     qw = wqkv.shape[1] - 2 * HD
     heads = qw // HD
@@ -957,7 +958,7 @@
     whole = lambda shape: pl.BlockSpec(shape, lambda i: (0, 0))
     shape = jax.ShapeDtypeStruct
     return pl.pallas_call(
-        functools.partial(attn_forward_kernel, n, heads, MOST // rows),
+        functools.partial(attn_forward_kernel, n, n_dp, heads, MOST // rows),
         grid=(length // rows,),
         in_specs=[
             blk(width),
@@ -968,7 +969,7 @@
             whole((1, HD)),
             blk(1),
             whole((1, length)),
-            whole(grad.shape),
+            ANY,
         ],
         out_specs=[
             blk(qw),
@@ -988,10 +989,10 @@
             shape((length, HD), BF16),
             shape((length, qw), BF16),
             shape((length, HD), F32),
-            shape((n,) + grad.shape, BF16),
+            shape(wrows.shape, BF16),
         ],
         scratch_shapes=[pltpu.VMEM((rows, qw), F32), pltpu.VMEM((rows, qw), F32)]
-        + gather_sems(n),
+        + [DMA((n_dp,)), DMA((n_dp,))],
         compiler_params=pltpu.CompilerParams(
             collective_id=7, has_side_effects=True, vmem_limit_bytes=VMEM_LIMIT
         ),
@@ -999,7 +1000,7 @@
             flops=35 * 10**9, transcendentals=0, bytes_accessed=30 * 2**20
         ),
         name="attn_forward",
-    )(normed, wqkv, cosine, sine, qgain, kgain, doc[:, None], doc[None, :], grad)
+    )(normed, wqkv, cosine, sine, qgain, kgain, doc[:, None], doc[None, :], wrows)
 
 
 def attn_backward_kernel(
@@ -1368,6 +1369,8 @@
     place = lax.axis_index("dp")
     reach = n_dp - hop
     spots = (jnp.minimum(place + reach, n_dp - 1), jnp.maximum(place - reach, 0))
+    if got is not None:
+        got = lax.optimization_barrier(got)
     blocks = [lax.dynamic_index_in_dim(grads, spot, 0, False) for spot in spots]
     if got is not None:
         blocks = [(b.astype(F32) + g.astype(F32)).astype(BF16) for b, g in zip(blocks, got)]
@@ -1429,7 +1432,7 @@
     gain_query = small[:, 2 * cut : 2 * cut + hcut].reshape(1, HD)
     gain_key = small[:, 2 * cut + hcut : kinds].reshape(1, HD)
     wqkv = lax.all_gather(cols.reshape(n_ctx * depth, qw + 2 * HD), "dp", axis=0, tiled=True)
-    wrows = lax.all_gather(after_of(w_out, small), "dp", axis=0, tiled=False)
+    wrows = lax.all_gather(w_out, "dp", axis=0, tiled=False)
 
     inputs = layer_input.reshape(tokens, width)
     top_own = out_grad.reshape(tokens, width)
@@ -1439,7 +1442,7 @@
     info = jnp.concatenate(
         [probs, doc_ids.reshape(1, tokens).astype(F32), jnp.zeros((7, tokens), F32)], axis=0
     )
-    normed, info = first(n_ctx, inputs, gain_attn, info)
+    normed, info, top_all = first(n_ctx, inputs, gain_attn, info, top_own)
     normed = normed.reshape(length, width)
     doc = info[:, n_experts].reshape(length).astype(jnp.int32)
     my_probs = lax.dynamic_slice_in_dim(info, ctx_index * own_e, own_e, 1)
@@ -1451,13 +1454,13 @@
     sine = jnp.sin(angles)
     cosine = jnp.concatenate([cosine, cosine], axis=1)
     sine = jnp.concatenate([-sine, sine], axis=1)
-    qlin, klin, q, k, v, attn, total, top_all = attn_forward(
-        n_ctx, normed, wqkv, cosine, sine, gain_query, gain_key, doc, top_own, tokens
-    )
+    qlin, klin, q, k, v, attn, total, wout = attn_forward(
+        n_ctx, n_dp, normed, wqkv, cosine, sine, gain_query, gain_key, doc, wrows, tokens
+    )
+    wout = wout.reshape(qw, width)
     top_all = top_all.reshape(length, width)
     blocks = (n_ctx, tokens, width)
-    after, normed2, wout = middle(n_ctx, n_dp, attn, wrows, inputs, gain_ffn)
-    wout = wout.reshape(qw, width)
+    after, normed2 = middle(n_ctx, attn, wout, inputs, gain_ffn)
     normed2 = normed2.reshape(length, width)
 
     z = lax.axis_index("dp").astype(jnp.int32).reshape(1)
@@ -1494,10 +1497,6 @@
         grads0 = (grads,)
     got = None
     for hop in range(2, n_dp + 1):
-        if hop == 2:
-            up, down, grads = lax.optimization_barrier((up, down, grads))
-        else:
-            up, down, got = lax.optimization_barrier((up, down, got))
         if hop < n_dp:
             up, down = line_hop(up, down, n_dp, hop)
             sources1 += [(up, "up", hop, 0), (down, "down", hop, 0)]

time: 1140 us -> 1240 us (1.088)
  waiting for transfers between devices: 254 us -> 382 us
  Pallas kernels: 767 us -> 718 us
    ppermute x3, waiting for transfers between devices: 144 us -> 239 us  [reduce_hop(): lax.ppermute(blocks[0], 'dp', up)]
    all_gather x2, waiting for transfers between devices: 14.8 us -> 90.7 us  [per_device(): full = lax.all_gather(blocks0[index], 'dp', axis=0, tiled=False)]
    ppermute x3, waiting for transfers between devices: 53.3 us -> 0.01 us  [line_hop(): lax.ppermute(block_down, 'dp', down)]
    all_gather x1, waiting for transfers between devices: 0.01 us -> 47.4 us  [per_device(): lax.all_gather(cols.reshape(n_ctx * depth, qw + 2 * HD), 'dp', axis=0, ti...]
    reduce_scatter x1, waiting for transfers between devices: 38.3 us -> 0.02 us  [per_device(): lax.psum_scatter(grads1.reshape(3 * width, hidden), 'dp', scatter_dimensi...]
    pallas_call x7, Pallas kernels: 465 us -> 434 us  [comm_call(): pl.pallas_call(kernel, out_shape=outs, in_specs=in_specs, out_specs=out_s...]
    pallas_call x1, Pallas kernels: 55.2 us -> 37.3 us  [attn_forward(): pl.pallas_call(functools.partial(attn_forward_kernel, n, n_dp, heads, MOS...]
  transfers between devices with their start and end apart: 19 -> 19, of which waited for: 8 -> 5; matrix products, arithmetic and copies ran while one was open for 4% -> 4% of each run, Pallas kernels for 46% -> 39%
where the time goes in v6:
time: 1240 us; the launch traced here: 1230 us
  Pallas kernels  718 us (58%)
  waiting for transfers between devices  382 us (31%)
  starting transfers between devices  42.5 us (3%)
  local copies, waits for them, and re-layouts  34.2 us (3%)
  other arithmetic  24.5 us (2%)
  between operations  14.9 us (1%)
    pallas_call x7, Pallas kernels, comm_call(): pl.pallas_call(kernel, out_shape=outs, in_specs=in_specs, out_specs=out_s...  434 us
    ppermute x3, waiting for transfers between devices, reduce_hop(): lax.ppermute(blocks[0], 'dp', up)  239 us
    pallas_call x3, Pallas kernels, expert(): pl.pallas_call(functools.partial(expert_kernel, len(before) > 0, low, len...  164 us
    all_gather x2, waiting for transfers between devices, per_device(): full = lax.all_gather(blocks0[index], 'dp', axis=0, tiled=False)  90.7 us
    pallas_call x1, Pallas kernels, attn_backward(): pl.pallas_call(functools.partial(attn_backward_kernel, n, n_dp, heads, MO...  67.1 us
    all_gather x1, waiting for transfers between devices, per_device(): lax.all_gather(cols.reshape(n_ctx * depth, qw + 2 * HD), 'dp', axis=0, ti...  47.4 us
    pallas_call x1, Pallas kernels, attn_forward(): pl.pallas_call(functools.partial(attn_forward_kernel, n, n_dp, heads, MOS...  37.3 us
  transfers between devices with their start and end apart: 19, of which 5 were waited for; matrix products, arithmetic and copies ran while one was open for 4% of the time, Pallas kernels for 39%

profile of v6, /device:TPU:14, one launch (start us, length us, event | category | flops | bytes accessed | tf_op | source)
XLA Modules:
  0.0 1225.4 jit_solution(2019242628727016366)
XLA Ops:
  7.3 2.8 slice_bitcast_fusion
  10.0 1.7 slice_bitcast_fusion.1
  11.8 3.3 pack.2
  17.7 17.6 %shard_map.255 = (bf16[8,64,768]{2,1,0:T(8,128)(2,1)}, f32[4,8,8,128]{3,2,1,0:T(8,128)}) custom-call(bf16[8,64,768]{2,1,0:T(8,128)(2,1)} %maximum_bitcast_fusion.cols_ref, f32[8,128]{1,0:T(8,128)} %fusion.15.small_ref), custom_call_target="tpu_custom_call" | custom-call | bytes 24000000 | tf_op jit(solution)/shard_map/pallas_call | solution.py:429
  37.0 3.3 pack.3.rest_2_
  40.3 90.7 %all-gather.14.cloned.1.call-done = bf16[6144,512]{1,0:T(8,128)(2,1)} async-done(((bf16[1536,512]{1,0:T(8,128)(2,1)}), bf16[6144,512]{1,0:T(8,128)(2,1)}) %all-gather.14.cloned.1.call-update) | async-done | bytes 6291472 | tf_op jit(solution)/shard_map/all_gather | solution.py:1489
  131.0 2.4 collective-permute-start
  133.4 3.6 collective-permute-start.1
  139.9 78.9 %shard_map.256 = (bf16[8,256,2048]{2,1,0:T(8,128)(2,1)}, f32[8,24,256]{2,1,0:T(8,128)}, bf16[8,256,2048]{2,1,0:T(8,128)(2,1)}) custom-call(bf16[256,2048]{1,0:T(8,128)(2,1)} %bitcast.93, f32[1,2048]{1,0:T(1,128)} %reshape.167.gain_ref, f32[24,256]{1,0:T(8,128)} %maximum_maximum_fusion.info_ref, bf16[256,2048]{1,0:T(8,128)(2,1)} %bitcast.102), custom_call_target="tpu_custom_call" | custom-call | bytes 270000000 | tf_op jit(solution)/shard_map/pallas_call | solution.py:429
  219.6 1.3 copy.47.docc_ref
  222.9 3.9 fusion.6
  226.8 1.9 pad_maximum_fusion
  228.7 1.7 fusion.16
  230.4 4.0 collective-permute-start.2
  234.4 12.1 collective-permute-start.3
  246.6 47.4 %all-gather.8.cloned.1.call-done.wqkv_ref = bf16[2048,768]{1,0:T(8,128)(2,1)} async-done(((bf16[512,768]{1,0:T(8,128)(2,1)}), bf16[2048,768]{1,0:T(8,128)(2,1)}) %all-gather.8.cloned.1.call-update) | async-done | bytes 3145744 | tf_op jit(solution)/shard_map/all_gather | solution.py:1434
  293.9 37.3 %attn_forward.1 = (f32[2048,512]{1,0:T(8,128)}, f32[2048,128]{1,0:T(8,128)}, bf16[2048,512]{1,0:T(8,128)(2,1)}, bf16[2048,128]{1,0:T(8,128)(2,1)}, bf16[2048,128...) custom-call(bf16[2048,2048]{1,0:T(8,128)(2,1)} %bitcast.100, ...), custom_call_target="tpu_custom_call" | custom-call | flops 35000000512 | bytes 31457280 | tf_op jit(solution)/shard_map/attn_forward/pallas_call | solution.py:960
  331.3 87.7 %shard_map.257 = (f32[256,2048]{1,0:T(8,128)}, bf16[8,256,2048]{2,1,0:T(8,128)(2,1)}) custom-call(bf16[2048,512]{1,0:T(8,128)(2,1)} %get-tuple-element.65.attn_ref, bf16[512,2048]{1,0:T(8,128)(2,1)} %bitcast.104, bf16[256,2048]{1,0:T(8,128)(2,1)} %bitcast.94, f32[1,2048]{1,0:T(1,128)} %reshape.174.gain_ref), custom_call_target="tpu_custom_call" | custom-call | bytes 315000000 | tf_op jit(solution)/shard_map/pallas_call | solution.py:429
  419.0 32.5 %expert.3 = (bf16[2048,2048]{1,0:T(8,128)(2,1)}, bf16[2048,2048]{1,0:T(8,128)(2,1)}, bf16[4,1536,768]{2,1,0:T(8,128)(2,1)}) custom-call(s32[1]{0:T(128)} %bitcast.z_ref, bf16[2048,2048]{1,0:T(8,128)(2,1)} %bitcast.128, bf16[2048,2048]{1,0:T(8,128)(2,1)} %bitcast.125, f32[2048,1]{1,0:T(8,128)} %get-tuple-element.123.prob_ref, bf16[4,1536,256]{2,1,0:T(8,128)(2,1)} %bitcast.134), custom_call_target="tpu_custom_call" | custom-call | flops 19327352832 | bytes 41943040 | tf_op jit(solution)/shard_map/expert/pallas_call | solution.py:1279
  452.4 5.6 collective-permute-start.5
  458.0 55.3 %expert.4 = (bf16[2048,2048]{1,0:T(8,128)(2,1)}, bf16[2048,2048]{1,0:T(8,128)(2,1)}, bf16[4,1536,768]{2,1,0:T(8,128)(2,1)}) custom-call(s32[1]{0:T(128)} %bitcast.z_ref, bf16[2048,2048]{1,0:T(8,128)(2,1)} %bitcast.129, bf16[2048,2048]{1,0:T(8,128)(2,1)} %bitcast.126, f32[2048,1]{1,0:T(8,128)} %get-tuple-element.123.prob_ref, ...), custom_call_target="tpu_custom_call", output_to_operand_aliasing={{2}: (4, {})} | custom-call | flops 38654705664 | bytes 41943040 | tf_op jit(solution)/shard_map/expert/pallas_call | solution.py:1279
  513.4 1.4 copy-done.23
  514.8 76.2 %expert.5 = (bf16[2048,2048]{1,0:T(8,128)(2,1)}, bf16[2048,2048]{1,0:T(8,128)(2,1)}, bf16[4,1536,768]{2,1,0:T(8,128)(2,1)}) custom-call(s32[1]{0:T(128)} %bitcast.z_ref, bf16[2048,2048]{1,0:T(8,128)(2,1)} %bitcast.130, bf16[2048,2048]{1,0:T(8,128)(2,1)} %bitcast.127, f32[2048,1]{1,0:T(8,128)} %get-tuple-element.124.prob_ref, ...), custom_call_target="tpu_custom_call" | custom-call | flops 57982058496 | bytes 41943040 | tf_op jit(solution)/shard_map/expert/pallas_call | solution.py:1279
  590.9 84.5 %shard_map.258 = (f32[256,2048]{1,0:T(8,128)}, f32[8,2048]{1,0:T(8,128)}, bf16[8,256,2048]{2,1,0:T(8,128)(2,1)}) custom-call(bf16[8,256,2048]{2,1,0:T(8,128)(2,1)} %bitcast.98, f32[256,2048]{1,0:T(8,128)} %get-tuple-element.78.after_ref, bf16[256,2048]{1,0:T(8,128)(2,1)} %bitcast.103, f32[1,2048]{1,0:T(1,128)} %reshape.174.gain_ref), custom_call_target="tpu_custom_call" | custom-call | bytes 285000000 | tf_op jit(solution)/shard_map/pallas_call | solution.py:429
  675.5 9.1 convolution_convert_fusion
  684.6 67.1 %attn_backward.1 = (bf16[2048,768]{1,0:T(8,128)(2,1)}, f32[8,128]{1,0:T(8,128)}, bf16[4,128,2048]{2,1,0:T(8,128)(2,1)}) custom-call(bf16[2048,2048]{1,0:T(8,128)(2,1)} %bitcast.132, bf16[512,2048]{1,0:T(8,128)(2,1)} %bitcast.105, bf16[2048,512]{1,0:T(8,128)(2,1)} %get-tuple-element.65.attn_ref, f32[2048,128]{1,0:T(8,128)} %get-tuple-element.81.total_ref, ...), custom_call_target="tpu_custom_call" | custom-call | flops 60000002048 | bytes 31457280 | tf_op jit(solution)/shard_map/attn_backward/pallas_call | solution.py:1127
  751.9 55.3 %shard_map.259 = (f32[256,2048]{1,0:T(8,128)}, f32[8,2048]{1,0:T(8,128)}, bf16[2048,768]{1,0:T(8,128)(2,1)}) custom-call(bf16[2048,768]{1,0:T(8,128)(2,1)} %get-tuple-element.87.grad_ref, bf16[2048,768]{1,0:T(8,128)(2,1)} %all-gather.8.cloned.1.call-done.wqkv_ref, bf16[256,2048]{1,0:T(8,128)(2,1)} %bitcast.95, f32[256,2048]{1,0:T(8,128)} %get-tuple-element.88.mid_ref, ...), custom_call_target="tpu_custom_call" | custom-call | bytes 180000000 | tf_op jit(solution)/shard_map/pallas_call | solution.py:429
  808.0 4.9 dynamic-slice_bitcast_fusion
  812.9 1.3 collective-permute-start.6
  814.1 2.1 collective-permute-start.7
  816.2 99.9 %collective-permute-done.6 = bf16[1536,768]{1,0:T(8,128)(2,1)S(1)} collective-permute-done((bf16[1536,768]{1,0:T(8,128)(2,1)}, bf16[1536,768]{1,0:T(8,128)(2,1)S(1)}, u32[]{:S(2)}, u32[]{:S(2)}) %collective-permute-start.6) | collective-permute-done | bytes 2359328 | tf_op jit(solution)/shard_map/ppermute | solution.py:1379
  916.1 1.4 copy-done.3
  917.5 6.3 fusion.1
  923.8 3.1 collective-permute-start.8
  926.9 1.3 collective-permute-start.9
  928.2 138.8 %collective-permute-done.8 = bf16[1536,768]{1,0:T(8,128)(2,1)} collective-permute-done((bf16[1536,768]{1,0:T(8,128)(2,1)}, bf16[1536,768]{1,0:T(8,128)(2,1)}, u32[]{:S(2)}, u32[]{:S(2)}) %collective-permute-start.8) | collective-permute-done | bytes 2359328 | tf_op jit(solution)/shard_map/ppermute | solution.py:1379
  1067.0 2.9 collective-permute-done.9
  1069.9 7.1 fusion
  1076.9 2.0 collective-permute-start.10
  1079.0 4.0 collective-permute-start.11
  1086.6 95.8 %shard_map.260 = (bf16[256,2048]{1,0:T(8,128)(2,1)}, f32[8,128]{1,0:T(8,128)}) custom-call(bf16[8,256,2048]{2,1,0:T(8,128)(2,1)} %bitcast.99, f32[256,2048]{1,0:T(8,128)} %get-tuple-element.78.after_ref, f32[8,4,8,128]{3,2,1,0:T(8,128)} %copy_bitcast_fusion.3.small_ref), custom_call_target="tpu_custom_call" | custom-call | bytes 150000000 | tf_op jit(solution)/shard_map/pallas_call | solution.py:429
  1182.5 1.3 fusion.20
  1183.8 1.3 fusion.19
  1185.1 2.1 convert_element_type.88
  1187.3 14.0 %shard_map.261 = (f32[64,4096]{1,0:T(8,128)}, f32[64,512]{1,0:T(8,128)}, f32[64,512]{1,0:T(8,128)}) custom-call(bf16[8,64,768]{2,1,0:T(8,128)(2,1)} %bitcast.110), custom_call_target="tpu_custom_call" | custom-call | bytes 30000000 | tf_op jit(solution)/shard_map/pallas_call | solution.py:429
  1201.4 1.4 copy-done.2
  1202.7 9.4 unpack.1
  1214.1 1.3 copy.72
  (111 shorter events, 20.0 us)
Async XLA Ops:
  7.2 9.5 copy-start
  7.2 2.8 copy-start.6
  7.2 2.8 copy-start.7
  7.2 123.8 %all-gather.14.cloned.1.call-start = ((), (), s32[]{:S(2)}) async-start(), calls=%async_computation.9 | async-start | bytes 7864320 | tf_op jit(solution)/shard_map/all_gather | solution.py:1489
  11.7 4.2 copy-start.10
  11.7 4.2 copy-start.18
  11.7 4.2 copy-start.19
  11.7 4.2 copy-start.20
  11.8 4.2 copy-start.21
  11.8 4.9 copy-start.13
  15.1 231.4 %all-gather.10.cloned.1.call-start = ((), (), s32[]{:S(2)}) async-start(), calls=%async_computation.7 | async-start | bytes 2621440 | tf_op jit(solution)/shard_map/all_gather | solution.py:1435
  15.9 278.1 %all-gather.8.cloned.1.call-start = ((), (), s32[]{:S(2)}) async-start(), calls=%async_computation.3 | async-start | bytes 3932160 | tf_op jit(solution)/shard_map/all_gather | solution.py:1434
  35.4 383.6 %all-gather.12.cloned.1.call-start = ((), (), s32[]{:S(2)}) async-start(), calls=%async_computation.8 | async-start | bytes 3932160 | tf_op jit(solution)/shard_map/all_gather | solution.py:1489
  36.0 1149.2 %reduce-scatter.6.cloned.1.call-start = ((), (), s32[]{:S(2)}) async-start(), calls=%async_computation.5 | async-start | bytes 2621440 | tf_op jit(solution)/shard_map/reduce_scatter | solution.py:1534
  37.0 100.8 %copy-start.17 = (s32[1,256]{1,0:T(1,128)S(1)}, s32[1,256]{1,0:T(1,128)}, u32[]{:S(2)}) copy-start(s32[1,256]{1,0:T(1,128)} %param.17) | copy-start | bytes 3076
  37.0 102.2 %copy-start.15 = (f32[1,256,8]{1,2,0:T(8,128)S(1)}, f32[1,256,8]{1,2,0:T(8,128)}, u32[]{:S(2)}) copy-start(f32[1,256,8]{1,2,0:T(8,128)} %param.19) | copy-start | bytes 24580
  37.0 102.2 %copy-start.16 = (s32[1,256,8]{1,2,0:T(8,128)S(1)}, s32[1,256,8]{1,2,0:T(8,128)}, u32[]{:S(2)}) copy-start(s32[1,256,8]{1,2,0:T(8,128)} %param.18) | copy-start | bytes 24580
  131.0 99.4 %collective-permute-start = (bf16[1536,768]{1,0:T(8,128)(2,1)}, bf16[1536,768]{1,0:T(8,128)(2,1)S(1)}, u32[]{:S(2)}, u32[]{:S(2)}) collective-permute-start(bf16[1536,768]{1,0:T(8,128)(2,1)} %pack.3.rest_2_), channel_id=1, source_target_pairs={{0,8},{8,16},{16,24},{1,9},{9,17},{17,25},{2,10},{10,18},{18,26},{... | collective-permute-start | bytes 7077896 | tf_op jit(solution)/shard_map/ppermute | solution.py:1365
  133.4 101.0 %collective-permute-start.1 = (bf16[1536,768]{1,0:T(8,128)(2,1)}, bf16[1536,768]{1,0:T(8,128)(2,1)}, u32[]{:S(2)}, u32[]{:S(2)}) collective-permute-start(bf16[1536,768]{1,0:T(8,128)(2,1)} %pack.3.rest_2_), channel_id=1, source_target_pairs={{8,0},{16,8},{24,16},{9,1},{17,9},{25,17},{10,2},{18,10},{26,18},{... | collective-permute-start | bytes 7077896 | tf_op jit(solution)/shard_map/ppermute | solution.py:1365
  219.6 7.2 copy-start.14
  230.4 100.9 %copy-start.22 = (bf16[1536,768]{1,0:T(8,128)(2,1)}, bf16[1536,768]{1,0:T(8,128)(2,1)S(1)}, u32[]{:S(2)}) copy-start(bf16[1536,768]{1,0:T(8,128)(2,1)S(1)} %collective-permute-done.rest_3_) | copy-start | bytes 7077892
  230.4 221.2 %collective-permute-start.2 = (bf16[1536,768]{1,0:T(8,128)(2,1)S(1)}, bf16[1536,768]{1,0:T(8,128)(2,1)}, u32[]{:S(2)}, u32[]{:S(2)}) collective-permute-start(bf16[1536,768]{1,0:T(8,128)(2,1)S(1)} %collective-permute-done.rest_3_), channel_id=1, source_target_pairs={{8,16},{16,24},{9,17},{17,25},{10,18},{18,26},{11,19},{19,27},{12,... | collective-permute-start | bytes 7077896 | tf_op jit(solution)/shard_map/ppermute | solution.py:1365
  234.4 218.0 %collective-permute-start.3 = (bf16[1536,768]{1,0:T(8,128)(2,1)}, bf16[1536,768]{1,0:T(8,128)(2,1)}, u32[]{:S(2)}, u32[]{:S(2)}) collective-permute-start(bf16[1536,768]{1,0:T(8,128)(2,1)} %collective-permute-done.1.rest_4_), channel_id=1, source_target_pairs={{8,0},{16,8},{9,1},{17,9},{10,2},{18,10},{11,3},{19,11},{12,4},{20... | collective-permute-start | bytes 7077896 | tf_op jit(solution)/shard_map/ppermute | solution.py:1365
  451.6 61.7 %collective-permute-start.4 = (bf16[1536,768]{1,0:T(8,128)(2,1)}, bf16[1536,768]{1,0:T(8,128)(2,1)S(1)}, u32[]{:S(2)}, u32[]{:S(2)}) collective-permute-start(bf16[1536,768]{1,0:T(8,128)(2,1)} %collective-permute-done.2.rest_5_), channel_id=1, source_target_pairs={{16,24},{17,25},{18,26},{19,27},{20,28},{21,29},{22,30},{23,31}} | collective-permute-start | bytes 7077896 | tf_op jit(solution)/shard_map/ppermute | solution.py:1365
  452.4 60.9 %collective-permute-start.5 = (bf16[1536,768]{1,0:T(8,128)(2,1)}, bf16[1536,768]{1,0:T(8,128)(2,1)}, u32[]{:S(2)}, u32[]{:S(2)}) collective-permute-start(bf16[1536,768]{1,0:T(8,128)(2,1)} %collective-permute-done.3.rest_6_), channel_id=1, source_target_pairs={{8,0},{9,1},{10,2},{11,3},{12,4},{13,5},{14,6},{15,7}} | collective-permute-start | bytes 7077896 | tf_op jit(solution)/shard_map/ppermute | solution.py:1365
  513.3 1.4 copy-start.23
  590.9 84.6 %copy-start.4 = (bf16[2048,512]{1,0:T(8,128)(2,1)S(1)}, bf16[2048,512]{1,0:T(8,128)(2,1)}, u32[]{:S(2)}) copy-start(bf16[2048,512]{1,0:T(8,128)(2,1)} %get-tuple-element.65.attn_ref) | copy-start | bytes 6291460
  751.8 435.4 %reduce-scatter.4.cloned.1.call-start = ((), (), s32[]{:S(2)}) async-start(), calls=%async_computation.4 | async-start | bytes 3932160 | tf_op jit(solution)/shard_map/reduce_scatter | solution.py:1537
  807.2 394.1 %reduce-scatter.8.cloned.1.call-start = ((), (), s32[]{:S(2)}) async-start(), calls=%async_computation.6 | async-start | bytes 11796480 | tf_op jit(solution)/shard_map/reduce_scatter | solution.py:1505
  812.9 103.3 %collective-permute-start.6 = (bf16[1536,768]{1,0:T(8,128)(2,1)}, bf16[1536,768]{1,0:T(8,128)(2,1)S(1)}, u32[]{:S(2)}, u32[]{:S(2)}) collective-permute-start(bf16[1536,768]{1,0:T(8,128)(2,1)} %get-tuple-element.116), channel_id=1, source_target_pairs={{0,8},{1,9},{2,10},{3,11},{4,12},{5,13},{6,14},{7,15}} | collective-permute-start | bytes 7077896 | tf_op jit(solution)/shard_map/ppermute | solution.py:1379
  814.1 103.4 %collective-permute-start.7 = (bf16[1536,768]{1,0:T(8,128)(2,1)}, bf16[1536,768]{1,0:T(8,128)(2,1)}, u32[]{:S(2)}, u32[]{:S(2)}) collective-permute-start(bf16[1536,768]{1,0:T(8,128)(2,1)} %get-tuple-element.115), channel_id=1, source_target_pairs={{24,16},{25,17},{26,18},{27,19},{28,20},{29,21},{30,22},{31,23}} | collective-permute-start | bytes 7077896 | tf_op jit(solution)/shard_map/ppermute | solution.py:1379
  916.1 1.4 copy-start.3
  923.8 143.2 %collective-permute-start.8 = (bf16[1536,768]{1,0:T(8,128)(2,1)}, bf16[1536,768]{1,0:T(8,128)(2,1)}, u32[]{:S(2)}, u32[]{:S(2)}) collective-permute-start(bf16[1536,768]{1,0:T(8,128)(2,1)} %get-tuple-element.114), channel_id=1, source_target_pairs={{0,8},{8,16},{1,9},{9,17},{2,10},{10,18},{3,11},{11,19},{4,12},{12... | collective-permute-start | bytes 7077896 | tf_op jit(solution)/shard_map/ppermute | solution.py:1379
  926.9 143.0 %collective-permute-start.9 = (bf16[1536,768]{1,0:T(8,128)(2,1)S(1)}, bf16[1536,768]{1,0:T(8,128)(2,1)}, u32[]{:S(2)}, u32[]{:S(2)}) collective-permute-start(bf16[1536,768]{1,0:T(8,128)(2,1)S(1)} %get-tuple-element.113), channel_id=1, source_target_pairs={{16,8},{24,16},{17,9},{25,17},{18,10},{26,18},{19,11},{27,19},{20,... | collective-permute-start | bytes 7077896 | tf_op jit(solution)/shard_map/ppermute | solution.py:1379
  1076.9 124.4 %collective-permute-start.10 = (bf16[1536,768]{1,0:T(8,128)(2,1)}, bf16[1536,768]{1,0:T(8,128)(2,1)S(1)}, u32[]{:S(2)}, u32[]{:S(2)}) collective-permute-start(bf16[1536,768]{1,0:T(8,128)(2,1)} %get-tuple-element.112), channel_id=1, source_target_pairs={{0,8},{8,16},{16,24},{1,9},{9,17},{17,25},{2,10},{10,18},{18,26},{... | collective-permute-start | bytes 7077896 | tf_op jit(solution)/shard_map/ppermute | solution.py:1379
  1079.0 122.4 %collective-permute-start.11 = (bf16[1536,768]{1,0:T(8,128)(2,1)}, bf16[1536,768]{1,0:T(8,128)(2,1)}, u32[]{:S(2)}, u32[]{:S(2)}) collective-permute-start(bf16[1536,768]{1,0:T(8,128)(2,1)} %get-tuple-element.111), channel_id=1, source_target_pairs={{8,0},{16,8},{24,16},{9,1},{17,9},{25,17},{10,2},{18,10},{26,18},{... | collective-permute-start | bytes 7077896 | tf_op jit(solution)/shard_map/ppermute | solution.py:1379
  1201.3 10.9 copy-start.8
  1201.3 1.4 copy-start.2
  1212.1 2.0 copy-start.5
  1214.1 1.9 copy-start.9
  1214.1 2.9 copy-start.12
  1214.1 3.6 copy-start.11
  1214.1 4.2 copy-start.1
Sparse Core Ops, SparseCore 0:
  15.2 115.7 all-gather.13
  132.6 78.7 all-gather.9
  213.0 80.9 all-gather.7
  295.4 79.1 all-gather.11
  751.9 43.1 reduce-scatter.5
  807.4 104.0 reduce-scatter.3
  913.8 258.7 reduce-scatter.7

commit v7 on v6

--- a/solution.py
+++ b/solution.py
@@ -1322,22 +1322,29 @@
     )(w_gate, w_up, w_down)
 
 
-def unpack_kernel(z_ref, one_ref, all_ref, up_ref, down_ref, dg_ref, du_ref, dd_ref, own, sem):
+def unpack_kernel(
+    z_ref, one_ref, all_ref, up0_ref, down0_ref, up1_ref, down1_ref, dg_ref, du_ref, dd_ref, own, sem
+):
     copy = pltpu.make_async_copy(all_ref.at[z_ref[0]], own, sem)
     copy.start()
     cut = dg_ref.shape[1]
+    half = up0_ref.shape[0]
     piece = [slice(k * cut, (k + 1) * cut) for k in range(3)]
     dg_ref[1] = one_ref[piece[0], :].astype(F32)
     du_ref[1] = one_ref[piece[1], :].astype(F32)
     dd_ref[1] = jnp.transpose(one_ref[piece[2], :].astype(F32))
     copy.wait()
 
-    def total(at):
-        return own[at, :].astype(F32) + up_ref[at, :].astype(F32) + down_ref[at, :].astype(F32)
-
-    dg_ref[0] = total(piece[0])
-    du_ref[0] = total(piece[1])
-    dd_ref[0] = jnp.transpose(total(piece[2]))
+    def total(low, high):
+        shift, up, down = (0, up0_ref, down0_ref) if high <= half else (half, up1_ref, down1_ref)
+        there = slice(low - shift, high - shift)
+        value = own[low:high, :].astype(F32)
+        return value + up[there, :].astype(F32) + down[there, :].astype(F32)
+
+    dg_ref[0] = total(0, cut)
+    du_ref[0, : half - cut] = total(cut, half)
+    du_ref[0, half - cut :] = total(half, 2 * cut)
+    dd_ref[0] = jnp.transpose(total(2 * cut, 3 * cut))
 
 
 def unpack(z, one, grads, got):
@@ -1346,7 +1353,7 @@
     shape = jax.ShapeDtypeStruct
     return pl.pallas_call(
         unpack_kernel,
-        in_specs=[pl.BlockSpec(memory_space=pltpu.SMEM), VM, ANY, VM, VM],
+        in_specs=[pl.BlockSpec(memory_space=pltpu.SMEM), VM, ANY, VM, VM, VM, VM],
         out_specs=[VM] * 3,
         out_shape=[
             shape((2, cut, hidden), F32),
@@ -1365,18 +1372,26 @@
     return lax.ppermute(block_up, "dp", up), lax.ppermute(block_down, "dp", down)
 
 
-def reduce_hop(grads, got, n_dp, hop):
+def reduce_hop(grads, got, n_dp, hop, rows, before):
     place = lax.axis_index("dp")
     reach = n_dp - hop
+    zero = jnp.int32(0)
+    size = (1, rows[1] - rows[0], grads.shape[2])
     spots = (jnp.minimum(place + reach, n_dp - 1), jnp.maximum(place - reach, 0))
     if got is not None:
-        got = lax.optimization_barrier(got)
-    blocks = [lax.dynamic_index_in_dim(grads, spot, 0, False) for spot in spots]
+        got = lax.optimization_barrier((*got, *before))[:2]
+    elif before:
+        grads = after_of(grads, *before)
+    blocks = [
+        lax.dynamic_slice(grads, (spot.astype(jnp.int32), jnp.int32(rows[0]), zero), size)[0]
+        for spot in spots
+    ]
     if got is not None:
         blocks = [(b.astype(F32) + g.astype(F32)).astype(BF16) for b, g in zip(blocks, got)]
     up = [(i, i + 1) for i in range(hop)]
     down = [(i, i - 1) for i in range(n_dp - hop, n_dp)]
-    return lax.ppermute(blocks[0], "dp", up), lax.ppermute(blocks[1], "dp", down)
+    sent = lax.ppermute(blocks[0], "dp", up), lax.ppermute(blocks[1], "dp", down)
+    return sent, tuple(blocks)
 
 
 def after_of(value, *others):
@@ -1495,12 +1510,15 @@
             sources1 += [(up, "up", 1, 0), (down, "down", 1, 0)]
         carried, grads = run(0, [(full, "all", 0, 0)], carried, low, grads0)
         grads0 = (grads,)
-    got = None
+    rows_all = 3 * (width // n_dp)
+    spans = {"a": (0, rows_all // 2), "b": (rows_all // 2, rows_all)}
+    got, before = {tag: None for tag in spans}, ()
     for hop in range(2, n_dp + 1):
         if hop < n_dp:
             up, down = line_hop(up, down, n_dp, hop)
             sources1 += [(up, "up", hop, 0), (down, "down", hop, 0)]
-        got = reduce_hop(grads, got, n_dp, hop - 1)
+        for tag, rows in spans.items():
+            got[tag], before = reduce_hop(grads, got[tag], n_dp, hop - 1, rows, before)
     (moe, rows_grad), grads1 = run(1, sources1, carried, 0, ())
     done1 = lax.psum_scatter(
         grads1.reshape(3 * width, hidden), "dp", scatter_dimension=0, tiled=True
@@ -1550,7 +1568,7 @@
     layer_output, packed = close(n_ctx, n_dp, moe.reshape(blocks), after, packed)
     packed = packed.reshape(1024)
     query_w, key_w, value_w = post(n_ctx, qkv_w.reshape(n_ctx, depth, qw + 2 * HD))
-    gate_w, up_w, down_w = unpack(z, done1, grads, got)
+    gate_w, up_w, down_w = unpack(z, done1, grads, got["a"] + got["b"])
     return (
         layer_output.reshape(1, tokens, width),
         input_grad.reshape(1, tokens, width),

time: 1240 us -> 1200 us (0.968)
  waiting for transfers between devices: 382 us -> 344 us
    ppermute x3 -> x6, waiting for transfers between devices: 239 us -> 157 us  [reduce_hop(): lax.ppermute(blocks[0], 'dp', up)]
    reduce_scatter x1, waiting for transfers between devices: 0.02 us -> 37.2 us  [per_device(): lax.psum_scatter(grads1.reshape(3 * width, hidden), 'dp', scatter_dimensi...]
    ppermute x3 -> x6, starting transfers between devices: 6.36 us -> 21 us  [reduce_hop(): lax.ppermute(blocks[0], 'dp', up)]
  transfers between devices with their start and end apart: 19 -> 25, of which waited for: 5 -> 7; matrix products, arithmetic and copies ran while one was open for 4% -> 4% of each run, Pallas kernels for 39% -> 40%
where the time goes in v7:
time: 1200 us; the launch traced here: 1190 us
  Pallas kernels  712 us (59%)
  waiting for transfers between devices  344 us (29%)
  starting transfers between devices  50.4 us (4%)
  local copies, waits for them, and re-layouts  31.7 us (3%)
  other arithmetic  28.3 us (2%)
  between operations  15 us (1%)
    pallas_call x7, Pallas kernels, comm_call(): pl.pallas_call(kernel, out_shape=outs, in_specs=in_specs, out_specs=out_s...  428 us
    pallas_call x3, Pallas kernels, expert(): pl.pallas_call(functools.partial(expert_kernel, len(before) > 0, low, len...  164 us
    ppermute x6, waiting for transfers between devices, reduce_hop(): lax.ppermute(blocks[0], 'dp', up)  157 us
    all_gather x2, waiting for transfers between devices, per_device(): full = lax.all_gather(blocks0[index], 'dp', axis=0, tiled=False)  90.7 us
    pallas_call x1, Pallas kernels, attn_backward(): pl.pallas_call(functools.partial(attn_backward_kernel, n, n_dp, heads, MO...  67.1 us
    all_gather x1, waiting for transfers between devices, per_device(): lax.all_gather(cols.reshape(n_ctx * depth, qw + 2 * HD), 'dp', axis=0, ti...  57.3 us
    pallas_call x1, Pallas kernels, attn_forward(): pl.pallas_call(functools.partial(attn_forward_kernel, n, n_dp, heads, MOS...  37.3 us
    reduce_scatter x1, waiting for transfers between devices, per_device(): lax.psum_scatter(grads1.reshape(3 * width, hidden), 'dp', scatter_dimensi...  37.2 us
  transfers between devices with their start and end apart: 25, of which 7 were waited for; matrix products, arithmetic and copies ran while one was open for 4% of the time, Pallas kernels for 40%

profile of v7, /device:TPU:14, one launch (start us, length us, event | category | flops | bytes accessed | tf_op | source)
XLA Modules:
  0.0 1190.1 jit_solution(15139553620404590138)
XLA Ops:
  7.3 2.8 slice_bitcast_fusion
  10.0 1.7 slice_bitcast_fusion.1
  11.7 3.3 pack.2
  17.7 17.7 %shard_map.255 = (bf16[8,64,768]{2,1,0:T(8,128)(2,1)}, f32[4,8,8,128]{3,2,1,0:T(8,128)}) custom-call(bf16[8,64,768]{2,1,0:T(8,128)(2,1)} %maximum_bitcast_fusion.cols_ref, f32[8,128]{1,0:T(8,128)} %fusion.19.small_ref), custom_call_target="tpu_custom_call" | custom-call | bytes 24000000 | tf_op jit(solution)/shard_map/pallas_call | solution.py:429
  37.0 3.3 pack.3.rest_2_
  40.3 90.6 %all-gather.14.cloned.1.call-done = bf16[6144,512]{1,0:T(8,128)(2,1)} async-done(((bf16[1536,512]{1,0:T(8,128)(2,1)}), bf16[6144,512]{1,0:T(8,128)(2,1)}) %all-gather.14.cloned.1.call-update) | async-done | bytes 6291472 | tf_op jit(solution)/shard_map/all_gather | solution.py:1504
  131.0 2.4 collective-permute-start
  133.4 3.6 collective-permute-start.1
  139.9 78.9 %shard_map.256 = (bf16[8,256,2048]{2,1,0:T(8,128)(2,1)}, f32[8,24,256]{2,1,0:T(8,128)}, bf16[8,256,2048]{2,1,0:T(8,128)(2,1)}) custom-call(bf16[256,2048]{1,0:T(8,128)(2,1)} %bitcast.109, f32[1,2048]{1,0:T(1,128)} %reshape.175.gain_ref, f32[24,256]{1,0:T(8,128)} %maximum_maximum_fusion.info_ref, bf16[256,2048]{1,0:T(8,128)(2,1)} %bitcast.118), custom_call_target="tpu_custom_call" | custom-call | bytes 270000000 | tf_op jit(solution)/shard_map/pallas_call | solution.py:429
  222.9 3.9 fusion.10
  226.8 1.9 pad_maximum_fusion
  228.7 1.7 fusion.20
  230.4 4.1 collective-permute-start.2
  234.5 2.1 collective-permute-start.3
  236.6 57.3 %all-gather.8.cloned.1.call-done.wqkv_ref = bf16[2048,768]{1,0:T(8,128)(2,1)} async-done(((bf16[512,768]{1,0:T(8,128)(2,1)}), bf16[2048,768]{1,0:T(8,128)(2,1)}) %all-gather.8.cloned.1.call-update) | async-done | bytes 3145744 | tf_op jit(solution)/shard_map/all_gather | solution.py:1449
  293.9 37.3 %attn_forward.1 = (f32[2048,512]{1,0:T(8,128)}, f32[2048,128]{1,0:T(8,128)}, bf16[2048,512]{1,0:T(8,128)(2,1)}, bf16[2048,128]{1,0:T(8,128)(2,1)}, bf16[2048,128...) custom-call(bf16[2048,2048]{1,0:T(8,128)(2,1)} %bitcast.116, ...), custom_call_target="tpu_custom_call" | custom-call | flops 35000000512 | bytes 31457280 | tf_op jit(solution)/shard_map/attn_forward/pallas_call | solution.py:960
  331.2 87.8 %shard_map.257 = (f32[256,2048]{1,0:T(8,128)}, bf16[8,256,2048]{2,1,0:T(8,128)(2,1)}) custom-call(bf16[2048,512]{1,0:T(8,128)(2,1)} %get-tuple-element.70.attn_ref, bf16[512,2048]{1,0:T(8,128)(2,1)} %bitcast.120, bf16[256,2048]{1,0:T(8,128)(2,1)} %bitcast.110, f32[1,2048]{1,0:T(1,128)} %reshape.182.gain_ref), custom_call_target="tpu_custom_call" | custom-call | bytes 315000000 | tf_op jit(solution)/shard_map/pallas_call | solution.py:429
  419.0 32.4 %expert.3 = (bf16[2048,2048]{1,0:T(8,128)(2,1)}, bf16[2048,2048]{1,0:T(8,128)(2,1)}, bf16[4,1536,768]{2,1,0:T(8,128)(2,1)}) custom-call(s32[1]{0:T(128)} %bitcast.z_ref, bf16[2048,2048]{1,0:T(8,128)(2,1)} %bitcast.144, bf16[2048,2048]{1,0:T(8,128)(2,1)} %bitcast.141, f32[2048,1]{1,0:T(8,128)} %get-tuple-element.139.prob_ref, bf16[4,1536,256]{2,1,0:T(8,128)(2,1)} %bitcast.150), custom_call_target="tpu_custom_call" | custom-call | flops 19327352832 | bytes 41943040 | tf_op jit(solution)/shard_map/expert/pallas_call | solution.py:1279
  452.3 5.6 collective-permute-start.5
  457.9 55.3 %expert.4 = (bf16[2048,2048]{1,0:T(8,128)(2,1)}, bf16[2048,2048]{1,0:T(8,128)(2,1)}, bf16[4,1536,768]{2,1,0:T(8,128)(2,1)}) custom-call(s32[1]{0:T(128)} %bitcast.z_ref, bf16[2048,2048]{1,0:T(8,128)(2,1)} %bitcast.145, bf16[2048,2048]{1,0:T(8,128)(2,1)} %bitcast.142, f32[2048,1]{1,0:T(8,128)} %get-tuple-element.139.prob_ref, ...), custom_call_target="tpu_custom_call", output_to_operand_aliasing={{2}: (4, {})} | custom-call | flops 38654705664 | bytes 41943040 | tf_op jit(solution)/shard_map/expert/pallas_call | solution.py:1279
  514.6 76.1 %expert.5 = (bf16[2048,2048]{1,0:T(8,128)(2,1)}, bf16[2048,2048]{1,0:T(8,128)(2,1)}, bf16[4,1536,768]{2,1,0:T(8,128)(2,1)}) custom-call(s32[1]{0:T(128)} %bitcast.z_ref, bf16[2048,2048]{1,0:T(8,128)(2,1)} %bitcast.146, bf16[2048,2048]{1,0:T(8,128)(2,1)} %bitcast.143, f32[2048,1]{1,0:T(8,128)} %get-tuple-element.140.prob_ref, ...), custom_call_target="tpu_custom_call" | custom-call | flops 57982058496 | bytes 41943040 | tf_op jit(solution)/shard_map/expert/pallas_call | solution.py:1279
  590.8 84.6 %shard_map.258 = (f32[256,2048]{1,0:T(8,128)}, f32[8,2048]{1,0:T(8,128)}, bf16[8,256,2048]{2,1,0:T(8,128)(2,1)}) custom-call(bf16[8,256,2048]{2,1,0:T(8,128)(2,1)} %bitcast.114, f32[256,2048]{1,0:T(8,128)} %get-tuple-element.83.after_ref, bf16[256,2048]{1,0:T(8,128)(2,1)} %bitcast.119, f32[1,2048]{1,0:T(1,128)} %reshape.182.gain_ref), custom_call_target="tpu_custom_call" | custom-call | bytes 285000000 | tf_op jit(solution)/shard_map/pallas_call | solution.py:429
  675.3 9.1 convolution_convert_fusion
  684.5 67.1 %attn_backward.1 = (bf16[2048,768]{1,0:T(8,128)(2,1)}, f32[8,128]{1,0:T(8,128)}, bf16[4,128,2048]{2,1,0:T(8,128)(2,1)}) custom-call(bf16[2048,2048]{1,0:T(8,128)(2,1)} %bitcast.148, bf16[512,2048]{1,0:T(8,128)(2,1)} %bitcast.121, bf16[2048,512]{1,0:T(8,128)(2,1)} %get-tuple-element.70.attn_ref, f32[2048,128]{1,0:T(8,128)} %get-tuple-element.86.total_ref, ...), custom_call_target="tpu_custom_call" | custom-call | flops 60000002048 | bytes 31457280 | tf_op jit(solution)/shard_map/attn_backward/pallas_call | solution.py:1127
  751.7 55.4 %shard_map.259 = (f32[256,2048]{1,0:T(8,128)}, f32[8,2048]{1,0:T(8,128)}, bf16[2048,768]{1,0:T(8,128)(2,1)}) custom-call(bf16[2048,768]{1,0:T(8,128)(2,1)} %get-tuple-element.92.grad_ref, bf16[2048,768]{1,0:T(8,128)(2,1)} %all-gather.8.cloned.1.call-done.wqkv_ref, bf16[256,2048]{1,0:T(8,128)(2,1)} %bitcast.111, f32[256,2048]{1,0:T(8,128)} %get-tuple-element.93.mid_ref, ...), custom_call_target="tpu_custom_call" | custom-call | bytes 180000000 | tf_op jit(solution)/shard_map/pallas_call | solution.py:429
  807.8 3.2 dynamic-slice_bitcast_fusion.2
  812.3 1.7 collective-permute-start.7
  814.0 2.0 dynamic-slice_bitcast_fusion
  817.3 1.8 collective-permute-start.11
  819.0 48.3 %collective-permute-done.6 = bf16[768,768]{1,0:T(8,128)(2,1)} collective-permute-done((bf16[768,768]{1,0:T(8,128)(2,1)}, bf16[768,768]{1,0:T(8,128)(2,1)}, u32[]{:S(2)}, u32[]{:S(2)}) %collective-permute-start.6) | collective-permute-done | bytes 1179680 | tf_op jit(solution)/shard_map/ppermute | solution.py:1393
  867.3 4.3 fusion.5
  871.6 5.6 collective-permute-start.8
  878.6 38.1 %collective-permute-done.10 = bf16[768,768]{1,0:T(8,128)(2,1)} collective-permute-done((bf16[768,768]{1,0:T(8,128)(2,1)S(1)}, bf16[768,768]{1,0:T(8,128)(2,1)}, u32[]{:S(2)}, u32[]{:S(2)}) %collective-permute-start.10) | collective-permute-done | bytes 1179680 | tf_op jit(solution)/shard_map/ppermute | solution.py:1393
  916.6 4.3 fusion.3
  920.9 4.3 collective-permute-start.14
  926.5 30.2 %collective-permute-done.8 = bf16[768,768]{1,0:T(8,128)(2,1)} collective-permute-done((bf16[768,768]{1,0:T(8,128)(2,1)}, bf16[768,768]{1,0:T(8,128)(2,1)}, u32[]{:S(2)}, u32[]{:S(2)}) %collective-permute-start.8) | collective-permute-done | bytes 1179680 | tf_op jit(solution)/shard_map/ppermute | solution.py:1393
  956.7 4.3 fusion.2
  961.0 4.3 collective-permute-start.12
  965.3 1.9 collective-permute-start.13
  967.2 40.1 %collective-permute-done.14 = bf16[768,768]{1,0:T(8,128)(2,1)} collective-permute-done((bf16[768,768]{1,0:T(8,128)(2,1)}, bf16[768,768]{1,0:T(8,128)(2,1)}, u32[]{:S(2)}, u32[]{:S(2)}) %collective-permute-start.14) | collective-permute-done | bytes 1179680 | tf_op jit(solution)/shard_map/ppermute | solution.py:1393
  1007.3 4.3 fusion
  1011.5 4.3 collective-permute-start.16
  1015.8 2.6 collective-permute-start.17
  1022.1 89.2 %shard_map.260 = (bf16[256,2048]{1,0:T(8,128)(2,1)}, f32[8,128]{1,0:T(8,128)}) custom-call(bf16[8,256,2048]{2,1,0:T(8,128)(2,1)} %bitcast.115, f32[256,2048]{1,0:T(8,128)} %get-tuple-element.83.after_ref, f32[8,4,8,128]{3,2,1,0:T(8,128)} %copy_bitcast_fusion.3.small_ref), custom_call_target="tpu_custom_call" | custom-call | bytes 150000000 | tf_op jit(solution)/shard_map/pallas_call | solution.py:429
  1114.0 2.1 convert_element_type.136
  1116.2 14.0 %shard_map.261 = (f32[64,4096]{1,0:T(8,128)}, f32[64,512]{1,0:T(8,128)}, f32[64,512]{1,0:T(8,128)}) custom-call(bf16[8,64,768]{2,1,0:T(8,128)(2,1)} %bitcast.126), custom_call_target="tpu_custom_call" | custom-call | bytes 30000000 | tf_op jit(solution)/shard_map/pallas_call | solution.py:429
  1130.3 37.2 %reduce-scatter.8.cloned.1.call-done.one_ref = bf16[1536,768]{1,0:T(8,128)(2,1)} async-done(((bf16[6144,768]{1,0:T(8,128)(2,1)}), bf16[1536,768]{1,0:T(8,128)(2,1)}) %reduce-scatter.8.cloned.1.call-update) | async-done | bytes 2359312 | tf_op jit(solution)/shard_map/reduce_scatter | solution.py:1523
  1167.5 9.3 unpack.1
  (126 shorter events, 32.0 us)
Async XLA Ops:
  7.2 9.5 copy-start
  7.2 2.8 copy-start.4
  7.2 2.8 copy-start.5
  7.2 123.8 %all-gather.14.cloned.1.call-start = ((), (), s32[]{:S(2)}) async-start(), calls=%async_computation.9 | async-start | bytes 7864320 | tf_op jit(solution)/shard_map/all_gather | solution.py:1504
  11.7 4.2 copy-start.10
  15.0 0.9 copy-start.19
  15.0 0.9 copy-start.20
  15.1 0.9 copy-start.21
  15.1 1.6 copy-start.13
  15.1 221.5 %all-gather.10.cloned.1.call-start = ((), (), s32[]{:S(2)}) async-start(), calls=%async_computation.7 | async-start | bytes 2621440 | tf_op jit(solution)/shard_map/all_gather | solution.py:1450
  15.8 278.1 %all-gather.8.cloned.1.call-start = ((), (), s32[]{:S(2)}) async-start(), calls=%async_computation.3 | async-start | bytes 3932160 | tf_op jit(solution)/shard_map/all_gather | solution.py:1449
  35.4 383.6 %all-gather.12.cloned.1.call-start = ((), (), s32[]{:S(2)}) async-start(), calls=%async_computation.8 | async-start | bytes 3932160 | tf_op jit(solution)/shard_map/all_gather | solution.py:1504
  36.0 1078.0 %reduce-scatter.6.cloned.1.call-start = ((), (), s32[]{:S(2)}) async-start(), calls=%async_computation.5 | async-start | bytes 2621440 | tf_op jit(solution)/shard_map/reduce_scatter | solution.py:1552
  37.0 100.8 %copy-start.17 = (s32[1,256]{1,0:T(1,128)S(1)}, s32[1,256]{1,0:T(1,128)}, u32[]{:S(2)}) copy-start(s32[1,256]{1,0:T(1,128)} %param.17) | copy-start | bytes 3076
  37.0 102.1 %copy-start.15 = (f32[1,256,8]{1,2,0:T(8,128)S(1)}, f32[1,256,8]{1,2,0:T(8,128)}, u32[]{:S(2)}) copy-start(f32[1,256,8]{1,2,0:T(8,128)} %param.19) | copy-start | bytes 24580
  37.0 102.1 %copy-start.16 = (s32[1,256,8]{1,2,0:T(8,128)S(1)}, s32[1,256,8]{1,2,0:T(8,128)}, u32[]{:S(2)}) copy-start(s32[1,256,8]{1,2,0:T(8,128)} %param.18) | copy-start | bytes 24580
  131.0 99.4 %collective-permute-start = (bf16[1536,768]{1,0:T(8,128)(2,1)}, bf16[1536,768]{1,0:T(8,128)(2,1)S(1)}, u32[]{:S(2)}, u32[]{:S(2)}) collective-permute-start(bf16[1536,768]{1,0:T(8,128)(2,1)} %pack.3.rest_2_), channel_id=1, source_target_pairs={{0,8},{8,16},{16,24},{1,9},{9,17},{17,25},{2,10},{10,18},{18,26},{... | collective-permute-start | bytes 7077896 | tf_op jit(solution)/shard_map/ppermute | solution.py:1372
  133.4 101.1 %collective-permute-start.1 = (bf16[1536,768]{1,0:T(8,128)(2,1)}, bf16[1536,768]{1,0:T(8,128)(2,1)}, u32[]{:S(2)}, u32[]{:S(2)}) collective-permute-start(bf16[1536,768]{1,0:T(8,128)(2,1)} %pack.3.rest_2_), channel_id=1, source_target_pairs={{8,0},{16,8},{24,16},{9,1},{17,9},{25,17},{10,2},{18,10},{26,18},{... | collective-permute-start | bytes 7077896 | tf_op jit(solution)/shard_map/ppermute | solution.py:1372
  219.6 7.2 copy-start.14
  230.4 100.8 %copy-start.22 = (bf16[1536,768]{1,0:T(8,128)(2,1)}, bf16[1536,768]{1,0:T(8,128)(2,1)S(1)}, u32[]{:S(2)}) copy-start(bf16[1536,768]{1,0:T(8,128)(2,1)S(1)} %collective-permute-done.rest_3_) | copy-start | bytes 7077892
  230.4 221.1 %collective-permute-start.2 = (bf16[1536,768]{1,0:T(8,128)(2,1)S(1)}, bf16[1536,768]{1,0:T(8,128)(2,1)}, u32[]{:S(2)}, u32[]{:S(2)}) collective-permute-start(bf16[1536,768]{1,0:T(8,128)(2,1)S(1)} %collective-permute-done.rest_3_), channel_id=1, source_target_pairs={{8,16},{16,24},{9,17},{17,25},{10,18},{18,26},{11,19},{19,27},{12,... | collective-permute-start | bytes 7077896 | tf_op jit(solution)/shard_map/ppermute | solution.py:1372
  234.5 217.8 %collective-permute-start.3 = (bf16[1536,768]{1,0:T(8,128)(2,1)}, bf16[1536,768]{1,0:T(8,128)(2,1)}, u32[]{:S(2)}, u32[]{:S(2)}) collective-permute-start(bf16[1536,768]{1,0:T(8,128)(2,1)} %collective-permute-done.1.rest_4_), channel_id=1, source_target_pairs={{8,0},{16,8},{9,1},{17,9},{10,2},{18,10},{11,3},{19,11},{12,4},{20... | collective-permute-start | bytes 7077896 | tf_op jit(solution)/shard_map/ppermute | solution.py:1372
  451.5 61.7 %collective-permute-start.4 = (bf16[1536,768]{1,0:T(8,128)(2,1)}, bf16[1536,768]{1,0:T(8,128)(2,1)S(1)}, u32[]{:S(2)}, u32[]{:S(2)}) collective-permute-start(bf16[1536,768]{1,0:T(8,128)(2,1)} %collective-permute-done.2.rest_5_), channel_id=1, source_target_pairs={{16,24},{17,25},{18,26},{19,27},{20,28},{21,29},{22,30},{23,31}} | collective-permute-start | bytes 7077896 | tf_op jit(solution)/shard_map/ppermute | solution.py:1372
  452.3 60.9 %collective-permute-start.5 = (bf16[1536,768]{1,0:T(8,128)(2,1)}, bf16[1536,768]{1,0:T(8,128)(2,1)}, u32[]{:S(2)}, u32[]{:S(2)}) collective-permute-start(bf16[1536,768]{1,0:T(8,128)(2,1)} %collective-permute-done.3.rest_6_), channel_id=1, source_target_pairs={{8,0},{9,1},{10,2},{11,3},{12,4},{13,5},{14,6},{15,7}} | collective-permute-start | bytes 7077896 | tf_op jit(solution)/shard_map/ppermute | solution.py:1372
  513.2 1.4 copy-start.23
  590.8 84.6 %copy-start.2 = (bf16[2048,512]{1,0:T(8,128)(2,1)S(1)}, bf16[2048,512]{1,0:T(8,128)(2,1)}, u32[]{:S(2)}) copy-start(bf16[2048,512]{1,0:T(8,128)(2,1)} %get-tuple-element.70.attn_ref) | copy-start | bytes 6291460
  751.6 364.6 %reduce-scatter.4.cloned.1.call-start = ((), (), s32[]{:S(2)}) async-start(), calls=%async_computation.4 | async-start | bytes 3932160 | tf_op jit(solution)/shard_map/reduce_scatter | solution.py:1555
  807.1 360.4 %reduce-scatter.8.cloned.1.call-start = ((), (), s32[]{:S(2)}) async-start(), calls=%async_computation.6 | async-start | bytes 11796480 | tf_op jit(solution)/shard_map/reduce_scatter | solution.py:1523
  811.0 56.3 %collective-permute-start.6 = (bf16[768,768]{1,0:T(8,128)(2,1)}, bf16[768,768]{1,0:T(8,128)(2,1)}, u32[]{:S(2)}, u32[]{:S(2)}) collective-permute-start(bf16[768,768]{1,0:T(8,128)(2,1)} %get-tuple-element.132), channel_id=1, source_target_pairs={{0,8},{1,9},{2,10},{3,11},{4,12},{5,13},{6,14},{7,15}} | collective-permute-start | bytes 3538952 | tf_op jit(solution)/shard_map/ppermute | solution.py:1393
  812.3 55.0 %collective-permute-start.7 = (bf16[768,768]{1,0:T(8,128)(2,1)}, bf16[768,768]{1,0:T(8,128)(2,1)}, u32[]{:S(2)}, u32[]{:S(2)}) collective-permute-start(bf16[768,768]{1,0:T(8,128)(2,1)} %get-tuple-element.131), channel_id=1, source_target_pairs={{24,16},{25,17},{26,18},{27,19},{28,20},{29,21},{30,22},{31,23}} | collective-permute-start | bytes 3538952 | tf_op jit(solution)/shard_map/ppermute | solution.py:1393
  816.0 100.7 %collective-permute-start.10 = (bf16[768,768]{1,0:T(8,128)(2,1)S(1)}, bf16[768,768]{1,0:T(8,128)(2,1)}, u32[]{:S(2)}, u32[]{:S(2)}) collective-permute-start(bf16[768,768]{1,0:T(8,128)(2,1)S(1)} %get-tuple-element.130), channel_id=1, source_target_pairs={{0,8},{1,9},{2,10},{3,11},{4,12},{5,13},{6,14},{7,15}} | collective-permute-start | bytes 3538952 | tf_op jit(solution)/shard_map/ppermute | solution.py:1393
  817.3 99.4 %collective-permute-start.11 = (bf16[768,768]{1,0:T(8,128)(2,1)S(1)}, bf16[768,768]{1,0:T(8,128)(2,1)}, u32[]{:S(2)}, u32[]{:S(2)}) collective-permute-start(bf16[768,768]{1,0:T(8,128)(2,1)S(1)} %get-tuple-element.129), channel_id=1, source_target_pairs={{24,16},{25,17},{26,18},{27,19},{28,20},{29,21},{30,22},{31,23}} | collective-permute-start | bytes 3538952 | tf_op jit(solution)/shard_map/ppermute | solution.py:1393
  871.6 85.1 %collective-permute-start.8 = (bf16[768,768]{1,0:T(8,128)(2,1)}, bf16[768,768]{1,0:T(8,128)(2,1)}, u32[]{:S(2)}, u32[]{:S(2)}) collective-permute-start(bf16[768,768]{1,0:T(8,128)(2,1)} %get-tuple-element.128), channel_id=1, source_target_pairs={{0,8},{8,16},{1,9},{9,17},{2,10},{10,18},{3,11},{11,19},{4,12},{12... | collective-permute-start | bytes 3538952 | tf_op jit(solution)/shard_map/ppermute | solution.py:1393
  877.3 79.4 %collective-permute-start.9 = (bf16[768,768]{1,0:T(8,128)(2,1)}, bf16[768,768]{1,0:T(8,128)(2,1)}, u32[]{:S(2)}, u32[]{:S(2)}) collective-permute-start(bf16[768,768]{1,0:T(8,128)(2,1)} %get-tuple-element.127), channel_id=1, source_target_pairs={{16,8},{24,16},{17,9},{25,17},{18,10},{26,18},{19,11},{27,19},{20,... | collective-permute-start | bytes 3538952 | tf_op jit(solution)/shard_map/ppermute | solution.py:1393
  920.9 86.3 %collective-permute-start.14 = (bf16[768,768]{1,0:T(8,128)(2,1)}, bf16[768,768]{1,0:T(8,128)(2,1)}, u32[]{:S(2)}, u32[]{:S(2)}) collective-permute-start(bf16[768,768]{1,0:T(8,128)(2,1)} %get-tuple-element.126), channel_id=1, source_target_pairs={{0,8},{8,16},{1,9},{9,17},{2,10},{10,18},{3,11},{11,19},{4,12},{12... | collective-permute-start | bytes 3538952 | tf_op jit(solution)/shard_map/ppermute | solution.py:1393
  925.2 82.0 %collective-permute-start.15 = (bf16[768,768]{1,0:T(8,128)(2,1)}, bf16[768,768]{1,0:T(8,128)(2,1)}, u32[]{:S(2)}, u32[]{:S(2)}) collective-permute-start(bf16[768,768]{1,0:T(8,128)(2,1)} %get-tuple-element.125), channel_id=1, source_target_pairs={{16,8},{24,16},{17,9},{25,17},{18,10},{26,18},{19,11},{27,19},{20,... | collective-permute-start | bytes 3538952 | tf_op jit(solution)/shard_map/ppermute | solution.py:1393
  961.0 169.2 %collective-permute-start.12 = (bf16[768,768]{1,0:T(8,128)(2,1)}, bf16[768,768]{1,0:T(8,128)(2,1)S(1)}, u32[]{:S(2)}, u32[]{:S(2)}) collective-permute-start(bf16[768,768]{1,0:T(8,128)(2,1)} %get-tuple-element.124), channel_id=1, source_target_pairs={{0,8},{8,16},{16,24},{1,9},{9,17},{17,25},{2,10},{10,18},{18,26},{... | collective-permute-start | bytes 3538952 | tf_op jit(solution)/shard_map/ppermute | solution.py:1393
  965.3 165.0 %collective-permute-start.13 = (bf16[768,768]{1,0:T(8,128)(2,1)}, bf16[768,768]{1,0:T(8,128)(2,1)S(1)}, u32[]{:S(2)}, u32[]{:S(2)}) collective-permute-start(bf16[768,768]{1,0:T(8,128)(2,1)} %get-tuple-element.123), channel_id=1, source_target_pairs={{8,0},{16,8},{24,16},{9,1},{17,9},{25,17},{10,2},{18,10},{26,18},{... | collective-permute-start | bytes 3538952 | tf_op jit(solution)/shard_map/ppermute | solution.py:1393
  1011.5 118.7 %collective-permute-start.16 = (bf16[768,768]{1,0:T(8,128)(2,1)}, bf16[768,768]{1,0:T(8,128)(2,1)}, u32[]{:S(2)}, u32[]{:S(2)}) collective-permute-start(bf16[768,768]{1,0:T(8,128)(2,1)} %get-tuple-element.122), channel_id=1, source_target_pairs={{0,8},{8,16},{16,24},{1,9},{9,17},{17,25},{2,10},{10,18},{18,26},{... | collective-permute-start | bytes 3538952 | tf_op jit(solution)/shard_map/ppermute | solution.py:1393
  1015.8 114.4 %collective-permute-start.17 = (bf16[768,768]{1,0:T(8,128)(2,1)}, bf16[768,768]{1,0:T(8,128)(2,1)}, u32[]{:S(2)}, u32[]{:S(2)}) collective-permute-start(bf16[768,768]{1,0:T(8,128)(2,1)} %get-tuple-element.121), channel_id=1, source_target_pairs={{8,0},{16,8},{24,16},{9,1},{17,9},{25,17},{10,2},{18,10},{26,18},{... | collective-permute-start | bytes 3538952 | tf_op jit(solution)/shard_map/ppermute | solution.py:1393
  1130.2 46.6 %copy-start.8 = (bf16[256,2048]{1,0:T(8,128)(2,1)S(1)}, bf16[256,2048]{1,0:T(8,128)(2,1)}, u32[]{:S(2)}) copy-start(bf16[256,2048]{1,0:T(8,128)(2,1)} %get-tuple-element.97) | copy-start | bytes 3145732
  1130.2 37.3 %copy-start.6 = (bf16[768,768]{1,0:T(8,128)(2,1)}, bf16[768,768]{1,0:T(8,128)(2,1)S(1)}, u32[]{:S(2)}) copy-start(bf16[768,768]{1,0:T(8,128)(2,1)S(1)} %collective-permute-done.12.up0_ref) | copy-start | bytes 3538948
  1130.2 37.2 %copy-start.7 = (bf16[768,768]{1,0:T(8,128)(2,1)}, bf16[768,768]{1,0:T(8,128)(2,1)S(1)}, u32[]{:S(2)}) copy-start(bf16[768,768]{1,0:T(8,128)(2,1)S(1)} %collective-permute-done.13.down0_ref) | copy-start | bytes 3538948
  1176.8 2.0 copy-start.3
  1178.7 2.0 copy-start.9
  1178.7 4.3 copy-start.1
  1180.7 1.0 copy-start.12
  1180.7 1.7 copy-start.11
  (1 other events, 0.9 us)
Sparse Core Ops, SparseCore 0:
  15.2 115.7 all-gather.13
  132.5 78.7 all-gather.9
  213.0 80.9 all-gather.7
  295.3 79.1 all-gather.11
  751.7 43.1 reduce-scatter.5
  807.2 105.4 reduce-scatter.3
  915.0 252.3 reduce-scatter.7

commit v8 on v7

--- a/solution.py
+++ b/solution.py
@@ -227,7 +227,6 @@
         self.square = plane.chips == 4
         self.order = [3, 1, 2, 0] if self.square else far_first(plane.chips) + [0]
         self.send, self.recv = send, recv
-        self.sent = []
         half = mine.shape[1] // 2
         self.halves = [pl.ds(0, half), pl.ds(half, half)]
 
@@ -243,9 +242,7 @@
         )
 
     def go(self, s, h, to):
-        copy = self.copy(s, h, to)
-        copy.start()
-        self.sent.append(copy)
+        self.copy(s, h, to).start()
 
     def ready(self, s):
         if self.square:
@@ -257,7 +254,21 @@
             elif s == 2:
                 self.go(2, 1, 2)
         elif s:
-            copy = push(
+            push(
+                self.mine.at[s],
+                self.landed.at[s],
+                self.send.at[s],
+                self.recv.at[s],
+                "ctx",
+                self.plane.same(s),
+            ).start()
+
+    def sends(self):
+        if self.square:
+            hops = ((3, 0, 1), (3, 1, 2), (1, 0, 1), (2, 1, 2), (2, 0, 2), (1, 1, 1))
+            return [self.copy(*hop) for hop in hops]
+        return [
+            push(
                 self.mine.at[s],
                 self.landed.at[s],
                 self.send.at[s],
@@ -265,17 +276,14 @@
                 "ctx",
                 self.plane.same(s),
             )
-            copy.start()
-            self.sent.append(copy)
-
-    def settle(self, extra=None):
+            for s in self.order
+            if s
+        ]
+
+    def relay(self):
         mine, landed = self.mine, self.landed
         half = mine.shape[1] // 2
         if not self.square:
-            if extra is not None:
-                extra()
-            for copy in self.sent:
-                copy.wait_recv()
             return
         for s, h in ((2, 0), (1, 1)):
             self.copy(3, h, 1).wait_recv()
@@ -286,12 +294,22 @@
                 mine[s, rows, :] = total.astype(BF16)
 
             by_rows(half, add)
-            self.go(s, h, s)
-        if extra is not None:
-            extra()
+            self.copy(s, h, s).start()
+
+    def gathered(self):
+        if not self.square:
+            for copy in self.sends():
+                copy.wait_recv()
+            return
         for s in (1, 2):
             for h in (0, 1):
                 self.copy(s, h, s).wait_recv()
+
+    def settle(self, extra=None):
+        self.relay()
+        if extra is not None:
+            extra()
+        self.gathered()
 
     def total(self, at):
         value = self.mine[0, at, :].astype(F32)
@@ -300,7 +318,7 @@
         return value
 
     def finish(self):
-        for copy in self.sent:
+        for copy in self.sends():
             copy.wait_send()
 
 
@@ -327,7 +345,7 @@
             self.across[s].start()
             self.loads[s].start()
 
-    def run(self, extra=None):
+    def pairs(self):
         mine, other = self.mine, self.other
         for s in self.order:
             self.loads[s].wait()
@@ -339,8 +357,9 @@
 
             by_rows(mine.shape[1], add)
             self.spread.ready(s)
-        if extra is not None:
-            extra()
+
+    def run(self):
+        self.pairs()
         self.spread.settle()
 
     def total(self, at):
@@ -750,19 +769,7 @@
     )
 
 
-def last_kernel(
-    n,
-    grad_ref,
-    wqkv_ref,
-    x_ref,
-    mid_ref,
-    gain_ref,
-    *rest,
-):
-    fused = n == 8
-    normed_ref, rest = (rest[0], rest[1:]) if fused else (None, rest)
-    out_ref, apart_ref, rest = rest[0], rest[1], rest[2:]
-    wgrad_ref, scratch = (rest[0], rest[1:]) if fused else (None, rest)
+def last_kernel(n, grad_ref, wqkv_ref, x_ref, mid_ref, gain_ref, out_ref, apart_ref, *scratch):
     plane = Plane(n)
     plane.meet()
     apart_ref[...] = jnp.zeros_like(apart_ref)
@@ -774,14 +781,7 @@
 
     sums = Product(plane, value, *scratch[:8])
     sums.start()
-
-    def weights():
-        def fill(at):
-            wgrad_ref[at, :] = dot(normed_ref[:, at], grad_ref[...], TN).astype(BF16)
-
-        by_cols(normed_ref.shape[1], fill)
-
-    sums.run(weights if fused else None)
+    sums.run()
 
     def norm(at):
         value = x_ref[at, :].astype(F32)
@@ -795,17 +795,14 @@
     sums.finish()
 
 
-def last(n, grad, wqkv, x, mid, gain, normed):
+def last(n, grad, wqkv, x, mid, gain):
     shape = jax.ShapeDtypeStruct
-    outs = [shape(mid.shape, F32), shape((8, mid.shape[1]), F32)]
-    more = [normed] if n == 8 else []
-    outs += [shape(wqkv.shape, BF16) for _ in more]
-    got = comm_call(
+    return comm_call(
         functools.partial(last_kernel, n),
         5,
-        outs,
-        [VM] * len(outs),
-        [VM] * (5 + len(more)),
+        [shape(mid.shape, F32), shape((8, mid.shape[1]), F32)],
+        [VM, VM],
+        [VM] * 5,
         product_scratch(n, *mid.shape),
         60,
         grad,
@@ -813,42 +810,29 @@
         x,
         mid,
         gain,
-        *more,
-    )
-    return got if more else (*got, dot(normed, grad, TN).astype(BF16))
-
-
-def close_kernel(n, n_dp, part_ref, after_ref, small_ref, out_ref, sum_ref, *scratch):
+    )
+
+
+def gains_kernel(n, n_dp, small_ref, sum_ref, *scratch):
     meet(
         [("ctx", flip(lax.axis_index("ctx"), s, n)) for s in range(1, n)]
         + [("dp", flip(lax.axis_index("dp"), s, n_dp)) for s in range(1, n_dp)]
     )
-    plane = Plane(n)
-    sums = Scatter(plane, part_ref, *scratch[:8])
-    sums.start()
-    gains = Gains(n, n_dp, small_ref, *scratch[8:])
+    gains = Gains(n, n_dp, small_ref, *scratch)
     gains.start()
-    sums.run(gains.middle)
-
-    def add(at):
-        out_ref[at, :] = (after_ref[at, :] + sums.total(at)).astype(BF16)
-
-    by_rows(after_ref.shape[0], add)
-    sums.finish()
+    gains.middle()
     sum_ref[...] = gains.finish()
 
 
-def close(n, n_dp, part, after, small):
-    shape = jax.ShapeDtypeStruct
+def gains_sum(n, n_dp, small):
     tile = small.shape[2:]
     return comm_call(
-        functools.partial(close_kernel, n, n_dp),
-        6,
-        [shape(after.shape, BF16), shape(tile, F32)],
-        [VM, VM],
-        [ANY, VM, VM],
-        scatter_scratch(n, *after.shape)
-        + [
+        functools.partial(gains_kernel, n, n_dp),
+        8,
+        jax.ShapeDtypeStruct(tile, F32),
+        VM,
+        [VM],
+        [
             pltpu.VMEM((n, n_dp) + tile, F32),
             pltpu.VMEM((n_dp,) + tile, F32),
             pltpu.VMEM((n_dp,) + tile, F32),
@@ -857,9 +841,7 @@
             DMA((n_dp,)),
             DMA((n_dp,)),
         ],
-        50,
-        part,
-        after,
+        10,
         small,
     )
 
@@ -1024,9 +1006,12 @@
     docc_ref,
     docr_ref,
     wgrad_ref,
+    moe_ref,
+    after_ref,
     dqkv_ref,
     gains_ref,
     swapped_ref,
+    final_ref,
     dk_ref,
     dv_ref,
     dqa_ref,
@@ -1034,16 +1019,24 @@
 ):
     step = pl.program_id(0)
 
+    steps = pl.num_programs(0)
+
+    def scatter():
+        return Scatter(Plane(n), moe_ref, *sems[2:])
+
     @pl.when(step == 0)
     def _():
         meet_all(n)
-        RowSwap(n, n_dp, wgrad_ref, swapped_ref, *sems, True).start()
-
-    @pl.when(step == pl.num_programs(0) - 1)
+        scatter().start()
+        RowSwap(n, n_dp, wgrad_ref, swapped_ref, *sems[:2], True).start()
+
+    @pl.when(step == 2)
     def _():
-        swap = RowSwap(n, n_dp, wgrad_ref, swapped_ref, *sems, True)
-        swap.arrive()
-        swap.finish()
+        scatter().pairs()
+
+    @pl.when(step == steps - 2)
+    def _():
+        scatter().spread.relay()
 
     rows = branch_ref.shape[0]
     here = pl.ds(pl.multiple_of(step * rows, rows), rows)
@@ -1114,14 +1107,25 @@
             return carry
 
         lax.fori_loop(0, pl.num_programs(0), finish, 0)
-
-
-def attn_backward(n, n_dp, wgrad, branch, wout, attn, total, q, k, v, qlin, klin, cosine, sine, qgain, kgain, doc, rows):
+        sums = scatter()
+        sums.spread.gathered()
+
+        def add(at):
+            final_ref[at, :] = (after_ref[at, :] + sums.total(at)).astype(BF16)
+
+        by_rows(rows, add)
+        sums.finish()
+        swap = RowSwap(n, n_dp, wgrad_ref, swapped_ref, *sems[:2], True)
+        swap.arrive()
+        swap.finish()
+
+
+def attn_backward(n, n_dp, wgrad, moe, after, branch, wout, attn, total, q, k, v, qlin, klin, cosine, sine, qgain, kgain, doc, rows):
     length, width = branch.shape
     qw = wout.shape[0]
     heads = qw // HD
     blk = lambda cols: pl.BlockSpec((rows, cols), lambda i: (i, 0))
-    whole = lambda shape: pl.BlockSpec(shape, lambda i: (0, 0))
+    whole = lambda shape: pl.BlockSpec(shape, lambda i: (0, 0), pipeline_mode=pl.Buffered(1))
     shape = jax.ShapeDtypeStruct
     full = whole((length, HD))
     return pl.pallas_call(
@@ -1144,12 +1148,15 @@
             blk(1),
             whole((1, length)),
             ANY,
+            ANY,
+            whole(after.shape),
         ],
-        out_specs=[whole((length, qw + 2 * HD)), whole((8, HD)), ANY],
+        out_specs=[whole((length, qw + 2 * HD)), whole((8, HD)), ANY, whole(after.shape)],
         out_shape=[
             shape((length, qw + 2 * HD), BF16),
             shape((8, HD), F32),
             shape(wgrad.shape, BF16),
+            shape(after.shape, BF16),
         ],
         scratch_shapes=[
             pltpu.VMEM((length, HD), F32),
@@ -1157,7 +1164,8 @@
             pltpu.VMEM((rows, qw), F32),
             DMA((n_dp,)),
             DMA((n_dp,)),
-        ],
+        ]
+        + scatter_scratch(n, *after.shape),
         compiler_params=pltpu.CompilerParams(
             collective_id=9, has_side_effects=True, vmem_limit_bytes=VMEM_LIMIT
         ),
@@ -1165,7 +1173,7 @@
             flops=60 * 10**9, transcendentals=0, bytes_accessed=30 * 2**20
         ),
         name="attn_backward",
-    )(branch, wout, attn, total, q, k, v, qlin, klin, cosine, sine, qgain, kgain, doc[:, None], doc[None, :], wgrad)
+    )(branch, wout, attn, total, q, k, v, qlin, klin, cosine, sine, qgain, kgain, doc[:, None], doc[None, :], wgrad, moe, after)
 
 
 def expert_kernel(chained, low, aliased, plan, z_ref, n2_ref, top_ref, prob_ref, *rest):
@@ -1529,10 +1537,12 @@
     branch = branch.reshape(length, width)
 
     out_w = dot(attn, branch, TN).astype(BF16).reshape(n_dp, qw // n_dp, width)
-    dqkv, gains, out_w = attn_backward(
+    dqkv, gains, out_w, layer_output = attn_backward(
         n_ctx,
         n_dp,
         out_w,
+        moe.reshape(blocks),
+        after,
         branch,
         wout,
         attn,
@@ -1549,10 +1559,11 @@
         doc,
         tokens,
     )
+    qkv_w = dot(normed, dqkv, TN).astype(BF16)
+    qkv_w = lax.psum_scatter(qkv_w, "dp", scatter_dimension=0, tiled=True)
     out_w = lax.psum_scatter(out_w.reshape(qw, width), "dp", scatter_dimension=0, tiled=True)
     out_w = out_w.astype(F32)
-    input_grad, attn_part, qkv_w = last(n_ctx, dqkv, wqkv, inputs, mid, gain_attn, normed)
-    qkv_w = lax.psum_scatter(qkv_w, "dp", scatter_dimension=0, tiled=True)
+    input_grad, attn_part = last(n_ctx, dqkv, wqkv, inputs, mid, gain_attn)
     n_all = n_dp * n_ctx
     packed = jnp.concatenate(
         [
@@ -1565,7 +1576,7 @@
         axis=1,
     )
     packed = packed.reshape(n_dp, n_ctx, 8, HD).transpose(1, 0, 2, 3)
-    layer_output, packed = close(n_ctx, n_dp, moe.reshape(blocks), after, packed)
+    packed = gains_sum(n_ctx, n_dp, packed)
     packed = packed.reshape(1024)
     query_w, key_w, value_w = post(n_ctx, qkv_w.reshape(n_ctx, depth, qw + 2 * HD))
     gate_w, up_w, down_w = unpack(z, done1, grads, got["a"] + got["b"])

time: 1200 us -> 1180 us (0.983)
  Pallas kernels: 712 us -> 660 us
  waiting for transfers between devices: 344 us -> 367 us
    pallas_call x7, Pallas kernels: 428 us -> 372 us  [comm_call(): pl.pallas_call(kernel, out_shape=outs, in_specs=in_specs, out_specs=out_s...]
    reduce_scatter x1, waiting for transfers between devices: 37.2 us -> 71.6 us  [per_device(): lax.psum_scatter(grads1.reshape(3 * width, hidden), 'dp', scatter_dimensi...]
  transfers between devices with their start and end apart: 25 -> 25, of which waited for: 7 -> 7; matrix products, arithmetic and copies ran while one was open for 4% -> 5% of each run, Pallas kernels for 40% -> 35%
where the time goes in v8:
time: 1180 us; the launch traced here: 1170 us
  Pallas kernels  660 us (56%)
  waiting for transfers between devices  367 us (31%)
  starting transfers between devices  49.6 us (4%)
  local copies, waits for them, and re-layouts  31.6 us (3%)
  other arithmetic  28.4 us (2%)
  matrix products  20.5 us (2%)
  between operations  15 us (1%)
    pallas_call x7, Pallas kernels, comm_call(): pl.pallas_call(kernel, out_shape=outs, in_specs=in_specs, out_specs=out_s...  372 us
    pallas_call x3, Pallas kernels, expert(): pl.pallas_call(functools.partial(expert_kernel, len(before) > 0, low, len...  164 us
    ppermute x6, waiting for transfers between devices, reduce_hop(): lax.ppermute(blocks[0], 'dp', up)  146 us
    all_gather x2, waiting for transfers between devices, per_device(): full = lax.all_gather(blocks0[index], 'dp', axis=0, tiled=False)  90.7 us
    reduce_scatter x1, waiting for transfers between devices, per_device(): lax.psum_scatter(grads1.reshape(3 * width, hidden), 'dp', scatter_dimensi...  71.6 us
    pallas_call x1, Pallas kernels, attn_backward(): pl.pallas_call(functools.partial(attn_backward_kernel, n, n_dp, heads, MO...  70.4 us
    all_gather x1, waiting for transfers between devices, per_device(): lax.all_gather(cols.reshape(n_ctx * depth, qw + 2 * HD), 'dp', axis=0, ti...  57.3 us
    pallas_call x1, Pallas kernels, attn_forward(): pl.pallas_call(functools.partial(attn_forward_kernel, n, n_dp, heads, MOS...  37.3 us
  transfers between devices with their start and end apart: 25, of which 7 were waited for; matrix products, arithmetic and copies ran while one was open for 5% of the time, Pallas kernels for 35%

profile of v8, /device:TPU:14, one launch (start us, length us, event | category | flops | bytes accessed | tf_op | source)
XLA Modules:
  0.0 1171.9 jit_solution(16943021344722027571)
XLA Ops:
  7.3 2.8 slice_bitcast_fusion
  10.0 1.7 slice_bitcast_fusion.1
  11.7 3.3 pack.2
  17.7 17.6 %shard_map.255 = (bf16[8,64,768]{2,1,0:T(8,128)(2,1)}, f32[4,8,8,128]{3,2,1,0:T(8,128)}) custom-call(bf16[8,64,768]{2,1,0:T(8,128)(2,1)} %maximum_bitcast_fusion.cols_ref, f32[8,128]{1,0:T(8,128)} %fusion.19.small_ref), custom_call_target="tpu_custom_call" | custom-call | bytes 24000000 | tf_op jit(solution)/shard_map/pallas_call | solution.py:448
  37.0 3.3 pack.3.rest_2_
  40.3 90.6 %all-gather.14.cloned.1.call-done = bf16[6144,512]{1,0:T(8,128)(2,1)} async-done(((bf16[1536,512]{1,0:T(8,128)(2,1)}), bf16[6144,512]{1,0:T(8,128)(2,1)}) %all-gather.14.cloned.1.call-update) | async-done | bytes 6291472 | tf_op jit(solution)/shard_map/all_gather | solution.py:1512
  131.0 2.4 collective-permute-start
  133.4 3.6 collective-permute-start.1
  139.9 78.9 %shard_map.256 = (bf16[8,256,2048]{2,1,0:T(8,128)(2,1)}, f32[8,24,256]{2,1,0:T(8,128)}, bf16[8,256,2048]{2,1,0:T(8,128)(2,1)}) custom-call(bf16[256,2048]{1,0:T(8,128)(2,1)} %bitcast.113, f32[1,2048]{1,0:T(1,128)} %reshape.175.gain_ref, f32[24,256]{1,0:T(8,128)} %maximum_maximum_fusion.info_ref, bf16[256,2048]{1,0:T(8,128)(2,1)} %bitcast.117), custom_call_target="tpu_custom_call" | custom-call | bytes 270000000 | tf_op jit(solution)/shard_map/pallas_call | solution.py:448
  222.9 3.9 fusion.10
  226.8 1.9 pad_maximum_fusion
  230.4 4.0 collective-permute-start.2
  234.5 2.1 collective-permute-start.3
  236.6 57.3 %all-gather.8.cloned.1.call-done.wqkv_ref = bf16[2048,768]{1,0:T(8,128)(2,1)} async-done(((bf16[512,768]{1,0:T(8,128)(2,1)}), bf16[2048,768]{1,0:T(8,128)(2,1)}) %all-gather.8.cloned.1.call-update) | async-done | bytes 3145744 | tf_op jit(solution)/shard_map/all_gather | solution.py:1457
  293.9 37.3 %attn_forward.1 = (f32[2048,512]{1,0:T(8,128)}, f32[2048,128]{1,0:T(8,128)}, bf16[2048,512]{1,0:T(8,128)(2,1)}, bf16[2048,128]{1,0:T(8,128)(2,1)}, bf16[2048,128...) custom-call(bf16[2048,2048]{1,0:T(8,128)(2,1)} %bitcast.140, ...), custom_call_target="tpu_custom_call" | custom-call | flops 35000000512 | bytes 31457280 | tf_op jit(solution)/shard_map/attn_forward/pallas_call | solution.py:942
  331.2 87.6 %shard_map.257 = (f32[256,2048]{1,0:T(8,128)}, bf16[8,256,2048]{2,1,0:T(8,128)(2,1)}) custom-call(bf16[2048,512]{1,0:T(8,128)(2,1)} %get-tuple-element.68.attn_ref, bf16[512,2048]{1,0:T(8,128)(2,1)} %bitcast.119, bf16[256,2048]{1,0:T(8,128)(2,1)} %bitcast.114, f32[1,2048]{1,0:T(1,128)} %reshape.182.gain_ref), custom_call_target="tpu_custom_call" | custom-call | bytes 315000000 | tf_op jit(solution)/shard_map/pallas_call | solution.py:448
  418.8 32.5 %expert.3 = (bf16[2048,2048]{1,0:T(8,128)(2,1)}, bf16[2048,2048]{1,0:T(8,128)(2,1)}, bf16[4,1536,768]{2,1,0:T(8,128)(2,1)}) custom-call(s32[1]{0:T(128)} %bitcast.z_ref, bf16[2048,2048]{1,0:T(8,128)(2,1)} %bitcast.145, bf16[2048,2048]{1,0:T(8,128)(2,1)} %bitcast.142, f32[2048,1]{1,0:T(8,128)} %get-tuple-element.135.prob_ref, bf16[4,1536,256]{2,1,0:T(8,128)(2,1)} %bitcast.151), custom_call_target="tpu_custom_call" | custom-call | flops 19327352832 | bytes 41943040 | tf_op jit(solution)/shard_map/expert/pallas_call | solution.py:1287
  452.2 5.6 collective-permute-start.5
  457.8 55.3 %expert.4 = (bf16[2048,2048]{1,0:T(8,128)(2,1)}, bf16[2048,2048]{1,0:T(8,128)(2,1)}, bf16[4,1536,768]{2,1,0:T(8,128)(2,1)}) custom-call(s32[1]{0:T(128)} %bitcast.z_ref, bf16[2048,2048]{1,0:T(8,128)(2,1)} %bitcast.146, bf16[2048,2048]{1,0:T(8,128)(2,1)} %bitcast.143, f32[2048,1]{1,0:T(8,128)} %get-tuple-element.135.prob_ref, ...), custom_call_target="tpu_custom_call", output_to_operand_aliasing={{2}: (4, {})} | custom-call | flops 38654705664 | bytes 41943040 | tf_op jit(solution)/shard_map/expert/pallas_call | solution.py:1287
  514.6 76.1 %expert.5 = (bf16[2048,2048]{1,0:T(8,128)(2,1)}, bf16[2048,2048]{1,0:T(8,128)(2,1)}, bf16[4,1536,768]{2,1,0:T(8,128)(2,1)}) custom-call(s32[1]{0:T(128)} %bitcast.z_ref, bf16[2048,2048]{1,0:T(8,128)(2,1)} %bitcast.147, bf16[2048,2048]{1,0:T(8,128)(2,1)} %bitcast.144, f32[2048,1]{1,0:T(8,128)} %get-tuple-element.136.prob_ref, ...), custom_call_target="tpu_custom_call" | custom-call | flops 57982058496 | bytes 41943040 | tf_op jit(solution)/shard_map/expert/pallas_call | solution.py:1287
  590.7 84.6 %shard_map.258 = (f32[256,2048]{1,0:T(8,128)}, f32[8,2048]{1,0:T(8,128)}, bf16[8,256,2048]{2,1,0:T(8,128)(2,1)}) custom-call(bf16[8,256,2048]{2,1,0:T(8,128)(2,1)} %bitcast.116, f32[256,2048]{1,0:T(8,128)} %get-tuple-element.81.after_ref, bf16[256,2048]{1,0:T(8,128)(2,1)} %bitcast.118, f32[1,2048]{1,0:T(1,128)} %reshape.182.gain_ref), custom_call_target="tpu_custom_call" | custom-call | bytes 285000000 | tf_op jit(solution)/shard_map/pallas_call | solution.py:448
  675.3 9.1 convolution_convert_fusion.1
  684.4 70.4 %attn_backward.1 = (bf16[2048,768]{1,0:T(8,128)(2,1)}, f32[8,128]{1,0:T(8,128)}, bf16[4,128,2048]{2,1,0:T(8,128)(2,1)}, bf16[256,2048]{1,0:T(8,128)(2,1)}) custom-call(bf16[2048,2048]{1,0:T(8,128)(2,1)} %bitcast.149, bf16[512,2048]{1,0:T(8,128)(2,1)} %bitcast.120, bf16[2048,512]{1,0:T(8,128)(2,1)} %get-tuple-element.68.attn_ref, ...), custom_call_target="tpu_custom_call" | custom-call | flops 60000002048 | bytes 31457280 | tf_op jit(solution)/shard_map/attn_backward/pallas_call | solution.py:1131
  754.9 11.4 convolution_convert_fusion
  767.1 3.2 dynamic-slice_bitcast_fusion.2
  771.6 1.7 collective-permute-start.7
  773.3 1.8 dynamic-slice_bitcast_fusion
  776.4 1.8 collective-permute-start.11
  778.2 44.0 %collective-permute-done.6 = bf16[768,768]{1,0:T(8,128)(2,1)} collective-permute-done((bf16[768,768]{1,0:T(8,128)(2,1)}, bf16[768,768]{1,0:T(8,128)(2,1)}, u32[]{:S(2)}, u32[]{:S(2)}) %collective-permute-start.6) | collective-permute-done | bytes 1179680 | tf_op jit(solution)/shard_map/ppermute | solution.py:1401
  822.1 4.3 fusion.5
  826.4 4.4 collective-permute-start.8
  832.1 32.9 %collective-permute-done.10 = bf16[768,768]{1,0:T(8,128)(2,1)} collective-permute-done((bf16[768,768]{1,0:T(8,128)(2,1)S(1)}, bf16[768,768]{1,0:T(8,128)(2,1)}, u32[]{:S(2)}, u32[]{:S(2)}) %collective-permute-start.10) | collective-permute-done | bytes 1179680 | tf_op jit(solution)/shard_map/ppermute | solution.py:1401
  865.0 4.3 fusion.3
  869.3 4.4 collective-permute-start.14
  875.0 40.5 %collective-permute-done.8 = bf16[768,768]{1,0:T(8,128)(2,1)} collective-permute-done((bf16[768,768]{1,0:T(8,128)(2,1)}, bf16[768,768]{1,0:T(8,128)(2,1)}, u32[]{:S(2)}, u32[]{:S(2)}) %collective-permute-start.8) | collective-permute-done | bytes 1179680 | tf_op jit(solution)/shard_map/ppermute | solution.py:1401
  915.6 4.3 fusion.2
  919.8 4.4 collective-permute-start.12
  924.3 1.9 collective-permute-start.13
  926.2 28.2 %collective-permute-done.14 = bf16[768,768]{1,0:T(8,128)(2,1)} collective-permute-done((bf16[768,768]{1,0:T(8,128)(2,1)}, bf16[768,768]{1,0:T(8,128)(2,1)}, u32[]{:S(2)}, u32[]{:S(2)}) %collective-permute-start.14) | collective-permute-done | bytes 1179680 | tf_op jit(solution)/shard_map/ppermute | solution.py:1401
  954.4 4.3 fusion
  958.7 4.4 collective-permute-start.16
  963.2 2.5 collective-permute-start.17
  965.7 52.1 %shard_map.259 = (f32[256,2048]{1,0:T(8,128)}, f32[8,2048]{1,0:T(8,128)}) custom-call(bf16[2048,768]{1,0:T(8,128)(2,1)} %get-tuple-element.91.grad_ref, bf16[2048,768]{1,0:T(8,128)(2,1)} %all-gather.8.cloned.1.call-done.wqkv_ref, bf16[256,2048]{1,0:T(8,128)(2,1)} %bitcast.115, f32[256,2048]{1,0:T(8,128)} %get-tuple-element.92.mid_ref, ...), custom_call_target="tpu_custom_call" | custom-call | bytes 180000000 | tf_op jit(solution)/shard_map/pallas_call | solution.py:448
  1021.5 36.9 %shard_map.260 = f32[8,128]{1,0:T(8,128)} custom-call(f32[8,4,8,128]{3,2,1,0:T(8,128)} %copy_bitcast_fusion.3.small_ref), custom_call_target="tpu_custom_call" | custom-call | bytes 30000000 | tf_op jit(solution)/shard_map/pallas_call | solution.py:448
  1061.1 2.1 convert_element_type.140
  1063.2 14.5 %shard_map.261 = (f32[64,4096]{1,0:T(8,128)}, f32[64,512]{1,0:T(8,128)}, f32[64,512]{1,0:T(8,128)}) custom-call(bf16[8,64,768]{2,1,0:T(8,128)(2,1)} %bitcast.125), custom_call_target="tpu_custom_call" | custom-call | bytes 30000000 | tf_op jit(solution)/shard_map/pallas_call | solution.py:448
  1077.7 71.6 %reduce-scatter.8.cloned.1.call-done.one_ref = bf16[1536,768]{1,0:T(8,128)(2,1)} async-done(((bf16[6144,768]{1,0:T(8,128)(2,1)}), bf16[1536,768]{1,0:T(8,128)(2,1)}) %reduce-scatter.8.cloned.1.call-update) | async-done | bytes 2359312 | tf_op jit(solution)/shard_map/reduce_scatter | solution.py:1531
  1149.3 9.3 unpack.1
  (127 shorter events, 33.6 us)
Async XLA Ops:
  7.2 9.5 copy-start
  7.2 2.8 copy-start.4
  7.2 2.8 copy-start.5
  7.2 123.8 %all-gather.14.cloned.1.call-start = ((), (), s32[]{:S(2)}) async-start(), calls=%async_computation.9 | async-start | bytes 7864320 | tf_op jit(solution)/shard_map/all_gather | solution.py:1512
  11.7 4.2 copy-start.10
  15.0 0.9 copy-start.19
  15.0 0.9 copy-start.20
  15.1 0.9 copy-start.21
  15.1 1.6 copy-start.13
  15.1 221.5 %all-gather.10.cloned.1.call-start = ((), (), s32[]{:S(2)}) async-start(), calls=%async_computation.7 | async-start | bytes 2621440 | tf_op jit(solution)/shard_map/all_gather | solution.py:1458
  15.8 278.1 %all-gather.8.cloned.1.call-start = ((), (), s32[]{:S(2)}) async-start(), calls=%async_computation.3 | async-start | bytes 3932160 | tf_op jit(solution)/shard_map/all_gather | solution.py:1457
  35.4 383.4 %all-gather.12.cloned.1.call-start = ((), (), s32[]{:S(2)}) async-start(), calls=%async_computation.8 | async-start | bytes 3932160 | tf_op jit(solution)/shard_map/all_gather | solution.py:1512
  36.0 1025.1 %reduce-scatter.6.cloned.1.call-start = ((), (), s32[]{:S(2)}) async-start(), calls=%async_computation.5 | async-start | bytes 2621440 | tf_op jit(solution)/shard_map/reduce_scatter | solution.py:1564
  37.0 100.8 %copy-start.17 = (s32[1,256]{1,0:T(1,128)S(1)}, s32[1,256]{1,0:T(1,128)}, u32[]{:S(2)}) copy-start(s32[1,256]{1,0:T(1,128)} %param.17) | copy-start | bytes 3076
  37.0 102.1 %copy-start.15 = (f32[1,256,8]{1,2,0:T(8,128)S(1)}, f32[1,256,8]{1,2,0:T(8,128)}, u32[]{:S(2)}) copy-start(f32[1,256,8]{1,2,0:T(8,128)} %param.19) | copy-start | bytes 24580
  37.0 102.1 %copy-start.16 = (s32[1,256,8]{1,2,0:T(8,128)S(1)}, s32[1,256,8]{1,2,0:T(8,128)}, u32[]{:S(2)}) copy-start(s32[1,256,8]{1,2,0:T(8,128)} %param.18) | copy-start | bytes 24580
  131.0 99.4 %collective-permute-start = (bf16[1536,768]{1,0:T(8,128)(2,1)}, bf16[1536,768]{1,0:T(8,128)(2,1)S(1)}, u32[]{:S(2)}, u32[]{:S(2)}) collective-permute-start(bf16[1536,768]{1,0:T(8,128)(2,1)} %pack.3.rest_2_), channel_id=1, source_target_pairs={{0,8},{8,16},{16,24},{1,9},{9,17},{17,25},{2,10},{10,18},{18,26},{... | collective-permute-start | bytes 7077896 | tf_op jit(solution)/shard_map/ppermute | solution.py:1380
  133.4 101.0 %collective-permute-start.1 = (bf16[1536,768]{1,0:T(8,128)(2,1)}, bf16[1536,768]{1,0:T(8,128)(2,1)}, u32[]{:S(2)}, u32[]{:S(2)}) collective-permute-start(bf16[1536,768]{1,0:T(8,128)(2,1)} %pack.3.rest_2_), channel_id=1, source_target_pairs={{8,0},{16,8},{24,16},{9,1},{17,9},{25,17},{10,2},{18,10},{26,18},{... | collective-permute-start | bytes 7077896 | tf_op jit(solution)/shard_map/ppermute | solution.py:1380
  219.6 7.2 copy-start.14
  230.4 100.8 %copy-start.22 = (bf16[1536,768]{1,0:T(8,128)(2,1)}, bf16[1536,768]{1,0:T(8,128)(2,1)S(1)}, u32[]{:S(2)}) copy-start(bf16[1536,768]{1,0:T(8,128)(2,1)S(1)} %collective-permute-done.rest_3_) | copy-start | bytes 7077892
  230.4 220.9 %collective-permute-start.2 = (bf16[1536,768]{1,0:T(8,128)(2,1)S(1)}, bf16[1536,768]{1,0:T(8,128)(2,1)}, u32[]{:S(2)}, u32[]{:S(2)}) collective-permute-start(bf16[1536,768]{1,0:T(8,128)(2,1)S(1)} %collective-permute-done.rest_3_), channel_id=1, source_target_pairs={{8,16},{16,24},{9,17},{17,25},{10,18},{18,26},{11,19},{19,27},{12,... | collective-permute-start | bytes 7077896 | tf_op jit(solution)/shard_map/ppermute | solution.py:1380
  234.5 217.7 %collective-permute-start.3 = (bf16[1536,768]{1,0:T(8,128)(2,1)}, bf16[1536,768]{1,0:T(8,128)(2,1)}, u32[]{:S(2)}, u32[]{:S(2)}) collective-permute-start(bf16[1536,768]{1,0:T(8,128)(2,1)} %collective-permute-done.1.rest_4_), channel_id=1, source_target_pairs={{8,0},{16,8},{9,1},{17,9},{10,2},{18,10},{11,3},{19,11},{12,4},{20... | collective-permute-start | bytes 7077896 | tf_op jit(solution)/shard_map/ppermute | solution.py:1380
  451.3 61.8 %collective-permute-start.4 = (bf16[1536,768]{1,0:T(8,128)(2,1)}, bf16[1536,768]{1,0:T(8,128)(2,1)S(1)}, u32[]{:S(2)}, u32[]{:S(2)}) collective-permute-start(bf16[1536,768]{1,0:T(8,128)(2,1)} %collective-permute-done.2.rest_5_), channel_id=1, source_target_pairs={{16,24},{17,25},{18,26},{19,27},{20,28},{21,29},{22,30},{23,31}} | collective-permute-start | bytes 7077896 | tf_op jit(solution)/shard_map/ppermute | solution.py:1380
  452.2 61.0 %collective-permute-start.5 = (bf16[1536,768]{1,0:T(8,128)(2,1)}, bf16[1536,768]{1,0:T(8,128)(2,1)}, u32[]{:S(2)}, u32[]{:S(2)}) collective-permute-start(bf16[1536,768]{1,0:T(8,128)(2,1)} %collective-permute-done.3.rest_6_), channel_id=1, source_target_pairs={{8,0},{9,1},{10,2},{11,3},{12,4},{13,5},{14,6},{15,7}} | collective-permute-start | bytes 7077896 | tf_op jit(solution)/shard_map/ppermute | solution.py:1380
  513.1 1.4 copy-start.23
  590.7 84.6 %copy-start.2 = (bf16[2048,512]{1,0:T(8,128)(2,1)S(1)}, bf16[2048,512]{1,0:T(8,128)(2,1)}, u32[]{:S(2)}) copy-start(bf16[2048,512]{1,0:T(8,128)(2,1)} %get-tuple-element.68.attn_ref) | copy-start | bytes 6291460
  754.9 308.3 %reduce-scatter.4.cloned.1.call-start = ((), (), s32[]{:S(2)}) async-start(), calls=%async_computation.4 | async-start | bytes 3932160 | tf_op jit(solution)/shard_map/reduce_scatter | solution.py:1563
  766.3 383.0 %reduce-scatter.8.cloned.1.call-start = ((), (), s32[]{:S(2)}) async-start(), calls=%async_computation.6 | async-start | bytes 11796480 | tf_op jit(solution)/shard_map/reduce_scatter | solution.py:1531
  770.3 51.9 %collective-permute-start.6 = (bf16[768,768]{1,0:T(8,128)(2,1)}, bf16[768,768]{1,0:T(8,128)(2,1)}, u32[]{:S(2)}, u32[]{:S(2)}) collective-permute-start(bf16[768,768]{1,0:T(8,128)(2,1)} %get-tuple-element.128), channel_id=1, source_target_pairs={{0,8},{1,9},{2,10},{3,11},{4,12},{5,13},{6,14},{7,15}} | collective-permute-start | bytes 3538952 | tf_op jit(solution)/shard_map/ppermute | solution.py:1401
  771.6 50.6 %collective-permute-start.7 = (bf16[768,768]{1,0:T(8,128)(2,1)}, bf16[768,768]{1,0:T(8,128)(2,1)}, u32[]{:S(2)}, u32[]{:S(2)}) collective-permute-start(bf16[768,768]{1,0:T(8,128)(2,1)} %get-tuple-element.127), channel_id=1, source_target_pairs={{24,16},{25,17},{26,18},{27,19},{28,20},{29,21},{30,22},{31,23}} | collective-permute-start | bytes 3538952 | tf_op jit(solution)/shard_map/ppermute | solution.py:1401
  775.1 89.9 %collective-permute-start.10 = (bf16[768,768]{1,0:T(8,128)(2,1)S(1)}, bf16[768,768]{1,0:T(8,128)(2,1)}, u32[]{:S(2)}, u32[]{:S(2)}) collective-permute-start(bf16[768,768]{1,0:T(8,128)(2,1)S(1)} %get-tuple-element.126), channel_id=1, source_target_pairs={{0,8},{1,9},{2,10},{3,11},{4,12},{5,13},{6,14},{7,15}} | collective-permute-start | bytes 3538952 | tf_op jit(solution)/shard_map/ppermute | solution.py:1401
  776.4 88.6 %collective-permute-start.11 = (bf16[768,768]{1,0:T(8,128)(2,1)S(1)}, bf16[768,768]{1,0:T(8,128)(2,1)}, u32[]{:S(2)}, u32[]{:S(2)}) collective-permute-start(bf16[768,768]{1,0:T(8,128)(2,1)S(1)} %get-tuple-element.125), channel_id=1, source_target_pairs={{24,16},{25,17},{26,18},{27,19},{28,20},{29,21},{30,22},{31,23}} | collective-permute-start | bytes 3538952 | tf_op jit(solution)/shard_map/ppermute | solution.py:1401
  826.4 89.1 %collective-permute-start.8 = (bf16[768,768]{1,0:T(8,128)(2,1)}, bf16[768,768]{1,0:T(8,128)(2,1)}, u32[]{:S(2)}, u32[]{:S(2)}) collective-permute-start(bf16[768,768]{1,0:T(8,128)(2,1)} %get-tuple-element.124), channel_id=1, source_target_pairs={{0,8},{8,16},{1,9},{9,17},{2,10},{10,18},{3,11},{11,19},{4,12},{12... | collective-permute-start | bytes 3538952 | tf_op jit(solution)/shard_map/ppermute | solution.py:1401
  830.8 84.7 %collective-permute-start.9 = (bf16[768,768]{1,0:T(8,128)(2,1)}, bf16[768,768]{1,0:T(8,128)(2,1)}, u32[]{:S(2)}, u32[]{:S(2)}) collective-permute-start(bf16[768,768]{1,0:T(8,128)(2,1)} %get-tuple-element.123), channel_id=1, source_target_pairs={{16,8},{24,16},{17,9},{25,17},{18,10},{26,18},{19,11},{27,19},{20,... | collective-permute-start | bytes 3538952 | tf_op jit(solution)/shard_map/ppermute | solution.py:1401
  869.3 85.1 %collective-permute-start.14 = (bf16[768,768]{1,0:T(8,128)(2,1)}, bf16[768,768]{1,0:T(8,128)(2,1)}, u32[]{:S(2)}, u32[]{:S(2)}) collective-permute-start(bf16[768,768]{1,0:T(8,128)(2,1)} %get-tuple-element.122), channel_id=1, source_target_pairs={{0,8},{8,16},{1,9},{9,17},{2,10},{10,18},{3,11},{11,19},{4,12},{12... | collective-permute-start | bytes 3538952 | tf_op jit(solution)/shard_map/ppermute | solution.py:1401
  873.7 80.7 %collective-permute-start.15 = (bf16[768,768]{1,0:T(8,128)(2,1)}, bf16[768,768]{1,0:T(8,128)(2,1)}, u32[]{:S(2)}, u32[]{:S(2)}) collective-permute-start(bf16[768,768]{1,0:T(8,128)(2,1)} %get-tuple-element.121), channel_id=1, source_target_pairs={{16,8},{24,16},{17,9},{25,17},{18,10},{26,18},{19,11},{27,19},{20,... | collective-permute-start | bytes 3538952 | tf_op jit(solution)/shard_map/ppermute | solution.py:1401
  919.8 157.8 %collective-permute-start.12 = (bf16[768,768]{1,0:T(8,128)(2,1)}, bf16[768,768]{1,0:T(8,128)(2,1)S(1)}, u32[]{:S(2)}, u32[]{:S(2)}) collective-permute-start(bf16[768,768]{1,0:T(8,128)(2,1)} %get-tuple-element.120), channel_id=1, source_target_pairs={{0,8},{8,16},{16,24},{1,9},{9,17},{17,25},{2,10},{10,18},{18,26},{... | collective-permute-start | bytes 3538952 | tf_op jit(solution)/shard_map/ppermute | solution.py:1401
  924.3 153.4 %collective-permute-start.13 = (bf16[768,768]{1,0:T(8,128)(2,1)}, bf16[768,768]{1,0:T(8,128)(2,1)S(1)}, u32[]{:S(2)}, u32[]{:S(2)}) collective-permute-start(bf16[768,768]{1,0:T(8,128)(2,1)} %get-tuple-element.119), channel_id=1, source_target_pairs={{8,0},{16,8},{24,16},{9,1},{17,9},{25,17},{10,2},{18,10},{26,18},{... | collective-permute-start | bytes 3538952 | tf_op jit(solution)/shard_map/ppermute | solution.py:1401
  958.7 119.0 %collective-permute-start.16 = (bf16[768,768]{1,0:T(8,128)(2,1)}, bf16[768,768]{1,0:T(8,128)(2,1)}, u32[]{:S(2)}, u32[]{:S(2)}) collective-permute-start(bf16[768,768]{1,0:T(8,128)(2,1)} %get-tuple-element.118), channel_id=1, source_target_pairs={{0,8},{8,16},{16,24},{1,9},{9,17},{17,25},{2,10},{10,18},{18,26},{... | collective-permute-start | bytes 3538952 | tf_op jit(solution)/shard_map/ppermute | solution.py:1401
  963.2 114.6 %collective-permute-start.17 = (bf16[768,768]{1,0:T(8,128)(2,1)}, bf16[768,768]{1,0:T(8,128)(2,1)}, u32[]{:S(2)}, u32[]{:S(2)}) collective-permute-start(bf16[768,768]{1,0:T(8,128)(2,1)} %get-tuple-element.117), channel_id=1, source_target_pairs={{8,0},{16,8},{24,16},{9,1},{17,9},{25,17},{10,2},{18,10},{26,18},{... | collective-permute-start | bytes 3538952 | tf_op jit(solution)/shard_map/ppermute | solution.py:1401
  1077.7 80.9 %copy-start.8 = (bf16[256,2048]{1,0:T(8,128)(2,1)S(1)}, bf16[256,2048]{1,0:T(8,128)(2,1)}, u32[]{:S(2)}) copy-start(bf16[256,2048]{1,0:T(8,128)(2,1)} %get-tuple-element.90) | copy-start | bytes 3145732
  1077.7 71.6 %copy-start.6 = (bf16[768,768]{1,0:T(8,128)(2,1)}, bf16[768,768]{1,0:T(8,128)(2,1)S(1)}, u32[]{:S(2)}) copy-start(bf16[768,768]{1,0:T(8,128)(2,1)S(1)} %collective-permute-done.12.up0_ref) | copy-start | bytes 3538948
  1077.7 71.6 %copy-start.7 = (bf16[768,768]{1,0:T(8,128)(2,1)}, bf16[768,768]{1,0:T(8,128)(2,1)S(1)}, u32[]{:S(2)}) copy-start(bf16[768,768]{1,0:T(8,128)(2,1)S(1)} %collective-permute-done.13.down0_ref) | copy-start | bytes 3538948
  1158.6 2.0 copy-start.3
  1160.6 2.0 copy-start.9
  1160.6 4.3 copy-start.1
  1162.5 1.0 copy-start.12
  1162.5 1.7 copy-start.11
  (1 other events, 0.9 us)
Sparse Core Ops, SparseCore 0:
  15.2 115.7 all-gather.13
  132.5 78.7 all-gather.9
  213.0 80.8 all-gather.7
  295.3 79.1 all-gather.11
  755.0 61.5 reduce-scatter.5
  819.3 108.6 reduce-scatter.3
  930.4 218.8 reduce-scatter.7

commit v9 on v8

--- a/solution.py
+++ b/solution.py
@@ -580,10 +580,10 @@
     for c in range(n):
         query_ref[:, c * qw : (c + 1) * qw] = blocks[c, :, :qw].astype(F32)
     for g in range(KV):
-        for out, at in ((key_ref, qw), (value_ref, qw + HD)):
-            total = blocks[g * share, :, at : at + HD].astype(F32)
-            for c in range(1, share):
-                total = total + blocks[g * share + c, :, at : at + HD].astype(F32)
+        for out, kind in ((key_ref, 0), (value_ref, 1)):
+            total = blocks[g * share + kind, :, qw:].astype(F32)
+            for c in range(2 + kind, share, 2):
+                total = total + blocks[g * share + c, :, qw:].astype(F32)
             out[:, g * HD : (g + 1) * HD] = total
     for copy in copies:
         copy.wait_send()
@@ -870,6 +870,7 @@
     wout_ref,
     acc_ref,
     sum_ref,
+    mate_ref,
     *sems,
 ):
     step = pl.program_id(0)
@@ -877,7 +878,18 @@
     @pl.when(step == 0)
     def _():
         meet_all(n)
-        RowSwap(n, n_dp, rows_ref, wout_ref, *sems, False).start()
+        copy = push(
+            wqkv_ref.at[:, pl.ds(heads * HD, HD)],
+            mate_ref,
+            sems[2],
+            sems[3],
+            "ctx",
+            Plane(n).mate,
+        )
+        copy.start()
+        RowSwap(n, n_dp, rows_ref, wout_ref, *sems[:2], False).start()
+        copy.wait_recv()
+        copy.wait_send()
 
     rows = normed_ref.shape[0]
     lin = dot(normed_ref[...], wqkv_ref[...])
@@ -890,10 +902,13 @@
         part = lin[:, cols]
         qlin_ref[:, cols] = part
         q_ref[:, cols] = head_forward(part, qgain_ref[...], cosine, sine).astype(BF16)
-    key_lin = lin[:, qw : qw + HD]
+    own = lin[:, qw:]
+    other = dot(normed_ref[...], mate_ref[...])
+    first_core = lax.axis_index("ctx") % 2 == 0
+    key_lin = jnp.where(first_core, own, other)
     klin_ref[...] = key_lin
     k_ref[here, :] = head_forward(key_lin, kgain_ref[...], cosine, sine).astype(BF16)
-    v_ref[here, :] = lin[:, qw + HD :].astype(BF16)
+    v_ref[here, :] = jnp.where(first_core, other, own).astype(BF16)
     acc_ref[...] = jnp.zeros_like(acc_ref)
     sum_ref[...] = jnp.zeros_like(sum_ref)
     row_pos = step * rows + lax.broadcasted_iota(jnp.int32, (rows, rows), 0)
@@ -927,14 +942,14 @@
 
     @pl.when(step == pl.num_programs(0) - 1)
     def _():
-        swap = RowSwap(n, n_dp, rows_ref, wout_ref, *sems, False)
+        swap = RowSwap(n, n_dp, rows_ref, wout_ref, *sems[:2], False)
         swap.arrive()
         swap.finish()
 
 
 def attn_forward(n, n_dp, normed, wqkv, cosine, sine, qgain, kgain, doc, wrows, rows):
     length, width = normed.shape
-    qw = wqkv.shape[1] - 2 * HD
+    qw = wqkv.shape[1] - HD
     heads = qw // HD
     blk = lambda cols: pl.BlockSpec((rows, cols), lambda i: (i, 0))
     whole = lambda shape: pl.BlockSpec(shape, lambda i: (0, 0))
@@ -973,8 +988,12 @@
             shape((length, HD), F32),
             shape(wrows.shape, BF16),
         ],
-        scratch_shapes=[pltpu.VMEM((rows, qw), F32), pltpu.VMEM((rows, qw), F32)]
-        + [DMA((n_dp,)), DMA((n_dp,))],
+        scratch_shapes=[
+            pltpu.VMEM((rows, qw), F32),
+            pltpu.VMEM((rows, qw), F32),
+            pltpu.VMEM((width, HD), BF16),
+        ]
+        + [DMA((n_dp,)), DMA((n_dp,)), DMA(()), DMA(())],
         compiler_params=pltpu.CompilerParams(
             collective_id=7, has_side_effects=True, vmem_limit_bytes=VMEM_LIMIT
         ),
@@ -1015,6 +1034,8 @@
     dk_ref,
     dv_ref,
     dqa_ref,
+    give_ref,
+    take_ref,
     *sems,
 ):
     step = pl.program_id(0)
@@ -1022,7 +1043,7 @@
     steps = pl.num_programs(0)
 
     def scatter():
-        return Scatter(Plane(n), moe_ref, *sems[2:])
+        return Scatter(Plane(n), moe_ref, *sems[2:10])
 
     @pl.when(step == 0)
     def _():
@@ -1100,13 +1121,15 @@
             grad, gain_part = head_backward(
                 klin_ref[at, :], kgain_ref[...], cos_ref[at, :], sin_ref[at, :], dk_ref[at, :] * SCALE
             )
-            qw = heads * HD
-            dqkv_ref[at, qw : qw + HD] = grad.astype(BF16)
-            dqkv_ref[at, qw + HD :] = dv_ref[at, :].astype(BF16)
+            first_core = lax.axis_index("ctx") % 2 == 0
+            dk_ref[at, :] = jnp.where(first_core, grad, dv_ref[at, :])
+            give_ref[at, :] = jnp.where(first_core, dv_ref[at, :], grad).astype(BF16)
             gains_ref[1:2, :] += gain_part
             return carry
 
         lax.fori_loop(0, pl.num_programs(0), finish, 0)
+        trade = push(give_ref, take_ref, sems[10], sems[11], "ctx", Plane(n).mate)
+        trade.start()
         sums = scatter()
         sums.spread.gathered()
 
@@ -1115,6 +1138,16 @@
 
         by_rows(rows, add)
         sums.finish()
+        trade.wait_recv()
+
+        def join(block, carry):
+            at = pl.ds(pl.multiple_of(block * rows, rows), rows)
+            total = dk_ref[at, :] + take_ref[at, :].astype(F32)
+            dqkv_ref[at, heads * HD :] = total.astype(BF16)
+            return carry
+
+        lax.fori_loop(0, pl.num_programs(0), join, 0)
+        trade.wait_send()
         swap = RowSwap(n, n_dp, wgrad_ref, swapped_ref, *sems[:2], True)
         swap.arrive()
         swap.finish()
@@ -1151,9 +1184,9 @@
             ANY,
             whole(after.shape),
         ],
-        out_specs=[whole((length, qw + 2 * HD)), whole((8, HD)), ANY, whole(after.shape)],
+        out_specs=[whole((length, qw + HD)), whole((8, HD)), ANY, whole(after.shape)],
         out_shape=[
-            shape((length, qw + 2 * HD), BF16),
+            shape((length, qw + HD), BF16),
             shape((8, HD), F32),
             shape(wgrad.shape, BF16),
             shape(after.shape, BF16),
@@ -1162,10 +1195,13 @@
             pltpu.VMEM((length, HD), F32),
             pltpu.VMEM((length, HD), F32),
             pltpu.VMEM((rows, qw), F32),
+            pltpu.VMEM((length, HD), BF16),
+            pltpu.VMEM((length, HD), BF16),
             DMA((n_dp,)),
             DMA((n_dp,)),
         ]
-        + scatter_scratch(n, *after.shape),
+        + scatter_scratch(n, *after.shape)
+        + [DMA(()), DMA(())],
         compiler_params=pltpu.CompilerParams(
             collective_id=9, has_side_effects=True, vmem_limit_bytes=VMEM_LIMIT
         ),
@@ -1440,13 +1476,10 @@
     kinds = 2 * (cut + hcut)
     small = jnp.concatenate([attn_gain, ffn_gain, query_gain, key_gain]).astype(F32)
     small = jnp.pad(small, (0, 1024 - kinds)).reshape(8, HD)
+    even = (jnp.arange(n_ctx) % 2 == 0)[None, :, None]
+    wide = [jnp.repeat(w.reshape(depth, KV, HD), share, axis=1) for w in (w_key, w_value)]
     cols = jnp.concatenate(
-        [
-            w_query.reshape(depth, n_ctx, qw),
-            jnp.repeat(w_key.reshape(depth, KV, HD), share, axis=1),
-            jnp.repeat(w_value.reshape(depth, KV, HD), share, axis=1),
-        ],
-        axis=2,
+        [w_query.reshape(depth, n_ctx, qw), jnp.where(even, wide[0], wide[1])], axis=2
     ).transpose(1, 0, 2)
     cols, small = prep(n_ctx, n_dp, cols, small)
     small = small.reshape(n_dp * n_ctx, 1024)
@@ -1454,7 +1487,7 @@
     gain_ffn = small[:, cut : 2 * cut].reshape(1, width)
     gain_query = small[:, 2 * cut : 2 * cut + hcut].reshape(1, HD)
     gain_key = small[:, 2 * cut + hcut : kinds].reshape(1, HD)
-    wqkv = lax.all_gather(cols.reshape(n_ctx * depth, qw + 2 * HD), "dp", axis=0, tiled=True)
+    wqkv = lax.all_gather(cols.reshape(n_ctx * depth, qw + HD), "dp", axis=0, tiled=True)
     wrows = lax.all_gather(w_out, "dp", axis=0, tiled=False)
 
     inputs = layer_input.reshape(tokens, width)
@@ -1511,7 +1544,8 @@
     for index, (low, high) in enumerate(cuts):
         full = lax.all_gather(blocks0[index], "dp", axis=0, tiled=False)
         if index == 1:
-            (block1,) = pack([(0, hidden)], w_gate[1], w_up[1], w_down[1])
+            later = lax.optimization_barrier((w_gate[1], w_up[1], w_down[1], *carried))[:3]
+            (block1,) = pack([(0, hidden)], *later)
             sources1 = [(block1, "up", 0, 0)]
             up = down = after_of(block1, full)
             up, down = line_hop(up, down, n_dp, 1)
@@ -1578,7 +1612,7 @@
     packed = packed.reshape(n_dp, n_ctx, 8, HD).transpose(1, 0, 2, 3)
     packed = gains_sum(n_ctx, n_dp, packed)
     packed = packed.reshape(1024)
-    query_w, key_w, value_w = post(n_ctx, qkv_w.reshape(n_ctx, depth, qw + 2 * HD))
+    query_w, key_w, value_w = post(n_ctx, qkv_w.reshape(n_ctx, depth, qw + HD))
     gate_w, up_w, down_w = unpack(z, done1, grads, got["a"] + got["b"])
     return (
         layer_output.reshape(1, tokens, width),

time: 1180 us -> 1130 us (0.958)
  waiting for transfers between devices: 367 us -> 311 us
    ppermute x3, waiting for transfers between devices: 0.01 us -> 96.4 us  [line_hop(): lax.ppermute(block_up, 'dp', up)]
    all_gather x2, waiting for transfers between devices: 90.7 us -> 0.02 us  [per_device(): full = lax.all_gather(blocks0[index], 'dp', axis=0, tiled=False)]
    all_gather x1, waiting for transfers between devices: 57.3 us -> 0.01 us  [per_device(): lax.all_gather(cols.reshape(n_ctx * depth, qw + HD), 'dp', axis=0, tiled=...]
  transfers between devices with their start and end apart: 25 -> 25, of which waited for: 7 -> 8; matrix products, arithmetic and copies ran while one was open for 5% -> 6% of each run, Pallas kernels for 35% -> 38%
where the time goes in v9:
time: 1130 us; the launch traced here: 1120 us
  Pallas kernels  662 us (59%)
  waiting for transfers between devices  311 us (28%)
  starting transfers between devices  49.8 us (4%)
  local copies, waits for them, and re-layouts  30.4 us (3%)
  other arithmetic  28.4 us (3%)
  matrix products  20.2 us (2%)
  between operations  14.9 us (1%)
    pallas_call x7, Pallas kernels, comm_call(): pl.pallas_call(kernel, out_shape=outs, in_specs=in_specs, out_specs=out_s...  368 us
    pallas_call x3, Pallas kernels, expert(): pl.pallas_call(functools.partial(expert_kernel, len(before) > 0, low, len...  164 us
    ppermute x6, waiting for transfers between devices, reduce_hop(): lax.ppermute(blocks[0], 'dp', up)  144 us
    ppermute x3, waiting for transfers between devices, line_hop(): lax.ppermute(block_up, 'dp', up)  96.4 us
    pallas_call x1, Pallas kernels, attn_backward(): pl.pallas_call(functools.partial(attn_backward_kernel, n, n_dp, heads, MO...  71.6 us
    reduce_scatter x1, waiting for transfers between devices, per_device(): lax.psum_scatter(grads1.reshape(3 * width, hidden), 'dp', scatter_dimensi...  65.4 us
    pallas_call x1, Pallas kernels, attn_forward(): pl.pallas_call(functools.partial(attn_forward_kernel, n, n_dp, heads, MOS...  41.8 us
  transfers between devices with their start and end apart: 25, of which 8 were waited for; matrix products, arithmetic and copies ran while one was open for 6% of the time, Pallas kernels for 38%

profile of v9, /device:TPU:14, one launch (start us, length us, event | category | flops | bytes accessed | tf_op | source)
XLA Modules:
  0.0 1116.7 jit_solution(3342007006048014319)
XLA Ops:
  11.8 15.4 %shard_map.255 = (bf16[8,64,640]{2,1,0:T(8,128)(2,1)}, f32[4,8,8,128]{3,2,1,0:T(8,128)}) custom-call(bf16[8,64,640]{2,1,0:T(8,128)(2,1)} %maximum_bitcast_fusion.cols_ref, f32[8,128]{1,0:T(8,128)} %fusion.19.small_ref), custom_call_target="tpu_custom_call" | custom-call | bytes 24000000 | tf_op jit(solution)/shard_map/pallas_call | solution.py:448
  31.1 3.3 pack.2
  38.0 81.0 %shard_map.256 = (bf16[8,256,2048]{2,1,0:T(8,128)(2,1)}, f32[8,24,256]{2,1,0:T(8,128)}, bf16[8,256,2048]{2,1,0:T(8,128)(2,1)}) custom-call(bf16[256,2048]{1,0:T(8,128)(2,1)} %bitcast.113, f32[1,2048]{1,0:T(1,128)} %reshape.185.gain_ref, f32[24,256]{1,0:T(8,128)} %maximum_maximum_fusion.info_ref, bf16[256,2048]{1,0:T(8,128)(2,1)} %bitcast.119), custom_call_target="tpu_custom_call" | custom-call | bytes 270000000 | tf_op jit(solution)/shard_map/pallas_call | solution.py:448
  123.0 3.9 fusion.10
  126.9 1.9 pad_maximum_fusion
  130.5 41.8 %attn_forward.1 = (f32[2048,512]{1,0:T(8,128)}, f32[2048,128]{1,0:T(8,128)}, bf16[2048,512]{1,0:T(8,128)(2,1)}, bf16[2048,128]{1,0:T(8,128)(2,1)}, bf16[2048,128...) custom-call(bf16[2048,2048]{1,0:T(8,128)(2,1)} %bitcast.140, ...), custom_call_target="tpu_custom_call" | custom-call | flops 35000000512 | bytes 31457280 | tf_op jit(solution)/shard_map/attn_forward/pallas_call | solution.py:957
  172.3 86.8 %shard_map.257 = (f32[256,2048]{1,0:T(8,128)}, bf16[8,256,2048]{2,1,0:T(8,128)(2,1)}) custom-call(bf16[2048,512]{1,0:T(8,128)(2,1)} %get-tuple-element.71.attn_ref, bf16[512,2048]{1,0:T(8,128)(2,1)} %bitcast.121, bf16[256,2048]{1,0:T(8,128)(2,1)} %bitcast.114, f32[1,2048]{1,0:T(1,128)} %reshape.192.gain_ref), custom_call_target="tpu_custom_call" | custom-call | bytes 315000000 | tf_op jit(solution)/shard_map/pallas_call | solution.py:448
  259.2 32.6 %expert.3 = (bf16[2048,2048]{1,0:T(8,128)(2,1)}, bf16[2048,2048]{1,0:T(8,128)(2,1)}, bf16[4,1536,768]{2,1,0:T(8,128)(2,1)}) custom-call(s32[1]{0:T(128)} %bitcast.z_ref, bf16[2048,2048]{1,0:T(8,128)(2,1)} %bitcast.145, bf16[2048,2048]{1,0:T(8,128)(2,1)} %bitcast.142, f32[2048,1]{1,0:T(8,128)} %get-tuple-element.141.prob_ref, bf16[4,1536,256]{2,1,0:T(8,128)(2,1)} %bitcast.151), custom_call_target="tpu_custom_call" | custom-call | flops 19327352832 | bytes 41943040 | tf_op jit(solution)/shard_map/expert/pallas_call | solution.py:1323
  291.8 3.3 pack.3.rest_2_
  295.2 3.8 collective-permute-start
  298.9 2.2 collective-permute-start.1
  301.1 49.6 %collective-permute-done.rest_3_ = bf16[1536,768]{1,0:T(8,128)(2,1)S(1)} collective-permute-done((bf16[1536,768]{1,0:T(8,128)(2,1)}, bf16[1536,768]{1,0:T(8,128)(2,1)S(1)}, u32[]{:S(2)}, u32[]{:S(2)}) %collective-permute-start) | collective-permute-done | bytes 2359328 | tf_op jit(solution)/shard_map/ppermute | solution.py:1416
  350.7 5.2 collective-permute-start.2
  355.9 1.9 collective-permute-start.3
  357.9 46.8 %collective-permute-done.2.rest_5_ = bf16[1536,768]{1,0:T(8,128)(2,1)} collective-permute-done((bf16[1536,768]{1,0:T(8,128)(2,1)S(1)}, bf16[1536,768]{1,0:T(8,128)(2,1)}, u32[]{:S(2)}, u32[]{:S(2)}) %collective-permute-start.2) | collective-permute-done | bytes 2359328 | tf_op jit(solution)/shard_map/ppermute | solution.py:1416
  404.7 2.1 collective-permute-start.4
  406.8 3.5 collective-permute-done.3.rest_6_
  410.3 3.6 collective-permute-start.5
  413.9 55.3 %expert.4 = (bf16[2048,2048]{1,0:T(8,128)(2,1)}, bf16[2048,2048]{1,0:T(8,128)(2,1)}, bf16[4,1536,768]{2,1,0:T(8,128)(2,1)}) custom-call(s32[1]{0:T(128)} %bitcast.z_ref, bf16[2048,2048]{1,0:T(8,128)(2,1)} %bitcast.146, bf16[2048,2048]{1,0:T(8,128)(2,1)} %bitcast.143, f32[2048,1]{1,0:T(8,128)} %get-tuple-element.141.prob_ref, ...), custom_call_target="tpu_custom_call", output_to_operand_aliasing={{2}: (4, {})} | custom-call | flops 38654705664 | bytes 41943040 | tf_op jit(solution)/shard_map/expert/pallas_call | solution.py:1323
  469.2 76.0 %expert.5 = (bf16[2048,2048]{1,0:T(8,128)(2,1)}, bf16[2048,2048]{1,0:T(8,128)(2,1)}, bf16[4,1536,768]{2,1,0:T(8,128)(2,1)}) custom-call(s32[1]{0:T(128)} %bitcast.z_ref, bf16[2048,2048]{1,0:T(8,128)(2,1)} %bitcast.147, bf16[2048,2048]{1,0:T(8,128)(2,1)} %bitcast.144, f32[2048,1]{1,0:T(8,128)} %get-tuple-element.142.prob_ref, ...), custom_call_target="tpu_custom_call" | custom-call | flops 57982058496 | bytes 41943040 | tf_op jit(solution)/shard_map/expert/pallas_call | solution.py:1323
  545.2 83.6 %shard_map.258 = (f32[256,2048]{1,0:T(8,128)}, f32[8,2048]{1,0:T(8,128)}, bf16[8,256,2048]{2,1,0:T(8,128)(2,1)}) custom-call(bf16[8,256,2048]{2,1,0:T(8,128)(2,1)} %bitcast.118, f32[256,2048]{1,0:T(8,128)} %get-tuple-element.87.after_ref, bf16[256,2048]{1,0:T(8,128)(2,1)} %bitcast.120, f32[1,2048]{1,0:T(1,128)} %reshape.192.gain_ref), custom_call_target="tpu_custom_call" | custom-call | bytes 285000000 | tf_op jit(solution)/shard_map/pallas_call | solution.py:448
  628.8 9.1 convolution_convert_fusion.1
  637.9 71.6 %attn_backward.1 = (bf16[2048,640]{1,0:T(8,128)(2,1)}, f32[8,128]{1,0:T(8,128)}, bf16[4,128,2048]{2,1,0:T(8,128)(2,1)}, bf16[256,2048]{1,0:T(8,128)(2,1)}) custom-call(bf16[2048,2048]{1,0:T(8,128)(2,1)} %bitcast.149, bf16[512,2048]{1,0:T(8,128)(2,1)} %bitcast.122, bf16[2048,512]{1,0:T(8,128)(2,1)} %get-tuple-element.71.attn_ref, ...), custom_call_target="tpu_custom_call" | custom-call | flops 60000002048 | bytes 31457280 | tf_op jit(solution)/shard_map/attn_backward/pallas_call | solution.py:1164
  709.6 11.1 convolution_convert_fusion
  721.5 3.2 dynamic-slice_bitcast_fusion.2
  726.0 1.7 collective-permute-start.7
  727.7 1.8 dynamic-slice_bitcast_fusion
  730.7 1.8 collective-permute-start.11
  732.5 42.8 %collective-permute-done.6 = bf16[768,768]{1,0:T(8,128)(2,1)} collective-permute-done((bf16[768,768]{1,0:T(8,128)(2,1)}, bf16[768,768]{1,0:T(8,128)(2,1)}, u32[]{:S(2)}, u32[]{:S(2)}) %collective-permute-start.6) | collective-permute-done | bytes 1179680 | tf_op jit(solution)/shard_map/ppermute | solution.py:1437
  775.4 4.3 fusion.5
  779.7 4.4 collective-permute-start.8
  785.4 32.4 %collective-permute-done.10 = bf16[768,768]{1,0:T(8,128)(2,1)} collective-permute-done((bf16[768,768]{1,0:T(8,128)(2,1)S(1)}, bf16[768,768]{1,0:T(8,128)(2,1)}, u32[]{:S(2)}, u32[]{:S(2)}) %collective-permute-start.10) | collective-permute-done | bytes 1179680 | tf_op jit(solution)/shard_map/ppermute | solution.py:1437
  817.8 4.3 fusion.3
  822.0 4.5 collective-permute-start.14
  827.8 40.2 %collective-permute-done.8 = bf16[768,768]{1,0:T(8,128)(2,1)} collective-permute-done((bf16[768,768]{1,0:T(8,128)(2,1)}, bf16[768,768]{1,0:T(8,128)(2,1)}, u32[]{:S(2)}, u32[]{:S(2)}) %collective-permute-start.8) | collective-permute-done | bytes 1179680 | tf_op jit(solution)/shard_map/ppermute | solution.py:1437
  868.1 4.3 fusion.2
  872.4 4.4 collective-permute-start.12
  876.8 1.9 collective-permute-start.13
  878.7 28.5 %collective-permute-done.14 = bf16[768,768]{1,0:T(8,128)(2,1)} collective-permute-done((bf16[768,768]{1,0:T(8,128)(2,1)}, bf16[768,768]{1,0:T(8,128)(2,1)}, u32[]{:S(2)}, u32[]{:S(2)}) %collective-permute-start.14) | collective-permute-done | bytes 1179680 | tf_op jit(solution)/shard_map/ppermute | solution.py:1437
  907.2 4.3 fusion
  911.5 4.5 collective-permute-start.16
  916.0 2.5 collective-permute-start.17
  918.5 51.1 %shard_map.259 = (f32[256,2048]{1,0:T(8,128)}, f32[8,2048]{1,0:T(8,128)}) custom-call(bf16[2048,640]{1,0:T(8,128)(2,1)} %get-tuple-element.97.grad_ref, bf16[2048,640]{1,0:T(8,128)(2,1)} %all-gather.8.cloned.1.call-done.wqkv_ref, bf16[256,2048]{1,0:T(8,128)(2,1)} %bitcast.115, f32[256,2048]{1,0:T(8,128)} %get-tuple-element.98.mid_ref, ...), custom_call_target="tpu_custom_call" | custom-call | bytes 180000000 | tf_op jit(solution)/shard_map/pallas_call | solution.py:448
  973.2 38.0 %shard_map.260 = f32[8,128]{1,0:T(8,128)} custom-call(f32[8,4,8,128]{3,2,1,0:T(8,128)} %copy_bitcast_fusion.3.small_ref), custom_call_target="tpu_custom_call" | custom-call | bytes 30000000 | tf_op jit(solution)/shard_map/pallas_call | solution.py:448
  1013.9 2.1 convert_element_type.140
  1016.1 12.6 %shard_map.261 = (f32[64,4096]{1,0:T(8,128)}, f32[64,512]{1,0:T(8,128)}, f32[64,512]{1,0:T(8,128)}) custom-call(bf16[8,64,640]{2,1,0:T(8,128)(2,1)} %bitcast.127), custom_call_target="tpu_custom_call" | custom-call | bytes 30000000 | tf_op jit(solution)/shard_map/pallas_call | solution.py:448
  1028.7 65.4 %reduce-scatter.8.cloned.1.call-done.one_ref = bf16[1536,768]{1,0:T(8,128)(2,1)} async-done(((bf16[6144,768]{1,0:T(8,128)(2,1)}), bf16[1536,768]{1,0:T(8,128)(2,1)}) %reduce-scatter.8.cloned.1.call-update) | async-done | bytes 2359312 | tf_op jit(solution)/shard_map/reduce_scatter | solution.py:1565
  1094.1 9.3 unpack.1
  (126 shorter events, 36.1 us)
Async XLA Ops:
  7.2 2.1 copy-start
  7.2 3.0 copy-start.18
  7.2 3.0 copy-start.19
  7.2 3.0 copy-start.20
  7.2 3.0 copy-start.21
  7.2 123.3 %all-gather.10.cloned.1.call-start = ((), (), s32[]{:S(2)}) async-start(), calls=%async_computation.7 | async-start | bytes 2621440 | tf_op jit(solution)/shard_map/all_gather | solution.py:1491
  8.0 122.5 %all-gather.8.cloned.1.call-start = ((), (), s32[]{:S(2)}) async-start(), calls=%async_computation.3 | async-start | bytes 3276800 | tf_op jit(solution)/shard_map/all_gather | solution.py:1490
  8.0 19.3 %copy-start.4 = (bf16[2,768,512]{2,1,0:T(8,128)(2,1)S(1)}, bf16[2,768,512]{2,1,0:T(8,128)(2,1)}, u32[]{:S(2)}) copy-start(bf16[2,768,512]{2,1,0:T(8,128)(2,1)} %param.30) | copy-start | bytes 4718596
  11.8 16.8 %copy-start.5 = (bf16[2,512,768]{2,1,0:T(8,128)(2,1)S(1)}, bf16[2,512,768]{2,1,0:T(8,128)(2,1)}, u32[]{:S(2)}) copy-start(bf16[2,512,768]{2,1,0:T(8,128)(2,1)} %param.29) | copy-start | bytes 4718596
  27.3 231.9 %all-gather.12.cloned.1.call-start = ((), (), s32[]{:S(2)}) async-start(), calls=%async_computation.8 | async-start | bytes 3932160 | tf_op jit(solution)/shard_map/all_gather | solution.py:1545
  27.4 2.0 copy-start.6
  31.1 4.0 copy-start.11
  31.1 4.8 copy-start.17
  31.1 6.2 copy-start.15
  31.1 6.2 copy-start.16
  34.4 260.8 %all-gather.14.cloned.1.call-start = ((), (), s32[]{:S(2)}) async-start(), calls=%async_computation.9 | async-start | bytes 7864320 | tf_op jit(solution)/shard_map/all_gather | solution.py:1545
  35.0 979.0 %reduce-scatter.6.cloned.1.call-start = ((), (), s32[]{:S(2)}) async-start(), calls=%async_computation.5 | async-start | bytes 2621440 | tf_op jit(solution)/shard_map/reduce_scatter | solution.py:1598
  119.8 7.2 copy-start.14
  295.2 55.6 %collective-permute-start = (bf16[1536,768]{1,0:T(8,128)(2,1)}, bf16[1536,768]{1,0:T(8,128)(2,1)S(1)}, u32[]{:S(2)}, u32[]{:S(2)}) collective-permute-start(bf16[1536,768]{1,0:T(8,128)(2,1)} %pack.3.rest_2_), channel_id=1, source_target_pairs={{0,8},{8,16},{16,24},{1,9},{9,17},{17,25},{2,10},{10,18},{18,26},{... | collective-permute-start | bytes 7077896 | tf_op jit(solution)/shard_map/ppermute | solution.py:1416
  298.9 57.0 %collective-permute-start.1 = (bf16[1536,768]{1,0:T(8,128)(2,1)}, bf16[1536,768]{1,0:T(8,128)(2,1)S(1)}, u32[]{:S(2)}, u32[]{:S(2)}) collective-permute-start(bf16[1536,768]{1,0:T(8,128)(2,1)} %pack.3.rest_2_), channel_id=1, source_target_pairs={{8,0},{16,8},{24,16},{9,1},{17,9},{25,17},{10,2},{18,10},{26,18},{... | collective-permute-start | bytes 7077896 | tf_op jit(solution)/shard_map/ppermute | solution.py:1416
  350.7 118.5 %copy-start.22 = (bf16[1536,768]{1,0:T(8,128)(2,1)}, bf16[1536,768]{1,0:T(8,128)(2,1)S(1)}, u32[]{:S(2)}) copy-start(bf16[1536,768]{1,0:T(8,128)(2,1)S(1)} %collective-permute-done.rest_3_) | copy-start | bytes 7077892
  350.7 53.9 %collective-permute-start.2 = (bf16[1536,768]{1,0:T(8,128)(2,1)S(1)}, bf16[1536,768]{1,0:T(8,128)(2,1)}, u32[]{:S(2)}, u32[]{:S(2)}) collective-permute-start(bf16[1536,768]{1,0:T(8,128)(2,1)S(1)} %collective-permute-done.rest_3_), channel_id=1, source_target_pairs={{8,16},{16,24},{9,17},{17,25},{10,18},{18,26},{11,19},{19,27},{12,... | collective-permute-start | bytes 7077896 | tf_op jit(solution)/shard_map/ppermute | solution.py:1416
  355.9 48.8 %copy-start.23 = (bf16[1536,768]{1,0:T(8,128)(2,1)}, bf16[1536,768]{1,0:T(8,128)(2,1)S(1)}, u32[]{:S(2)}) copy-start(bf16[1536,768]{1,0:T(8,128)(2,1)S(1)} %collective-permute-done.1.rest_4_) | copy-start | bytes 7077892
  355.9 54.4 %collective-permute-start.3 = (bf16[1536,768]{1,0:T(8,128)(2,1)S(1)}, bf16[1536,768]{1,0:T(8,128)(2,1)}, u32[]{:S(2)}, u32[]{:S(2)}) collective-permute-start(bf16[1536,768]{1,0:T(8,128)(2,1)S(1)} %collective-permute-done.1.rest_4_), channel_id=1, source_target_pairs={{8,0},{16,8},{9,1},{17,9},{10,2},{18,10},{11,3},{19,11},{12,4},{20... | collective-permute-start | bytes 7077896 | tf_op jit(solution)/shard_map/ppermute | solution.py:1416
  404.7 64.5 %collective-permute-start.4 = (bf16[1536,768]{1,0:T(8,128)(2,1)}, bf16[1536,768]{1,0:T(8,128)(2,1)}, u32[]{:S(2)}, u32[]{:S(2)}) collective-permute-start(bf16[1536,768]{1,0:T(8,128)(2,1)} %collective-permute-done.2.rest_5_), channel_id=1, source_target_pairs={{16,24},{17,25},{18,26},{19,27},{20,28},{21,29},{22,30},{23,31}} | collective-permute-start | bytes 7077896 | tf_op jit(solution)/shard_map/ppermute | solution.py:1416
  410.3 58.9 %collective-permute-start.5 = (bf16[1536,768]{1,0:T(8,128)(2,1)}, bf16[1536,768]{1,0:T(8,128)(2,1)}, u32[]{:S(2)}, u32[]{:S(2)}) collective-permute-start(bf16[1536,768]{1,0:T(8,128)(2,1)} %collective-permute-done.3.rest_6_), channel_id=1, source_target_pairs={{8,0},{9,1},{10,2},{11,3},{12,4},{13,5},{14,6},{15,7}} | collective-permute-start | bytes 7077896 | tf_op jit(solution)/shard_map/ppermute | solution.py:1416
  545.2 83.6 %copy-start.2 = (bf16[2048,512]{1,0:T(8,128)(2,1)S(1)}, bf16[2048,512]{1,0:T(8,128)(2,1)}, u32[]{:S(2)}) copy-start(bf16[2048,512]{1,0:T(8,128)(2,1)} %get-tuple-element.71.attn_ref) | copy-start | bytes 6291460
  709.6 306.5 %reduce-scatter.4.cloned.1.call-start = ((), (), s32[]{:S(2)}) async-start(), calls=%async_computation.4 | async-start | bytes 3276800 | tf_op jit(solution)/shard_map/reduce_scatter | solution.py:1597
  720.7 373.4 %reduce-scatter.8.cloned.1.call-start = ((), (), s32[]{:S(2)}) async-start(), calls=%async_computation.6 | async-start | bytes 11796480 | tf_op jit(solution)/shard_map/reduce_scatter | solution.py:1565
  724.7 50.7 %collective-permute-start.6 = (bf16[768,768]{1,0:T(8,128)(2,1)}, bf16[768,768]{1,0:T(8,128)(2,1)}, u32[]{:S(2)}, u32[]{:S(2)}) collective-permute-start(bf16[768,768]{1,0:T(8,128)(2,1)} %get-tuple-element.134), channel_id=1, source_target_pairs={{0,8},{1,9},{2,10},{3,11},{4,12},{5,13},{6,14},{7,15}} | collective-permute-start | bytes 3538952 | tf_op jit(solution)/shard_map/ppermute | solution.py:1437
  726.0 49.4 %collective-permute-start.7 = (bf16[768,768]{1,0:T(8,128)(2,1)}, bf16[768,768]{1,0:T(8,128)(2,1)}, u32[]{:S(2)}, u32[]{:S(2)}) collective-permute-start(bf16[768,768]{1,0:T(8,128)(2,1)} %get-tuple-element.133), channel_id=1, source_target_pairs={{24,16},{25,17},{26,18},{27,19},{28,20},{29,21},{30,22},{31,23}} | collective-permute-start | bytes 3538952 | tf_op jit(solution)/shard_map/ppermute | solution.py:1437
  729.4 88.3 %collective-permute-start.10 = (bf16[768,768]{1,0:T(8,128)(2,1)S(1)}, bf16[768,768]{1,0:T(8,128)(2,1)}, u32[]{:S(2)}, u32[]{:S(2)}) collective-permute-start(bf16[768,768]{1,0:T(8,128)(2,1)S(1)} %get-tuple-element.132), channel_id=1, source_target_pairs={{0,8},{1,9},{2,10},{3,11},{4,12},{5,13},{6,14},{7,15}} | collective-permute-start | bytes 3538952 | tf_op jit(solution)/shard_map/ppermute | solution.py:1437
  730.7 87.0 %collective-permute-start.11 = (bf16[768,768]{1,0:T(8,128)(2,1)S(1)}, bf16[768,768]{1,0:T(8,128)(2,1)}, u32[]{:S(2)}, u32[]{:S(2)}) collective-permute-start(bf16[768,768]{1,0:T(8,128)(2,1)S(1)} %get-tuple-element.131), channel_id=1, source_target_pairs={{24,16},{25,17},{26,18},{27,19},{28,20},{29,21},{30,22},{31,23}} | collective-permute-start | bytes 3538952 | tf_op jit(solution)/shard_map/ppermute | solution.py:1437
  779.7 88.4 %collective-permute-start.8 = (bf16[768,768]{1,0:T(8,128)(2,1)}, bf16[768,768]{1,0:T(8,128)(2,1)}, u32[]{:S(2)}, u32[]{:S(2)}) collective-permute-start(bf16[768,768]{1,0:T(8,128)(2,1)} %get-tuple-element.130), channel_id=1, source_target_pairs={{0,8},{8,16},{1,9},{9,17},{2,10},{10,18},{3,11},{11,19},{4,12},{12... | collective-permute-start | bytes 3538952 | tf_op jit(solution)/shard_map/ppermute | solution.py:1437
  784.1 84.0 %collective-permute-start.9 = (bf16[768,768]{1,0:T(8,128)(2,1)}, bf16[768,768]{1,0:T(8,128)(2,1)}, u32[]{:S(2)}, u32[]{:S(2)}) collective-permute-start(bf16[768,768]{1,0:T(8,128)(2,1)} %get-tuple-element.129), channel_id=1, source_target_pairs={{16,8},{24,16},{17,9},{25,17},{18,10},{26,18},{19,11},{27,19},{20,... | collective-permute-start | bytes 3538952 | tf_op jit(solution)/shard_map/ppermute | solution.py:1437
  822.0 85.2 %collective-permute-start.14 = (bf16[768,768]{1,0:T(8,128)(2,1)}, bf16[768,768]{1,0:T(8,128)(2,1)}, u32[]{:S(2)}, u32[]{:S(2)}) collective-permute-start(bf16[768,768]{1,0:T(8,128)(2,1)} %get-tuple-element.128), channel_id=1, source_target_pairs={{0,8},{8,16},{1,9},{9,17},{2,10},{10,18},{3,11},{11,19},{4,12},{12... | collective-permute-start | bytes 3538952 | tf_op jit(solution)/shard_map/ppermute | solution.py:1437
  826.5 80.7 %collective-permute-start.15 = (bf16[768,768]{1,0:T(8,128)(2,1)}, bf16[768,768]{1,0:T(8,128)(2,1)}, u32[]{:S(2)}, u32[]{:S(2)}) collective-permute-start(bf16[768,768]{1,0:T(8,128)(2,1)} %get-tuple-element.127), channel_id=1, source_target_pairs={{16,8},{24,16},{17,9},{25,17},{18,10},{26,18},{19,11},{27,19},{20,... | collective-permute-start | bytes 3538952 | tf_op jit(solution)/shard_map/ppermute | solution.py:1437
  872.4 156.3 %collective-permute-start.12 = (bf16[768,768]{1,0:T(8,128)(2,1)}, bf16[768,768]{1,0:T(8,128)(2,1)S(1)}, u32[]{:S(2)}, u32[]{:S(2)}) collective-permute-start(bf16[768,768]{1,0:T(8,128)(2,1)} %get-tuple-element.126), channel_id=1, source_target_pairs={{0,8},{8,16},{16,24},{1,9},{9,17},{17,25},{2,10},{10,18},{18,26},{... | collective-permute-start | bytes 3538952 | tf_op jit(solution)/shard_map/ppermute | solution.py:1437
  876.8 151.9 %collective-permute-start.13 = (bf16[768,768]{1,0:T(8,128)(2,1)}, bf16[768,768]{1,0:T(8,128)(2,1)S(1)}, u32[]{:S(2)}, u32[]{:S(2)}) collective-permute-start(bf16[768,768]{1,0:T(8,128)(2,1)} %get-tuple-element.125), channel_id=1, source_target_pairs={{8,0},{16,8},{24,16},{9,1},{17,9},{25,17},{10,2},{18,10},{26,18},{... | collective-permute-start | bytes 3538952 | tf_op jit(solution)/shard_map/ppermute | solution.py:1437
  911.5 117.2 %collective-permute-start.16 = (bf16[768,768]{1,0:T(8,128)(2,1)}, bf16[768,768]{1,0:T(8,128)(2,1)}, u32[]{:S(2)}, u32[]{:S(2)}) collective-permute-start(bf16[768,768]{1,0:T(8,128)(2,1)} %get-tuple-element.124), channel_id=1, source_target_pairs={{0,8},{8,16},{16,24},{1,9},{9,17},{17,25},{2,10},{10,18},{18,26},{... | collective-permute-start | bytes 3538952 | tf_op jit(solution)/shard_map/ppermute | solution.py:1437
  916.0 112.7 %collective-permute-start.17 = (bf16[768,768]{1,0:T(8,128)(2,1)}, bf16[768,768]{1,0:T(8,128)(2,1)}, u32[]{:S(2)}, u32[]{:S(2)}) collective-permute-start(bf16[768,768]{1,0:T(8,128)(2,1)} %get-tuple-element.123), channel_id=1, source_target_pairs={{8,0},{16,8},{24,16},{9,1},{17,9},{25,17},{10,2},{18,10},{26,18},{... | collective-permute-start | bytes 3538952 | tf_op jit(solution)/shard_map/ppermute | solution.py:1437
  1028.6 74.8 %copy-start.9 = (bf16[256,2048]{1,0:T(8,128)(2,1)S(1)}, bf16[256,2048]{1,0:T(8,128)(2,1)}, u32[]{:S(2)}) copy-start(bf16[256,2048]{1,0:T(8,128)(2,1)} %get-tuple-element.96) | copy-start | bytes 3145732
  1028.7 65.5 %copy-start.7 = (bf16[768,768]{1,0:T(8,128)(2,1)}, bf16[768,768]{1,0:T(8,128)(2,1)S(1)}, u32[]{:S(2)}) copy-start(bf16[768,768]{1,0:T(8,128)(2,1)S(1)} %collective-permute-done.12.up0_ref) | copy-start | bytes 3538948
  1028.7 65.5 %copy-start.8 = (bf16[768,768]{1,0:T(8,128)(2,1)}, bf16[768,768]{1,0:T(8,128)(2,1)S(1)}, u32[]{:S(2)}) copy-start(bf16[768,768]{1,0:T(8,128)(2,1)S(1)} %collective-permute-done.13.down0_ref) | copy-start | bytes 3538948
  1103.4 2.0 copy-start.3
  1105.4 2.0 copy-start.10
  1105.4 4.3 copy-start.1
  1107.4 1.7 copy-start.12
  (1 other events, 1.0 us)
Sparse Core Ops, SparseCore 0:
  9.6 46.7 all-gather.9
  58.0 54.5 all-gather.7
  114.7 61.7 all-gather.11
  178.5 113.3 all-gather.13
  709.7 58.9 reduce-scatter.5
  771.4 94.0 reduce-scatter.3
  867.9 226.2 reduce-scatter.7

commit v10 on v9

--- a/solution.py
+++ b/solution.py
@@ -505,8 +505,45 @@
     meet([("ctx", flip(me, s, n)) for s in range(1, n)])
 
 
-def prep_kernel(n, n_dp, cols_ref, small_ref, out_ref, all_ref, *sems):
-    send, recv, local, gsend, grecv, zsend, zrecv = sems
+class Pack:
+    def __init__(self, e, sources, buffers, sems):
+        self.buffers = buffers
+        self.loads = [
+            pltpu.make_async_copy(source.at[e], buffer, sems.at[k])
+            for k, (source, buffer) in enumerate(zip(sources, buffers))
+        ]
+
+    def start(self):
+        for load in self.loads:
+            load.start()
+
+    def write(self, cuts, outs):
+        for load in self.loads:
+            load.wait()
+        gate, up, down = self.buffers
+        cut = gate.shape[0]
+        for (low, high), out in zip(cuts, outs):
+            out[:cut, :] = gate[:, low:high]
+            out[cut : 2 * cut, :] = up[:, low:high]
+            out[2 * cut :, :] = jnp.transpose(down[low:high, :].astype(F32)).astype(BF16)
+
+
+def pack_scratch(weights):
+    return [pltpu.VMEM(w.shape[1:], BF16) for w in weights] + [DMA((3,))]
+
+
+def pack_shapes(cuts, weights):
+    cut = weights[0].shape[1]
+    return [jax.ShapeDtypeStruct((3 * cut, high - low), BF16) for low, high in cuts]
+
+
+def prep_kernel(n, n_dp, cuts, cols_ref, small_ref, *rest):
+    sources, rest = rest[:3], rest[3:]
+    out_ref, all_ref, rest = rest[0], rest[1], rest[2:]
+    packed, rest = rest[: len(cuts)], rest[len(cuts) :]
+    pack = Pack(0, sources, rest[:3], rest[3])
+    pack.start()
+    send, recv, local, gsend, grecv, zsend, zrecv = rest[4:]
     me, row = lax.axis_index("ctx"), lax.axis_index("dp")
     meet(
         [("ctx", flip(me, s, n)) for s in range(1, n)]
@@ -519,6 +556,7 @@
         smalls.append(push(small_ref, all_ref.at[row, me], gsend.at[s], grecv.at[s], "ctx", peer))
         smalls[-1].start()
     own, copies = swap_all(n, cols_ref, out_ref, send, recv, local)
+    pack.write(cuts, packed)
     for copy in smalls:
         copy.wait_recv()
     planes = []
@@ -593,18 +631,20 @@
     return [DMA((n,)), DMA((n,)), DMA(()), DMA((n,)), DMA((n,)), DMA((n_dp,)), DMA((n_dp,))]
 
 
-def prep(n, n_dp, cols, small):
+def prep(n, n_dp, cols, small, cuts, weights):
     shape = jax.ShapeDtypeStruct
     return comm_call(
-        functools.partial(prep_kernel, n, n_dp),
+        functools.partial(prep_kernel, n, n_dp, cuts),
         0,
-        [shape(cols.shape, cols.dtype), shape((n_dp, n) + small.shape, F32)],
-        [ANY, VM],
-        [ANY, VM],
-        swap_sems(n, n_dp),
+        [shape(cols.shape, cols.dtype), shape((n_dp, n) + small.shape, F32)]
+        + pack_shapes(cuts, weights),
+        [ANY, VM] + [VM] * len(cuts),
+        [ANY, VM, ANY, ANY, ANY],
+        pack_scratch(weights) + swap_sems(n, n_dp),
         8,
         cols,
         small,
+        *weights,
     )
 
 
@@ -628,8 +668,14 @@
 
 
 def first_kernel(
-    n, x_ref, gain_ref, info_ref, grad_ref, nall_ref, iall_ref, gall_ref, low, *sems
+    n, cuts, x_ref, gain_ref, info_ref, grad_ref, *rest
 ):
+    sources, rest = rest[:3], rest[3:]
+    nall_ref, iall_ref, gall_ref, rest = rest[0], rest[1], rest[2], rest[3:]
+    packed, rest = rest[: len(cuts)], rest[len(cuts) :]
+    pack = Pack(1, sources, rest[:3], rest[3])
+    low, sems = rest[4], rest[5:]
+    pack.start()
     plane = Plane(n)
     plane.meet()
     infos = Gather(plane, info_ref, iall_ref, *sems[0:3])
@@ -644,6 +690,7 @@
     normed.start()
     grads = gather_of(plane, grad_ref, gall_ref, *sems[6:9])
     grads.start()
+    pack.write(cuts, packed)
     infos.forward()
     normed.forward()
     grads.forward()
@@ -652,16 +699,17 @@
     grads.finish()
 
 
-def first(n, x, gain, info, grad):
+def first(n, x, gain, info, grad, cuts, weights):
     shape = jax.ShapeDtypeStruct
     many = lambda array, kind: shape((n,) + array.shape, kind)
     return comm_call(
-        functools.partial(first_kernel, n),
+        functools.partial(first_kernel, n, cuts),
         2,
-        [many(x, BF16), many(info, F32), many(grad, BF16)],
-        [ANY] * 3,
-        [VM] * 4,
-        [pltpu.VMEM(x.shape, BF16)]
+        [many(x, BF16), many(info, F32), many(grad, BF16)] + pack_shapes(cuts, weights),
+        [ANY] * 3 + [VM] * len(cuts),
+        [VM] * 4 + [ANY] * 3,
+        pack_scratch(weights)
+        + [pltpu.VMEM(x.shape, BF16)]
         + [DMA((n,)), DMA((n,)), DMA(())]
         + gather_sems(n)
         + gather_sems(n),
@@ -670,6 +718,7 @@
         gain,
         info,
         grad,
+        *weights,
     )
 
 
@@ -1347,25 +1396,6 @@
     )(z, n2, top, prob, *grads, *before, *[entry[0] for entry in sources])
 
 
-def pack_kernel(cuts, gate_ref, up_ref, down_ref, *outs):
-    cut = gate_ref.shape[0]
-    for (low, high), out in zip(cuts, outs):
-        out[:cut, :] = gate_ref[:, low:high]
-        out[cut : 2 * cut, :] = up_ref[:, low:high]
-        out[2 * cut :, :] = jnp.transpose(down_ref[low:high, :].astype(F32)).astype(BF16)
-
-
-def pack(cuts, w_gate, w_up, w_down):
-    cut = w_gate.shape[0]
-    return pl.pallas_call(
-        functools.partial(pack_kernel, cuts),
-        in_specs=[VM] * 3,
-        out_specs=[VM] * len(cuts),
-        out_shape=[jax.ShapeDtypeStruct((3 * cut, high - low), BF16) for low, high in cuts],
-        name="pack",
-    )(w_gate, w_up, w_down)
-
-
 def unpack_kernel(
     z_ref, one_ref, all_ref, up0_ref, down0_ref, up1_ref, down1_ref, dg_ref, du_ref, dd_ref, own, sem
 ):
@@ -1481,7 +1511,11 @@
     cols = jnp.concatenate(
         [w_query.reshape(depth, n_ctx, qw), jnp.where(even, wide[0], wide[1])], axis=2
     ).transpose(1, 0, 2)
-    cols, small = prep(n_ctx, n_dp, cols, small)
+    hidden = w_gate.shape[2]
+    cuts = ((0, 256), (256, hidden))
+    cols, small, *blocks0 = prep(
+        n_ctx, n_dp, cols, small, cuts, (w_gate, w_up, w_down)
+    )
     small = small.reshape(n_dp * n_ctx, 1024)
     gain_attn = small[:, :cut].reshape(1, width)
     gain_ffn = small[:, cut : 2 * cut].reshape(1, width)
@@ -1498,7 +1532,9 @@
     info = jnp.concatenate(
         [probs, doc_ids.reshape(1, tokens).astype(F32), jnp.zeros((7, tokens), F32)], axis=0
     )
-    normed, info, top_all = first(n_ctx, inputs, gain_attn, info, top_own)
+    normed, info, top_all, block1 = first(
+        n_ctx, inputs, gain_attn, info, top_own, ((0, hidden),), (w_gate, w_up, w_down)
+    )
     normed = normed.reshape(length, width)
     doc = info[:, n_experts].reshape(length).astype(jnp.int32)
     my_probs = lax.dynamic_slice_in_dim(info, ctx_index * own_e, own_e, 1)
@@ -1538,14 +1574,10 @@
         )
         return (moe, rows_grad), grads
 
-    cuts = [(0, 256), (256, hidden)]
-    blocks0 = pack(cuts, w_gate[0], w_up[0], w_down[0])
     carried, grads0 = (), ()
     for index, (low, high) in enumerate(cuts):
         full = lax.all_gather(blocks0[index], "dp", axis=0, tiled=False)
         if index == 1:
-            later = lax.optimization_barrier((w_gate[1], w_up[1], w_down[1], *carried))[:3]
-            (block1,) = pack([(0, hidden)], *later)
             sources1 = [(block1, "up", 0, 0)]
             up = down = after_of(block1, full)
             up, down = line_hop(up, down, n_dp, 1)

time: 1130 us -> 1180 us (1.044)
  waiting for transfers between devices: 311 us -> 371 us
    all_gather x1, waiting for transfers between devices: 0.01 us -> 56.9 us  [per_device(): lax.all_gather(cols.reshape(n_ctx * depth, qw + HD), 'dp', axis=0, tiled=...]
    all_gather x2, waiting for transfers between devices: 0.02 us -> 30.7 us  [per_device(): full = lax.all_gather(blocks0[index], 'dp', axis=0, tiled=False)]
    ppermute x3, waiting for transfers between devices: 96.4 us -> 70.2 us  [line_hop(): lax.ppermute(block_up, 'dp', up)]
  transfers between devices with their start and end apart: 25 -> 25, of which waited for: 8 -> 8; matrix products, arithmetic and copies ran while one was open for 6% -> 5% of each run, Pallas kernels for 38% -> 34%
where the time goes in v10:
time: 1180 us; the launch traced here: 1170 us
  Pallas kernels  653 us (55%)
  waiting for transfers between devices  371 us (31%)
  starting transfers between devices  51.2 us (4%)
  other arithmetic  28.4 us (2%)
  local copies, waits for them, and re-layouts  28 us (2%)
  matrix products  20.2 us (2%)
  between operations  15.3 us (1%)
    pallas_call x7, Pallas kernels, comm_call(): pl.pallas_call(kernel, out_shape=outs, in_specs=in_specs, out_specs=out_s...  368 us
    pallas_call x3, Pallas kernels, expert(): pl.pallas_call(functools.partial(expert_kernel, len(before) > 0, low, len...  164 us
    ppermute x6, waiting for transfers between devices, reduce_hop(): lax.ppermute(blocks[0], 'dp', up)  146 us
    pallas_call x1, Pallas kernels, attn_backward(): pl.pallas_call(functools.partial(attn_backward_kernel, n, n_dp, heads, MO...  71.3 us
    ppermute x3, waiting for transfers between devices, line_hop(): lax.ppermute(block_up, 'dp', up)  70.2 us
    reduce_scatter x1, waiting for transfers between devices, per_device(): lax.psum_scatter(grads1.reshape(3 * width, hidden), 'dp', scatter_dimensi...  65.3 us
    all_gather x1, waiting for transfers between devices, per_device(): lax.all_gather(cols.reshape(n_ctx * depth, qw + HD), 'dp', axis=0, tiled=...  56.9 us
    pallas_call x1, Pallas kernels, attn_forward(): pl.pallas_call(functools.partial(attn_forward_kernel, n, n_dp, heads, MOS...  41 us
  transfers between devices with their start and end apart: 25, of which 8 were waited for; matrix products, arithmetic and copies ran while one was open for 5% of the time, Pallas kernels for 34%

profile of v10, /device:TPU:14, one launch (start us, length us, event | category | flops | bytes accessed | tf_op | source)
XLA Modules:
  0.0 1167.0 jit_solution(12050556994319084971)
XLA Ops:
  10.9 13.7 %shard_map.255 = (bf16[8,64,640]{2,1,0:T(8,128)(2,1)}, f32[4,8,8,128]{3,2,1,0:T(8,128)}, bf16[1536,256]{1,0:T(8,128)(2,1)}, bf16[1536,512]{1,0:T(8,128)(2,1)}) custom-call(bf16[8,64,640]{2,1,0:T(8,128)(2,1)} %maximum_bitcast_fusion.cols_ref, f32[8,128]{1,0:T(8,128)} %fusion.19.small_ref, bf16[2,512,768]{2,1,0:T(8,128)(2,1)} %rest_0_.3, ...), custom_call_target="tpu_custom_call" | custom-call | bytes 24000000 | tf_op jit(solution)/shard_map/pallas_call | solution.py:448
  27.9 80.1 %shard_map.256 = (bf16[8,256,2048]{2,1,0:T(8,128)(2,1)}, f32[8,24,256]{2,1,0:T(8,128)}, bf16[8,256,2048]{2,1,0:T(8,128)(2,1)}, bf16[1536,768]{1,0:T(8,128)(2,1)}) custom-call(bf16[256,2048]{1,0:T(8,128)(2,1)} %bitcast.101, f32[1,2048]{1,0:T(1,128)} %reshape.185.gain_ref, f32[24,256]{1,0:T(8,128)} %maximum_maximum_fusion.info_ref, ...), custom_call_target="tpu_custom_call" | custom-call | bytes 270000000 | tf_op jit(solution)/shard_map/pallas_call | solution.py:448
  108.0 30.6 %all-gather.14.cloned.1.call-done = bf16[6144,512]{1,0:T(8,128)(2,1)} async-done(((bf16[1536,512]{1,0:T(8,128)(2,1)}), bf16[6144,512]{1,0:T(8,128)(2,1)}) %all-gather.14.cloned.1.call-update) | async-done | bytes 6291472 | tf_op jit(solution)/shard_map/all_gather | solution.py:1579
  138.7 4.4 collective-permute-start
  143.0 2.3 collective-permute-start.1
  147.6 1.3 copy.47.docc_ref
  150.8 3.9 fusion.10
  154.7 1.9 pad_maximum_fusion
  156.7 1.6 fusion.21
  158.3 70.2 %collective-permute-done.rest_3_ = bf16[1536,768]{1,0:T(8,128)(2,1)S(1)} collective-permute-done((bf16[1536,768]{1,0:T(8,128)(2,1)}, bf16[1536,768]{1,0:T(8,128)(2,1)S(1)}, u32[]{:S(2)}, u32[]{:S(2)}) %collective-permute-start) | collective-permute-done | bytes 2359328 | tf_op jit(solution)/shard_map/ppermute | solution.py:1446
  228.5 4.6 collective-permute-start.2
  233.1 2.4 collective-permute-start.3
  235.6 56.9 %all-gather.8.cloned.1.call-done.wqkv_ref = bf16[2048,640]{1,0:T(8,128)(2,1)} async-done(((bf16[512,640]{1,0:T(8,128)(2,1)}), bf16[2048,640]{1,0:T(8,128)(2,1)}) %all-gather.8.cloned.1.call-update) | async-done | bytes 2621456 | tf_op jit(solution)/shard_map/all_gather | solution.py:1524
  292.5 41.0 %attn_forward.1 = (f32[2048,512]{1,0:T(8,128)}, f32[2048,128]{1,0:T(8,128)}, bf16[2048,512]{1,0:T(8,128)(2,1)}, bf16[2048,128]{1,0:T(8,128)(2,1)}, bf16[2048,128...) custom-call(bf16[2048,2048]{1,0:T(8,128)(2,1)} %bitcast.128, ...), custom_call_target="tpu_custom_call" | custom-call | flops 35000000512 | bytes 31457280 | tf_op jit(solution)/shard_map/attn_forward/pallas_call | solution.py:1006
  333.4 87.7 %shard_map.257 = (f32[256,2048]{1,0:T(8,128)}, bf16[8,256,2048]{2,1,0:T(8,128)(2,1)}) custom-call(bf16[2048,512]{1,0:T(8,128)(2,1)} %get-tuple-element.69.attn_ref, bf16[512,2048]{1,0:T(8,128)(2,1)} %bitcast.109, bf16[256,2048]{1,0:T(8,128)(2,1)} %bitcast.102, f32[1,2048]{1,0:T(1,128)} %reshape.192.gain_ref), custom_call_target="tpu_custom_call" | custom-call | bytes 315000000 | tf_op jit(solution)/shard_map/pallas_call | solution.py:448
  421.2 32.5 %expert.3 = (bf16[2048,2048]{1,0:T(8,128)(2,1)}, bf16[2048,2048]{1,0:T(8,128)(2,1)}, bf16[4,1536,768]{2,1,0:T(8,128)(2,1)}) custom-call(s32[1]{0:T(128)} %bitcast.z_ref, bf16[2048,2048]{1,0:T(8,128)(2,1)} %bitcast.133, bf16[2048,2048]{1,0:T(8,128)(2,1)} %bitcast.130, f32[2048,1]{1,0:T(8,128)} %get-tuple-element.131.prob_ref, bf16[4,1536,256]{2,1,0:T(8,128)(2,1)} %bitcast.139), custom_call_target="tpu_custom_call" | custom-call | flops 19327352832 | bytes 41943040 | tf_op jit(solution)/shard_map/expert/pallas_call | solution.py:1372
  454.5 5.6 collective-permute-start.5
  460.2 55.3 %expert.4 = (bf16[2048,2048]{1,0:T(8,128)(2,1)}, bf16[2048,2048]{1,0:T(8,128)(2,1)}, bf16[4,1536,768]{2,1,0:T(8,128)(2,1)}) custom-call(s32[1]{0:T(128)} %bitcast.z_ref, bf16[2048,2048]{1,0:T(8,128)(2,1)} %bitcast.134, bf16[2048,2048]{1,0:T(8,128)(2,1)} %bitcast.131, f32[2048,1]{1,0:T(8,128)} %get-tuple-element.131.prob_ref, ...), custom_call_target="tpu_custom_call", output_to_operand_aliasing={{2}: (4, {})} | custom-call | flops 38654705664 | bytes 41943040 | tf_op jit(solution)/shard_map/expert/pallas_call | solution.py:1372
  515.5 1.4 copy-done.20
  516.9 76.0 %expert.5 = (bf16[2048,2048]{1,0:T(8,128)(2,1)}, bf16[2048,2048]{1,0:T(8,128)(2,1)}, bf16[4,1536,768]{2,1,0:T(8,128)(2,1)}) custom-call(s32[1]{0:T(128)} %bitcast.z_ref, bf16[2048,2048]{1,0:T(8,128)(2,1)} %bitcast.135, bf16[2048,2048]{1,0:T(8,128)(2,1)} %bitcast.132, f32[2048,1]{1,0:T(8,128)} %get-tuple-element.132.prob_ref, ...), custom_call_target="tpu_custom_call" | custom-call | flops 57982058496 | bytes 41943040 | tf_op jit(solution)/shard_map/expert/pallas_call | solution.py:1372
  592.9 84.5 %shard_map.258 = (f32[256,2048]{1,0:T(8,128)}, f32[8,2048]{1,0:T(8,128)}, bf16[8,256,2048]{2,1,0:T(8,128)(2,1)}) custom-call(bf16[8,256,2048]{2,1,0:T(8,128)(2,1)} %bitcast.106, f32[256,2048]{1,0:T(8,128)} %get-tuple-element.83.after_ref, bf16[256,2048]{1,0:T(8,128)(2,1)} %bitcast.108, f32[1,2048]{1,0:T(1,128)} %reshape.192.gain_ref), custom_call_target="tpu_custom_call" | custom-call | bytes 285000000 | tf_op jit(solution)/shard_map/pallas_call | solution.py:448
  677.4 9.1 convolution_convert_fusion.1
  686.6 71.3 %attn_backward.1 = (bf16[2048,640]{1,0:T(8,128)(2,1)}, f32[8,128]{1,0:T(8,128)}, bf16[4,128,2048]{2,1,0:T(8,128)(2,1)}, bf16[256,2048]{1,0:T(8,128)(2,1)}) custom-call(bf16[2048,2048]{1,0:T(8,128)(2,1)} %bitcast.137, bf16[512,2048]{1,0:T(8,128)(2,1)} %bitcast.110, bf16[2048,512]{1,0:T(8,128)(2,1)} %get-tuple-element.69.attn_ref, ...), custom_call_target="tpu_custom_call" | custom-call | flops 60000002048 | bytes 31457280 | tf_op jit(solution)/shard_map/attn_backward/pallas_call | solution.py:1213
  758.0 11.1 convolution_convert_fusion
  769.8 3.2 dynamic-slice_bitcast_fusion.2
  774.3 1.7 collective-permute-start.7
  776.0 1.8 dynamic-slice_bitcast_fusion
  779.1 1.8 collective-permute-start.11
  780.9 44.4 %collective-permute-done.6 = bf16[768,768]{1,0:T(8,128)(2,1)} collective-permute-done((bf16[768,768]{1,0:T(8,128)(2,1)}, bf16[768,768]{1,0:T(8,128)(2,1)}, u32[]{:S(2)}, u32[]{:S(2)}) %collective-permute-start.6) | collective-permute-done | bytes 1179680 | tf_op jit(solution)/shard_map/ppermute | solution.py:1467
  825.3 4.3 fusion.5
  829.6 4.4 collective-permute-start.8
  835.3 32.4 %collective-permute-done.10 = bf16[768,768]{1,0:T(8,128)(2,1)} collective-permute-done((bf16[768,768]{1,0:T(8,128)(2,1)S(1)}, bf16[768,768]{1,0:T(8,128)(2,1)}, u32[]{:S(2)}, u32[]{:S(2)}) %collective-permute-start.10) | collective-permute-done | bytes 1179680 | tf_op jit(solution)/shard_map/ppermute | solution.py:1467
  867.7 4.3 fusion.3
  872.0 4.5 collective-permute-start.14
  877.8 40.2 %collective-permute-done.8 = bf16[768,768]{1,0:T(8,128)(2,1)} collective-permute-done((bf16[768,768]{1,0:T(8,128)(2,1)}, bf16[768,768]{1,0:T(8,128)(2,1)}, u32[]{:S(2)}, u32[]{:S(2)}) %collective-permute-start.8) | collective-permute-done | bytes 1179680 | tf_op jit(solution)/shard_map/ppermute | solution.py:1467
  918.0 4.3 fusion.2
  922.3 4.4 collective-permute-start.12
  926.8 1.9 collective-permute-start.13
  928.7 28.5 %collective-permute-done.14 = bf16[768,768]{1,0:T(8,128)(2,1)} collective-permute-done((bf16[768,768]{1,0:T(8,128)(2,1)}, bf16[768,768]{1,0:T(8,128)(2,1)}, u32[]{:S(2)}, u32[]{:S(2)}) %collective-permute-start.14) | collective-permute-done | bytes 1179680 | tf_op jit(solution)/shard_map/ppermute | solution.py:1467
  957.2 4.3 fusion
  961.5 4.5 collective-permute-start.16
  966.0 2.5 collective-permute-start.17
  968.5 51.3 %shard_map.259 = (f32[256,2048]{1,0:T(8,128)}, f32[8,2048]{1,0:T(8,128)}) custom-call(bf16[2048,640]{1,0:T(8,128)(2,1)} %get-tuple-element.93.grad_ref, bf16[2048,640]{1,0:T(8,128)(2,1)} %all-gather.8.cloned.1.call-done.wqkv_ref, bf16[256,2048]{1,0:T(8,128)(2,1)} %bitcast.103, f32[256,2048]{1,0:T(8,128)} %get-tuple-element.94.mid_ref, ...), custom_call_target="tpu_custom_call" | custom-call | bytes 180000000 | tf_op jit(solution)/shard_map/pallas_call | solution.py:448
  1023.4 37.9 %shard_map.260 = f32[8,128]{1,0:T(8,128)} custom-call(f32[8,4,8,128]{3,2,1,0:T(8,128)} %copy_bitcast_fusion.3.small_ref), custom_call_target="tpu_custom_call" | custom-call | bytes 30000000 | tf_op jit(solution)/shard_map/pallas_call | solution.py:448
  1064.0 2.1 convert_element_type.140
  1066.1 12.7 %shard_map.261 = (f32[64,4096]{1,0:T(8,128)}, f32[64,512]{1,0:T(8,128)}, f32[64,512]{1,0:T(8,128)}) custom-call(bf16[8,64,640]{2,1,0:T(8,128)(2,1)} %bitcast.115), custom_call_target="tpu_custom_call" | custom-call | bytes 30000000 | tf_op jit(solution)/shard_map/pallas_call | solution.py:448
  1078.8 65.3 %reduce-scatter.8.cloned.1.call-done.one_ref = bf16[1536,768]{1,0:T(8,128)(2,1)} async-done(((bf16[6144,768]{1,0:T(8,128)(2,1)}), bf16[1536,768]{1,0:T(8,128)(2,1)}) %reduce-scatter.8.cloned.1.call-update) | async-done | bytes 2359312 | tf_op jit(solution)/shard_map/reduce_scatter | solution.py:1597
  1144.1 9.3 unpack.1
  (116 shorter events, 30.3 us)
Async XLA Ops:
  7.2 1.2 copy-start
  7.2 3.1 copy-start.15
  7.2 3.1 copy-start.16
  7.2 3.0 copy-start.17
  7.2 3.0 copy-start.18
  7.2 131.4 %all-gather.14.cloned.1.call-start = ((), (), s32[]{:S(2)}) async-start(), calls=%async_computation.9 | async-start | bytes 7864320 | tf_op jit(solution)/shard_map/all_gather | solution.py:1579
  24.7 1.6 copy-start.10
  24.7 2.4 copy-start.14
  24.7 2.5 copy-start.12
  24.7 2.5 copy-start.13
  24.8 210.8 %all-gather.10.cloned.1.call-start = ((), (), s32[]{:S(2)}) async-start(), calls=%async_computation.7 | async-start | bytes 2621440 | tf_op jit(solution)/shard_map/all_gather | solution.py:1525
  25.5 267.0 %all-gather.8.cloned.1.call-start = ((), (), s32[]{:S(2)}) async-start(), calls=%async_computation.3 | async-start | bytes 3276800 | tf_op jit(solution)/shard_map/all_gather | solution.py:1524
  26.2 394.9 %all-gather.12.cloned.1.call-start = ((), (), s32[]{:S(2)}) async-start(), calls=%async_computation.8 | async-start | bytes 3932160 | tf_op jit(solution)/shard_map/all_gather | solution.py:1579
  138.7 89.9 %collective-permute-start = (bf16[1536,768]{1,0:T(8,128)(2,1)}, bf16[1536,768]{1,0:T(8,128)(2,1)S(1)}, u32[]{:S(2)}, u32[]{:S(2)}) collective-permute-start(bf16[1536,768]{1,0:T(8,128)(2,1)} %get-tuple-element.81.rest_2_), channel_id=1, source_target_pairs={{0,8},{8,16},{16,24},{1,9},{9,17},{17,25},{2,10},{10,18},{18,26},{... | collective-permute-start | bytes 7077896 | tf_op jit(solution)/shard_map/ppermute | solution.py:1446
  143.0 90.1 %collective-permute-start.1 = (bf16[1536,768]{1,0:T(8,128)(2,1)}, bf16[1536,768]{1,0:T(8,128)(2,1)}, u32[]{:S(2)}, u32[]{:S(2)}) collective-permute-start(bf16[1536,768]{1,0:T(8,128)(2,1)} %get-tuple-element.81.rest_2_), channel_id=1, source_target_pairs={{8,0},{16,8},{24,16},{9,1},{17,9},{25,17},{10,2},{18,10},{26,18},{... | collective-permute-start | bytes 7077896 | tf_op jit(solution)/shard_map/ppermute | solution.py:1446
  145.3 918.6 %reduce-scatter.6.cloned.1.call-start = ((), (), s32[]{:S(2)}) async-start(), calls=%async_computation.5 | async-start | bytes 2621440 | tf_op jit(solution)/shard_map/reduce_scatter | solution.py:1630
  147.5 7.2 copy-start.11
  228.5 104.9 %copy-start.19 = (bf16[1536,768]{1,0:T(8,128)(2,1)}, bf16[1536,768]{1,0:T(8,128)(2,1)S(1)}, u32[]{:S(2)}) copy-start(bf16[1536,768]{1,0:T(8,128)(2,1)S(1)} %collective-permute-done.rest_3_) | copy-start | bytes 7077892
  228.5 225.2 %collective-permute-start.2 = (bf16[1536,768]{1,0:T(8,128)(2,1)S(1)}, bf16[1536,768]{1,0:T(8,128)(2,1)}, u32[]{:S(2)}, u32[]{:S(2)}) collective-permute-start(bf16[1536,768]{1,0:T(8,128)(2,1)S(1)} %collective-permute-done.rest_3_), channel_id=1, source_target_pairs={{8,16},{16,24},{9,17},{17,25},{10,18},{18,26},{11,19},{19,27},{12,... | collective-permute-start | bytes 7077896 | tf_op jit(solution)/shard_map/ppermute | solution.py:1446
  233.1 221.4 %collective-permute-start.3 = (bf16[1536,768]{1,0:T(8,128)(2,1)}, bf16[1536,768]{1,0:T(8,128)(2,1)}, u32[]{:S(2)}, u32[]{:S(2)}) collective-permute-start(bf16[1536,768]{1,0:T(8,128)(2,1)} %collective-permute-done.1.rest_4_), channel_id=1, source_target_pairs={{8,0},{16,8},{9,1},{17,9},{10,2},{18,10},{11,3},{19,11},{12,4},{20... | collective-permute-start | bytes 7077896 | tf_op jit(solution)/shard_map/ppermute | solution.py:1446
  453.7 61.8 %collective-permute-start.4 = (bf16[1536,768]{1,0:T(8,128)(2,1)}, bf16[1536,768]{1,0:T(8,128)(2,1)S(1)}, u32[]{:S(2)}, u32[]{:S(2)}) collective-permute-start(bf16[1536,768]{1,0:T(8,128)(2,1)} %collective-permute-done.2.rest_5_), channel_id=1, source_target_pairs={{16,24},{17,25},{18,26},{19,27},{20,28},{21,29},{22,30},{23,31}} | collective-permute-start | bytes 7077896 | tf_op jit(solution)/shard_map/ppermute | solution.py:1446
  454.5 61.0 %collective-permute-start.5 = (bf16[1536,768]{1,0:T(8,128)(2,1)}, bf16[1536,768]{1,0:T(8,128)(2,1)}, u32[]{:S(2)}, u32[]{:S(2)}) collective-permute-start(bf16[1536,768]{1,0:T(8,128)(2,1)} %collective-permute-done.3.rest_6_), channel_id=1, source_target_pairs={{8,0},{9,1},{10,2},{11,3},{12,4},{13,5},{14,6},{15,7}} | collective-permute-start | bytes 7077896 | tf_op jit(solution)/shard_map/ppermute | solution.py:1446
  515.5 1.4 copy-start.20
  592.9 84.6 %copy-start.2 = (bf16[2048,512]{1,0:T(8,128)(2,1)S(1)}, bf16[2048,512]{1,0:T(8,128)(2,1)}, u32[]{:S(2)}) copy-start(bf16[2048,512]{1,0:T(8,128)(2,1)} %get-tuple-element.69.attn_ref) | copy-start | bytes 6291460
  757.9 308.2 %reduce-scatter.4.cloned.1.call-start = ((), (), s32[]{:S(2)}) async-start(), calls=%async_computation.4 | async-start | bytes 3276800 | tf_op jit(solution)/shard_map/reduce_scatter | solution.py:1629
  769.0 375.1 %reduce-scatter.8.cloned.1.call-start = ((), (), s32[]{:S(2)}) async-start(), calls=%async_computation.6 | async-start | bytes 11796480 | tf_op jit(solution)/shard_map/reduce_scatter | solution.py:1597
  773.0 52.3 %collective-permute-start.6 = (bf16[768,768]{1,0:T(8,128)(2,1)}, bf16[768,768]{1,0:T(8,128)(2,1)}, u32[]{:S(2)}, u32[]{:S(2)}) collective-permute-start(bf16[768,768]{1,0:T(8,128)(2,1)} %get-tuple-element.130), channel_id=1, source_target_pairs={{0,8},{1,9},{2,10},{3,11},{4,12},{5,13},{6,14},{7,15}} | collective-permute-start | bytes 3538952 | tf_op jit(solution)/shard_map/ppermute | solution.py:1467
  774.3 51.1 %collective-permute-start.7 = (bf16[768,768]{1,0:T(8,128)(2,1)}, bf16[768,768]{1,0:T(8,128)(2,1)}, u32[]{:S(2)}, u32[]{:S(2)}) collective-permute-start(bf16[768,768]{1,0:T(8,128)(2,1)} %get-tuple-element.129), channel_id=1, source_target_pairs={{24,16},{25,17},{26,18},{27,19},{28,20},{29,21},{30,22},{31,23}} | collective-permute-start | bytes 3538952 | tf_op jit(solution)/shard_map/ppermute | solution.py:1467
  777.8 89.9 %collective-permute-start.10 = (bf16[768,768]{1,0:T(8,128)(2,1)S(1)}, bf16[768,768]{1,0:T(8,128)(2,1)}, u32[]{:S(2)}, u32[]{:S(2)}) collective-permute-start(bf16[768,768]{1,0:T(8,128)(2,1)S(1)} %get-tuple-element.128), channel_id=1, source_target_pairs={{0,8},{1,9},{2,10},{3,11},{4,12},{5,13},{6,14},{7,15}} | collective-permute-start | bytes 3538952 | tf_op jit(solution)/shard_map/ppermute | solution.py:1467
  779.1 88.6 %collective-permute-start.11 = (bf16[768,768]{1,0:T(8,128)(2,1)S(1)}, bf16[768,768]{1,0:T(8,128)(2,1)}, u32[]{:S(2)}, u32[]{:S(2)}) collective-permute-start(bf16[768,768]{1,0:T(8,128)(2,1)S(1)} %get-tuple-element.127), channel_id=1, source_target_pairs={{24,16},{25,17},{26,18},{27,19},{28,20},{29,21},{30,22},{31,23}} | collective-permute-start | bytes 3538952 | tf_op jit(solution)/shard_map/ppermute | solution.py:1467
  829.6 88.4 %collective-permute-start.8 = (bf16[768,768]{1,0:T(8,128)(2,1)}, bf16[768,768]{1,0:T(8,128)(2,1)}, u32[]{:S(2)}, u32[]{:S(2)}) collective-permute-start(bf16[768,768]{1,0:T(8,128)(2,1)} %get-tuple-element.126), channel_id=1, source_target_pairs={{0,8},{8,16},{1,9},{9,17},{2,10},{10,18},{3,11},{11,19},{4,12},{12... | collective-permute-start | bytes 3538952 | tf_op jit(solution)/shard_map/ppermute | solution.py:1467
  834.0 84.0 %collective-permute-start.9 = (bf16[768,768]{1,0:T(8,128)(2,1)}, bf16[768,768]{1,0:T(8,128)(2,1)}, u32[]{:S(2)}, u32[]{:S(2)}) collective-permute-start(bf16[768,768]{1,0:T(8,128)(2,1)} %get-tuple-element.125), channel_id=1, source_target_pairs={{16,8},{24,16},{17,9},{25,17},{18,10},{26,18},{19,11},{27,19},{20,... | collective-permute-start | bytes 3538952 | tf_op jit(solution)/shard_map/ppermute | solution.py:1467
  872.0 85.2 %collective-permute-start.14 = (bf16[768,768]{1,0:T(8,128)(2,1)}, bf16[768,768]{1,0:T(8,128)(2,1)}, u32[]{:S(2)}, u32[]{:S(2)}) collective-permute-start(bf16[768,768]{1,0:T(8,128)(2,1)} %get-tuple-element.124), channel_id=1, source_target_pairs={{0,8},{8,16},{1,9},{9,17},{2,10},{10,18},{3,11},{11,19},{4,12},{12... | collective-permute-start | bytes 3538952 | tf_op jit(solution)/shard_map/ppermute | solution.py:1467
  876.5 80.7 %collective-permute-start.15 = (bf16[768,768]{1,0:T(8,128)(2,1)}, bf16[768,768]{1,0:T(8,128)(2,1)}, u32[]{:S(2)}, u32[]{:S(2)}) collective-permute-start(bf16[768,768]{1,0:T(8,128)(2,1)} %get-tuple-element.123), channel_id=1, source_target_pairs={{16,8},{24,16},{17,9},{25,17},{18,10},{26,18},{19,11},{27,19},{20,... | collective-permute-start | bytes 3538952 | tf_op jit(solution)/shard_map/ppermute | solution.py:1467
  922.3 156.5 %collective-permute-start.12 = (bf16[768,768]{1,0:T(8,128)(2,1)}, bf16[768,768]{1,0:T(8,128)(2,1)S(1)}, u32[]{:S(2)}, u32[]{:S(2)}) collective-permute-start(bf16[768,768]{1,0:T(8,128)(2,1)} %get-tuple-element.122), channel_id=1, source_target_pairs={{0,8},{8,16},{16,24},{1,9},{9,17},{17,25},{2,10},{10,18},{18,26},{... | collective-permute-start | bytes 3538952 | tf_op jit(solution)/shard_map/ppermute | solution.py:1467
  926.8 152.1 %collective-permute-start.13 = (bf16[768,768]{1,0:T(8,128)(2,1)}, bf16[768,768]{1,0:T(8,128)(2,1)S(1)}, u32[]{:S(2)}, u32[]{:S(2)}) collective-permute-start(bf16[768,768]{1,0:T(8,128)(2,1)} %get-tuple-element.121), channel_id=1, source_target_pairs={{8,0},{16,8},{24,16},{9,1},{17,9},{25,17},{10,2},{18,10},{26,18},{... | collective-permute-start | bytes 3538952 | tf_op jit(solution)/shard_map/ppermute | solution.py:1467
  961.5 117.3 %collective-permute-start.16 = (bf16[768,768]{1,0:T(8,128)(2,1)}, bf16[768,768]{1,0:T(8,128)(2,1)}, u32[]{:S(2)}, u32[]{:S(2)}) collective-permute-start(bf16[768,768]{1,0:T(8,128)(2,1)} %get-tuple-element.120), channel_id=1, source_target_pairs={{0,8},{8,16},{16,24},{1,9},{9,17},{17,25},{2,10},{10,18},{18,26},{... | collective-permute-start | bytes 3538952 | tf_op jit(solution)/shard_map/ppermute | solution.py:1467
  966.0 112.9 %collective-permute-start.17 = (bf16[768,768]{1,0:T(8,128)(2,1)}, bf16[768,768]{1,0:T(8,128)(2,1)}, u32[]{:S(2)}, u32[]{:S(2)}) collective-permute-start(bf16[768,768]{1,0:T(8,128)(2,1)} %get-tuple-element.119), channel_id=1, source_target_pairs={{8,0},{16,8},{24,16},{9,1},{17,9},{25,17},{10,2},{18,10},{26,18},{... | collective-permute-start | bytes 3538952 | tf_op jit(solution)/shard_map/ppermute | solution.py:1467
  1078.8 74.7 %copy-start.6 = (bf16[256,2048]{1,0:T(8,128)(2,1)S(1)}, bf16[256,2048]{1,0:T(8,128)(2,1)}, u32[]{:S(2)}) copy-start(bf16[256,2048]{1,0:T(8,128)(2,1)} %get-tuple-element.92) | copy-start | bytes 3145732
  1078.8 65.3 %copy-start.4 = (bf16[768,768]{1,0:T(8,128)(2,1)}, bf16[768,768]{1,0:T(8,128)(2,1)S(1)}, u32[]{:S(2)}) copy-start(bf16[768,768]{1,0:T(8,128)(2,1)S(1)} %collective-permute-done.12.up0_ref) | copy-start | bytes 3538948
  1078.8 65.3 %copy-start.5 = (bf16[768,768]{1,0:T(8,128)(2,1)}, bf16[768,768]{1,0:T(8,128)(2,1)S(1)}, u32[]{:S(2)}) copy-start(bf16[768,768]{1,0:T(8,128)(2,1)S(1)} %collective-permute-done.13.down0_ref) | copy-start | bytes 3538948
  1153.4 2.0 copy-start.3
  1155.4 2.0 copy-start.7
  1155.4 4.3 copy-start.1
  1157.3 1.0 copy-start.9
  1157.3 1.7 copy-start.8
Sparse Core Ops, SparseCore 0:
  24.9 113.7 all-gather.13
  140.2 78.2 all-gather.9
  220.1 72.3 all-gather.7
  293.9 79.0 all-gather.11
  758.0 62.1 reduce-scatter.5
  823.0 92.4 reduce-scatter.3
  917.8 226.2 reduce-scatter.7

commit v11 on v10

--- a/solution.py
+++ b/solution.py
@@ -815,6 +815,138 @@
         after,
         grad,
         gain,
+    )
+
+
+def halfway_kernel(
+    n,
+    n_dp,
+    part_ref,
+    n2_ref,
+    gg_ref,
+    ug_ref,
+    after_ref,
+    grad_ref,
+    gain_ref,
+    mid_ref,
+    fpart_ref,
+    low_ref,
+    wgrad_ref,
+    n2,
+    gg,
+    ug,
+    wgrad,
+    lsem,
+    wsem,
+    *scratch,
+):
+    loads = [
+        pltpu.make_async_copy(src, dst, lsem.at[k])
+        for k, (src, dst) in enumerate(((n2_ref, n2), (gg_ref, gg), (ug_ref, ug)))
+    ]
+    plane = Plane(n)
+    plane.meet()
+    sums = Scatter(plane, part_ref, *scratch)
+    sums.start()
+    for load in loads:
+        load.start()
+    fpart_ref[...] = jnp.zeros_like(fpart_ref)
+    sums.pairs()
+    for load in loads:
+        load.wait()
+    cut = wgrad.shape[1] // 2
+
+    def weights(kind, source):
+        copies = []
+        for z in range(n_dp):
+            here = slice(z * cut, (z + 1) * cut)
+            there = slice(kind * cut, (kind + 1) * cut)
+            wgrad[z, there, :] = dot(n2[:, here], source[...], TN).astype(BF16)
+            copies.append(
+                pltpu.make_async_copy(
+                    wgrad.at[z, pl.ds(kind * cut, cut), :],
+                    wgrad_ref.at[z, pl.ds(kind * cut, cut), :],
+                    wsem.at[kind, z],
+                )
+            )
+            copies[-1].start()
+        return copies
+
+    copies = weights(0, gg)
+    sums.spread.relay()
+    copies += weights(1, ug)
+    sums.spread.gathered()
+
+    def norm(at):
+        value = after_ref[at, :]
+        inv = rms_parts(value)
+        unit = value * inv
+        grad = sums.total(at)
+        fpart_ref[0:1, :] += jnp.sum(grad * unit, axis=0, keepdims=True)
+        mid = grad_ref[at, :].astype(F32) + rms_back(grad, unit, inv, gain_ref[...])
+        mid_ref[at, :] = mid
+        low_ref[at, :] = mid.astype(BF16)
+
+    by_rows(after_ref.shape[0], norm)
+    sums.finish()
+    for copy in copies:
+        copy.wait()
+
+
+def halfway(n, n_dp, part, n2, gg, ug, after, grad, gain):
+    shape = jax.ShapeDtypeStruct
+    width, hidden = n2.shape[1], gg.shape[1]
+    out = (n_dp, 2 * width // n_dp, hidden)
+    return comm_call(
+        functools.partial(halfway_kernel, n, n_dp),
+        4,
+        [
+            shape(after.shape, F32),
+            shape((8, after.shape[1]), F32),
+            shape(after.shape, BF16),
+            shape(out, BF16),
+        ],
+        [VM, VM, VM, ANY],
+        [ANY, ANY, ANY, ANY, VM, VM, VM],
+        [
+            pltpu.VMEM(n2.shape, BF16),
+            pltpu.VMEM(gg.shape, BF16),
+            pltpu.VMEM(gg.shape, BF16),
+            pltpu.VMEM(out, BF16),
+            DMA((3,)),
+            DMA((2, n_dp)),
+        ]
+        + scatter_scratch(n, *after.shape),
+        50,
+        part,
+        n2,
+        gg,
+        ug,
+        after,
+        grad,
+        gain,
+    )
+
+
+def share_kernel(n, low_ref, all_ref, *sems):
+    plane = Plane(n)
+    plane.meet()
+    gather = gather_of(plane, low_ref, all_ref, *sems)
+    gather.start()
+    gather.forward()
+    gather.finish()
+
+
+def share_rows(n, low):
+    return comm_call(
+        functools.partial(share_kernel, n),
+        10,
+        jax.ShapeDtypeStruct((n,) + low.shape, BF16),
+        ANY,
+        [VM],
+        gather_sems(n),
+        45,
+        low,
     )
 
 
@@ -1136,18 +1268,19 @@
         key = k_ref[at, :]
         val = v_ref[at, :]
         allowed = (docc_ref[...] == docr_ref[:, at]) & (block * rows + col_off <= row_pos)
-        dk = jnp.zeros((rows, HD), F32)
-        dv = jnp.zeros((rows, HD), F32)
-        for head in range(heads):
-            cols = slice(head * HD, (head + 1) * HD)
-            query = q_ref[:, cols]
-            score = dot(query, key, NT) * SCALE2
-            expo = jnp.where(allowed, jnp.exp2(score), 0.0)
-            prod = dot(grads[head], val, NT)
-            score_grad = (expo * (prod - shifts[head])).astype(BF16)
-            dv += dot(expo.astype(BF16), grads[head], TN)
-            dk += dot(score_grad, query, TN)
-            dqa_ref[:, cols] += dot(score_grad, key)
+        columns = [slice(head * HD, (head + 1) * HD) for head in range(heads)]
+        queries = [q_ref[:, cols] for cols in columns]
+        scores = [dot(query, key, NT) for query in queries]
+        prods = [dot(grad, val, NT) for grad in grads]
+        expos = [jnp.where(allowed, jnp.exp2(score * SCALE2), 0.0) for score in scores]
+        score_grads = [
+            (expo * (prod - shift)).astype(BF16) for expo, prod, shift in zip(expos, prods, shifts)
+        ]
+        expos = [expo.astype(BF16) for expo in expos]
+        dv = sum(dot(expo, grad, TN) for expo, grad in zip(expos, grads))
+        dk = sum(dot(each, query, TN) for each, query in zip(score_grads, queries))
+        for cols, each in zip(columns, score_grads):
+            dqa_ref[:, cols] += dot(each, key)
         dk_ref[at, :] += dk
         dv_ref[at, :] += dv
         return carry
@@ -1261,15 +1394,19 @@
     )(branch, wout, attn, total, q, k, v, qlin, klin, cosine, sine, qgain, kgain, doc[:, None], doc[None, :], wgrad, moe, after)
 
 
-def expert_kernel(chained, low, aliased, plan, z_ref, n2_ref, top_ref, prob_ref, *rest):
+def expert_kernel(chained, low, aliased, split, plan, z_ref, n2_ref, top_ref, prob_ref, *rest):
     if aliased:
         rest = rest[1:]
     if chained:
         moe_in, row_in = rest[:2]
         rest = rest[2:]
     sources, rest = rest[: len(plan)], rest[len(plan) :]
-    moe_ref, row_ref, grads_ref, wg_ref, wu_ref, wd_ref = rest[:6]
-    ag_ref, au_ref, ad_ref, stage, wsem, sem = rest[6:]
+    moe_ref, row_ref, rest = rest[0], rest[1], rest[2:]
+    if split:
+        gg_ref, ug_ref, rest = rest[0], rest[1], rest[2:]
+    grads_ref, wg_ref, wu_ref, wd_ref, rest = *rest[:4], rest[4:]
+    sums, (stage, wsem, sem) = rest[:-3], rest[-3:]
+    ad_ref = sums[-1]
     step = pl.program_id(0)
     rows, width = n2_ref.shape
     parts, cut, hidden = wd_ref.shape
@@ -1300,9 +1437,8 @@
                     load()
                 else:
                     pl.when(wanted)(load)
-        ag_ref[...] = jnp.zeros_like(ag_ref)
-        au_ref[...] = jnp.zeros_like(au_ref)
-        ad_ref[...] = jnp.zeros_like(ad_ref)
+        for each in sums:
+            each[...] = jnp.zeros_like(each)
         for index in range(3):
             for owner in range(parts):
                 block = weights[index].at[owner]
@@ -1333,14 +1469,18 @@
     if chained:
         row = row + row_in[...].astype(F32)
     row_ref[...] = row.astype(BF16)
-    ag_ref[...] += dot(n2, gate_grad, TN).reshape(parts, cut, hidden)
-    au_ref[...] += dot(n2, up_grad, TN).reshape(parts, cut, hidden)
+    if split:
+        gg_ref[...] = gate_grad
+        ug_ref[...] = up_grad
+    else:
+        sums[0][...] += dot(n2, gate_grad, TN).reshape(parts, cut, hidden)
+        sums[1][...] += dot(n2, up_grad, TN).reshape(parts, cut, hidden)
 
     @pl.when(step == pl.num_programs(0) - 1)
     def _():
         copies = []
         pieces = [
-            (acc, place, z) for z in range(parts) for place, acc in enumerate((ag_ref, au_ref, ad_ref))
+            (acc, place, z) for z in range(parts) for place, acc in enumerate(sums)
         ]
         for index, (acc, place, z) in enumerate(pieces):
             slot = index % 2
@@ -1359,32 +1499,34 @@
         copies[-1].wait()
 
 
-def expert(z, n2, top, prob, n_dp, sources, before, rows, low, full, grads):
+def expert(z, n2, top, prob, n_dp, sources, before, rows, low, full, grads, split):
     length, width = n2.shape
     cut = width // n_dp
     hidden = sources[0][0].shape[-1]
     blk = pl.BlockSpec((rows, width), lambda i: (i, 0))
     col = pl.BlockSpec((rows, 1), lambda i: (i, 0))
+    thin = pl.BlockSpec((rows, hidden), lambda i: (i, 0))
     shape = jax.ShapeDtypeStruct
     plan = tuple(entry[1:] for entry in sources)
     weight = pltpu.VMEM((n_dp, cut, hidden), BF16)
     total = pltpu.VMEM((n_dp, cut, hidden), F32)
     return pl.pallas_call(
-        functools.partial(expert_kernel, len(before) > 0, low, len(grads) > 0, plan),
+        functools.partial(expert_kernel, len(before) > 0, low, len(grads) > 0, split, plan),
         grid=(length // rows,),
         in_specs=[pl.BlockSpec(memory_space=pltpu.SMEM), blk, blk, col]
         + [ANY] * len(grads)
         + [blk] * len(before)
         + [ANY] * len(sources),
-        out_specs=[blk, blk, ANY],
+        out_specs=[blk, blk] + [thin] * (2 * split) + [ANY],
         out_shape=[
             shape((length, width), BF16),
             shape((length, width), BF16),
-            shape((n_dp, 3 * cut, full), BF16),
-        ],
+        ]
+        + [shape((length, hidden), BF16)] * (2 * split)
+        + [shape((n_dp, cut if split else 3 * cut, full), BF16)],
         input_output_aliases={4: 2} if grads else {},
         scratch_shapes=[weight] * 3
-        + [total] * 3
+        + [total] * (1 if split else 3)
         + [pltpu.VMEM((2, cut, hidden), BF16), DMA((3, n_dp)), DMA((2,))],
         compiler_params=pltpu.CompilerParams(vmem_limit_bytes=VMEM_LIMIT),
         cost_estimate=pl.CostEstimate(
@@ -1397,16 +1539,16 @@
 
 
 def unpack_kernel(
-    z_ref, one_ref, all_ref, up0_ref, down0_ref, up1_ref, down1_ref, dg_ref, du_ref, dd_ref, own, sem
+    z_ref, pair_ref, down_one_ref, all_ref, up0_ref, down0_ref, up1_ref, down1_ref, dg_ref, du_ref, dd_ref, own, sem
 ):
     copy = pltpu.make_async_copy(all_ref.at[z_ref[0]], own, sem)
     copy.start()
     cut = dg_ref.shape[1]
     half = up0_ref.shape[0]
-    piece = [slice(k * cut, (k + 1) * cut) for k in range(3)]
-    dg_ref[1] = one_ref[piece[0], :].astype(F32)
-    du_ref[1] = one_ref[piece[1], :].astype(F32)
-    dd_ref[1] = jnp.transpose(one_ref[piece[2], :].astype(F32))
+    piece = [slice(k * cut, (k + 1) * cut) for k in range(2)]
+    dg_ref[1] = pair_ref[piece[0], :].astype(F32)
+    du_ref[1] = pair_ref[piece[1], :].astype(F32)
+    dd_ref[1] = jnp.transpose(down_one_ref[...].astype(F32))
     copy.wait()
 
     def total(low, high):
@@ -1421,13 +1563,13 @@
     dd_ref[0] = jnp.transpose(total(2 * cut, 3 * cut))
 
 
-def unpack(z, one, grads, got):
-    rows, hidden = one.shape
-    cut = rows // 3
+def unpack(z, pair, one, grads, got):
+    cut, hidden = one.shape
+    rows = 3 * cut
     shape = jax.ShapeDtypeStruct
     return pl.pallas_call(
         unpack_kernel,
-        in_specs=[pl.BlockSpec(memory_space=pltpu.SMEM), VM, ANY, VM, VM, VM, VM],
+        in_specs=[pl.BlockSpec(memory_space=pltpu.SMEM), VM, VM, ANY, VM, VM, VM, VM],
         out_specs=[VM] * 3,
         out_shape=[
             shape((2, cut, hidden), F32),
@@ -1437,7 +1579,7 @@
         scratch_shapes=[pltpu.VMEM((rows, hidden), BF16), DMA(())],
         compiler_params=pltpu.CompilerParams(vmem_limit_bytes=VMEM_LIMIT),
         name="unpack",
-    )(z, one, grads, *got)
+    )(z, pair, one, grads, *got)
 
 
 def line_hop(block_up, block_down, n_dp, hop):
@@ -1558,8 +1700,8 @@
     z = lax.axis_index("dp").astype(jnp.int32).reshape(1)
     hidden = w_gate.shape[2]
 
-    def run(e, sources, carried, low, grads):
-        moe, rows_grad, grads = expert(
+    def run(e, sources, carried, low, grads, split=False):
+        moe, rows_grad, *grads = expert(
             z,
             normed2,
             top_all,
@@ -1571,6 +1713,7 @@
             low,
             hidden,
             grads,
+            split,
         )
         return (moe, rows_grad), grads
 
@@ -1582,7 +1725,7 @@
             up = down = after_of(block1, full)
             up, down = line_hop(up, down, n_dp, 1)
             sources1 += [(up, "up", 1, 0), (down, "down", 1, 0)]
-        carried, grads = run(0, [(full, "all", 0, 0)], carried, low, grads0)
+        carried, (grads,) = run(0, [(full, "all", 0, 0)], carried, low, grads0)
         grads0 = (grads,)
     rows_all = 3 * (width // n_dp)
     spans = {"a": (0, rows_all // 2), "b": (rows_all // 2, rows_all)}
@@ -1593,13 +1736,27 @@
             sources1 += [(up, "up", hop, 0), (down, "down", hop, 0)]
         for tag, rows in spans.items():
             got[tag], before = reduce_hop(grads, got[tag], n_dp, hop - 1, rows, before)
-    (moe, rows_grad), grads1 = run(1, sources1, carried, 0, ())
-    done1 = lax.psum_scatter(
-        grads1.reshape(3 * width, hidden), "dp", scatter_dimension=0, tiled=True
-    )
-    mid, ffn_part, branch = turn(
-        n_ctx, rows_grad.reshape(blocks), after, top_own, gain_ffn
-    )
+    split = n_ctx == 8
+    (moe, rows_grad), grads1 = run(1, sources1, carried, 0, (), split)
+    rows_grad = rows_grad.reshape(blocks)
+    if split:
+        gate_grad, up_grad, down_grad = grads1
+        done_d = lax.psum_scatter(
+            down_grad.reshape(width, hidden), "dp", scatter_dimension=0, tiled=True
+        )
+        mid, ffn_part, low_mid, pair_grad = halfway(
+            n_ctx, n_dp, rows_grad, normed2, gate_grad, up_grad, after, top_own, gain_ffn
+        )
+        done_gu = lax.psum_scatter(
+            pair_grad.reshape(2 * width, hidden), "dp", scatter_dimension=0, tiled=True
+        )
+        branch = share_rows(n_ctx, low_mid)
+    else:
+        done = lax.psum_scatter(
+            grads1[0].reshape(3 * width, hidden), "dp", scatter_dimension=0, tiled=True
+        )
+        done_gu, done_d = done[: 2 * width // n_dp], done[2 * width // n_dp :]
+        mid, ffn_part, branch = turn(n_ctx, rows_grad, after, top_own, gain_ffn)
     branch = branch.reshape(length, width)
 
     out_w = dot(attn, branch, TN).astype(BF16).reshape(n_dp, qw // n_dp, width)
@@ -1645,7 +1802,7 @@
     packed = gains_sum(n_ctx, n_dp, packed)
     packed = packed.reshape(1024)
     query_w, key_w, value_w = post(n_ctx, qkv_w.reshape(n_ctx, depth, qw + HD))
-    gate_w, up_w, down_w = unpack(z, done1, grads, got["a"] + got["b"])
+    gate_w, up_w, down_w = unpack(z, done_gu, done_d, grads, got["a"] + got["b"])
     return (
         layer_output.reshape(1, tokens, width),
         input_grad.reshape(1, tokens, width),

time: 1180 us -> 1160 us (0.983)
  Pallas kernels: 653 us -> 625 us
  waiting for transfers between devices: 371 us -> 386 us
    pallas_call x3, Pallas kernels: 164 us -> 148 us  [expert(): pl.pallas_call(functools.partial(expert_kernel, len(before) > 0, low, len...]
    reduce_scatter x1 -> x2, waiting for transfers between devices: 65.3 us -> 80.1 us  [the longest x1 80.1 us: per_device(): lax.psum_scatter(pair_grad.reshape(2 * width, hidden), 'dp', scatter_dime...]
    pallas_call x7 -> x8, Pallas kernels: 368 us -> 359 us  [comm_call(): pl.pallas_call(kernel, out_shape=outs, in_specs=in_specs, out_specs=out_s...]
  transfers between devices with their start and end apart: 25 -> 26, of which waited for: 8 -> 8; matrix products, arithmetic and copies ran while one was open for 5% -> 5% of each run, Pallas kernels for 34% -> 34%
where the time goes in v11:
time: 1160 us; the launch traced here: 1150 us
  Pallas kernels  625 us (54%)
  waiting for transfers between devices  386 us (33%)
  starting transfers between devices  50.6 us (4%)
  other arithmetic  28.4 us (2%)
  local copies, waits for them, and re-layouts  28 us (2%)
  matrix products  20.4 us (2%)
  between operations  15 us (1%)
    pallas_call x8, Pallas kernels, comm_call(): pl.pallas_call(kernel, out_shape=outs, in_specs=in_specs, out_specs=out_s...  359 us
    pallas_call x3, Pallas kernels, expert(): pl.pallas_call(functools.partial(expert_kernel, len(before) > 0, low, len...  148 us
    ppermute x6, waiting for transfers between devices, reduce_hop(): lax.ppermute(blocks[0], 'dp', up)  145 us
    reduce_scatter x1, waiting for transfers between devices, per_device(): lax.psum_scatter(pair_grad.reshape(2 * width, hidden), 'dp', scatter_dime...  80.1 us
    ppermute x3, waiting for transfers between devices, line_hop(): lax.ppermute(block_up, 'dp', up)  70.2 us
    pallas_call x1, Pallas kernels, attn_backward(): pl.pallas_call(functools.partial(attn_backward_kernel, n, n_dp, heads, MO...  68.1 us
    all_gather x1, waiting for transfers between devices, per_device(): lax.all_gather(cols.reshape(n_ctx * depth, qw + HD), 'dp', axis=0, tiled=...  57.3 us
    pallas_call x1, Pallas kernels, attn_forward(): pl.pallas_call(functools.partial(attn_forward_kernel, n, n_dp, heads, MOS...  41 us
  transfers between devices with their start and end apart: 26, of which 8 were waited for; matrix products, arithmetic and copies ran while one was open for 5% of the time, Pallas kernels for 34%

profile of v11, /device:TPU:14, one launch (start us, length us, event | category | flops | bytes accessed | tf_op | source)
XLA Modules:
  0.0 1153.6 jit_solution(6128268369766913082)
XLA Ops:
  10.9 13.7 %shard_map.255 = (bf16[8,64,640]{2,1,0:T(8,128)(2,1)}, f32[4,8,8,128]{3,2,1,0:T(8,128)}, bf16[1536,256]{1,0:T(8,128)(2,1)}, bf16[1536,512]{1,0:T(8,128)(2,1)}) custom-call(bf16[8,64,640]{2,1,0:T(8,128)(2,1)} %maximum_bitcast_fusion.cols_ref, f32[8,128]{1,0:T(8,128)} %fusion.19.small_ref, bf16[2,512,768]{2,1,0:T(8,128)(2,1)} %rest_0_.3, ...), custom_call_target="tpu_custom_call" | custom-call | bytes 24000000 | tf_op jit(solution)/shard_map/pallas_call | solution.py:448
  27.9 80.1 %shard_map.256 = (bf16[8,256,2048]{2,1,0:T(8,128)(2,1)}, f32[8,24,256]{2,1,0:T(8,128)}, bf16[8,256,2048]{2,1,0:T(8,128)(2,1)}, bf16[1536,768]{1,0:T(8,128)(2,1)}) custom-call(bf16[256,2048]{1,0:T(8,128)(2,1)} %bitcast.102, f32[1,2048]{1,0:T(1,128)} %reshape.188.gain_ref, f32[24,256]{1,0:T(8,128)} %maximum_maximum_fusion.info_ref, ...), custom_call_target="tpu_custom_call" | custom-call | bytes 270000000 | tf_op jit(solution)/shard_map/pallas_call | solution.py:448
  108.1 30.6 %all-gather.14.cloned.1.call-done = bf16[6144,512]{1,0:T(8,128)(2,1)} async-done(((bf16[1536,512]{1,0:T(8,128)(2,1)}), bf16[6144,512]{1,0:T(8,128)(2,1)}) %all-gather.14.cloned.1.call-update) | async-done | bytes 6291472 | tf_op jit(solution)/shard_map/all_gather | solution.py:1722
  138.7 4.4 collective-permute-start
  143.0 2.3 collective-permute-start.1
  150.8 3.9 fusion.10
  154.7 1.9 pad_maximum_fusion
  156.7 1.6 fusion.21
  158.3 70.2 %collective-permute-done.rest_3_ = bf16[1536,768]{1,0:T(8,128)(2,1)S(1)} collective-permute-done((bf16[1536,768]{1,0:T(8,128)(2,1)}, bf16[1536,768]{1,0:T(8,128)(2,1)S(1)}, u32[]{:S(2)}, u32[]{:S(2)}) %collective-permute-start) | collective-permute-done | bytes 2359328 | tf_op jit(solution)/shard_map/ppermute | solution.py:1588
  228.5 4.6 collective-permute-start.2
  233.1 2.1 collective-permute-start.3
  235.2 57.3 %all-gather.8.cloned.1.call-done.wqkv_ref = bf16[2048,640]{1,0:T(8,128)(2,1)} async-done(((bf16[512,640]{1,0:T(8,128)(2,1)}), bf16[2048,640]{1,0:T(8,128)(2,1)}) %all-gather.8.cloned.1.call-update) | async-done | bytes 2621456 | tf_op jit(solution)/shard_map/all_gather | solution.py:1666
  292.5 41.0 %attn_forward.1 = (f32[2048,512]{1,0:T(8,128)}, f32[2048,128]{1,0:T(8,128)}, bf16[2048,512]{1,0:T(8,128)(2,1)}, bf16[2048,128]{1,0:T(8,128)(2,1)}, bf16[2048,128...) custom-call(bf16[2048,2048]{1,0:T(8,128)(2,1)} %bitcast.136, ...), custom_call_target="tpu_custom_call" | custom-call | flops 35000000512 | bytes 31457280 | tf_op jit(solution)/shard_map/attn_forward/pallas_call | solution.py:1138
  333.5 87.7 %shard_map.257 = (f32[256,2048]{1,0:T(8,128)}, bf16[8,256,2048]{2,1,0:T(8,128)(2,1)}) custom-call(bf16[2048,512]{1,0:T(8,128)(2,1)} %get-tuple-element.72.attn_ref, bf16[512,2048]{1,0:T(8,128)(2,1)} %bitcast.117, bf16[256,2048]{1,0:T(8,128)(2,1)} %bitcast.103, f32[1,2048]{1,0:T(1,128)} %reshape.195.gain_ref), custom_call_target="tpu_custom_call" | custom-call | bytes 315000000 | tf_op jit(solution)/shard_map/pallas_call | solution.py:448
  421.2 32.4 %expert.3 = (bf16[2048,2048]{1,0:T(8,128)(2,1)}, bf16[2048,2048]{1,0:T(8,128)(2,1)}, bf16[4,1536,768]{2,1,0:T(8,128)(2,1)}) custom-call(s32[1]{0:T(128)} %bitcast.z_ref, bf16[2048,2048]{1,0:T(8,128)(2,1)} %bitcast.108, bf16[2048,2048]{1,0:T(8,128)(2,1)} %bitcast.138, f32[2048,1]{1,0:T(8,128)} %get-tuple-element.137.prob_ref, bf16[4,1536,256]{2,1,0:T(8,128)(2,1)} %bitcast.142), custom_call_target="tpu_custom_call" | custom-call | flops 19327352832 | bytes 41943040 | tf_op jit(solution)/shard_map/expert/pallas_call | solution.py:1513
  454.4 5.6 collective-permute-start.5
  460.0 55.5 %expert.4 = (bf16[2048,2048]{1,0:T(8,128)(2,1)}, bf16[2048,2048]{1,0:T(8,128)(2,1)}, bf16[4,1536,768]{2,1,0:T(8,128)(2,1)}) custom-call(s32[1]{0:T(128)} %bitcast.z_ref, bf16[2048,2048]{1,0:T(8,128)(2,1)} %bitcast.109, bf16[2048,2048]{1,0:T(8,128)(2,1)} %bitcast.139, f32[2048,1]{1,0:T(8,128)} %get-tuple-element.137.prob_ref, ...), custom_call_target="tpu_custom_call", output_to_operand_aliasing={{2}: (4, {})} | custom-call | flops 38654705664 | bytes 41943040 | tf_op jit(solution)/shard_map/expert/pallas_call | solution.py:1513
  515.6 1.4 copy-done.20
  517.0 59.6 %expert.5 = (bf16[2048,2048]{1,0:T(8,128)(2,1)}, bf16[2048,2048]{1,0:T(8,128)(2,1)}, bf16[2048,768]{1,0:T(8,128)(2,1)}, bf16[2048,768]{1,0:T(8,128)(2,1)}, bf16[4,512,768]{2,1,0:T(8,128)(2,1)}) custom-call(s32[1]{0:T(128)} %bitcast.z_ref, bf16[2048,2048]{1,0:T(8,128)(2,1)} %bitcast.110, bf16[2048,2048]{1,0:T(8,128)(2,1)} %bitcast.140, ...), custom_call_target="tpu_custom_call" | custom-call | flops 57982058496 | bytes 41943040 | tf_op jit(solution)/shard_map/expert/pallas_call | solution.py:1513
  576.6 45.9 %shard_map.258 = (f32[256,2048]{1,0:T(8,128)}, f32[8,2048]{1,0:T(8,128)}, bf16[256,2048]{1,0:T(8,128)(2,1)}, bf16[4,1024,768]{2,1,0:T(8,128)(2,1)}) custom-call(bf16[8,256,2048]{2,1,0:T(8,128)(2,1)} %bitcast.112, bf16[2048,2048]{1,0:T(8,128)(2,1)} %bitcast.111, bf16[2048,768]{1,0:T(8,128)(2,1)} %get-tuple-element.86.gg_ref, ...), custom_call_target="tpu_custom_call" | custom-call | bytes 150000000 | tf_op jit(solution)/shard_map/pallas_call | solution.py:448
  622.5 41.6 %shard_map.259 = bf16[8,256,2048]{2,1,0:T(8,128)(2,1)} custom-call(bf16[256,2048]{1,0:T(8,128)(2,1)} %get-tuple-element.89.low_ref), custom_call_target="tpu_custom_call" | custom-call | bytes 135000000 | tf_op jit(solution)/shard_map/pallas_call | solution.py:448
  664.2 9.1 convolution_convert_fusion.1
  673.3 68.1 %attn_backward.1 = (bf16[2048,640]{1,0:T(8,128)(2,1)}, f32[8,128]{1,0:T(8,128)}, bf16[4,128,2048]{2,1,0:T(8,128)(2,1)}, bf16[256,2048]{1,0:T(8,128)(2,1)}) custom-call(bf16[2048,2048]{1,0:T(8,128)(2,1)} %bitcast.107, bf16[512,2048]{1,0:T(8,128)(2,1)} %bitcast.118, bf16[2048,512]{1,0:T(8,128)(2,1)} %get-tuple-element.72.attn_ref, ...), custom_call_target="tpu_custom_call" | custom-call | flops 60000002048 | bytes 31457280 | tf_op jit(solution)/shard_map/attn_backward/pallas_call | solution.py:1346
  741.5 11.3 convolution_convert_fusion
  754.3 3.2 dynamic-slice_bitcast_fusion.2
  758.8 1.7 collective-permute-start.7
  760.5 1.8 dynamic-slice_bitcast_fusion
  763.6 1.7 collective-permute-start.11
  765.3 44.5 %collective-permute-done.6 = bf16[768,768]{1,0:T(8,128)(2,1)} collective-permute-done((bf16[768,768]{1,0:T(8,128)(2,1)}, bf16[768,768]{1,0:T(8,128)(2,1)}, u32[]{:S(2)}, u32[]{:S(2)}) %collective-permute-start.6) | collective-permute-done | bytes 1179680 | tf_op jit(solution)/shard_map/ppermute | solution.py:1609
  809.9 4.3 fusion.5
  814.1 4.4 collective-permute-start.8
  819.8 32.4 %collective-permute-done.10 = bf16[768,768]{1,0:T(8,128)(2,1)} collective-permute-done((bf16[768,768]{1,0:T(8,128)(2,1)S(1)}, bf16[768,768]{1,0:T(8,128)(2,1)}, u32[]{:S(2)}, u32[]{:S(2)}) %collective-permute-start.10) | collective-permute-done | bytes 1179680 | tf_op jit(solution)/shard_map/ppermute | solution.py:1609
  852.2 4.3 fusion.3
  856.5 4.5 collective-permute-start.14
  862.3 40.2 %collective-permute-done.8 = bf16[768,768]{1,0:T(8,128)(2,1)} collective-permute-done((bf16[768,768]{1,0:T(8,128)(2,1)}, bf16[768,768]{1,0:T(8,128)(2,1)}, u32[]{:S(2)}, u32[]{:S(2)}) %collective-permute-start.8) | collective-permute-done | bytes 1179680 | tf_op jit(solution)/shard_map/ppermute | solution.py:1609
  902.5 4.3 fusion.2
  906.8 4.4 collective-permute-start.12
  911.3 1.9 collective-permute-start.13
  913.2 28.0 %collective-permute-done.14 = bf16[768,768]{1,0:T(8,128)(2,1)} collective-permute-done((bf16[768,768]{1,0:T(8,128)(2,1)}, bf16[768,768]{1,0:T(8,128)(2,1)}, u32[]{:S(2)}, u32[]{:S(2)}) %collective-permute-start.14) | collective-permute-done | bytes 1179680 | tf_op jit(solution)/shard_map/ppermute | solution.py:1609
  941.2 4.3 fusion
  945.5 4.4 collective-permute-start.16
  950.0 2.4 collective-permute-start.17
  952.4 51.0 %shard_map.260 = (f32[256,2048]{1,0:T(8,128)}, f32[8,2048]{1,0:T(8,128)}) custom-call(bf16[2048,640]{1,0:T(8,128)(2,1)} %get-tuple-element.98.grad_ref, bf16[2048,640]{1,0:T(8,128)(2,1)} %all-gather.8.cloned.1.call-done.wqkv_ref, bf16[256,2048]{1,0:T(8,128)(2,1)} %bitcast.104, f32[256,2048]{1,0:T(8,128)} %get-tuple-element.99.mid_ref, ...), custom_call_target="tpu_custom_call" | custom-call | bytes 180000000 | tf_op jit(solution)/shard_map/pallas_call | solution.py:448
  1007.1 26.4 %shard_map.261 = f32[8,128]{1,0:T(8,128)} custom-call(f32[8,4,8,128]{3,2,1,0:T(8,128)} %copy_bitcast_fusion.3.small_ref), custom_call_target="tpu_custom_call" | custom-call | bytes 30000000 | tf_op jit(solution)/shard_map/pallas_call | solution.py:448
  1036.2 2.1 convert_element_type.140
  1038.3 12.5 %shard_map.262 = (f32[64,4096]{1,0:T(8,128)}, f32[64,512]{1,0:T(8,128)}, f32[64,512]{1,0:T(8,128)}) custom-call(bf16[8,64,640]{2,1,0:T(8,128)(2,1)} %bitcast.123), custom_call_target="tpu_custom_call" | custom-call | bytes 30000000 | tf_op jit(solution)/shard_map/pallas_call | solution.py:448
  1050.9 80.1 %reduce-scatter.9.cloned.1.call-done.pair_ref = bf16[1024,768]{1,0:T(8,128)(2,1)} async-done(((bf16[4096,768]{1,0:T(8,128)(2,1)}), bf16[1024,768]{1,0:T(8,128)(2,1)}) %reduce-scatter.9.cloned.1.call-update) | async-done | bytes 1572880 | tf_op jit(solution)/shard_map/reduce_scatter | solution.py:1750
  1131.0 9.3 unpack.1
  (120 shorter events, 32.4 us)
Async XLA Ops:
  7.2 1.2 copy-start
  7.2 3.1 copy-start.15
  7.2 3.1 copy-start.16
  7.2 3.0 copy-start.17
  7.2 3.0 copy-start.18
  7.2 131.4 %all-gather.14.cloned.1.call-start = ((), (), s32[]{:S(2)}) async-start(), calls=%async_computation.11 | async-start | bytes 7864320 | tf_op jit(solution)/shard_map/all_gather | solution.py:1722
  24.7 1.6 copy-start.10
  24.7 2.4 copy-start.14
  24.7 2.5 copy-start.12
  24.7 2.5 copy-start.13
  24.8 210.4 %all-gather.10.cloned.1.call-start = ((), (), s32[]{:S(2)}) async-start(), calls=%async_computation.9 | async-start | bytes 2621440 | tf_op jit(solution)/shard_map/all_gather | solution.py:1667
  25.5 267.0 %all-gather.8.cloned.1.call-start = ((), (), s32[]{:S(2)}) async-start(), calls=%async_computation.4 | async-start | bytes 3276800 | tf_op jit(solution)/shard_map/all_gather | solution.py:1666
  26.2 394.9 %all-gather.12.cloned.1.call-start = ((), (), s32[]{:S(2)}) async-start(), calls=%async_computation.10 | async-start | bytes 3932160 | tf_op jit(solution)/shard_map/all_gather | solution.py:1722
  138.7 89.9 %collective-permute-start = (bf16[1536,768]{1,0:T(8,128)(2,1)}, bf16[1536,768]{1,0:T(8,128)(2,1)S(1)}, u32[]{:S(2)}, u32[]{:S(2)}) collective-permute-start(bf16[1536,768]{1,0:T(8,128)(2,1)} %get-tuple-element.84.rest_2_), channel_id=1, source_target_pairs={{0,8},{8,16},{16,24},{1,9},{9,17},{17,25},{2,10},{10,18},{18,26},{... | collective-permute-start | bytes 7077896 | tf_op jit(solution)/shard_map/ppermute | solution.py:1588
  143.0 90.1 %collective-permute-start.1 = (bf16[1536,768]{1,0:T(8,128)(2,1)}, bf16[1536,768]{1,0:T(8,128)(2,1)}, u32[]{:S(2)}, u32[]{:S(2)}) collective-permute-start(bf16[1536,768]{1,0:T(8,128)(2,1)} %get-tuple-element.84.rest_2_), channel_id=1, source_target_pairs={{8,0},{16,8},{24,16},{9,1},{17,9},{25,17},{10,2},{18,10},{26,18},{... | collective-permute-start | bytes 7077896 | tf_op jit(solution)/shard_map/ppermute | solution.py:1588
  145.3 890.8 %reduce-scatter.7.cloned.1.call-start = ((), (), s32[]{:S(2)}) async-start(), calls=%async_computation.6 | async-start | bytes 2621440 | tf_op jit(solution)/shard_map/reduce_scatter | solution.py:1787
  147.6 7.2 copy-start.11
  228.5 104.9 %copy-start.19 = (bf16[1536,768]{1,0:T(8,128)(2,1)}, bf16[1536,768]{1,0:T(8,128)(2,1)S(1)}, u32[]{:S(2)}) copy-start(bf16[1536,768]{1,0:T(8,128)(2,1)S(1)} %collective-permute-done.rest_3_) | copy-start | bytes 7077892
  228.5 225.1 %collective-permute-start.2 = (bf16[1536,768]{1,0:T(8,128)(2,1)S(1)}, bf16[1536,768]{1,0:T(8,128)(2,1)}, u32[]{:S(2)}, u32[]{:S(2)}) collective-permute-start(bf16[1536,768]{1,0:T(8,128)(2,1)S(1)} %collective-permute-done.rest_3_), channel_id=1, source_target_pairs={{8,16},{16,24},{9,17},{17,25},{10,18},{18,26},{11,19},{19,27},{12,... | collective-permute-start | bytes 7077896 | tf_op jit(solution)/shard_map/ppermute | solution.py:1588
  233.1 221.3 %collective-permute-start.3 = (bf16[1536,768]{1,0:T(8,128)(2,1)}, bf16[1536,768]{1,0:T(8,128)(2,1)}, u32[]{:S(2)}, u32[]{:S(2)}) collective-permute-start(bf16[1536,768]{1,0:T(8,128)(2,1)} %collective-permute-done.1.rest_4_), channel_id=1, source_target_pairs={{8,0},{16,8},{9,1},{17,9},{10,2},{18,10},{11,3},{19,11},{12,4},{20... | collective-permute-start | bytes 7077896 | tf_op jit(solution)/shard_map/ppermute | solution.py:1588
  453.6 62.0 %collective-permute-start.4 = (bf16[1536,768]{1,0:T(8,128)(2,1)}, bf16[1536,768]{1,0:T(8,128)(2,1)S(1)}, u32[]{:S(2)}, u32[]{:S(2)}) collective-permute-start(bf16[1536,768]{1,0:T(8,128)(2,1)} %collective-permute-done.2.rest_5_), channel_id=1, source_target_pairs={{16,24},{17,25},{18,26},{19,27},{20,28},{21,29},{22,30},{23,31}} | collective-permute-start | bytes 7077896 | tf_op jit(solution)/shard_map/ppermute | solution.py:1588
  454.4 61.1 %collective-permute-start.5 = (bf16[1536,768]{1,0:T(8,128)(2,1)}, bf16[1536,768]{1,0:T(8,128)(2,1)}, u32[]{:S(2)}, u32[]{:S(2)}) collective-permute-start(bf16[1536,768]{1,0:T(8,128)(2,1)} %collective-permute-done.3.rest_6_), channel_id=1, source_target_pairs={{8,0},{9,1},{10,2},{11,3},{12,4},{13,5},{14,6},{15,7}} | collective-permute-start | bytes 7077896 | tf_op jit(solution)/shard_map/ppermute | solution.py:1588
  515.6 1.5 copy-start.20
  622.5 41.7 %copy-start.2 = (bf16[2048,512]{1,0:T(8,128)(2,1)S(1)}, bf16[2048,512]{1,0:T(8,128)(2,1)}, u32[]{:S(2)}) copy-start(bf16[2048,512]{1,0:T(8,128)(2,1)} %get-tuple-element.72.attn_ref) | copy-start | bytes 6291460
  741.5 296.8 %reduce-scatter.5.cloned.1.call-start = ((), (), s32[]{:S(2)}) async-start(), calls=%async_computation.5 | async-start | bytes 3276800 | tf_op jit(solution)/shard_map/reduce_scatter | solution.py:1786
  752.8 298.1 %reduce-scatter.11.cloned.1.call-start = ((), (), s32[]{:S(2)}) async-start(), calls=%async_computation.8 | async-start | bytes 3932160 | tf_op jit(solution)/shard_map/reduce_scatter | solution.py:1744
  753.6 377.4 %reduce-scatter.9.cloned.1.call-start = ((), (), s32[]{:S(2)}) async-start(), calls=%async_computation.7 | async-start | bytes 7864320 | tf_op jit(solution)/shard_map/reduce_scatter | solution.py:1750
  757.5 52.3 %collective-permute-start.6 = (bf16[768,768]{1,0:T(8,128)(2,1)}, bf16[768,768]{1,0:T(8,128)(2,1)}, u32[]{:S(2)}, u32[]{:S(2)}) collective-permute-start(bf16[768,768]{1,0:T(8,128)(2,1)} %get-tuple-element.136), channel_id=1, source_target_pairs={{0,8},{1,9},{2,10},{3,11},{4,12},{5,13},{6,14},{7,15}} | collective-permute-start | bytes 3538952 | tf_op jit(solution)/shard_map/ppermute | solution.py:1609
  758.8 51.0 %collective-permute-start.7 = (bf16[768,768]{1,0:T(8,128)(2,1)}, bf16[768,768]{1,0:T(8,128)(2,1)}, u32[]{:S(2)}, u32[]{:S(2)}) collective-permute-start(bf16[768,768]{1,0:T(8,128)(2,1)} %get-tuple-element.135), channel_id=1, source_target_pairs={{24,16},{25,17},{26,18},{27,19},{28,20},{29,21},{30,22},{31,23}} | collective-permute-start | bytes 3538952 | tf_op jit(solution)/shard_map/ppermute | solution.py:1609
  762.3 89.9 %collective-permute-start.10 = (bf16[768,768]{1,0:T(8,128)(2,1)S(1)}, bf16[768,768]{1,0:T(8,128)(2,1)}, u32[]{:S(2)}, u32[]{:S(2)}) collective-permute-start(bf16[768,768]{1,0:T(8,128)(2,1)S(1)} %get-tuple-element.134), channel_id=1, source_target_pairs={{0,8},{1,9},{2,10},{3,11},{4,12},{5,13},{6,14},{7,15}} | collective-permute-start | bytes 3538952 | tf_op jit(solution)/shard_map/ppermute | solution.py:1609
  763.6 88.6 %collective-permute-start.11 = (bf16[768,768]{1,0:T(8,128)(2,1)S(1)}, bf16[768,768]{1,0:T(8,128)(2,1)}, u32[]{:S(2)}, u32[]{:S(2)}) collective-permute-start(bf16[768,768]{1,0:T(8,128)(2,1)S(1)} %get-tuple-element.133), channel_id=1, source_target_pairs={{24,16},{25,17},{26,18},{27,19},{28,20},{29,21},{30,22},{31,23}} | collective-permute-start | bytes 3538952 | tf_op jit(solution)/shard_map/ppermute | solution.py:1609
  814.1 88.4 %collective-permute-start.8 = (bf16[768,768]{1,0:T(8,128)(2,1)}, bf16[768,768]{1,0:T(8,128)(2,1)}, u32[]{:S(2)}, u32[]{:S(2)}) collective-permute-start(bf16[768,768]{1,0:T(8,128)(2,1)} %get-tuple-element.132), channel_id=1, source_target_pairs={{0,8},{8,16},{1,9},{9,17},{2,10},{10,18},{3,11},{11,19},{4,12},{12... | collective-permute-start | bytes 3538952 | tf_op jit(solution)/shard_map/ppermute | solution.py:1609
  818.5 84.0 %collective-permute-start.9 = (bf16[768,768]{1,0:T(8,128)(2,1)}, bf16[768,768]{1,0:T(8,128)(2,1)}, u32[]{:S(2)}, u32[]{:S(2)}) collective-permute-start(bf16[768,768]{1,0:T(8,128)(2,1)} %get-tuple-element.131), channel_id=1, source_target_pairs={{16,8},{24,16},{17,9},{25,17},{18,10},{26,18},{19,11},{27,19},{20,... | collective-permute-start | bytes 3538952 | tf_op jit(solution)/shard_map/ppermute | solution.py:1609
  856.5 84.7 %collective-permute-start.14 = (bf16[768,768]{1,0:T(8,128)(2,1)}, bf16[768,768]{1,0:T(8,128)(2,1)}, u32[]{:S(2)}, u32[]{:S(2)}) collective-permute-start(bf16[768,768]{1,0:T(8,128)(2,1)} %get-tuple-element.130), channel_id=1, source_target_pairs={{0,8},{8,16},{1,9},{9,17},{2,10},{10,18},{3,11},{11,19},{4,12},{12... | collective-permute-start | bytes 3538952 | tf_op jit(solution)/shard_map/ppermute | solution.py:1609
  861.0 80.2 %collective-permute-start.15 = (bf16[768,768]{1,0:T(8,128)(2,1)}, bf16[768,768]{1,0:T(8,128)(2,1)}, u32[]{:S(2)}, u32[]{:S(2)}) collective-permute-start(bf16[768,768]{1,0:T(8,128)(2,1)} %get-tuple-element.129), channel_id=1, source_target_pairs={{16,8},{24,16},{17,9},{25,17},{18,10},{26,18},{19,11},{27,19},{20,... | collective-permute-start | bytes 3538952 | tf_op jit(solution)/shard_map/ppermute | solution.py:1609
  906.8 144.0 %collective-permute-start.12 = (bf16[768,768]{1,0:T(8,128)(2,1)}, bf16[768,768]{1,0:T(8,128)(2,1)S(1)}, u32[]{:S(2)}, u32[]{:S(2)}) collective-permute-start(bf16[768,768]{1,0:T(8,128)(2,1)} %get-tuple-element.128), channel_id=1, source_target_pairs={{0,8},{8,16},{16,24},{1,9},{9,17},{17,25},{2,10},{10,18},{18,26},{... | collective-permute-start | bytes 3538952 | tf_op jit(solution)/shard_map/ppermute | solution.py:1609
  911.3 139.6 %collective-permute-start.13 = (bf16[768,768]{1,0:T(8,128)(2,1)}, bf16[768,768]{1,0:T(8,128)(2,1)S(1)}, u32[]{:S(2)}, u32[]{:S(2)}) collective-permute-start(bf16[768,768]{1,0:T(8,128)(2,1)} %get-tuple-element.127), channel_id=1, source_target_pairs={{8,0},{16,8},{24,16},{9,1},{17,9},{25,17},{10,2},{18,10},{26,18},{... | collective-permute-start | bytes 3538952 | tf_op jit(solution)/shard_map/ppermute | solution.py:1609
  945.5 105.3 %collective-permute-start.16 = (bf16[768,768]{1,0:T(8,128)(2,1)}, bf16[768,768]{1,0:T(8,128)(2,1)}, u32[]{:S(2)}, u32[]{:S(2)}) collective-permute-start(bf16[768,768]{1,0:T(8,128)(2,1)} %get-tuple-element.126), channel_id=1, source_target_pairs={{0,8},{8,16},{16,24},{1,9},{9,17},{17,25},{2,10},{10,18},{18,26},{... | collective-permute-start | bytes 3538952 | tf_op jit(solution)/shard_map/ppermute | solution.py:1609
  950.0 100.9 %collective-permute-start.17 = (bf16[768,768]{1,0:T(8,128)(2,1)}, bf16[768,768]{1,0:T(8,128)(2,1)}, u32[]{:S(2)}, u32[]{:S(2)}) collective-permute-start(bf16[768,768]{1,0:T(8,128)(2,1)} %get-tuple-element.125), channel_id=1, source_target_pairs={{8,0},{16,8},{24,16},{9,1},{17,9},{25,17},{10,2},{18,10},{26,18},{... | collective-permute-start | bytes 3538952 | tf_op jit(solution)/shard_map/ppermute | solution.py:1609
  1050.8 89.5 %copy-start.6 = (bf16[256,2048]{1,0:T(8,128)(2,1)S(1)}, bf16[256,2048]{1,0:T(8,128)(2,1)}, u32[]{:S(2)}) copy-start(bf16[256,2048]{1,0:T(8,128)(2,1)} %get-tuple-element.97) | copy-start | bytes 3145732
  1050.8 80.2 %copy-start.4 = (bf16[768,768]{1,0:T(8,128)(2,1)}, bf16[768,768]{1,0:T(8,128)(2,1)S(1)}, u32[]{:S(2)}) copy-start(bf16[768,768]{1,0:T(8,128)(2,1)S(1)} %collective-permute-done.12.up0_ref) | copy-start | bytes 3538948
  1050.9 80.1 %copy-start.5 = (bf16[768,768]{1,0:T(8,128)(2,1)}, bf16[768,768]{1,0:T(8,128)(2,1)S(1)}, u32[]{:S(2)}) copy-start(bf16[768,768]{1,0:T(8,128)(2,1)S(1)} %collective-permute-done.13.down0_ref) | copy-start | bytes 3538948
  1140.3 2.0 copy-start.3
  1142.3 1.9 copy-start.7
  1142.3 2.9 copy-start.9
  1142.3 3.6 copy-start.8
  1142.3 4.2 copy-start.1
Sparse Core Ops, SparseCore 0:
  24.9 113.7 all-gather.13
  140.2 78.2 all-gather.9
  220.1 72.3 all-gather.7
  293.9 79.0 all-gather.11
  741.6 63.1 reduce-scatter.6
  807.5 92.4 reduce-scatter.4
  902.9 109.7 reduce-scatter.10
  1014.9 116.0 reduce-scatter.8

commit v12 on v11

--- a/solution.py
+++ b/solution.py
@@ -928,25 +928,68 @@
     )
 
 
-def share_kernel(n, low_ref, all_ref, *sems):
+def share_kernel(
+    n, low_ref, act_ref, deep_ref, prob_ref, moe_ref, all_ref, out_ref, act, deep, moe, lsem, osem, *sems
+):
+    loads = [
+        pltpu.make_async_copy(src, dst, lsem.at[k])
+        for k, (src, dst) in enumerate(((act_ref, act), (deep_ref, deep), (moe_ref, moe)))
+    ]
     plane = Plane(n)
     plane.meet()
     gather = gather_of(plane, low_ref, all_ref, *sems)
     gather.start()
+    for load in loads:
+        load.start()
+    rows = low_ref.shape[0]
+    parts, cut = deep.shape[:2]
+    stores = [
+        pltpu.make_async_copy(moe.at[pl.ds(k * rows, rows), :], out_ref.at[pl.ds(k * rows, rows), :], osem.at[k])
+        for k in range(n)
+    ]
+
+    def product(k):
+        here = slice(k * rows, (k + 1) * rows)
+        for z in range(parts):
+            cols = slice(z * cut, (z + 1) * cut)
+            out = dot(act[here, :], deep[z], NT).astype(BF16).astype(F32) * prob_ref[here, :]
+            moe[here, cols] = (moe[here, cols].astype(F32) + out).astype(BF16)
+        stores[k].start()
+
+    for load in loads:
+        load.wait()
+    for k in range(n // 2):
+        product(k)
     gather.forward()
+    for k in range(n // 2, n):
+        product(k)
     gather.finish()
-
-
-def share_rows(n, low):
+    for store in stores:
+        store.wait()
+
+
+def share_rows(n, low, act, deep, prob, moe):
+    shape = jax.ShapeDtypeStruct
     return comm_call(
         functools.partial(share_kernel, n),
         10,
-        jax.ShapeDtypeStruct((n,) + low.shape, BF16),
-        ANY,
-        [VM],
-        gather_sems(n),
+        [shape((n,) + low.shape, BF16), shape(moe.shape, BF16)],
+        [ANY, ANY],
+        [VM, ANY, ANY, VM, ANY],
+        [
+            pltpu.VMEM(act.shape, BF16),
+            pltpu.VMEM(deep.shape, BF16),
+            pltpu.VMEM(moe.shape, BF16),
+            DMA((3,)),
+            DMA((n,)),
+        ]
+        + gather_sems(n),
         45,
         low,
+        act,
+        deep,
+        prob,
+        moe,
     )
 
 
@@ -1397,14 +1440,19 @@
 def expert_kernel(chained, low, aliased, split, plan, z_ref, n2_ref, top_ref, prob_ref, *rest):
     if aliased:
         rest = rest[1:]
-    if chained:
+    if chained and split:
+        row_in, rest = rest[0], rest[1:]
+    elif chained:
         moe_in, row_in = rest[:2]
         rest = rest[2:]
     sources, rest = rest[: len(plan)], rest[len(plan) :]
     moe_ref, row_ref, rest = rest[0], rest[1], rest[2:]
     if split:
-        gg_ref, ug_ref, rest = rest[0], rest[1], rest[2:]
+        act_ref = moe_ref
+        gg_ref, ug_ref, deep_ref, rest = *rest[:3], rest[3:]
     grads_ref, wg_ref, wu_ref, wd_ref, rest = *rest[:4], rest[4:]
+    if split:
+        deep_sem, rest = rest[-1], rest[:-1]
     sums, (stage, wsem, sem) = rest[:-3], rest[-3:]
     ad_ref = sums[-1]
     step = pl.program_id(0)
@@ -1443,6 +1491,8 @@
             for owner in range(parts):
                 block = weights[index].at[owner]
                 pltpu.make_async_copy(block, block, wsem.at[index, owner]).wait()
+        if split:
+            pltpu.make_async_copy(wd_ref, deep_ref, deep_sem).start()
 
     n2 = n2_ref[...]
     prob = prob_ref[...]
@@ -1456,10 +1506,11 @@
     act_grad = jnp.zeros((rows, hidden), F32)
     for z in range(parts):
         cols = slice(z * cut, (z + 1) * cut)
-        out = dot(act, wd_ref[z], NT).astype(BF16).astype(F32) * prob
-        if chained:
-            out = out + moe_in[:, cols].astype(F32)
-        moe_ref[:, cols] = out.astype(BF16)
+        if not split:
+            out = dot(act, wd_ref[z], NT).astype(BF16).astype(F32) * prob
+            if chained:
+                out = out + moe_in[:, cols].astype(F32)
+            moe_ref[:, cols] = out.astype(BF16)
         route = (top_ref[:, cols].astype(F32) * prob).astype(BF16)
         act_grad += dot(route, wd_ref[z])
         ad_ref[z] += dot(route, act, TN)
@@ -1470,6 +1521,7 @@
         row = row + row_in[...].astype(F32)
     row_ref[...] = row.astype(BF16)
     if split:
+        act_ref[...] = act
         gg_ref[...] = gate_grad
         ug_ref[...] = up_grad
     else:
@@ -1497,6 +1549,8 @@
             copies[-1].start()
         copies[-2].wait()
         copies[-1].wait()
+        if split:
+            pltpu.make_async_copy(wd_ref, deep_ref, deep_sem).wait()
 
 
 def expert(z, n2, top, prob, n_dp, sources, before, rows, low, full, grads, split):
@@ -1517,17 +1571,19 @@
         + [ANY] * len(grads)
         + [blk] * len(before)
         + [ANY] * len(sources),
-        out_specs=[blk, blk] + [thin] * (2 * split) + [ANY],
+        out_specs=[thin if split else blk, blk] + ([thin, thin, ANY] if split else []) + [ANY],
         out_shape=[
-            shape((length, width), BF16),
+            shape((length, hidden if split else width), BF16),
             shape((length, width), BF16),
         ]
         + [shape((length, hidden), BF16)] * (2 * split)
+        + [shape((n_dp, cut, hidden), BF16)] * split
         + [shape((n_dp, cut if split else 3 * cut, full), BF16)],
         input_output_aliases={4: 2} if grads else {},
         scratch_shapes=[weight] * 3
         + [total] * (1 if split else 3)
-        + [pltpu.VMEM((2, cut, hidden), BF16), DMA((3, n_dp)), DMA((2,))],
+        + [pltpu.VMEM((2, cut, hidden), BF16), DMA((3, n_dp)), DMA((2,))]
+        + [DMA(())] * split,
         compiler_params=pltpu.CompilerParams(vmem_limit_bytes=VMEM_LIMIT),
         cost_estimate=pl.CostEstimate(
             flops=18 * length * width * hidden,
@@ -1737,10 +1793,11 @@
         for tag, rows in spans.items():
             got[tag], before = reduce_hop(grads, got[tag], n_dp, hop - 1, rows, before)
     split = n_ctx == 8
-    (moe, rows_grad), grads1 = run(1, sources1, carried, 0, (), split)
+    earlier = carried[1:] if split else carried
+    (moe, rows_grad), grads1 = run(1, sources1, earlier, 0, (), split)
     rows_grad = rows_grad.reshape(blocks)
     if split:
-        gate_grad, up_grad, down_grad = grads1
+        gate_grad, up_grad, deep, down_grad = grads1
         done_d = lax.psum_scatter(
             down_grad.reshape(width, hidden), "dp", scatter_dimension=0, tiled=True
         )
@@ -1750,7 +1807,7 @@
         done_gu = lax.psum_scatter(
             pair_grad.reshape(2 * width, hidden), "dp", scatter_dimension=0, tiled=True
         )
-        branch = share_rows(n_ctx, low_mid)
+        branch, moe = share_rows(n_ctx, low_mid, moe, deep, my_probs[:, 1:2], carried[0])
     else:
         done = lax.psum_scatter(
             grads1[0].reshape(3 * width, hidden), "dp", scatter_dimension=0, tiled=True

time: 1160 us -> 1160 us (level)
  no operation moved by 1% of the time
where the time goes in v12:
time: 1160 us; the launch traced here: 1150 us
  Pallas kernels  620 us (53%)
  waiting for transfers between devices  386 us (33%)
  starting transfers between devices  50.8 us (4%)
  other arithmetic  28.4 us (2%)
  local copies, waits for them, and re-layouts  28 us (2%)
  matrix products  20.4 us (2%)
  between operations  15.3 us (1%)
    pallas_call x8, Pallas kernels, comm_call(): pl.pallas_call(kernel, out_shape=outs, in_specs=in_specs, out_specs=out_s...  362 us
    ppermute x6, waiting for transfers between devices, reduce_hop(): lax.ppermute(blocks[0], 'dp', up)  146 us
    pallas_call x3, Pallas kernels, expert(): pl.pallas_call(functools.partial(expert_kernel, len(before) > 0, low, len...  140 us
    reduce_scatter x1, waiting for transfers between devices, per_device(): lax.psum_scatter(pair_grad.reshape(2 * width, hidden), 'dp', scatter_dime...  78.8 us
    ppermute x3, waiting for transfers between devices, line_hop(): lax.ppermute(block_up, 'dp', up)  70.2 us
    pallas_call x1, Pallas kernels, attn_backward(): pl.pallas_call(functools.partial(attn_backward_kernel, n, n_dp, heads, MO...  68.2 us
    all_gather x1, waiting for transfers between devices, per_device(): lax.all_gather(cols.reshape(n_ctx * depth, qw + HD), 'dp', axis=0, tiled=...  57.2 us
    pallas_call x1, Pallas kernels, attn_forward(): pl.pallas_call(functools.partial(attn_forward_kernel, n, n_dp, heads, MOS...  41 us
  transfers between devices with their start and end apart: 26, of which 8 were waited for; matrix products, arithmetic and copies ran while one was open for 5% of the time, Pallas kernels for 34%

profile of v12, /device:TPU:14, one launch (start us, length us, event | category | flops | bytes accessed | tf_op | source)
XLA Modules:
  0.0 1148.5 jit_solution(9958567262190660875)
XLA Ops:
  10.9 13.8 %shard_map.255 = (bf16[8,64,640]{2,1,0:T(8,128)(2,1)}, f32[4,8,8,128]{3,2,1,0:T(8,128)}, bf16[1536,256]{1,0:T(8,128)(2,1)}, bf16[1536,512]{1,0:T(8,128)(2,1)}) custom-call(bf16[8,64,640]{2,1,0:T(8,128)(2,1)} %maximum_bitcast_fusion.cols_ref, f32[8,128]{1,0:T(8,128)} %fusion.19.small_ref, bf16[2,512,768]{2,1,0:T(8,128)(2,1)} %rest_0_.3, ...), custom_call_target="tpu_custom_call" | custom-call | bytes 24000000 | tf_op jit(solution)/shard_map/pallas_call | solution.py:448
  27.9 80.1 %shard_map.256 = (bf16[8,256,2048]{2,1,0:T(8,128)(2,1)}, f32[8,24,256]{2,1,0:T(8,128)}, bf16[8,256,2048]{2,1,0:T(8,128)(2,1)}, bf16[1536,768]{1,0:T(8,128)(2,1)}) custom-call(bf16[256,2048]{1,0:T(8,128)(2,1)} %bitcast.102, f32[1,2048]{1,0:T(1,128)} %reshape.188.gain_ref, f32[24,256]{1,0:T(8,128)} %maximum_maximum_fusion.info_ref, ...), custom_call_target="tpu_custom_call" | custom-call | bytes 270000000 | tf_op jit(solution)/shard_map/pallas_call | solution.py:448
  108.1 30.6 %all-gather.14.cloned.1.call-done = bf16[6144,512]{1,0:T(8,128)(2,1)} async-done(((bf16[1536,512]{1,0:T(8,128)(2,1)}), bf16[6144,512]{1,0:T(8,128)(2,1)}) %all-gather.14.cloned.1.call-update) | async-done | bytes 6291472 | tf_op jit(solution)/shard_map/all_gather | solution.py:1778
  138.7 4.4 collective-permute-start
  143.1 2.3 collective-permute-start.1
  150.8 3.9 fusion.10
  154.8 1.9 pad_maximum_fusion
  156.7 1.7 fusion.21
  158.3 70.2 %collective-permute-done.rest_2_ = bf16[1536,768]{1,0:T(8,128)(2,1)S(1)} collective-permute-done((bf16[1536,768]{1,0:T(8,128)(2,1)}, bf16[1536,768]{1,0:T(8,128)(2,1)S(1)}, u32[]{:S(2)}, u32[]{:S(2)}) %collective-permute-start) | collective-permute-done | bytes 2359328 | tf_op jit(solution)/shard_map/ppermute | solution.py:1644
  228.5 4.6 collective-permute-start.2
  233.1 2.1 collective-permute-start.3
  235.3 57.2 %all-gather.8.cloned.1.call-done.wqkv_ref = bf16[2048,640]{1,0:T(8,128)(2,1)} async-done(((bf16[512,640]{1,0:T(8,128)(2,1)}), bf16[2048,640]{1,0:T(8,128)(2,1)}) %all-gather.8.cloned.1.call-update) | async-done | bytes 2621456 | tf_op jit(solution)/shard_map/all_gather | solution.py:1722
  292.5 41.0 %attn_forward.1 = (f32[2048,512]{1,0:T(8,128)}, f32[2048,128]{1,0:T(8,128)}, bf16[2048,512]{1,0:T(8,128)(2,1)}, bf16[2048,128]{1,0:T(8,128)(2,1)}, bf16[2048,128...) custom-call(bf16[2048,2048]{1,0:T(8,128)(2,1)} %bitcast.134, ...), custom_call_target="tpu_custom_call" | custom-call | flops 35000000512 | bytes 31457280 | tf_op jit(solution)/shard_map/attn_forward/pallas_call | solution.py:1181
  333.5 87.7 %shard_map.257 = (f32[256,2048]{1,0:T(8,128)}, bf16[8,256,2048]{2,1,0:T(8,128)(2,1)}) custom-call(bf16[2048,512]{1,0:T(8,128)(2,1)} %get-tuple-element.75.attn_ref, bf16[512,2048]{1,0:T(8,128)(2,1)} %bitcast.115, bf16[256,2048]{1,0:T(8,128)(2,1)} %bitcast.103, f32[1,2048]{1,0:T(1,128)} %reshape.195.gain_ref), custom_call_target="tpu_custom_call" | custom-call | bytes 315000000 | tf_op jit(solution)/shard_map/pallas_call | solution.py:448
  421.2 32.4 %expert.3 = (bf16[2048,2048]{1,0:T(8,128)(2,1)}, bf16[2048,2048]{1,0:T(8,128)(2,1)}, bf16[4,1536,768]{2,1,0:T(8,128)(2,1)}) custom-call(s32[1]{0:T(128)} %bitcast.z_ref, bf16[2048,2048]{1,0:T(8,128)(2,1)} %bitcast.106, bf16[2048,2048]{1,0:T(8,128)(2,1)} %bitcast.136, f32[2048,1]{1,0:T(8,128)} %get-tuple-element.143.prob_ref, bf16[4,1536,256]{2,1,0:T(8,128)(2,1)} %bitcast.143), custom_call_target="tpu_custom_call" | custom-call | flops 19327352832 | bytes 41943040 | tf_op jit(solution)/shard_map/expert/pallas_call | solution.py:1567
  454.5 5.8 collective-permute-start.5
  460.3 55.4 %expert.4 = (bf16[2048,2048]{1,0:T(8,128)(2,1)}, bf16[2048,2048]{1,0:T(8,128)(2,1)}, bf16[4,1536,768]{2,1,0:T(8,128)(2,1)}) custom-call(s32[1]{0:T(128)} %bitcast.z_ref, bf16[2048,2048]{1,0:T(8,128)(2,1)} %bitcast.107, bf16[2048,2048]{1,0:T(8,128)(2,1)} %bitcast.137, f32[2048,1]{1,0:T(8,128)} %get-tuple-element.143.prob_ref, ...), custom_call_target="tpu_custom_call", output_to_operand_aliasing={{2}: (4, {})} | custom-call | flops 38654705664 | bytes 41943040 | tf_op jit(solution)/shard_map/expert/pallas_call | solution.py:1567
  515.7 1.4 copy-done.20
  517.1 52.2 %expert.5 = (bf16[2048,768]{1,0:T(8,128)(2,1)}, bf16[2048,2048]{1,0:T(8,128)(2,1)}, bf16[2048,768]{1,0:T(8,128)(2,1)}, bf16[2048,768]{1,0:T(8,128)(2,1)}, bf16[4...) custom-call(s32[1]{0:T(128)} %bitcast.z_ref, bf16[2048,2048]{1,0:T(8,128)(2,1)} %bitcast.108, ...), custom_call_target="tpu_custom_call" | custom-call | flops 57982058496 | bytes 41943040 | tf_op jit(solution)/shard_map/expert/pallas_call | solution.py:1567
  569.3 46.1 %shard_map.258 = (f32[256,2048]{1,0:T(8,128)}, f32[8,2048]{1,0:T(8,128)}, bf16[256,2048]{1,0:T(8,128)(2,1)}, bf16[4,1024,768]{2,1,0:T(8,128)(2,1)}) custom-call(bf16[8,256,2048]{2,1,0:T(8,128)(2,1)} %bitcast.110, bf16[2048,2048]{1,0:T(8,128)(2,1)} %bitcast.109, bf16[2048,768]{1,0:T(8,128)(2,1)} %get-tuple-element.88.gg_ref, ...), custom_call_target="tpu_custom_call" | custom-call | bytes 150000000 | tf_op jit(solution)/shard_map/pallas_call | solution.py:448
  615.4 43.9 %shard_map.259 = (bf16[8,256,2048]{2,1,0:T(8,128)(2,1)}, bf16[2048,2048]{1,0:T(8,128)(2,1)}) custom-call(bf16[256,2048]{1,0:T(8,128)(2,1)} %get-tuple-element.91.low_ref, bf16[2048,768]{1,0:T(8,128)(2,1)} %get-tuple-element.92.act_ref, bf16[4,512,768]{2,1,0:T(8,128)(2,1)} %get-tuple-element.93.deep_ref, f32[2048,1]{1,0:T(8,128)} %get-tuple-element.144.prob_ref, ...), custom_call_target="tpu_custom_call" | custom-call | bytes 135000000 | tf_op jit(solution)/shard_map/pallas_call | solution.py:448
  659.3 9.1 convolution_convert_fusion.1
  668.5 68.2 %attn_backward.1 = (bf16[2048,640]{1,0:T(8,128)(2,1)}, f32[8,128]{1,0:T(8,128)}, bf16[4,128,2048]{2,1,0:T(8,128)(2,1)}, bf16[256,2048]{1,0:T(8,128)(2,1)}) custom-call(bf16[2048,2048]{1,0:T(8,128)(2,1)} %bitcast.140, bf16[512,2048]{1,0:T(8,128)(2,1)} %bitcast.116, bf16[2048,512]{1,0:T(8,128)(2,1)} %get-tuple-element.75.attn_ref, ...), custom_call_target="tpu_custom_call" | custom-call | flops 60000002048 | bytes 31457280 | tf_op jit(solution)/shard_map/attn_backward/pallas_call | solution.py:1389
  736.8 11.3 convolution_convert_fusion
  749.6 3.2 dynamic-slice_bitcast_fusion.2
  754.1 1.7 collective-permute-start.7
  755.8 1.8 dynamic-slice_bitcast_fusion
  758.9 1.7 collective-permute-start.11
  760.6 44.5 %collective-permute-done.6 = bf16[768,768]{1,0:T(8,128)(2,1)} collective-permute-done((bf16[768,768]{1,0:T(8,128)(2,1)}, bf16[768,768]{1,0:T(8,128)(2,1)}, u32[]{:S(2)}, u32[]{:S(2)}) %collective-permute-start.6) | collective-permute-done | bytes 1179680 | tf_op jit(solution)/shard_map/ppermute | solution.py:1665
  805.1 4.3 fusion.5
  809.4 4.4 collective-permute-start.8
  815.1 32.4 %collective-permute-done.10 = bf16[768,768]{1,0:T(8,128)(2,1)} collective-permute-done((bf16[768,768]{1,0:T(8,128)(2,1)S(1)}, bf16[768,768]{1,0:T(8,128)(2,1)}, u32[]{:S(2)}, u32[]{:S(2)}) %collective-permute-start.10) | collective-permute-done | bytes 1179680 | tf_op jit(solution)/shard_map/ppermute | solution.py:1665
  847.5 4.3 fusion.3
  851.8 4.5 collective-permute-start.14
  857.6 40.2 %collective-permute-done.8 = bf16[768,768]{1,0:T(8,128)(2,1)} collective-permute-done((bf16[768,768]{1,0:T(8,128)(2,1)}, bf16[768,768]{1,0:T(8,128)(2,1)}, u32[]{:S(2)}, u32[]{:S(2)}) %collective-permute-start.8) | collective-permute-done | bytes 1179680 | tf_op jit(solution)/shard_map/ppermute | solution.py:1665
  897.8 4.3 fusion.2
  902.1 4.4 collective-permute-start.12
  906.5 1.9 collective-permute-start.13
  908.5 28.6 %collective-permute-done.14 = bf16[768,768]{1,0:T(8,128)(2,1)} collective-permute-done((bf16[768,768]{1,0:T(8,128)(2,1)}, bf16[768,768]{1,0:T(8,128)(2,1)}, u32[]{:S(2)}, u32[]{:S(2)}) %collective-permute-start.14) | collective-permute-done | bytes 1179680 | tf_op jit(solution)/shard_map/ppermute | solution.py:1665
  937.1 4.3 fusion
  941.4 4.5 collective-permute-start.16
  945.8 2.4 collective-permute-start.17
  948.2 51.1 %shard_map.260 = (f32[256,2048]{1,0:T(8,128)}, f32[8,2048]{1,0:T(8,128)}) custom-call(bf16[2048,640]{1,0:T(8,128)(2,1)} %get-tuple-element.104.grad_ref, bf16[2048,640]{1,0:T(8,128)(2,1)} %all-gather.8.cloned.1.call-done.wqkv_ref, bf16[256,2048]{1,0:T(8,128)(2,1)} %bitcast.104, f32[256,2048]{1,0:T(8,128)} %get-tuple-element.105.mid_ref, ...), custom_call_target="tpu_custom_call" | custom-call | bytes 180000000 | tf_op jit(solution)/shard_map/pallas_call | solution.py:448
  1003.0 26.3 %shard_map.261 = f32[8,128]{1,0:T(8,128)} custom-call(f32[8,4,8,128]{3,2,1,0:T(8,128)} %copy_bitcast_fusion.3.small_ref), custom_call_target="tpu_custom_call" | custom-call | bytes 30000000 | tf_op jit(solution)/shard_map/pallas_call | solution.py:448
  1032.0 2.1 convert_element_type.140
  1034.2 12.5 %shard_map.262 = (f32[64,4096]{1,0:T(8,128)}, f32[64,512]{1,0:T(8,128)}, f32[64,512]{1,0:T(8,128)}) custom-call(bf16[8,64,640]{2,1,0:T(8,128)(2,1)} %bitcast.121), custom_call_target="tpu_custom_call" | custom-call | bytes 30000000 | tf_op jit(solution)/shard_map/pallas_call | solution.py:448
  1046.8 78.8 %reduce-scatter.9.cloned.1.call-done.pair_ref = bf16[1024,768]{1,0:T(8,128)(2,1)} async-done(((bf16[4096,768]{1,0:T(8,128)(2,1)}), bf16[1024,768]{1,0:T(8,128)(2,1)}) %reduce-scatter.9.cloned.1.call-update) | async-done | bytes 1572880 | tf_op jit(solution)/shard_map/reduce_scatter | solution.py:1807
  1125.6 9.3 unpack.1
  (120 shorter events, 32.4 us)
Async XLA Ops:
  7.2 1.2 copy-start
  7.2 3.1 copy-start.15
  7.2 3.1 copy-start.16
  7.2 3.0 copy-start.17
  7.2 3.0 copy-start.18
  7.2 131.4 %all-gather.14.cloned.1.call-start = ((), (), s32[]{:S(2)}) async-start(), calls=%async_computation.11 | async-start | bytes 7864320 | tf_op jit(solution)/shard_map/all_gather | solution.py:1778
  24.7 1.6 copy-start.10
  24.7 2.4 copy-start.14
  24.7 2.5 copy-start.12
  24.7 2.5 copy-start.13
  24.8 210.5 %all-gather.10.cloned.1.call-start = ((), (), s32[]{:S(2)}) async-start(), calls=%async_computation.9 | async-start | bytes 2621440 | tf_op jit(solution)/shard_map/all_gather | solution.py:1723
  25.5 267.0 %all-gather.8.cloned.1.call-start = ((), (), s32[]{:S(2)}) async-start(), calls=%async_computation.4 | async-start | bytes 3276800 | tf_op jit(solution)/shard_map/all_gather | solution.py:1722
  26.3 395.0 %all-gather.12.cloned.1.call-start = ((), (), s32[]{:S(2)}) async-start(), calls=%async_computation.10 | async-start | bytes 3932160 | tf_op jit(solution)/shard_map/all_gather | solution.py:1778
  138.7 89.9 %collective-permute-start = (bf16[1536,768]{1,0:T(8,128)(2,1)}, bf16[1536,768]{1,0:T(8,128)(2,1)S(1)}, u32[]{:S(2)}, u32[]{:S(2)}) collective-permute-start(bf16[1536,768]{1,0:T(8,128)(2,1)} %get-tuple-element.86.rest_1_), channel_id=1, source_target_pairs={{0,8},{8,16},{16,24},{1,9},{9,17},{17,25},{2,10},{10,18},{18,26},{... | collective-permute-start | bytes 7077896 | tf_op jit(solution)/shard_map/ppermute | solution.py:1644
  143.1 90.1 %collective-permute-start.1 = (bf16[1536,768]{1,0:T(8,128)(2,1)}, bf16[1536,768]{1,0:T(8,128)(2,1)}, u32[]{:S(2)}, u32[]{:S(2)}) collective-permute-start(bf16[1536,768]{1,0:T(8,128)(2,1)} %get-tuple-element.86.rest_1_), channel_id=1, source_target_pairs={{8,0},{16,8},{24,16},{9,1},{17,9},{25,17},{10,2},{18,10},{26,18},{... | collective-permute-start | bytes 7077896 | tf_op jit(solution)/shard_map/ppermute | solution.py:1644
  145.4 886.7 %reduce-scatter.7.cloned.1.call-start = ((), (), s32[]{:S(2)}) async-start(), calls=%async_computation.6 | async-start | bytes 2621440 | tf_op jit(solution)/shard_map/reduce_scatter | solution.py:1844
  147.6 7.2 copy-start.11
  228.5 104.9 %copy-start.19 = (bf16[1536,768]{1,0:T(8,128)(2,1)}, bf16[1536,768]{1,0:T(8,128)(2,1)S(1)}, u32[]{:S(2)}) copy-start(bf16[1536,768]{1,0:T(8,128)(2,1)S(1)} %collective-permute-done.rest_2_) | copy-start | bytes 7077892
  228.5 225.1 %collective-permute-start.2 = (bf16[1536,768]{1,0:T(8,128)(2,1)S(1)}, bf16[1536,768]{1,0:T(8,128)(2,1)}, u32[]{:S(2)}, u32[]{:S(2)}) collective-permute-start(bf16[1536,768]{1,0:T(8,128)(2,1)S(1)} %collective-permute-done.rest_2_), channel_id=1, source_target_pairs={{8,16},{16,24},{9,17},{17,25},{10,18},{18,26},{11,19},{19,27},{12,... | collective-permute-start | bytes 7077896 | tf_op jit(solution)/shard_map/ppermute | solution.py:1644
  233.1 221.4 %collective-permute-start.3 = (bf16[1536,768]{1,0:T(8,128)(2,1)}, bf16[1536,768]{1,0:T(8,128)(2,1)}, u32[]{:S(2)}, u32[]{:S(2)}) collective-permute-start(bf16[1536,768]{1,0:T(8,128)(2,1)} %collective-permute-done.1.rest_3_), channel_id=1, source_target_pairs={{8,0},{16,8},{9,1},{17,9},{10,2},{18,10},{11,3},{19,11},{12,4},{20... | collective-permute-start | bytes 7077896 | tf_op jit(solution)/shard_map/ppermute | solution.py:1644
  453.7 62.0 %collective-permute-start.4 = (bf16[1536,768]{1,0:T(8,128)(2,1)}, bf16[1536,768]{1,0:T(8,128)(2,1)S(1)}, u32[]{:S(2)}, u32[]{:S(2)}) collective-permute-start(bf16[1536,768]{1,0:T(8,128)(2,1)} %collective-permute-done.2.rest_4_), channel_id=1, source_target_pairs={{16,24},{17,25},{18,26},{19,27},{20,28},{21,29},{22,30},{23,31}} | collective-permute-start | bytes 7077896 | tf_op jit(solution)/shard_map/ppermute | solution.py:1644
  454.5 61.2 %collective-permute-start.5 = (bf16[1536,768]{1,0:T(8,128)(2,1)}, bf16[1536,768]{1,0:T(8,128)(2,1)}, u32[]{:S(2)}, u32[]{:S(2)}) collective-permute-start(bf16[1536,768]{1,0:T(8,128)(2,1)} %collective-permute-done.3.rest_5_), channel_id=1, source_target_pairs={{8,0},{9,1},{10,2},{11,3},{12,4},{13,5},{14,6},{15,7}} | collective-permute-start | bytes 7077896 | tf_op jit(solution)/shard_map/ppermute | solution.py:1644
  515.7 1.4 copy-start.20
  615.4 43.9 %copy-start.2 = (bf16[2048,512]{1,0:T(8,128)(2,1)S(1)}, bf16[2048,512]{1,0:T(8,128)(2,1)}, u32[]{:S(2)}) copy-start(bf16[2048,512]{1,0:T(8,128)(2,1)} %get-tuple-element.75.attn_ref) | copy-start | bytes 6291460
  736.7 297.5 %reduce-scatter.5.cloned.1.call-start = ((), (), s32[]{:S(2)}) async-start(), calls=%async_computation.5 | async-start | bytes 3276800 | tf_op jit(solution)/shard_map/reduce_scatter | solution.py:1843
  748.1 298.7 %reduce-scatter.11.cloned.1.call-start = ((), (), s32[]{:S(2)}) async-start(), calls=%async_computation.8 | async-start | bytes 3932160 | tf_op jit(solution)/shard_map/reduce_scatter | solution.py:1801
  748.9 376.8 %reduce-scatter.9.cloned.1.call-start = ((), (), s32[]{:S(2)}) async-start(), calls=%async_computation.7 | async-start | bytes 7864320 | tf_op jit(solution)/shard_map/reduce_scatter | solution.py:1807
  752.8 52.3 %collective-permute-start.6 = (bf16[768,768]{1,0:T(8,128)(2,1)}, bf16[768,768]{1,0:T(8,128)(2,1)}, u32[]{:S(2)}, u32[]{:S(2)}) collective-permute-start(bf16[768,768]{1,0:T(8,128)(2,1)} %get-tuple-element.142), channel_id=1, source_target_pairs={{0,8},{1,9},{2,10},{3,11},{4,12},{5,13},{6,14},{7,15}} | collective-permute-start | bytes 3538952 | tf_op jit(solution)/shard_map/ppermute | solution.py:1665
  754.1 51.0 %collective-permute-start.7 = (bf16[768,768]{1,0:T(8,128)(2,1)}, bf16[768,768]{1,0:T(8,128)(2,1)}, u32[]{:S(2)}, u32[]{:S(2)}) collective-permute-start(bf16[768,768]{1,0:T(8,128)(2,1)} %get-tuple-element.141), channel_id=1, source_target_pairs={{24,16},{25,17},{26,18},{27,19},{28,20},{29,21},{30,22},{31,23}} | collective-permute-start | bytes 3538952 | tf_op jit(solution)/shard_map/ppermute | solution.py:1665
  757.6 89.9 %collective-permute-start.10 = (bf16[768,768]{1,0:T(8,128)(2,1)S(1)}, bf16[768,768]{1,0:T(8,128)(2,1)}, u32[]{:S(2)}, u32[]{:S(2)}) collective-permute-start(bf16[768,768]{1,0:T(8,128)(2,1)S(1)} %get-tuple-element.140), channel_id=1, source_target_pairs={{0,8},{1,9},{2,10},{3,11},{4,12},{5,13},{6,14},{7,15}} | collective-permute-start | bytes 3538952 | tf_op jit(solution)/shard_map/ppermute | solution.py:1665
  758.9 88.7 %collective-permute-start.11 = (bf16[768,768]{1,0:T(8,128)(2,1)S(1)}, bf16[768,768]{1,0:T(8,128)(2,1)}, u32[]{:S(2)}, u32[]{:S(2)}) collective-permute-start(bf16[768,768]{1,0:T(8,128)(2,1)S(1)} %get-tuple-element.139), channel_id=1, source_target_pairs={{24,16},{25,17},{26,18},{27,19},{28,20},{29,21},{30,22},{31,23}} | collective-permute-start | bytes 3538952 | tf_op jit(solution)/shard_map/ppermute | solution.py:1665
  809.4 88.4 %collective-permute-start.8 = (bf16[768,768]{1,0:T(8,128)(2,1)}, bf16[768,768]{1,0:T(8,128)(2,1)}, u32[]{:S(2)}, u32[]{:S(2)}) collective-permute-start(bf16[768,768]{1,0:T(8,128)(2,1)} %get-tuple-element.138), channel_id=1, source_target_pairs={{0,8},{8,16},{1,9},{9,17},{2,10},{10,18},{3,11},{11,19},{4,12},{12... | collective-permute-start | bytes 3538952 | tf_op jit(solution)/shard_map/ppermute | solution.py:1665
  813.8 84.0 %collective-permute-start.9 = (bf16[768,768]{1,0:T(8,128)(2,1)}, bf16[768,768]{1,0:T(8,128)(2,1)}, u32[]{:S(2)}, u32[]{:S(2)}) collective-permute-start(bf16[768,768]{1,0:T(8,128)(2,1)} %get-tuple-element.137), channel_id=1, source_target_pairs={{16,8},{24,16},{17,9},{25,17},{18,10},{26,18},{19,11},{27,19},{20,... | collective-permute-start | bytes 3538952 | tf_op jit(solution)/shard_map/ppermute | solution.py:1665
  851.8 85.2 %collective-permute-start.14 = (bf16[768,768]{1,0:T(8,128)(2,1)}, bf16[768,768]{1,0:T(8,128)(2,1)}, u32[]{:S(2)}, u32[]{:S(2)}) collective-permute-start(bf16[768,768]{1,0:T(8,128)(2,1)} %get-tuple-element.136), channel_id=1, source_target_pairs={{0,8},{8,16},{1,9},{9,17},{2,10},{10,18},{3,11},{11,19},{4,12},{12... | collective-permute-start | bytes 3538952 | tf_op jit(solution)/shard_map/ppermute | solution.py:1665
  856.3 80.7 %collective-permute-start.15 = (bf16[768,768]{1,0:T(8,128)(2,1)}, bf16[768,768]{1,0:T(8,128)(2,1)}, u32[]{:S(2)}, u32[]{:S(2)}) collective-permute-start(bf16[768,768]{1,0:T(8,128)(2,1)} %get-tuple-element.135), channel_id=1, source_target_pairs={{16,8},{24,16},{17,9},{25,17},{18,10},{26,18},{19,11},{27,19},{20,... | collective-permute-start | bytes 3538952 | tf_op jit(solution)/shard_map/ppermute | solution.py:1665
  902.1 144.6 %collective-permute-start.12 = (bf16[768,768]{1,0:T(8,128)(2,1)}, bf16[768,768]{1,0:T(8,128)(2,1)S(1)}, u32[]{:S(2)}, u32[]{:S(2)}) collective-permute-start(bf16[768,768]{1,0:T(8,128)(2,1)} %get-tuple-element.134), channel_id=1, source_target_pairs={{0,8},{8,16},{16,24},{1,9},{9,17},{17,25},{2,10},{10,18},{18,26},{... | collective-permute-start | bytes 3538952 | tf_op jit(solution)/shard_map/ppermute | solution.py:1665
  906.5 140.2 %collective-permute-start.13 = (bf16[768,768]{1,0:T(8,128)(2,1)}, bf16[768,768]{1,0:T(8,128)(2,1)S(1)}, u32[]{:S(2)}, u32[]{:S(2)}) collective-permute-start(bf16[768,768]{1,0:T(8,128)(2,1)} %get-tuple-element.133), channel_id=1, source_target_pairs={{8,0},{16,8},{24,16},{9,1},{17,9},{25,17},{10,2},{18,10},{26,18},{... | collective-permute-start | bytes 3538952 | tf_op jit(solution)/shard_map/ppermute | solution.py:1665
  941.4 105.4 %collective-permute-start.16 = (bf16[768,768]{1,0:T(8,128)(2,1)}, bf16[768,768]{1,0:T(8,128)(2,1)}, u32[]{:S(2)}, u32[]{:S(2)}) collective-permute-start(bf16[768,768]{1,0:T(8,128)(2,1)} %get-tuple-element.132), channel_id=1, source_target_pairs={{0,8},{8,16},{16,24},{1,9},{9,17},{17,25},{2,10},{10,18},{18,26},{... | collective-permute-start | bytes 3538952 | tf_op jit(solution)/shard_map/ppermute | solution.py:1665
  945.8 100.9 %collective-permute-start.17 = (bf16[768,768]{1,0:T(8,128)(2,1)}, bf16[768,768]{1,0:T(8,128)(2,1)}, u32[]{:S(2)}, u32[]{:S(2)}) collective-permute-start(bf16[768,768]{1,0:T(8,128)(2,1)} %get-tuple-element.131), channel_id=1, source_target_pairs={{8,0},{16,8},{24,16},{9,1},{17,9},{25,17},{10,2},{18,10},{26,18},{... | collective-permute-start | bytes 3538952 | tf_op jit(solution)/shard_map/ppermute | solution.py:1665
  1046.7 88.3 %copy-start.6 = (bf16[256,2048]{1,0:T(8,128)(2,1)S(1)}, bf16[256,2048]{1,0:T(8,128)(2,1)}, u32[]{:S(2)}) copy-start(bf16[256,2048]{1,0:T(8,128)(2,1)} %get-tuple-element.103) | copy-start | bytes 3145732
  1046.7 78.9 %copy-start.4 = (bf16[768,768]{1,0:T(8,128)(2,1)}, bf16[768,768]{1,0:T(8,128)(2,1)S(1)}, u32[]{:S(2)}) copy-start(bf16[768,768]{1,0:T(8,128)(2,1)S(1)} %collective-permute-done.12.up0_ref) | copy-start | bytes 3538948
  1046.7 78.9 %copy-start.5 = (bf16[768,768]{1,0:T(8,128)(2,1)}, bf16[768,768]{1,0:T(8,128)(2,1)S(1)}, u32[]{:S(2)}) copy-start(bf16[768,768]{1,0:T(8,128)(2,1)S(1)} %collective-permute-done.13.down0_ref) | copy-start | bytes 3538948
  1134.9 2.0 copy-start.3
  1136.9 1.9 copy-start.7
  1136.9 2.9 copy-start.9
  1136.9 3.6 copy-start.8
  1136.9 4.2 copy-start.1
Sparse Core Ops, SparseCore 0:
  24.9 113.7 all-gather.13
  140.3 78.2 all-gather.9
  220.1 72.3 all-gather.7
  293.9 79.0 all-gather.11
  736.8 63.1 reduce-scatter.6
  802.7 92.4 reduce-scatter.4
  897.5 109.7 reduce-scatter.10
  1009.6 116.0 reduce-scatter.8
